TPU v7x, 32 devices: a whole 2x2x4 slice. The times are simulated.
32 devices in a mesh: fs: 4 (over z), sp: 8 (over y, x, core).
Axes of the slice: x: 2, y: 2, z: 4, core: 2. Of those that a mesh axis runs over, the one named last changes fastest.
Arguments:
- layer_input: bfloat16 [8, 2048, 1024], P(None, ('fs', 'sp')), may hold values from -6 to 6
- first_gain: bfloat16 [1024], P('fs'), may hold values from 0.099609375 to 1.8984375
- first_shift: bfloat16 [1024], P('fs'), may hold values from -1.1953125 to 1.1953125
- joined_weight: bfloat16 [1024, 3072], P('fs'), may hold values from -0.1875 to 0.1875
- query_bias: bfloat16 [1024], P('fs'), may hold values from -1.1953125 to 1.1953125
- value_bias: bfloat16 [1024], P('fs'), may hold values from -1.1953125 to 1.1953125
- output_weight: bfloat16 [1024, 1024], P('fs'), may hold values from -0.5 to 0.5
- output_bias: bfloat16 [1024], P('fs'), may hold values from -1.1953125 to 1.1953125
- second_gain: bfloat16 [1024], P('fs'), may hold values from 0.099609375 to 1.8984375
- second_shift: bfloat16 [1024], P('fs'), may hold values from -1.1953125 to 1.1953125
- expand_weight: bfloat16 [1024, 4096], P('fs'), may hold values from -0.1875 to 0.1875
- expand_bias: bfloat16 [4096], P('fs'), may hold values from -1.1953125 to 1.1953125
- contract_weight: bfloat16 [4096, 1024], P('fs'), may hold values from -0.09375 to 0.09375
- contract_bias: bfloat16 [1024], P('fs'), may hold values from -1.1953125 to 1.1953125
- alibi_slopes: float32 [16], replicated, may hold values from 2.4414063e-05 to 0.04
- upstream: bfloat16 [8, 2048, 1024], P(None, ('fs', 'sp')), may hold values from -6 to 6
Outputs:
- layer_output: bfloat16 [8, 2048, 1024], P(None, ('fs', 'sp'))
- input_grad: bfloat16 [8, 2048, 1024], P(None, ('fs', 'sp'))
- first_gain_grad: float32 [1024], P(('fs', 'sp'))
- first_shift_grad: float32 [1024], P(('fs', 'sp'))
- joined_grad: float32 [1024, 3072], P(('fs', 'sp'))
- query_bias_grad: float32 [1024], P(('fs', 'sp'))
- value_bias_grad: float32 [1024], P(('fs', 'sp'))
- output_weight_grad: float32 [1024, 1024], P(('fs', 'sp'))
- output_bias_grad: float32 [1024], P(('fs', 'sp'))
- second_gain_grad: float32 [1024], P(('fs', 'sp'))
- second_shift_grad: float32 [1024], P(('fs', 'sp'))
- expand_grad: float32 [1024, 4096], P(('fs', 'sp'))
- expand_bias_grad: float32 [4096], P(('fs', 'sp'))
- contract_grad: float32 [4096, 1024], P(('fs', 'sp'))
- contract_bias_grad: float32 [1024], P(('fs', 'sp'))
All inputs are finite; a program needn't handle non-finite values.
Results may differ from a plain program's by a relative error of at most 0.014.
Values may be sent and summed in bfloat16 or wider, within the bound.
A program may use at most 256 MiB of HBM per device.

v0:
```python
import math

import jax
import jax.numpy as jnp
from jax import lax
from jax.sharding import PartitionSpec as P

norm_eps = 1e-05
gelu_coef = 0.7978845608028654
masked_value = -1e30


def normalize(values, norm_gain, norm_shift):
    center = values - jnp.mean(values, axis=-1, keepdims=True)
    variance = jnp.mean(center * center, axis=-1, keepdims=True)
    return center * lax.rsqrt(variance + norm_eps) * norm_gain + norm_shift


def gelu_tanh(values):
    return (
        0.5 * values * (1.0 + jnp.tanh(gelu_coef * (values + 0.044715 * values * values * values)))
    )


def matmul(left_side, right_side):
    return jnp.dot(left_side, right_side, preferred_element_type=jnp.float32)


def matmul_lt(left_side, right_side):
    return lax.dot_general(
        left_side, right_side, (((0,), (0,)), ((), ())), preferred_element_type=jnp.float32
    )


def matmul_rt(left_side, right_side):
    return lax.dot_general(
        left_side, right_side, (((1,), (1,)), ((), ())), preferred_element_type=jnp.float32
    )


def joined_bias_of(query_bias, value_bias, head_count):
    query_part = query_bias.astype(jnp.float32).reshape(head_count, -1)
    value_part = value_bias.astype(jnp.float32).reshape(head_count, -1)
    return jnp.stack([query_part, jnp.zeros_like(query_part), value_part], axis=1).reshape(-1)


def score_block(queries, key_rows, key_start, query_pos, slopes_here, score_scale):
    raw_scores = (
        jnp.einsum("qhd,khd->hqk", queries, key_rows, preferred_element_type=jnp.float32)
        * score_scale
    )
    key_pos = key_start + jnp.arange(key_rows.shape[0], dtype=jnp.int32)
    distance = (key_pos[None, :] - query_pos[:, None]).astype(jnp.float32)
    biased = raw_scores + slopes_here[:, None, None] * distance[None]
    return jnp.where((key_pos[None, :] <= query_pos[:, None])[None], biased, masked_value)


def per_device(
    layer_input,
    first_gain,
    first_shift,
    joined_weight,
    query_bias,
    value_bias,
    output_weight,
    output_bias,
    second_gain,
    second_shift,
    expand_weight,
    expand_bias,
    contract_weight,
    contract_bias,
    alibi_slopes,
    upstream,
):
    seq_count, piece_len, features = layer_input.shape
    sp_count = lax.axis_size("sp")
    fs_index = lax.axis_index("fs")
    sp_index = lax.axis_index("sp")
    head_count = alibi_slopes.shape[0]
    head_dim = features // head_count
    local_heads = head_count // sp_count
    local_span = piece_len * sp_count
    row_count = seq_count * piece_len
    score_scale = 1.0 / math.sqrt(head_dim)
    slopes_here = lax.dynamic_slice_in_dim(alibi_slopes, sp_index * local_heads, local_heads)
    query_pos = fs_index * local_span + jnp.arange(local_span, dtype=jnp.int32)
    block_count = fs_index + 1
    gain_one, shift_one, joined_full, qbias_full, vbias_full, out_full, obias_full = (
        lax.all_gather(first_gain, "fs", axis=0, tiled=True),
        lax.all_gather(first_shift, "fs", axis=0, tiled=True),
        lax.all_gather(joined_weight, "fs", axis=0, tiled=True),
        lax.all_gather(query_bias, "fs", axis=0, tiled=True),
        lax.all_gather(value_bias, "fs", axis=0, tiled=True),
        lax.all_gather(output_weight, "fs", axis=0, tiled=True),
        lax.all_gather(output_bias, "fs", axis=0, tiled=True),
    )
    tokens = layer_input.reshape(row_count, features).astype(jnp.float32)
    normed_f, norm_back_one = jax.vjp(
        normalize, tokens, gain_one.astype(jnp.float32), shift_one.astype(jnp.float32)
    )
    normed = normed_f.astype(jnp.bfloat16)
    joined_all = (
        matmul(normed, joined_full) + joined_bias_of(qbias_full, vbias_full, head_count)
    ).astype(jnp.bfloat16)
    packed = joined_all.reshape(seq_count, piece_len, sp_count, local_heads * 3 * head_dim)
    regrouped = lax.all_to_all(packed, "sp", split_axis=2, concat_axis=1, tiled=True)
    regrouped = regrouped.reshape(seq_count, local_span, local_heads, 3, head_dim)
    queries = regrouped[:, :, :, 0]
    key_rows = regrouped[:, :, :, 1]
    value_rows = regrouped[:, :, :, 2]
    keys_all, values_all = (
        lax.all_gather(key_rows, "fs", axis=1, tiled=True),
        lax.all_gather(value_rows, "fs", axis=1, tiled=True),
    )

    def forward_one(operands):
        seq_queries, seq_keys, seq_values = operands

        def stats_step(step_index, loop_state):
            running, row_total = loop_state
            key_start = step_index * local_span
            key_part = lax.dynamic_slice_in_dim(seq_keys, key_start, local_span, 0)
            scores = score_block(
                seq_queries, key_part, key_start, query_pos, slopes_here, score_scale
            )
            newest = jnp.maximum(running, jnp.max(scores, axis=-1))
            row_total = row_total * jnp.exp(running - newest) + jnp.sum(
                jnp.exp(scores - newest[..., None]), axis=-1
            )
            return (newest, row_total)

        initial = (
            jnp.full((local_heads, local_span), masked_value, jnp.float32),
            jnp.zeros((local_heads, local_span), jnp.float32),
        )
        running, row_total = lax.fori_loop(0, block_count, stats_step, initial)
        row_lse = running + jnp.log(row_total)

        def value_step(step_index, loop_state):
            accumulated, correction = loop_state
            key_start = step_index * local_span
            key_part = lax.dynamic_slice_in_dim(seq_keys, key_start, local_span, 0)
            value_part = lax.dynamic_slice_in_dim(seq_values, key_start, local_span, 0)
            scores = score_block(
                seq_queries, key_part, key_start, query_pos, slopes_here, score_scale
            )
            probs = jnp.exp(scores - row_lse[..., None])
            probs_low = probs.astype(jnp.bfloat16)
            remainder = (probs - probs_low.astype(jnp.float32)).astype(jnp.bfloat16)
            accumulated = accumulated + jnp.einsum(
                "hqk,khd->qhd", probs_low, value_part, preferred_element_type=jnp.float32
            )
            correction = correction + jnp.einsum(
                "hqk,khd->qhd", remainder, value_part, preferred_element_type=jnp.float32
            )
            return (accumulated, correction)

        zero_out = jnp.zeros((local_span, local_heads, head_dim), jnp.float32)
        accumulated, correction = lax.fori_loop(0, block_count, value_step, (zero_out, zero_out))
        return (accumulated.astype(jnp.bfloat16), row_lse, accumulated + correction)

    attended_heads, lse_all, exact_out = lax.map(forward_one, (queries, keys_all, values_all))
    heads_back = attended_heads.reshape(seq_count, local_span, 1, local_heads * head_dim)
    attended = lax.all_to_all(heads_back, "sp", split_axis=1, concat_axis=2, tiled=True).reshape(
        row_count, features
    )
    residual = tokens + (matmul(attended, out_full) + obias_full.astype(jnp.float32))
    gain_two, shift_two, expand_full, ebias_full, contract_full, cbias_full = (
        lax.all_gather(second_gain, "fs", axis=0, tiled=True),
        lax.all_gather(second_shift, "fs", axis=0, tiled=True),
        lax.all_gather(expand_weight, "fs", axis=0, tiled=True),
        lax.all_gather(expand_bias, "fs", axis=0, tiled=True),
        lax.all_gather(contract_weight, "fs", axis=0, tiled=True),
        lax.all_gather(contract_bias, "fs", axis=0, tiled=True),
    )
    second_f, norm_back_two = jax.vjp(
        normalize, residual, gain_two.astype(jnp.float32), shift_two.astype(jnp.float32)
    )
    second = second_f.astype(jnp.bfloat16)
    expanded = matmul(second, expand_full) + ebias_full.astype(jnp.float32)
    activated_f, gelu_back = jax.vjp(gelu_tanh, expanded)
    activated = activated_f.astype(jnp.bfloat16)
    result = residual + (matmul(activated, contract_full) + cbias_full.astype(jnp.float32))
    layer_output = result.astype(jnp.bfloat16).reshape(seq_count, piece_len, features)
    expand_full, contract_full = (
        lax.all_gather(expand_weight, "fs", axis=0, tiled=True),
        lax.all_gather(contract_weight, "fs", axis=0, tiled=True),
    )
    upstream_low = upstream.reshape(row_count, features)
    upstream_f = upstream_low.astype(jnp.float32)
    contract_grad = matmul_lt(activated, upstream_low)
    contract_bias_grad = jnp.sum(upstream_f, axis=0)
    act_grad = matmul_rt(upstream_low, contract_full)
    expand_diff = gelu_back(act_grad)[0].astype(jnp.bfloat16)
    expand_grad = matmul_lt(second, expand_diff)
    expand_bias_grad = jnp.sum(expand_diff.astype(jnp.float32), axis=0)
    second_back = matmul_rt(expand_diff, expand_full)
    resid_part, second_gain_grad, second_shift_grad = norm_back_two(second_back)
    residual_grad = upstream_f + resid_part
    mlp_grads = (
        lax.psum_scatter(second_gain_grad, ("fs", "sp"), scatter_dimension=0, tiled=True),
        lax.psum_scatter(second_shift_grad, ("fs", "sp"), scatter_dimension=0, tiled=True),
        lax.psum_scatter(expand_grad, ("fs", "sp"), scatter_dimension=0, tiled=True),
        lax.psum_scatter(expand_bias_grad, ("fs", "sp"), scatter_dimension=0, tiled=True),
        lax.psum_scatter(contract_grad, ("fs", "sp"), scatter_dimension=0, tiled=True),
        lax.psum_scatter(contract_bias_grad, ("fs", "sp"), scatter_dimension=0, tiled=True),
    )
    joined_full, out_full = (
        lax.all_gather(joined_weight, "fs", axis=0, tiled=True),
        lax.all_gather(output_weight, "fs", axis=0, tiled=True),
    )
    branch_diff = residual_grad.astype(jnp.bfloat16)
    output_weight_grad = matmul_lt(attended, branch_diff)
    output_bias_grad = jnp.sum(branch_diff.astype(jnp.float32), axis=0)
    attended_diff = matmul_rt(branch_diff, out_full).astype(jnp.bfloat16)
    diff_packed = attended_diff.reshape(seq_count, piece_len, sp_count, local_heads * head_dim)
    diff_heads = lax.all_to_all(diff_packed, "sp", split_axis=2, concat_axis=1, tiled=True)
    diff_heads = diff_heads.reshape(seq_count, local_span, local_heads, head_dim)
    delta_all = jnp.sum(diff_heads.astype(jnp.float32) * exact_out, axis=-1).transpose(0, 2, 1)

    def backward_one(operands):
        seq_queries, seq_keys, seq_values, seq_diff, seq_lse, row_delta = operands
        key_count = seq_keys.shape[0]

        def grad_step(step_index, loop_state):
            query_acc, key_terms = loop_state
            key_start = step_index * local_span
            key_part = lax.dynamic_slice_in_dim(seq_keys, key_start, local_span, 0)
            value_part = lax.dynamic_slice_in_dim(seq_values, key_start, local_span, 0)
            scores = score_block(
                seq_queries, key_part, key_start, query_pos, slopes_here, score_scale
            )
            probs = jnp.exp(scores - seq_lse[..., None])
            probs_low = probs.astype(jnp.bfloat16)
            prob_diff = jnp.einsum(
                "qhd,khd->hqk", seq_diff, value_part, preferred_element_type=jnp.float32
            )
            score_diff = (probs * (prob_diff - row_delta[..., None])).astype(jnp.bfloat16)
            query_acc = (
                query_acc
                + jnp.einsum(
                    "hqk,khd->qhd", score_diff, key_part, preferred_element_type=jnp.float32
                )
                * score_scale
            )
            key_diff = (
                jnp.einsum(
                    "hqk,qhd->khd", score_diff, seq_queries, preferred_element_type=jnp.float32
                )
                * score_scale
            )
            value_diff = jnp.einsum(
                "hqk,qhd->khd", probs_low, seq_diff, preferred_element_type=jnp.float32
            )
            key_terms = lax.dynamic_update_slice_in_dim(
                key_terms, jnp.stack([key_diff, value_diff], axis=2), key_start, 0
            )
            return (query_acc, key_terms)

        initial = (
            jnp.zeros((local_span, local_heads, head_dim), jnp.float32),
            jnp.zeros((key_count, local_heads, 2, head_dim), jnp.float32),
        )
        query_acc, key_terms = lax.fori_loop(0, block_count, grad_step, initial)
        return (
            query_acc.astype(jnp.bfloat16),
            key_terms.reshape(key_count, local_heads * 2 * head_dim),
        )

    query_diff, kv_terms = lax.map(
        backward_one, (queries, keys_all, values_all, diff_heads, lse_all, delta_all)
    )
    kv_diff = lax.psum_scatter(kv_terms.astype(jnp.bfloat16), "fs", scatter_dimension=1, tiled=True)
    kv_diff = kv_diff.reshape(seq_count, local_span, local_heads, 2, head_dim)
    joined_heads = jnp.concatenate([query_diff[:, :, :, None], kv_diff], axis=3)
    joined_heads = joined_heads.reshape(seq_count, local_span, 1, local_heads * 3 * head_dim)
    joined_diff = lax.all_to_all(
        joined_heads, "sp", split_axis=1, concat_axis=2, tiled=True
    ).reshape(row_count, 3 * features)
    joined_grad = matmul_lt(normed, joined_diff)
    column_sums = jnp.sum(joined_diff.astype(jnp.float32), axis=0).reshape(head_count, 3, head_dim)
    query_bias_grad = column_sums[:, 0].reshape(features)
    value_bias_grad = column_sums[:, 2].reshape(features)
    normed_back = matmul_rt(joined_diff, joined_full)
    input_part, first_gain_grad, first_shift_grad = norm_back_one(normed_back)
    input_grad = (
        (residual_grad + input_part).astype(jnp.bfloat16).reshape(seq_count, piece_len, features)
    )
    attn_grads = (
        lax.psum_scatter(first_gain_grad, ("fs", "sp"), scatter_dimension=0, tiled=True),
        lax.psum_scatter(first_shift_grad, ("fs", "sp"), scatter_dimension=0, tiled=True),
        lax.psum_scatter(joined_grad, ("fs", "sp"), scatter_dimension=0, tiled=True),
        lax.psum_scatter(query_bias_grad, ("fs", "sp"), scatter_dimension=0, tiled=True),
        lax.psum_scatter(value_bias_grad, ("fs", "sp"), scatter_dimension=0, tiled=True),
        lax.psum_scatter(output_weight_grad, ("fs", "sp"), scatter_dimension=0, tiled=True),
        lax.psum_scatter(output_bias_grad, ("fs", "sp"), scatter_dimension=0, tiled=True),
    )
    return (
        layer_output,
        input_grad,
        attn_grads[0],
        attn_grads[1],
        attn_grads[2],
        attn_grads[3],
        attn_grads[4],
        attn_grads[5],
        attn_grads[6],
        mlp_grads[0],
        mlp_grads[1],
        mlp_grads[2],
        mlp_grads[3],
        mlp_grads[4],
        mlp_grads[5],
    )


def solution(mesh):
    placed = (
        P(None, ("fs", "sp"), None),
        P("fs"),
        P("fs"),
        P("fs", None),
        P("fs"),
        P("fs"),
        P("fs", None),
        P("fs"),
        P("fs"),
        P("fs"),
        P("fs", None),
        P("fs"),
        P("fs", None),
        P("fs"),
        P(),
        P(None, ("fs", "sp"), None),
    )
    return jax.shard_map(
        per_device,
        mesh=mesh,
        in_specs=placed,
        out_specs=(
            P(None, ("fs", "sp"), None),
            P(None, ("fs", "sp"), None),
            P(("fs", "sp")),
            P(("fs", "sp")),
            P(("fs", "sp"), None),
            P(("fs", "sp")),
            P(("fs", "sp")),
            P(("fs", "sp"), None),
            P(("fs", "sp")),
            P(("fs", "sp")),
            P(("fs", "sp")),
            P(("fs", "sp"), None),
            P(("fs", "sp")),
            P(("fs", "sp"), None),
            P(("fs", "sp")),
        ),
        check_vma=False,
    )
```

profile of v0, /device:TPU:0, one launch (start us, length us, event | category | flops | bytes accessed | tf_op | source)
XLA Modules:
  0.0 1705.8 jit_solution(3027556152063594820)
XLA Ops:
  10.6 12.6 all-gather.3
  31.3 13.7 all-gather.4
  56.2 71.6 %all-gather.17.cloned.1.call-done = bf16[1024,3072]{1,0:T(8,128)(2,1)} async-done(((bf16[256,3072]{1,0:T(8,128)(2,1)}), bf16[1024,3072]{1,0:T(8,128)(2,1)}) %all-gather.17.cloned.1.call-update) | async-done | bytes 6291472 | tf_op jit(solution)/shard_map/all_gather | solution.py:92
  135.6 41.3 %all_to_all.60 = bf16[8,64,8,384]{3,1,0,2:T(8,128)(2,1)S(1)} all-to-all(bf16[8,64,8,384]{3,1,0,2:T(8,128)(2,1)S(1)} %copy.70), channel_id=1, replica_groups=mesh['fs'=4,'sp'=8] {'sp'}, dimensions={2} | all-to-all | bytes 6291456 | tf_op jit(solution)/shard_map/all_to_all | solution.py:107
  194.6 74.6 %all-gather.27.cloned.1.call-done = bf16[8,2048,2,1,64]{1,4,3,2,0:T(8,128)(2,1)} async-done(((bf16[8,512,2,1,64]{1,4,3,2,0:T(8,128)(2,1)}), bf16[8,2048,2,1,64]{1,4,3,2,0:T(8,128)(2,1)}) %all-gather.27.cloned.1.call-update) | async-done | bytes 4194320 | tf_op jit(solution)/shard_map/all_gather | solution.py:114
  269.2 80.8 %all-gather.25.cloned.1.call-done = bf16[8,2048,2,1,64]{1,4,3,2,0:T(8,128)(2,1)} async-done(((bf16[8,512,2,1,64]{1,4,3,2,0:T(8,128)(2,1)}), bf16[8,2048,2,1,64]{1,4,3,2,0:T(8,128)(2,1)}) %all-gather.25.cloned.1.call-update) | async-done | bytes 4194320 | tf_op jit(solution)/shard_map/all_gather | solution.py:113
  350.1 52.9 %while.69 = (s32[]{:T(128)}, bf16[8,512,2,64]{1,3,2,0:T(8,128)(2,1)S(1)}, f32[8,2,512]{2,1,0:T(2,128)S(1)}, f32[8,512,2,64]{1,3,2,0:T(8,128)}, bf16[8,2048,2,64]...) while((s32[]{:T(128)}, ...), condition=%wide.region_9.10_spmd.clone, body=%wide.region_2.9_spmd.clone.sunk | while | flops 279187968 | bytes 21733188 | solution.py:163
  408.2 94.2 %all-gather.8 = bf16[4,1,256]{2,1,0:T(2,128)(2,1)S(1)} all-gather(bf16[1,1,256]{2,1,0:T(2,128)(2,1)S(1)} %reshape.390), channel_id=1, replica_groups=mesh['fs'=4,'sp'=8] {'fs'}, dimensions={0}, use_global_device_ids=true | all-gather | bytes 2560 | tf_op jit(solution)/shard_map/all_gather | solution.py:171
  502.5 11.3 all-gather.7
  513.8 11.4 all-gather.6
  525.1 14.0 all_gather.61
  556.2 138.9 %all-gather.23.cloned.1.call-done = bf16[4096,1024]{1,0:T(8,128)(2,1)} async-done(((bf16[1024,1024]{1,0:T(8,128)(2,1)}), bf16[4096,1024]{1,0:T(8,128)(2,1)}) %all-gather.23.cloned.1.call-update) | async-done | bytes 8388624 | tf_op jit(solution)/shard_map/all_gather | solution.py:174
  695.1 15.6 convert_reduce_fusion
  726.1 15.3 all-to-all-done.2
  746.9 58.6 %while.71 = (s32[]{:T(128)}, bf16[8,512,2,64]{1,3,2,0:T(8,128)(2,1)}, bf16[8,2048,256]{1,2,0:T(8,128)(2,1)}, bf16[8,2048,2,64]{1,3,2,0:T(8,128)(2,1)}, bf16[8,20...) while((s32[]{:T(128)}, ...), condition=%wide.region_18.19_spmd.clone, body=%wide.region_15.18_spmd.clone.sunk | while | flops 341509120 | bytes 29135980 | solution.py:271
  811.6 15.5 fusion.67
  839.1 179.8 %reduce-scatter.6.cloned.1.call-done = bf16[8,512,256]{1,2,0:T(8,128)(2,1)} async-done(((bf16[8,2048,256]{1,2,0:T(8,128)(2,1)}), bf16[8,512,256]{1,2,0:T(8,128)(2,1)}) %reduce-scatter.6.cloned.1.call-update) | async-done | bytes 2097168 | tf_op jit(solution)/shard_map/reduce_scatter | solution.py:274
  1029.8 55.5 %all-to-all-done.3 = bf16[8,512,1,384]{3,0,2,1:T(8,128)(2,1)} async-done(((bf16[8,512,1,384]{3,0,2,1:T(8,128)(2,1)}), bf16[8,512,1,384]{3,0,2,1:T(8,128)(2,1)}, u32[]{:S(2)}, u32[]{:S(2)}) %all-to-all-start.3) | async-done | bytes 3145760 | tf_op jit(solution)/shard_map/all_to_all | solution.py:278
  1099.2 14.0 all-gather.9
  1113.4 13.0 add_convert_fusion.2
  1136.5 40.9 %all-reduce.9 = (f32[1024]{0:T(1024)S(1)}, f32[1024]{0:T(1024)S(1)}, f32[1024]{0:T(1024)S(1)}, f32[1024]{0:T(1024)S(1)}, f32[1024]{0:T(1024)S(1)}, /*index=5*/f3...) all-reduce(f32[1024]{0:T(1024)S(1)} %get-tuple-element.357, ...), channel_id=5, replica_groups=mesh['fs'=4,'sp'=8] {'fs','sp'}, use_global_device_ids=true, to_apply=%region_23.24.clone | all-reduce | flops 12288 | bytes 98304
  1185.9 162.4 %reduce-scatter.14.cloned.1.call-done = f32[128,1024]{1,0:T(8,128)} async-done(((f32[4096,1024]{1,0:T(8,128)}), f32[128,1024]{1,0:T(8,128)}) %reduce-scatter.14.cloned.1.call-update) | async-done | bytes 524304 | tf_op jit(solution)/shard_map/reduce_scatter | solution.py:206
  1348.3 187.4 %reduce-scatter.12.cloned.1.call-done = f32[32,4096]{1,0:T(8,128)} async-done(((f32[1024,4096]{1,0:T(8,128)}), f32[32,4096]{1,0:T(8,128)}) %reduce-scatter.12.cloned.1.call-update) | async-done | bytes 524304 | tf_op jit(solution)/shard_map/reduce_scatter | solution.py:204
  1535.7 163.2 %reduce-scatter.8.cloned.1.call-done = f32[32,3072]{1,0:T(8,128)} async-done(((f32[1024,3072]{1,0:T(8,128)}), f32[32,3072]{1,0:T(8,128)}) %reduce-scatter.8.cloned.1.call-update) | async-done | bytes 393232 | tf_op jit(solution)/shard_map/reduce_scatter | solution.py:293
  (599 shorter events, 313.4 us)
Async XLA Ops:
  7.2 46.5 %copy-start = (bf16[8,64,1024]{2,1,0:T(8,128)(2,1)S(1)}, bf16[8,64,1024]{2,1,0:T(8,128)(2,1)}, u32[]{:S(2)}) copy-start(bf16[8,64,1024]{2,1,0:T(8,128)(2,1)} %param.26) | copy-start | bytes 3145732
  7.2 120.7 %all-gather.17.cloned.1.call-start = ((), (), s32[]{:S(2)}) async-start(), calls=%async_computation.9 | async-start | bytes 7864320 | tf_op jit(solution)/shard_map/all_gather | solution.py:92
  7.9 261.3 %all-gather.27.cloned.1.call-start = ((), (), s32[]{:S(2)}) async-start(), calls=%async_computation.19 | async-start | bytes 5242880 | tf_op jit(solution)/shard_map/all_gather | solution.py:114
  23.3 33.0 %copy-start.23 = (f32[4,1,256]{2,1,0:T(1,128)}, f32[4,1,256]{2,1,0:T(1,128)S(1)}, u32[]{:S(2)}) copy-start(f32[4,1,256]{2,1,0:T(1,128)S(1)} %convert_element_type.160) | copy-start | bytes 12292
  53.9 80.3 %copy-start.25 = (f32[512]{0:T(512)}, f32[512]{0:T(512)S(1)}, u32[]{:S(2)}) copy-start(f32[512]{0:T(512)S(1)} %div.39) | copy-start | bytes 6148
  55.0 79.2 %copy-start.27 = (f32[512]{0:T(512)}, f32[512]{0:T(512)S(1)}, u32[]{:S(2)}) copy-start(f32[512]{0:T(512)S(1)} %rsqrt.23) | copy-start | bytes 6148
  192.0 158.1 %all-gather.25.cloned.1.call-start = ((), (), s32[]{:S(2)}) async-start(), calls=%async_computation.18 | async-start | bytes 5242880 | tf_op jit(solution)/shard_map/all_gather | solution.py:113
  192.7 348.3 %all-gather.19.cloned.1.call-start = ((), (), s32[]{:S(2)}) async-start(), calls=%async_computation.10 | async-start | bytes 2621440 | tf_op jit(solution)/shard_map/all_gather | solution.py:95
  193.3 352.5 %all-gather.21.cloned.1.call-start = ((), (), s32[]{:S(2)}) async-start(), calls=%async_computation.11 | async-start | bytes 10485760 | tf_op jit(solution)/shard_map/all_gather | solution.py:172
  193.9 501.2 %all-gather.23.cloned.1.call-start = ((), (), s32[]{:S(2)}) async-start(), calls=%async_computation.12 | async-start | bytes 10485760 | tf_op jit(solution)/shard_map/all_gather | solution.py:174
  403.1 122.1 %copy-start.40 = (bf16[1024]{0:T(1024)(128)(2,1)S(1)}, bf16[1024]{0:T(1024)(128)(2,1)}, u32[]{:S(2)}) copy-start(bf16[1024]{0:T(1024)(128)(2,1)} %param.37) | copy-start | bytes 6148
  404.5 134.6 %all-to-all-start.1 = ((bf16[8,512,1,128]{3,0,2,1:T(8,128)(2,1)}), bf16[8,512,1,128]{3,0,2,1:T(8,128)(2,1)S(1)}, u32[]{:S(2)}, u32[]{:S(2)}) async-start(bf16[8,512,1,128]{3,0,2,1:T(8,128)(2,1)} %copy.72), calls=%async_computation.1 | async-start | bytes 2097152 | tf_op jit(solution)/shard_map/all_to_all | solution.py:165
  502.5 43.3 %copy-start.38 = (f32[4,1,256]{2,1,0:T(1,128)}, f32[4,1,256]{2,1,0:T(1,128)S(1)}, u32[]{:S(2)}) copy-start(f32[4,1,256]{2,1,0:T(1,128)S(1)} %convert_element_type.163) | copy-start | bytes 12292
  544.2 172.0 %copy-start.11 = (f32[512,1024]{1,0:T(8,128)}, f32[512,1024]{1,0:T(8,128)S(1)}, u32[]{:S(2)}) copy-start(f32[512,1024]{1,0:T(8,128)S(1)} %get-tuple-element.501) | copy-start | bytes 6291460
  545.8 149.3 %copy-start.7 = (bf16[8,64,1024]{2,1,0:T(8,128)(2,1)S(1)}, bf16[8,64,1024]{2,1,0:T(8,128)(2,1)}, u32[]{:S(2)}) copy-start(bf16[8,64,1024]{2,1,0:T(8,128)(2,1)} %param.41) | copy-start | bytes 3145732
  722.4 19.0 %all-to-all-start.2 = ((bf16[8,64,8,128]{3,1,0,2:T(8,128)(2,1)}), bf16[8,64,8,128]{3,1,0,2:T(8,128)(2,1)S(1)}, u32[]{:S(2)}, u32[]{:S(2)}) async-start(bf16[8,64,8,128]{3,1,0,2:T(8,128)(2,1)} %copy.75), calls=%async_computation.2 | async-start | bytes 2097152 | tf_op jit(solution)/shard_map/all_to_all | solution.py:218
  726.0 292.9 %reduce-scatter.6.cloned.1.call-start = ((), (), s32[]{:S(2)}) async-start(), calls=%async_computation.13 | async-start | bytes 10485760 | tf_op jit(solution)/shard_map/reduce_scatter | solution.py:274
  805.5 380.4 %reduce-scatter.10.cloned.1.call-start = ((), (), s32[]{:S(2)}) async-start(), calls=%async_computation.15 | async-start | bytes 4325376 | tf_op jit(solution)/shard_map/reduce_scatter | solution.py:296
  810.4 537.9 %reduce-scatter.14.cloned.1.call-start = ((), (), s32[]{:S(2)}) async-start(), calls=%async_computation.17 | async-start | bytes 17301504 | tf_op jit(solution)/shard_map/reduce_scatter | solution.py:206
  827.1 708.6 %reduce-scatter.12.cloned.1.call-start = ((), (), s32[]{:S(2)}) async-start(), calls=%async_computation.16 | async-start | bytes 17301504 | tf_op jit(solution)/shard_map/reduce_scatter | solution.py:204
  1024.6 60.7 %all-to-all-start.3 = ((bf16[8,512,1,384]{3,0,2,1:T(8,128)(2,1)}), bf16[8,512,1,384]{3,0,2,1:T(8,128)(2,1)}, u32[]{:S(2)}, u32[]{:S(2)}) async-start(bf16[8,512,1,384]{3,0,2,1:T(8,128)(2,1)} %copy.77), calls=%async_computation.4 | async-start | bytes 6291456 | tf_op jit(solution)/shard_map/all_to_all | solution.py:278
  1029.2 669.6 %reduce-scatter.8.cloned.1.call-start = ((), (), s32[]{:S(2)}) async-start(), calls=%async_computation.14 | async-start | bytes 12976128 | tf_op jit(solution)/shard_map/reduce_scatter | solution.py:293
  1134.1 48.5 %copy-start.6 = (f32[512,1024]{1,0:T(8,128)S(1)}, f32[512,1024]{1,0:T(8,128)}, u32[]{:S(2)}) copy-start(f32[512,1024]{1,0:T(8,128)} %copy-done.5) | copy-start | bytes 6291460
  1134.1 48.5 %copy-start.30 = (f32[512]{0:T(512)S(1)}, f32[512]{0:T(512)}, u32[]{:S(2)}) copy-start(f32[512]{0:T(512)} %copy-done.29) | copy-start | bytes 6148
  (53 other events, 186.5 us)
Sparse Core Ops, SparseCore 0:
  9.6 118.2 all-gather.16
  192.1 77.0 all-gather.26
  270.8 79.2 all-gather.24
  351.4 44.2 all-gather.18
  397.1 148.6 all-gather.20
  547.2 147.7 all-gather.22
  805.6 213.2 reduce-scatter.5
  1021.8 144.5 reduce-scatter.9
  1169.3 178.9 reduce-scatter.13
  1351.0 184.6 reduce-scatter.11
  1542.3 156.5 reduce-scatter.7
where the time goes:
time: 1710 us
  waiting for transfers between devices  1130 us (66%)
  blocking collectives  270 us (16%)
  matrix products  137 us (8%)
  local copies, waits for them, and re-layouts  98.4 us (6%)
  other arithmetic  36.6 us (2%)
    reduce_scatter x1, waiting for transfers between devices, per_device(): lax.psum_scatter(expand_grad, ('fs', 'sp'), scatter_dimension=0, tiled=True)  187 us
    reduce_scatter x1, waiting for transfers between devices, per_device(): lax.psum_scatter(kv_terms.astype(jnp.bfloat16), 'fs', scatter_dimension=1...  180 us
    reduce_scatter x1, waiting for transfers between devices, per_device(): lax.psum_scatter(joined_grad, ('fs', 'sp'), scatter_dimension=0, tiled=True)  163 us
    reduce_scatter x1, waiting for transfers between devices, per_device(): lax.psum_scatter(contract_grad, ('fs', 'sp'), scatter_dimension=0, tiled=...  162 us
    all_gather x1, waiting for transfers between devices, per_device(): lax.all_gather(contract_weight, 'fs', axis=0, tiled=True)  139 us
    all_gather x1, blocking collectives, per_device(): lax.all_gather(second_shift, 'fs', axis=0, tiled=True)  94.2 us
    all_gather x1, waiting for transfers between devices, per_device(): lax.all_gather(key_rows, 'fs', axis=1, tiled=True)  80.8 us
    all_gather x1, waiting for transfers between devices, per_device(): lax.all_gather(value_rows, 'fs', axis=1, tiled=True)  74.6 us
  transfers between devices with their start and end apart: 14, of which 11 were waited for; matrix products, arithmetic and copies ran while one was open for 9% of the time, Pallas kernels for 0%

commit v1 on v0

v1 whole, which is shorter than its diff:
```python
import functools
import math

import jax
import jax.numpy as jnp
from jax import lax
from jax.experimental import pallas as pl
from jax.experimental.pallas import tpu as pltpu
from jax.sharding import PartitionSpec as P

norm_eps = 1e-05
gelu_coef = 0.7978845608028654
masked_value = -1e30
f32 = jnp.float32
bf16 = jnp.bfloat16
MESH = pl.DeviceIdType.MESH
HBM = pl.BlockSpec(memory_space=pl.ANY)
VMEM = pl.BlockSpec(memory_space=pltpu.VMEM)
vmem_bytes = 60 * 1024 * 1024


def normalize(values, norm_gain, norm_shift):
    center = values - jnp.mean(values, axis=-1, keepdims=True)
    variance = jnp.mean(center * center, axis=-1, keepdims=True)
    return center * lax.rsqrt(variance + norm_eps) * norm_gain + norm_shift


def gelu_tanh(values):
    return (
        0.5 * values * (1.0 + jnp.tanh(gelu_coef * (values + 0.044715 * values * values * values)))
    )


def matmul(left_side, right_side):
    return jnp.dot(left_side, right_side, preferred_element_type=f32)


def matmul_lt(left_side, right_side):
    return lax.dot_general(
        left_side, right_side, (((0,), (0,)), ((), ())), preferred_element_type=f32
    )


def matmul_rt(left_side, right_side):
    return lax.dot_general(
        left_side, right_side, (((1,), (1,)), ((), ())), preferred_element_type=f32
    )


def joined_bias_of(query_bias, value_bias, head_count):
    query_part = query_bias.astype(f32).reshape(head_count, -1)
    value_part = value_bias.astype(f32).reshape(head_count, -1)
    return jnp.stack([query_part, jnp.zeros_like(query_part), value_part], axis=1).reshape(-1)


def split_three(values):
    high = values.astype(bf16).astype(f32)
    rest = values - high
    middle = rest.astype(bf16).astype(f32)
    return high, middle, rest - middle


def key_columns(key_rows, slope, start):
    rows, width = key_rows.shape
    position = (start + lax.broadcasted_iota(jnp.int32, (rows, width), 0)).astype(f32)
    lane = lax.broadcasted_iota(jnp.int32, (rows, width), 1)
    high, middle, low = split_three(slope * position)
    extra = jnp.where(lane == 0, high, jnp.where(lane == 1, middle, jnp.where(lane == 2, low, 0.0)))
    return jnp.concatenate([key_rows.astype(f32), extra], axis=1).astype(bf16)


def query_columns(queries, scale):
    rows, width = queries.shape
    lane = lax.broadcasted_iota(jnp.int32, (rows, width), 1)
    ones = jnp.where(lane < 3, 1.0, 0.0)
    return jnp.concatenate([queries.astype(f32) * scale, ones], axis=1).astype(bf16)


def forward_kernel(heads, width, block, slopes, qkv, out, out_t, lse, keys, queries, values_t):
    seqs, length, _ = qkv.shape
    blocks = length // block
    scale = 1.0 / math.sqrt(width)

    def one_seq(b, _):
        def prepare(i, _):
            start = pl.multiple_of(i * block, block)
            rows = pl.ds(start, block)
            for h in range(heads):
                base = h * 3 * width
                keys[h, rows, :] = key_columns(
                    qkv[b, rows, base + width : base + 2 * width], slopes[h], start
                )
                queries[h, rows, :] = query_columns(qkv[b, rows, base : base + width], scale)
                value = qkv[b, rows, base + 2 * width : base + 3 * width]
                values_t[h, :, rows] = value.astype(f32).T.astype(bf16)
            return 0

        lax.fori_loop(0, blocks, prepare, 0)

        def one_block(i, _):
            rows = pl.ds(pl.multiple_of(i * block, block), block)
            query = [queries[h, rows, :] for h in range(heads)]

            def step(j, state, diagonal):
                columns = pl.ds(pl.multiple_of(j * block, block), block)
                result = []
                for h in range(heads):
                    top, total, acc = state[h]
                    scores = matmul_rt(keys[h, columns, :], query[h])
                    if diagonal:
                        key_at = lax.broadcasted_iota(jnp.int32, (block, block), 0)
                        query_at = lax.broadcasted_iota(jnp.int32, (block, block), 1)
                        scores = jnp.where(key_at <= query_at, scores, masked_value)
                    newest = jnp.maximum(top, jnp.max(scores, axis=0, keepdims=True))
                    shrink = jnp.exp(top - newest)
                    probs = jnp.exp(scores - newest)
                    total = total * shrink + jnp.sum(probs, axis=0, keepdims=True)
                    acc = acc * shrink + matmul(values_t[h, :, columns], probs.astype(bf16))
                    result.append((newest, total, acc))
                return tuple(result)

            state = tuple(
                (
                    jnp.full((1, block), masked_value, f32),
                    jnp.zeros((1, block), f32),
                    jnp.zeros((width, block), f32),
                )
                for h in range(heads)
            )
            state = lax.fori_loop(0, i, lambda j, s: step(j, s, False), state)
            state = step(i, state, True)
            finished = []
            for h in range(heads):
                top, total, acc = state[h]
                result = acc / total
                out_t[b, h, :, rows] = result
                lse[b, h, :, rows] = top + jnp.log(total)
                finished.append(result)
            joined = finished[0] if heads == 1 else jnp.concatenate(finished, axis=0)
            out[b, rows, :] = joined.T.astype(bf16)
            return 0

        lax.fori_loop(0, blocks, one_block, 0)
        return 0

    lax.fori_loop(0, seqs, one_seq, 0)


def attention_forward(qkv, slopes, heads, width):
    seqs, length, _ = qkv.shape
    block = min(512, length)
    return pl.pallas_call(
        functools.partial(forward_kernel, heads, width, block),
        name="attention_forward",
        out_shape=(
            jax.ShapeDtypeStruct((seqs, length, heads * width), bf16),
            jax.ShapeDtypeStruct((seqs, heads, width, length), f32),
            jax.ShapeDtypeStruct((seqs, heads, 1, length), f32),
        ),
        in_specs=[pl.BlockSpec(memory_space=pltpu.SMEM), VMEM],
        out_specs=(VMEM, VMEM, VMEM),
        scratch_shapes=[
            pltpu.VMEM((heads, length, 2 * width), bf16),
            pltpu.VMEM((heads, length, 2 * width), bf16),
            pltpu.VMEM((heads, width, length), bf16),
        ],
        compiler_params=pltpu.CompilerParams(vmem_limit_bytes=vmem_bytes),
    )(slopes, qkv)


def backward_kernel(
    heads, width, block, slopes, qkv, diff, out_t, lse, joined,
    keys, queries, keys_t, values, diffs, delta, query_acc,
):
    seqs, length, _ = qkv.shape
    blocks = length // block
    scale = 1.0 / math.sqrt(width)

    def one_seq(b, _):
        def prepare(i, _):
            start = pl.multiple_of(i * block, block)
            rows = pl.ds(start, block)
            for h in range(heads):
                base = h * 3 * width
                key = qkv[b, rows, base + width : base + 2 * width]
                keys[h, rows, :] = key_columns(key, slopes[h], start)
                keys_t[h, :, rows] = key.astype(f32).T.astype(bf16)
                queries[h, rows, :] = query_columns(qkv[b, rows, base : base + width], scale)
                values[h, rows, :] = qkv[b, rows, base + 2 * width : base + 3 * width]
                part = diff[b, rows, h * width : (h + 1) * width]
                diffs[h, rows, :] = part
                delta[h, :, rows] = jnp.sum(
                    part.astype(f32).T * out_t[b, h, :, rows], axis=0, keepdims=True
                )
                query_acc[h, :, rows] = jnp.zeros((width, block), f32)
            return 0

        lax.fori_loop(0, blocks, prepare, 0)

        def one_block(j, _):
            columns = pl.ds(pl.multiple_of(j * block, block), block)

            def step(i, state, diagonal):
                rows = pl.ds(pl.multiple_of(i * block, block), block)
                result = []
                for h in range(heads):
                    key_acc, value_acc = state[h]
                    query = queries[h, rows, :]
                    part = diffs[h, rows, :]
                    scores = matmul_rt(keys[h, columns, :], query)
                    probs = jnp.exp(scores - lse[b, h, :, rows])
                    if diagonal:
                        key_at = lax.broadcasted_iota(jnp.int32, (block, block), 0)
                        query_at = lax.broadcasted_iota(jnp.int32, (block, block), 1)
                        probs = jnp.where(key_at <= query_at, probs, 0.0)
                    prob_diff = matmul_rt(values[h, columns, :], part)
                    score_diff = (probs * (prob_diff - delta[h, :, rows])).astype(bf16)
                    value_acc = value_acc + matmul(probs.astype(bf16), part)
                    key_acc = key_acc + matmul(score_diff, query)
                    query_acc[h, :, rows] += matmul(keys_t[h, :, columns], score_diff)
                    result.append((key_acc, value_acc))
                return tuple(result)

            state = tuple(
                (jnp.zeros((block, 2 * width), f32), jnp.zeros((block, width), f32))
                for h in range(heads)
            )
            state = step(j, state, True)
            state = lax.fori_loop(j + 1, blocks, lambda i, s: step(i, s, False), state)
            for h in range(heads):
                base = h * 3 * width
                key_acc, value_acc = state[h]
                joined[b, columns, base + width : base + 2 * width] = key_acc[:, :width].astype(bf16)
                joined[b, columns, base + 2 * width : base + 3 * width] = value_acc.astype(bf16)
            return 0

        lax.fori_loop(0, blocks, one_block, 0)

        def finish(i, _):
            rows = pl.ds(pl.multiple_of(i * block, block), block)
            for h in range(heads):
                base = h * 3 * width
                joined[b, rows, base : base + width] = (
                    (query_acc[h, :, rows] * scale).T.astype(bf16)
                )
            return 0

        lax.fori_loop(0, blocks, finish, 0)
        return 0

    lax.fori_loop(0, seqs, one_seq, 0)


def attention_backward(qkv, diff, out_t, lse, slopes, heads, width):
    seqs, length, _ = qkv.shape
    block = min(512, length)
    return pl.pallas_call(
        functools.partial(backward_kernel, heads, width, block),
        name="attention_backward",
        out_shape=jax.ShapeDtypeStruct((seqs, length, heads * 3 * width), bf16),
        in_specs=[pl.BlockSpec(memory_space=pltpu.SMEM), VMEM, VMEM, VMEM, VMEM],
        out_specs=VMEM,
        scratch_shapes=[
            pltpu.VMEM((heads, length, 2 * width), bf16),
            pltpu.VMEM((heads, length, 2 * width), bf16),
            pltpu.VMEM((heads, width, length), bf16),
            pltpu.VMEM((heads, length, width), bf16),
            pltpu.VMEM((heads, length, width), bf16),
            pltpu.VMEM((heads, 1, length), f32),
            pltpu.VMEM((heads, width, length), f32),
        ],
        compiler_params=pltpu.CompilerParams(vmem_limit_bytes=vmem_bytes),
    )(slopes, qkv, diff, out_t, lse)


def to_own_seqs(values):
    seqs, piece, features = values.shape
    parts = lax.axis_size("fs")
    values = values.reshape(parts, seqs // parts, piece, features)
    return lax.all_to_all(values, "fs", split_axis=0, concat_axis=0).transpose(1, 0, 2, 3)


def from_own_seqs(values):
    own, parts, piece, features = values.shape
    values = lax.all_to_all(values.transpose(1, 0, 2, 3), "fs", split_axis=0, concat_axis=0)
    return values.reshape(parts * own, piece, features)


def to_heads(values):
    own, parts, piece, features = values.shape
    ranks = lax.axis_size("sp")
    values = values.reshape(own, parts, piece, ranks, features // ranks)
    values = lax.all_to_all(values, "sp", split_axis=3, concat_axis=2)
    return values.reshape(own, parts * ranks * piece, features // ranks)


def from_heads(values, parts, piece):
    own, _, features = values.shape
    ranks = lax.axis_size("sp")
    values = values.reshape(own, parts, ranks, piece, features)
    values = lax.all_to_all(values, "sp", split_axis=2, concat_axis=3)
    return values.reshape(own, parts, piece, ranks * features)


def per_device(
    layer_input,
    first_gain,
    first_shift,
    joined_weight,
    query_bias,
    value_bias,
    output_weight,
    output_bias,
    second_gain,
    second_shift,
    expand_weight,
    expand_bias,
    contract_weight,
    contract_bias,
    alibi_slopes,
    upstream,
):
    seqs, piece, features = layer_input.shape
    fs_count = lax.axis_size("fs")
    sp_count = lax.axis_size("sp")
    head_count = alibi_slopes.shape[0]
    width = features // head_count
    heads = head_count // sp_count
    rows = seqs * piece
    own = seqs // fs_count
    shape = (own, fs_count, piece)
    slopes = lax.dynamic_slice_in_dim(alibi_slopes, lax.axis_index("sp") * heads, heads)

    vectors = (
        first_gain, first_shift, query_bias, value_bias, output_bias,
        second_gain, second_shift, contract_bias, expand_bias,
    )
    packed = lax.all_gather(jnp.concatenate(vectors), "fs", axis=0)
    whole, at = [], 0
    for item in vectors:
        whole.append(packed[:, at : at + item.shape[0]].reshape(-1))
        at += item.shape[0]
    gain_one, shift_one, qbias, vbias, obias, gain_two, shift_two, cbias, ebias = [
        item.astype(f32) for item in whole
    ]
    gather = lambda item: lax.all_gather(item, "fs", axis=0, tiled=True)
    joined_full, out_full = gather(joined_weight), gather(output_weight)
    expand_full, contract_full = gather(expand_weight), gather(contract_weight)

    tokens = to_own_seqs(layer_input).reshape(rows, features).astype(f32)
    upstream_low = to_own_seqs(upstream).reshape(rows, features)

    normed_f, norm_back_one = jax.vjp(normalize, tokens, gain_one, shift_one)
    normed = normed_f.astype(bf16)
    joined_all = (matmul(normed, joined_full) + joined_bias_of(qbias, vbias, head_count)).astype(
        bf16
    )
    qkv = to_heads(joined_all.reshape(*shape, 3 * features))
    attended_heads, out_t, lse = attention_forward(qkv, slopes, heads, width)
    attended = from_heads(attended_heads, fs_count, piece).reshape(rows, features)

    residual = tokens + (matmul(attended, out_full) + obias)
    second_f, norm_back_two = jax.vjp(normalize, residual, gain_two, shift_two)
    second = second_f.astype(bf16)
    expanded = matmul(second, expand_full) + ebias
    activated_f, gelu_back = jax.vjp(gelu_tanh, expanded)
    activated = activated_f.astype(bf16)
    result = residual + (matmul(activated, contract_full) + cbias)
    layer_output = from_own_seqs(result.astype(bf16).reshape(*shape, features))

    upstream_f = upstream_low.astype(f32)
    contract_grad = matmul_lt(activated, upstream_low)
    contract_bias_grad = jnp.sum(upstream_f, axis=0)
    act_grad = matmul_rt(upstream_low, contract_full)
    expand_diff = gelu_back(act_grad)[0].astype(bf16)
    expand_grad = matmul_lt(second, expand_diff)
    expand_bias_grad = jnp.sum(expand_diff.astype(f32), axis=0)
    second_back = matmul_rt(expand_diff, expand_full)
    resid_part, second_gain_grad, second_shift_grad = norm_back_two(second_back)
    residual_grad = upstream_f + resid_part

    branch_diff = residual_grad.astype(bf16)
    output_weight_grad = matmul_lt(attended, branch_diff)
    output_bias_grad = jnp.sum(branch_diff.astype(f32), axis=0)
    attended_diff = matmul_rt(branch_diff, out_full).astype(bf16)
    diff_heads = to_heads(attended_diff.reshape(*shape, features))
    joined_heads = attention_backward(qkv, diff_heads, out_t, lse, slopes, heads, width)
    joined_diff = from_heads(joined_heads, fs_count, piece).reshape(rows, 3 * features)

    joined_grad = matmul_lt(normed, joined_diff)
    column_sums = jnp.sum(joined_diff.astype(f32), axis=0).reshape(head_count, 3, width)
    query_bias_grad = column_sums[:, 0].reshape(features)
    value_bias_grad = column_sums[:, 2].reshape(features)
    normed_back = matmul_rt(joined_diff, joined_full)
    input_part, first_gain_grad, first_shift_grad = norm_back_one(normed_back)
    input_grad = (residual_grad + input_part).astype(bf16)
    input_grad = from_own_seqs(input_grad.reshape(*shape, features))

    scatter = lambda item: lax.psum_scatter(
        item, ("fs", "sp"), scatter_dimension=0, tiled=True
    )
    vector_grads = (
        first_gain_grad, first_shift_grad, query_bias_grad, value_bias_grad, output_bias_grad,
        second_gain_grad, second_shift_grad, contract_bias_grad, expand_bias_grad,
    )
    devices = fs_count * sp_count
    packed = jnp.concatenate([item.reshape(devices, -1) for item in vector_grads], axis=1)
    packed = scatter(packed.reshape(-1))
    own_grads, at = [], 0
    for item in vector_grads:
        size = item.shape[0] // devices
        own_grads.append(packed[at : at + size])
        at += size
    g1, s1, qb, vb, ob, g2, s2, cb, eb = own_grads
    return (
        layer_output,
        input_grad,
        g1,
        s1,
        scatter(joined_grad),
        qb,
        vb,
        scatter(output_weight_grad),
        ob,
        g2,
        s2,
        scatter(expand_grad),
        eb,
        scatter(contract_grad),
        cb,
    )


def solution(mesh):
    tokens = P(None, ("fs", "sp"), None)
    both, both_rows = P(("fs", "sp")), P(("fs", "sp"), None)
    one, one_rows = P("fs"), P("fs", None)
    return jax.shard_map(
        per_device,
        mesh=mesh,
        in_specs=(
            tokens, one, one, one_rows, one, one, one_rows, one, one, one, one_rows, one,
            one_rows, one, P(), tokens,
        ),
        out_specs=(
            tokens, tokens, both, both, both_rows, both, both, both_rows, both, both, both,
            both_rows, both, both_rows, both,
        ),
        check_vma=False,
    )
```

time: 1710 us -> 1260 us (0.74)
  waiting for transfers between devices: 1130 us -> 816 us
  blocking collectives: 270 us -> 165 us
  Pallas kernels: 0 us -> 76.4 us
  local copies, waits for them, and re-layouts: 98.4 us -> 36.4 us
  matrix products: 137 us -> 106 us
  other arithmetic: 36.6 us -> 8.88 us
    reduce_scatter x5 -> x4, waiting for transfers between devices: 693 us -> 407 us  [per_device(): lax.psum_scatter(item, ('fs', 'sp'), scatter_dimension=0, tiled=True)]
    all_gather x9 -> x1, blocking collectives: 188 us -> 55.8 us  [per_device(): packed = lax.all_gather(jnp.concatenate(vectors), 'fs', axis=0)]
    all_gather x6 -> x4, waiting for transfers between devices: 367 us -> 286 us  [per_device(): gather = lambda item: lax.all_gather(item, 'fs', axis=0, tiled=True)]
    pallas_call x0 -> x2, Pallas kernels: none -> 76.4 us  [the longest x1 45.4 us: attention_backward(): pl.pallas_call(functools.partial(backward_kernel, heads, width, block), n...]
    all_to_all x3 -> x6, waiting for transfers between devices: 70.9 us -> 120 us  [the longest x2 64.3 us: from_heads(): values = lax.all_to_all(values, 'sp', split_axis=2, concat_axis=3)]
    squeeze x41 -> x0, local copies, waits for them, and re-layouts: 38.3 us -> none  [the longest x32 36.5 us: per_device(): lax.map(forward_one, (queries, keys_all, values_all))]
    dot_general x76 -> x4, matrix products: 72.3 us -> 35 us  [matmul(): return jnp.dot(left_side, right_side, preferred_element_type=f32)]
    all_to_all x1 -> x2, blocking collectives: 41.3 us -> 66.7 us  [to_heads(): values = lax.all_to_all(values, 'sp', split_axis=3, concat_axis=2)]
  transfers between devices with their start and end apart: 14 -> 14, of which waited for: 11 -> 10; matrix products, arithmetic and copies ran while one was open for 9% -> 10% of each run, Pallas kernels for 0% -> 6%
where the time goes in v1:
time: 1260 us; the launch traced here: 1250 us
  waiting for transfers between devices  816 us (65%)
  blocking collectives  165 us (13%)
  matrix products  106 us (8%)
  Pallas kernels  76.4 us (6%)
  local copies, waits for them, and re-layouts  36.4 us (3%)
  starting transfers between devices  27.5 us (2%)
  between operations  15.1 us (1%)
    reduce_scatter x4, waiting for transfers between devices, per_device(): lax.psum_scatter(item, ('fs', 'sp'), scatter_dimension=0, tiled=True)  407 us
    all_gather x4, waiting for transfers between devices, per_device(): gather = lambda item: lax.all_gather(item, 'fs', axis=0, tiled=True)  286 us
    all_to_all x2, blocking collectives, to_heads(): values = lax.all_to_all(values, 'sp', split_axis=3, concat_axis=2)  66.7 us
    all_to_all x2, waiting for transfers between devices, from_heads(): values = lax.all_to_all(values, 'sp', split_axis=2, concat_axis=3)  64.3 us
    all_gather x1, blocking collectives, per_device(): packed = lax.all_gather(jnp.concatenate(vectors), 'fs', axis=0)  55.8 us
    pallas_call x1, Pallas kernels, attention_backward(): pl.pallas_call(functools.partial(backward_kernel, heads, width, block), n...  45.4 us
    unnamed x1, blocking collectives  42.3 us
    dot_general x4, matrix products, matmul_lt(): lax.dot_general(left_side, right_side, (((0,), (0,)), ((), ())), preferre...  41.2 us
  transfers between devices with their start and end apart: 14, of which 10 were waited for; matrix products, arithmetic and copies ran while one was open for 10% of the time, Pallas kernels for 6%

profile of v1, /device:TPU:0, one launch (start us, length us, event | category | flops | bytes accessed | tf_op | source)
XLA Modules:
  0.0 1251.2 jit_solution(12109226285933564704)
XLA Ops:
  10.1 6.4 all-to-all-start
  18.2 55.8 %all-gather = bf16[12288]{0:T(1024)(128)(2,1)S(1)} all-gather(bf16[3072]{0:T(1024)(128)(2,1)S(1)} %constant_dynamic-update-slice_fusion), channel_id=2, replica_groups=mesh['fs'=4,'sp'=8] {'fs'}, dimensions={0}, use_global_device_ids=true | all-gather | bytes 30720 | tf_op jit(solution)/shard_map/all_gather | solution.py:338
  75.7 68.6 %all-gather.6.cloned.1.call-done = bf16[1024,3072]{1,0:T(8,128)(2,1)} async-done(((bf16[256,3072]{1,0:T(8,128)(2,1)}), bf16[1024,3072]{1,0:T(8,128)(2,1)}) %all-gather.6.cloned.1.call-update) | async-done | bytes 6291472 | tf_op jit(solution)/shard_map/all_gather | solution.py:346
  144.3 6.4 add_convert_fusion
  152.1 41.4 %all_to_all.80 = bf16[2,4,1,64,8,384]{5,3,1,0,2,4:T(8,128)(2,1)} all-to-all(bf16[2,4,1,64,8,384]{5,3,1,0,2,4:T(8,128)(2,1)S(1)} %copy.58), channel_id=1, replica_groups=mesh['fs'=4,'sp'=8] {'sp'}, dimensions={4} | all-to-all | bytes 6291456 | tf_op jit(solution)/shard_map/all_to_all | solution.py:293
  202.3 31.0 %attention_forward.1 = (bf16[2,2048,128]{2,1,0:T(8,128)(2,1)}, f32[2,2,64,2048]{3,2,1,0:T(8,128)}, f32[2,2,1,2048]{3,2,1,0:T(1,128)}) custom-call(f32[2]{0:T(128)} %dynamic_slice.3.slopes, bf16[2,2048,384]{2,1,0:T(8,128)(2,1)} %bitcast.148), custom_call_target="tpu_custom_call" | custom-call | tf_op jit(solution)/shard_map/attention_forward/pallas_call | solution.py:152
  235.6 15.2 %all-to-all-done.4 = bf16[4,2,64,1024]{3,2,1,0:T(8,128)(2,1)S(1)} async-done(((bf16[4,2,64,1024]{3,2,1,0:T(8,128)(2,1)}), bf16[4,2,64,1024]{3,2,1,0:T(8,128)(2,1)S(1)}, u32[]{:S(2)}, u32[]{:S(2)}) %all-to-all-start.4) | async-done | bytes 1048608 | tf_op jit(solution)/shard_map/all_to_all | solution.py:280
  256.7 13.8 %all-to-all-done.2 = bf16[2,4,8,64,1,128]{5,3,1,0,4,2:T(8,128)(2,1)} async-done(((bf16[2,4,8,64,1,128]{5,3,1,0,4,2:T(8,128)(2,1)}), bf16[2,4,8,64,1,128]{5,3,1,0,4,2:T(8,128)(2,1)}, u32[]{:S(2)}, u32[]{:S(2)}) %all-to-all-start.2) | async-done | bytes 1048608 | tf_op jit(solution)/shard_map/all_to_all | solution.py:301
  277.7 80.5 %all-gather.10.cloned.1.call-done = bf16[1024,4096]{1,0:T(8,128)(2,1)} async-done(((bf16[256,4096]{1,0:T(8,128)(2,1)}), bf16[1024,4096]{1,0:T(8,128)(2,1)}) %all-gather.10.cloned.1.call-update) | async-done | bytes 8388624 | tf_op jit(solution)/shard_map/all_gather | solution.py:346
  358.2 12.2 fusion.34
  370.4 136.7 %all-gather.12.cloned.1.call-done = bf16[4096,1024]{1,0:T(8,128)(2,1)} async-done(((bf16[1024,1024]{1,0:T(8,128)(2,1)}), bf16[4096,1024]{1,0:T(8,128)(2,1)}) %all-gather.12.cloned.1.call-update) | async-done | bytes 8388624 | tf_op jit(solution)/shard_map/all_gather | solution.py:346
  507.1 15.0 %convert_reduce_fusion = (f32[4096]{0:T(1024)S(1)}, bf16[512,4096]{1,0:T(8,128)(2,1)S(1)}) fusion(f32[512,4096]{1,0:T(8,128)} %fusion.34, f32[4096]{0:T(1024)S(1)} %bitcast.179, bf16[512,1024]{1,0:T(8,128)(2,1)S(1)} %bitcast.155, bf16[4096,1024]{1,0:T(8,128)(2,1)} %all-gather.12.cloned.1.call-done), kind=kOutput, calls=%fused_computation.10 | convolution fusion | flops 4351586304 | bytes 22052864 | tf_op jit(solution)/shard_map/dot_general | solution.py:45
  536.8 25.3 %all_to_all.81 = bf16[2,4,1,64,8,128]{5,3,1,0,2,4:T(8,128)(2,1)S(1)} all-to-all(bf16[2,4,1,64,8,128]{5,3,1,0,2,4:T(8,128)(2,1)S(1)} %copy.64), channel_id=1, replica_groups=mesh['fs'=4,'sp'=8] {'sp'}, dimensions={4} | all-to-all | bytes 2097152 | tf_op jit(solution)/shard_map/all_to_all | solution.py:293
  563.2 45.4 %attention_backward.1 = bf16[2,2048,384]{2,1,0:T(8,128)(2,1)} custom-call(f32[2]{0:T(128)} %dynamic_slice.3.slopes, bf16[2,2048,384]{2,1,0:T(8,128)(2,1)} %bitcast.149, bf16[2,2048,128]{2,1,0:T(8,128)(2,1)} %bitcast.157, f32[2,2,64,2048]{3,2,1,0:T(8,128)} %get-tuple-element.19.out_t, f32[2,2,1,2048]{3,2,1,0:T(1,128)} %get-tuple-element.20.lse), custom_call_target="tpu_custom_call" | custom-call | tf_op jit(solution)/shard_map/attention_backward/pallas_call | solution.py:257
  618.5 50.5 %all-to-all-done.6 = bf16[2,4,8,64,1,384]{5,3,1,0,4,2:T(8,128)(2,1)} async-done(((bf16[2,4,8,64,1,384]{5,3,1,0,4,2:T(8,128)(2,1)}), bf16[2,4,8,64,1,384]{5,3,1,0,4,2:T(8,128)(2,1)}, u32[]{:S(2)}, u32[]{:S(2)}) %all-to-all-start.6) | async-done | bytes 3145760 | tf_op jit(solution)/shard_map/all_to_all | solution.py:301
  681.8 14.2 %fusion.33 = f32[1024,4096]{1,0:T(8,128)} fusion(bf16[512,4096]{1,0:T(8,128)(2,1)} %copy-done.23, f32[512,1024]{1,0:T(8,128)} %copy-done.5, f32[1024]{0:T(1024)S(1)} %bitcast.187, f32[1024]{0:T(1024)S(1)} %bitcast.185, f32[512]{0:T(512)S(1)} %fusion.30, f32[512]{0:T(512)S(1)} %broadcast_multiply_fusion.1), kind=kOutput, calls=%fused_computation.80 | convolution fusion | flops 4297588736 | bytes 23080960 | tf_op jit(solution)/shard_map/dot_general | solution.py:39
  696.3 17.2 %fusion.35 = f32[4096,1024]{1,0:T(8,128)} fusion(bf16[512,1024]{1,0:T(8,128)(2,1)} %bitcast.156, f32[512,4096]{1,0:T(8,128)} %fusion.34, f32[4096]{0:T(1024)S(1)} %bitcast.180), kind=kOutput, calls=%fused_computation.82 | convolution fusion | flops 4315938816 | bytes 26230784 | tf_op jit(solution)/shard_map/dot_general | solution.py:39
  713.6 12.8 %add_convert_fusion.2 = bf16[512,1024]{1,0:T(8,128)(2,1)S(1)} fusion(f32[512,1024]{1,0:T(8,128)} %copy-done.5, bf16[4096,1024]{1,0:T(8,128)(2,1)} %all-gather.12.cloned.1.call-done, f32[1024]{0:T(1024)S(1)} %bitcast.189, f32[512,4096]{1,0:T(8,128)} %fusion.34, f32[4096]{0:T(1024)S(1)} %bitcast.181), kind=kOutput, calls=%fused_computation.42 | convolution fusion | flops 4317511680 | bytes 19943424 | tf_op jit(solution)/shard_map/dot_general | solution.py:35
  732.0 7.0 fusion.36
  742.5 40.4 %all-to-all-done.3 = bf16[4,2,64,1024]{3,2,1,0:T(8,128)(2,1)} async-done(((bf16[4,2,64,1024]{3,2,1,0:T(8,128)(2,1)}), bf16[4,2,64,1024]{3,2,1,0:T(8,128)(2,1)}, u32[]{:S(2)}, u32[]{:S(2)}) %all-to-all-start.3) | async-done | bytes 1048608 | tf_op jit(solution)/shard_map/all_to_all | solution.py:285
  789.8 42.3 %all-reduce = f32[12288]{0:T(1024)S(1)} all-reduce(f32[12288]{0:T(1024)S(1)} %reshape.291), channel_id=3, replica_groups=mesh['fs'=4,'sp'=8] {'fs','sp'}, use_global_device_ids=true, to_apply=%region_16.0.clone | all-reduce | flops 12288 | bytes 98304
  833.3 35.1 %reduce-scatter.5.cloned.1.call-done = f32[32,3072]{1,0:T(8,128)} async-done(((f32[1024,3072]{1,0:T(8,128)}), f32[32,3072]{1,0:T(8,128)}) %reduce-scatter.5.cloned.1.call-update) | async-done | bytes 393232 | tf_op jit(solution)/shard_map/reduce_scatter | solution.py:399
  868.4 184.7 %reduce-scatter.9.cloned.1.call-done = f32[32,4096]{1,0:T(8,128)} async-done(((f32[1024,4096]{1,0:T(8,128)}), f32[32,4096]{1,0:T(8,128)}) %reduce-scatter.9.cloned.1.call-update) | async-done | bytes 524304 | tf_op jit(solution)/shard_map/reduce_scatter | solution.py:399
  1053.1 187.5 %reduce-scatter.11.cloned.1.call-done = f32[128,1024]{1,0:T(8,128)} async-done(((f32[4096,1024]{1,0:T(8,128)}), f32[128,1024]{1,0:T(8,128)}) %reduce-scatter.11.cloned.1.call-update) | async-done | bytes 524304 | tf_op jit(solution)/shard_map/reduce_scatter | solution.py:399
  (158 shorter events, 90.6 us)
Async XLA Ops:
  7.2 137.2 %all-gather.6.cloned.1.call-start = ((), (), s32[]{:S(2)}) async-start(), calls=%async_computation.12 | async-start | bytes 7864320 | tf_op jit(solution)/shard_map/all_gather | solution.py:346
  7.9 264.5 %all-gather.8.cloned.1.call-start = ((), (), s32[]{:S(2)}) async-start(), calls=%async_computation.13 | async-start | bytes 2621440 | tf_op jit(solution)/shard_map/all_gather | solution.py:346
  8.7 349.5 %all-gather.10.cloned.1.call-start = ((), (), s32[]{:S(2)}) async-start(), calls=%async_computation.14 | async-start | bytes 10485760 | tf_op jit(solution)/shard_map/all_gather | solution.py:346
  9.4 7.7 copy-start.16
  9.4 7.9 copy-start.17
  9.4 8.1 copy-start.18
  9.5 8.3 copy-start.19
  9.5 8.5 copy-start.20
  9.5 8.7 copy-start.12
  9.5 497.6 %all-gather.12.cloned.1.call-start = ((), (), s32[]{:S(2)}) async-start(), calls=%async_computation.15 | async-start | bytes 10485760 | tf_op jit(solution)/shard_map/all_gather | solution.py:346
  10.1 64.4 %all-to-all-start = ((bf16[4,2,64,1024]{3,2,1,0:T(8,128)(2,1)}), bf16[4,2,64,1024]{3,2,1,0:T(8,128)(2,1)S(1)}, u32[]{:S(2)}, u32[]{:S(2)}) async-start(bf16[4,2,64,1024]{3,2,1,0:T(8,128)(2,1)} %bitcast), calls=%async_computation | async-start | bytes 2097152 | tf_op jit(solution)/shard_map/all_to_all | solution.py:280
  193.5 57.3 %all-to-all-start.4 = ((bf16[4,2,64,1024]{3,2,1,0:T(8,128)(2,1)}), bf16[4,2,64,1024]{3,2,1,0:T(8,128)(2,1)S(1)}, u32[]{:S(2)}, u32[]{:S(2)}) async-start(bf16[4,2,64,1024]{3,2,1,0:T(8,128)(2,1)} %bitcast.13), calls=%async_computation.4 | async-start | bytes 2097152 | tf_op jit(solution)/shard_map/all_to_all | solution.py:280
  250.8 19.6 %all-to-all-start.2 = ((bf16[2,4,8,64,1,128]{5,3,1,0,4,2:T(8,128)(2,1)}), bf16[2,4,8,64,1,128]{5,3,1,0,4,2:T(8,128)(2,1)}, u32[]{:S(2)}, u32[]{:S(2)}) async-start(bf16[2,4,8,64,1,128]{5,3,1,0,4,2:T(8,128)(2,1)} %copy.60), calls=%async_computation.2 | async-start | bytes 2097152 | tf_op jit(solution)/shard_map/all_to_all | solution.py:301
  255.1 578.2 %reduce-scatter.7.cloned.1.call-start = ((), (), s32[]{:S(2)}) async-start(), calls=%async_computation.17 | async-start | bytes 4325376 | tf_op jit(solution)/shard_map/reduce_scatter | solution.py:399
  255.5 251.6 %copy-start.2 = (bf16[2,4,64,1024]{3,2,1,0:T(8,128)(2,1)}, bf16[2,4,64,1024]{3,2,1,0:T(8,128)(2,1)S(1)}, u32[]{:S(2)}) copy-start(bf16[2,4,64,1024]{3,2,1,0:T(8,128)(2,1)S(1)} %copy.63) | copy-start | bytes 3145732
  507.1 15.0 %copy-start.6 = (f32[512,1024]{1,0:T(8,128)S(1)}, f32[512,1024]{1,0:T(8,128)}, u32[]{:S(2)}) copy-start(f32[512,1024]{1,0:T(8,128)} %copy-done.5) | copy-start | bytes 6291460
  507.1 15.0 %copy-start.21 = (bf16[1024,4096]{1,0:T(8,128)(2,1)S(1)}, bf16[1024,4096]{1,0:T(8,128)(2,1)}, u32[]{:S(2)}) copy-start(bf16[1024,4096]{1,0:T(8,128)(2,1)} %all-gather.10.cloned.1.call-done) | copy-start | bytes 25165828
  612.6 56.5 %all-to-all-start.6 = ((bf16[2,4,8,64,1,384]{5,3,1,0,4,2:T(8,128)(2,1)}), bf16[2,4,8,64,1,384]{5,3,1,0,4,2:T(8,128)(2,1)}, u32[]{:S(2)}, u32[]{:S(2)}) async-start(bf16[2,4,8,64,1,384]{5,3,1,0,4,2:T(8,128)(2,1)} %copy.66), calls=%async_computation.6 | async-start | bytes 6291456 | tf_op jit(solution)/shard_map/all_to_all | solution.py:301
  617.0 251.4 %reduce-scatter.5.cloned.1.call-start = ((), (), s32[]{:S(2)}) async-start(), calls=%async_computation.16 | async-start | bytes 12976128 | tf_op jit(solution)/shard_map/reduce_scatter | solution.py:399
  681.7 371.4 %reduce-scatter.9.cloned.1.call-start = ((), (), s32[]{:S(2)}) async-start(), calls=%async_computation.18 | async-start | bytes 17301504 | tf_op jit(solution)/shard_map/reduce_scatter | solution.py:399
  696.0 544.6 %reduce-scatter.11.cloned.1.call-start = ((), (), s32[]{:S(2)}) async-start(), calls=%async_computation.19 | async-start | bytes 17301504 | tf_op jit(solution)/shard_map/reduce_scatter | solution.py:399
  727.5 55.4 %all-to-all-start.3 = ((bf16[4,2,64,1024]{3,2,1,0:T(8,128)(2,1)}), bf16[4,2,64,1024]{3,2,1,0:T(8,128)(2,1)}, u32[]{:S(2)}, u32[]{:S(2)}) async-start(bf16[4,2,64,1024]{3,2,1,0:T(8,128)(2,1)} %bitcast.159), calls=%async_computation.3 | async-start | bytes 2097152 | tf_op jit(solution)/shard_map/all_to_all | solution.py:285
  741.4 45.0 %copy-start.1 = (bf16[4,2,64,1024]{3,2,1,0:T(8,128)(2,1)S(1)}, bf16[4,2,64,1024]{3,2,1,0:T(8,128)(2,1)}, u32[]{:S(2)}) copy-start(bf16[4,2,64,1024]{3,2,1,0:T(8,128)(2,1)} %copy-done) | copy-start | bytes 3145732
  782.9 50.4 %all-to-all-start.7 = ((bf16[4,2,64,1024]{3,2,1,0:T(8,128)(2,1)}), bf16[4,2,64,1024]{3,2,1,0:T(8,128)(2,1)S(1)}, u32[]{:S(2)}, u32[]{:S(2)}) async-start(bf16[4,2,64,1024]{3,2,1,0:T(8,128)(2,1)} %bitcast.145), calls=%async_computation.7 | async-start | bytes 2097152 | tf_op jit(solution)/shard_map/all_to_all | solution.py:285
  (14 other events, 48.9 us)
Sparse Core Ops, SparseCore 0:
  9.6 134.7 all-gather.5
  145.9 44.6 all-gather.7
  192.2 165.9 all-gather.9
  359.6 147.4 all-gather.11
  533.2 142.0 reduce-scatter.6
  681.8 186.5 reduce-scatter.4
  871.3 181.8 reduce-scatter.8
  1056.0 184.6 reduce-scatter.10

commit v2 on v1

--- a/solution.py
+++ b/solution.py
@@ -300,6 +300,399 @@
     values = values.reshape(own, parts, ranks, piece, features)
     values = lax.all_to_all(values, "sp", split_axis=2, concat_axis=3)
     return values.reshape(own, parts, piece, ranks * features)
+
+
+class Copies:
+    def __init__(self, send, recv):
+        self.send, self.recv, self.used, self.made = send, recv, 0, []
+
+    def start(self, source, target, device):
+        copy = pltpu.make_async_remote_copy(
+            src_ref=source,
+            dst_ref=target,
+            send_sem=self.send.at[self.used],
+            recv_sem=self.recv.at[self.used],
+            device_id=device,
+            device_id_type=MESH,
+        )
+        self.used += 1
+        self.made.append(copy)
+        copy.start()
+        return copy
+
+    def finish(self):
+        assert self.used == self.send.shape[0]
+        for copy in self.made:
+            copy.wait_send()
+
+
+class Locals:
+    def __init__(self, sems):
+        self.sems, self.used = sems, 0
+
+    def start(self, source, target):
+        copy = pltpu.make_async_copy(source, target, self.sems.at[self.used])
+        self.used += 1
+        copy.start()
+        return copy
+
+
+def arrive(copies):
+    for copy in copies:
+        copy.wait_recv()
+
+
+def greet(devices):
+    barrier = pltpu.get_barrier_semaphore()
+    for device in devices:
+        pl.semaphore_signal(barrier, inc=1, device_id=device, device_id_type=MESH)
+    pl.semaphore_wait(barrier, len(devices))
+
+
+def place():
+    z, s = lax.axis_index("fs"), lax.axis_index("sp")
+    along_x = s + 2 - 4 * ((s // 2) % 2)
+    along_y = s + 4 - 8 * (s // 4)
+    partner = s + 1 - 2 * (s % 2)
+    return z, s, along_x, along_y, partner
+
+
+def gather_kernel(count, *refs):
+    seq_in, vector_in, weights = refs[:2], refs[2], refs[3 : 3 + count]
+    refs = refs[3 + count :]
+    seq_out, vector_out, wholes = refs[:2], refs[2], refs[3 : 3 + count]
+    refs = refs[3 + count :]
+    seq_own, vector_own, weight_own = refs[:2], refs[2], refs[3 : 3 + count]
+    send, recv, local = refs[3 + count :]
+    z, s, along_x, along_y, partner = place()
+    diagonal = along_x + along_y - s
+    lines = [(lax.rem(z + k, 4), s) for k in range(1, 4)]
+    to_x, to_y, to_core = (z, along_x), (z, along_y), (z, partner)
+    copies, locals_ = Copies(send, recv), Locals(local)
+    greet(lines + [to_x, to_y, to_core])
+
+    own_in = [locals_.start(item.at[z], kept) for item, kept in zip(seq_in, seq_own)]
+    own_in.append(locals_.start(vector_in, vector_own))
+    own_in += [locals_.start(item, kept) for item, kept in zip(weights, weight_own)]
+    waiting = []
+    for to in lines:
+        waiting.append(copies.start(seq_in[0].at[to[0]], seq_out[0].at[:, z], to))
+        waiting.append(copies.start(vector_in, vector_out.at[z], to))
+    first = []
+    for item, whole in zip(weights, wholes):
+        first.append([copies.start(item.at[s], whole.at[z, s], to) for to in lines])
+    for to in lines:
+        waiting.append(copies.start(seq_in[1].at[to[0]], seq_out[1].at[:, z], to))
+    for copy in own_in:
+        copy.wait()
+    own_out = [locals_.start(kept, item.at[:, z]) for item, kept in zip(seq_out, seq_own)]
+    own_out.append(locals_.start(vector_own, vector_out.at[z]))
+    own_out += [locals_.start(kept, item.at[z]) for item, kept in zip(wholes, weight_own)]
+
+    def same(whole, where, to):
+        return copies.start(whole.at[where], whole.at[where], to)
+
+    second, third = [], []
+    for t in range(count + 2):
+        if t < count:
+            whole = wholes[t]
+            half = whole.shape[2] // 2
+            low, high, every = pl.ds(0, half), pl.ds(half, half), pl.ds(0, 2 * half)
+            arrive(first[t])
+            step = []
+            for k, _ in lines:
+                step.append(same(whole, (k, s, low), to_x))
+                step.append(same(whole, (k, s, high), to_y))
+                waiting.append(same(whole, (k, s, every), to_core))
+            second.append(step)
+        if 0 <= t - 1 < count:
+            whole = wholes[t - 1]
+            half = whole.shape[2] // 2
+            low, high = pl.ds(0, half), pl.ds(half, half)
+            arrive(second[t - 1])
+            step = []
+            for k, _ in lines:
+                step.append(same(whole, (k, s, low), to_y))
+                step.append(same(whole, (k, along_x, low), to_y))
+                step.append(same(whole, (k, s, high), to_x))
+                step.append(same(whole, (k, along_y, high), to_x))
+                waiting.append(same(whole, (k, along_x, low), to_core))
+                waiting.append(same(whole, (k, along_y, high), to_core))
+            third.append(step)
+        if 0 <= t - 2 < count:
+            whole = wholes[t - 2]
+            half = whole.shape[2] // 2
+            low, high = pl.ds(0, half), pl.ds(half, half)
+            arrive(third[t - 2])
+            for k, _ in lines:
+                waiting.append(same(whole, (k, along_y, low), to_core))
+                waiting.append(same(whole, (k, diagonal, low), to_core))
+                waiting.append(same(whole, (k, along_x, high), to_core))
+                waiting.append(same(whole, (k, diagonal, high), to_core))
+    arrive(waiting)
+    copies.finish()
+    for copy in own_out:
+        copy.wait()
+
+
+def gather_all(tokens, upstream, vector, weights):
+    seqs, piece, features = tokens.shape
+    own = seqs // 4
+    count = len(weights)
+    vector = vector.reshape(-1, 128)
+    cut = [item.reshape(8, item.shape[0] // 8, item.shape[1]) for item in weights]
+    seq_shape = (own, 4, piece, features)
+    copies = 9 + count * 42
+    out = pl.pallas_call(
+        functools.partial(gather_kernel, count),
+        name="gather_all",
+        out_shape=(
+            jax.ShapeDtypeStruct(seq_shape, bf16),
+            jax.ShapeDtypeStruct(seq_shape, bf16),
+            jax.ShapeDtypeStruct((4, *vector.shape), bf16),
+            *[jax.ShapeDtypeStruct((4, *item.shape), bf16) for item in cut],
+        ),
+        in_specs=[HBM] * (3 + count),
+        out_specs=(HBM,) * (3 + count),
+        scratch_shapes=[
+            pltpu.VMEM((own, piece, features), bf16),
+            pltpu.VMEM((own, piece, features), bf16),
+            pltpu.VMEM(vector.shape, bf16),
+            *[pltpu.VMEM(item.shape, bf16) for item in cut],
+            pltpu.SemaphoreType.DMA((copies,)),
+            pltpu.SemaphoreType.DMA((copies,)),
+            pltpu.SemaphoreType.DMA((2 * (3 + count),)),
+        ],
+        compiler_params=pltpu.CompilerParams(
+            collective_id=0, has_side_effects=True, vmem_limit_bytes=vmem_bytes
+        ),
+    )(
+        tokens.reshape(4, own, piece, features),
+        upstream.reshape(4, own, piece, features),
+        vector,
+        *cut,
+    )
+    wholes = [
+        whole.reshape(4 * item.shape[0], item.shape[1]) for whole, item in zip(out[3:], weights)
+    ]
+    return out[0], out[1], out[2].reshape(4, -1), wholes
+
+
+def heads_kernel(features, into, source, target, kept, send, recv, local):
+    z, s, _, _, _ = place()
+    copies, locals_ = Copies(send, recv), Locals(local)
+    peers = [(z, lax.rem(s + d, 8)) for d in range(1, 8)]
+
+    def columns(rank):
+        return pl.ds(pl.multiple_of(rank * features, 128), features)
+
+    def piece_for(rank):
+        return source.at[:, :, :, columns(rank)] if into else source.at[:, :, rank]
+
+    mine = target.at[:, :, s] if into else target.at[:, :, :, columns(s)]
+    own = locals_.start(piece_for(s), kept)
+    greet(peers)
+    waiting = [copies.start(piece_for(to[1]), mine, to) for to in peers]
+    own.wait()
+    own = locals_.start(kept, mine)
+    arrive(waiting)
+    copies.finish()
+    own.wait()
+
+
+def heads_call(values, collective, into, features):
+    own, parts, piece = values.shape[0], values.shape[1], values.shape[-2]
+    wide, tall = (own, parts, piece, 8 * features), (own, parts, 8, piece, features)
+    return pl.pallas_call(
+        functools.partial(heads_kernel, features, into),
+        name="to_heads" if into else "from_heads",
+        out_shape=jax.ShapeDtypeStruct(tall if into else wide, bf16),
+        in_specs=[HBM],
+        out_specs=HBM,
+        scratch_shapes=[
+            pltpu.VMEM((own, parts, piece, features), bf16),
+            pltpu.SemaphoreType.DMA((7,)),
+            pltpu.SemaphoreType.DMA((7,)),
+            pltpu.SemaphoreType.DMA((2,)),
+        ],
+        compiler_params=pltpu.CompilerParams(
+            collective_id=collective, has_side_effects=True, vmem_limit_bytes=vmem_bytes
+        ),
+    )(values)
+
+
+def add_blocks(steps, block_of):
+    def body(i, _):
+        target, others = block_of(i)
+        total = target[...].astype(f32)
+        for other in others:
+            total = total + other[...].astype(f32)
+        target[...] = total.astype(target.dtype)
+        return 0
+
+    lax.fori_loop(0, steps, body, 0)
+
+
+def reduce_kernel(count, *refs):
+    seq_in, vector_in, grads = refs[:2], refs[2], refs[3 : 3 + count]
+    refs = refs[3 + count :]
+    seq_out, vector_out, outs = refs[:2], refs[2], refs[3 : 3 + count]
+    refs = refs[3 + count :]
+    seq_own, vector_ranks, vector_sum, vector_lines = refs[:2], refs[2], refs[3], refs[4]
+    bufs = [refs[5 + 7 * t : 12 + 7 * t] for t in range(count)]
+    send, recv, local = refs[5 + 7 * count :]
+    z, s, along_x, along_y, partner = place()
+    core, chip = s % 2, s // 2
+    x, y = chip % 2, chip // 2
+    chip_x, chip_y = along_x // 2, along_y // 2
+    lines = [(lax.rem(z + k, 4), s) for k in range(1, 4)]
+    plane = [(z, lax.rem(s + d, 8)) for d in range(1, 8)]
+    to_x, to_y, to_core = (z, along_x), (z, along_y), (z, partner)
+    copies, locals_ = Copies(send, recv), Locals(local)
+    loads = [locals_.start(g.at[:, :, core], b[0]) for g, b in zip(grads, bufs)]
+    own_seq = [locals_.start(item.at[:, z], kept) for item, kept in zip(seq_in, seq_own)]
+    own_vector = locals_.start(vector_in.at[:, s], vector_ranks.at[0])
+    greet(lines + plane)
+
+    cores = [copies.start(g.at[:, :, 1 - core], b[1], to_core) for g, b in zip(grads, bufs)]
+    waiting = []
+    for to in lines:
+        for item, out in zip(seq_in, seq_out):
+            waiting.append(copies.start(item.at[:, to[0]], out.at[z], to))
+    vectors = [
+        copies.start(vector_in.at[:, to[1]], vector_ranks.at[d + 1], to)
+        for d, to in enumerate(plane)
+    ]
+    for copy in own_seq:
+        copy.wait()
+    own_out = [locals_.start(kept, out.at[z]) for kept, out in zip(seq_own, seq_out)]
+    second, third, fourth = [], [], []
+    for t in range(count + 3):
+        if t < count:
+            own, from_core, from_x, from_y = bufs[t][:4]
+            rows = own.shape[2]
+            half = rows // 2
+            low, high = pl.ds(0, half), pl.ds(half, half)
+            loads[t].wait()
+            arrive([cores[t]])
+            add_blocks(16, lambda i: (own.at[i // 4, i % 4], [from_core.at[i // 4, i % 4]]))
+            step = []
+            for k in range(2):
+                step.append(copies.start(own.at[:, 2 * k + 1 - x, low], from_x.at[:, k], to_x))
+                step.append(
+                    copies.start(own.at[:, 2 * (1 - y) + k, high], from_y.at[:, k], to_y)
+                )
+            second.append(step)
+        if 0 <= t - 1 < count:
+            own, _, from_x, from_y, late_y, late_x = bufs[t - 1][:6]
+            half = own.shape[2] // 2
+            low, high = pl.ds(0, half), pl.ds(half, half)
+            arrive(second[t - 1])
+            add_blocks(
+                8, lambda i: (own.at[i // 2, 2 * (i % 2) + x, low], [from_x.at[i // 2, i % 2]])
+            )
+            add_blocks(
+                8, lambda i: (own.at[i // 2, 2 * y + i % 2, high], [from_y.at[i // 2, i % 2]])
+            )
+            third.append(
+                [
+                    copies.start(own.at[:, chip_y, low], late_y, to_y),
+                    copies.start(own.at[:, chip_x, high], late_x, to_x),
+                ]
+            )
+        if 0 <= t - 2 < count:
+            own, _, _, _, late_y, late_x, from_z = bufs[t - 2]
+            half = own.shape[2] // 2
+            low, high = pl.ds(0, half), pl.ds(half, half)
+            arrive(third[t - 2])
+            add_blocks(4, lambda i: (own.at[i, chip, low], [late_y.at[i]]))
+            add_blocks(4, lambda i: (own.at[i, chip, high], [late_x.at[i]]))
+            fourth.append(
+                [copies.start(own.at[to[0], chip], from_z.at[k], to) for k, to in enumerate(lines)]
+            )
+        if t == 0:
+            own_vector.wait()
+            arrive(vectors)
+            total = vector_ranks[0]
+            for d in range(1, 8):
+                total = total + vector_ranks[d]
+            vector_sum[...] = total
+            vectors = [
+                copies.start(vector_sum.at[to[0]], vector_lines.at[k], to)
+                for k, to in enumerate(lines)
+            ]
+        if 0 <= t - 3 < count:
+            own, from_z = bufs[t - 3][0], bufs[t - 3][6]
+            arrive(fourth[t - 3])
+            total = own[z, chip].astype(f32)
+            for k in range(3):
+                total = total + from_z[k].astype(f32)
+            outs[t - 3][...] = total
+    arrive(vectors)
+    total = vector_sum[z]
+    for k in range(3):
+        total = total + vector_lines[k]
+    vector_out[...] = total
+    arrive(waiting)
+    copies.finish()
+    for copy in own_out:
+        copy.wait()
+
+
+def reduce_all(layer_output, input_grad, vector, grads):
+    own, parts, piece, features = layer_output.shape
+    count = len(grads)
+    lanes = vector.shape[-1]
+    padded = -(-lanes // 1024) * 1024
+    vector = jnp.pad(vector, ((0, 0), (0, padded - lanes))).reshape(4, 8, padded // 128, 128)
+    cut = [item.reshape(4, 4, 2, item.shape[0] // 32, item.shape[1]) for item in grads]
+    scratch = []
+    for item in cut:
+        rows, columns = item.shape[3:]
+        half = rows // 2
+        scratch += [
+            pltpu.VMEM((4, 4, rows, columns), bf16),
+            pltpu.VMEM((4, 4, rows, columns), bf16),
+            pltpu.VMEM((4, 2, half, columns), bf16),
+            pltpu.VMEM((4, 2, half, columns), bf16),
+            pltpu.VMEM((4, half, columns), bf16),
+            pltpu.VMEM((4, half, columns), bf16),
+            pltpu.VMEM((3, rows, columns), bf16),
+        ]
+    copies = 6 + 7 + 3 + count * 10
+    seq_shape = (4, own, piece, features)
+    out = pl.pallas_call(
+        functools.partial(reduce_kernel, count),
+        name="reduce_all",
+        out_shape=(
+            jax.ShapeDtypeStruct(seq_shape, bf16),
+            jax.ShapeDtypeStruct(seq_shape, bf16),
+            jax.ShapeDtypeStruct(vector.shape[2:], f32),
+            *[jax.ShapeDtypeStruct(item.shape[3:], f32) for item in cut],
+        ),
+        in_specs=[HBM] * (3 + count),
+        out_specs=(HBM, HBM) + (VMEM,) * (1 + count),
+        scratch_shapes=[
+            pltpu.VMEM((own, piece, features), bf16),
+            pltpu.VMEM((own, piece, features), bf16),
+            pltpu.VMEM((8, 4, padded // 128, 128), f32),
+            pltpu.VMEM((4, padded // 128, 128), f32),
+            pltpu.VMEM((3, padded // 128, 128), f32),
+            *scratch,
+            pltpu.SemaphoreType.DMA((copies,)),
+            pltpu.SemaphoreType.DMA((copies,)),
+            pltpu.SemaphoreType.DMA((count + 5,)),
+        ],
+        compiler_params=pltpu.CompilerParams(
+            collective_id=1, has_side_effects=True, vmem_limit_bytes=vmem_bytes
+        ),
+    )(layer_output, input_grad, vector, *cut)
+    return (
+        out[0].reshape(4 * own, piece, features),
+        out[1].reshape(4 * own, piece, features),
+        out[2].reshape(-1)[:lanes],
+        out[3:],
+    )
 
 
 def per_device(
@@ -335,7 +728,19 @@
         first_gain, first_shift, query_bias, value_bias, output_bias,
         second_gain, second_shift, contract_bias, expand_bias,
     )
-    packed = lax.all_gather(jnp.concatenate(vectors), "fs", axis=0)
+    fast = (fs_count, sp_count) == (4, 8) and own >= 1
+    weights = (joined_weight, output_weight, expand_weight, contract_weight)
+    if fast:
+        tokens, upstream_low, packed, weights = gather_all(
+            layer_input, upstream, jnp.concatenate(vectors), weights
+        )
+    else:
+        tokens, upstream_low = to_own_seqs(layer_input), to_own_seqs(upstream)
+        packed = lax.all_gather(jnp.concatenate(vectors), "fs", axis=0)
+        weights = [lax.all_gather(item, "fs", axis=0, tiled=True) for item in weights]
+    joined_full, out_full, expand_full, contract_full = weights
+    tokens = tokens.reshape(rows, features).astype(f32)
+    upstream_low = upstream_low.reshape(rows, features)
     whole, at = [], 0
     for item in vectors:
         whole.append(packed[:, at : at + item.shape[0]].reshape(-1))
@@ -343,21 +748,30 @@
     gain_one, shift_one, qbias, vbias, obias, gain_two, shift_two, cbias, ebias = [
         item.astype(f32) for item in whole
     ]
-    gather = lambda item: lax.all_gather(item, "fs", axis=0, tiled=True)
-    joined_full, out_full = gather(joined_weight), gather(output_weight)
-    expand_full, contract_full = gather(expand_weight), gather(contract_weight)
-
-    tokens = to_own_seqs(layer_input).reshape(rows, features).astype(f32)
-    upstream_low = to_own_seqs(upstream).reshape(rows, features)
+
+    def into_heads(values, collective):
+        if fast:
+            columns = values.shape[1] // 8
+            found = heads_call(values.reshape(*shape, -1), collective, True, columns)
+            return found.reshape(own, -1, columns)
+        return to_heads(values.reshape(*shape, -1))
+
+    def out_of_heads(values, collective):
+        if fast:
+            columns = values.shape[-1]
+            found = values.reshape(own, 4, 8, piece, columns)
+            found = heads_call(found, collective, False, columns)
+            return found.reshape(rows, -1)
+        return from_heads(values, fs_count, piece).reshape(rows, -1)
 
     normed_f, norm_back_one = jax.vjp(normalize, tokens, gain_one, shift_one)
     normed = normed_f.astype(bf16)
     joined_all = (matmul(normed, joined_full) + joined_bias_of(qbias, vbias, head_count)).astype(
         bf16
     )
-    qkv = to_heads(joined_all.reshape(*shape, 3 * features))
+    qkv = into_heads(joined_all, 2)
     attended_heads, out_t, lse = attention_forward(qkv, slopes, heads, width)
-    attended = from_heads(attended_heads, fs_count, piece).reshape(rows, features)
+    attended = out_of_heads(attended_heads, 3)
 
     residual = tokens + (matmul(attended, out_full) + obias)
     second_f, norm_back_two = jax.vjp(normalize, residual, gain_two, shift_two)
@@ -366,7 +780,7 @@
     activated_f, gelu_back = jax.vjp(gelu_tanh, expanded)
     activated = activated_f.astype(bf16)
     result = residual + (matmul(activated, contract_full) + cbias)
-    layer_output = from_own_seqs(result.astype(bf16).reshape(*shape, features))
+    layer_output = result.astype(bf16).reshape(*shape, features)
 
     upstream_f = upstream_low.astype(f32)
     contract_grad = matmul_lt(activated, upstream_low)
@@ -383,9 +797,9 @@
     output_weight_grad = matmul_lt(attended, branch_diff)
     output_bias_grad = jnp.sum(branch_diff.astype(f32), axis=0)
     attended_diff = matmul_rt(branch_diff, out_full).astype(bf16)
-    diff_heads = to_heads(attended_diff.reshape(*shape, features))
+    diff_heads = into_heads(attended_diff, 4)
     joined_heads = attention_backward(qkv, diff_heads, out_t, lse, slopes, heads, width)
-    joined_diff = from_heads(joined_heads, fs_count, piece).reshape(rows, 3 * features)
+    joined_diff = out_of_heads(joined_heads, 5)
 
     joined_grad = matmul_lt(normed, joined_diff)
     column_sums = jnp.sum(joined_diff.astype(f32), axis=0).reshape(head_count, 3, width)
@@ -393,19 +807,27 @@
     value_bias_grad = column_sums[:, 2].reshape(features)
     normed_back = matmul_rt(joined_diff, joined_full)
     input_part, first_gain_grad, first_shift_grad = norm_back_one(normed_back)
-    input_grad = (residual_grad + input_part).astype(bf16)
-    input_grad = from_own_seqs(input_grad.reshape(*shape, features))
-
-    scatter = lambda item: lax.psum_scatter(
-        item, ("fs", "sp"), scatter_dimension=0, tiled=True
-    )
+    input_grad = (residual_grad + input_part).astype(bf16).reshape(*shape, features)
+
     vector_grads = (
         first_gain_grad, first_shift_grad, query_bias_grad, value_bias_grad, output_bias_grad,
         second_gain_grad, second_shift_grad, contract_bias_grad, expand_bias_grad,
     )
     devices = fs_count * sp_count
     packed = jnp.concatenate([item.reshape(devices, -1) for item in vector_grads], axis=1)
-    packed = scatter(packed.reshape(-1))
+    grads = (contract_grad, expand_grad, joined_grad, output_weight_grad)
+    if fast:
+        layer_output, input_grad, packed, grads = reduce_all(
+            layer_output, input_grad, packed, [item.astype(bf16) for item in grads]
+        )
+    else:
+        layer_output, input_grad = from_own_seqs(layer_output), from_own_seqs(input_grad)
+        scatter = functools.partial(
+            lax.psum_scatter, axis_name=("fs", "sp"), scatter_dimension=0, tiled=True
+        )
+        packed = scatter(packed.reshape(-1))
+        grads = [scatter(item) for item in grads]
+    contract_grad, expand_grad, joined_grad, output_weight_grad = grads
     own_grads, at = [], 0
     for item in vector_grads:
         size = item.shape[0] // devices
@@ -417,16 +839,16 @@
         input_grad,
         g1,
         s1,
-        scatter(joined_grad),
+        joined_grad,
         qb,
         vb,
-        scatter(output_weight_grad),
+        output_weight_grad,
         ob,
         g2,
         s2,
-        scatter(expand_grad),
+        expand_grad,
         eb,
-        scatter(contract_grad),
+        contract_grad,
         cb,
     )
 

time: 1260 us -> 623 us (0.49)
  waiting for transfers between devices: 816 us -> 0 us
  Pallas kernels: 76.4 us -> 486 us
  blocking collectives: 165 us -> 0 us
  starting transfers between devices: 27.5 us -> 0 us
  local copies, waits for them, and re-layouts: 36.4 us -> 20.4 us
  between operations: 15.1 us -> 1.47 us
  matrix products: 106 us -> 93.2 us
    pallas_call x0 -> x6, Pallas kernels: none -> 409 us  [the longest x1 155 us: gather_all(): pl.pallas_call(functools.partial(gather_kernel, count), name='gather_all'...]
    reduce_scatter x4 -> x0, waiting for transfers between devices: 407 us -> none  [per_device(): lax.psum_scatter(item, ('fs', 'sp'), scatter_dimension=0, tiled=True)]
    all_gather x4 -> x0, waiting for transfers between devices: 286 us -> none  [per_device(): gather = lambda item: lax.all_gather(item, 'fs', axis=0, tiled=True)]
    all_to_all x6 -> x0, waiting for transfers between devices: 120 us -> none  [the longest x2 64.3 us: from_heads(): values = lax.all_to_all(values, 'sp', split_axis=2, concat_axis=3)]
    all_to_all x2 -> x0, blocking collectives: 66.7 us -> none  [to_heads(): values = lax.all_to_all(values, 'sp', split_axis=3, concat_axis=2)]
    all_gather x1 -> x0, blocking collectives: 55.8 us -> none  [per_device(): packed = lax.all_gather(jnp.concatenate(vectors), 'fs', axis=0)]
    unnamed x1 -> x0, blocking collectives: 42.3 us -> none
    all_to_all x6 -> x0, starting transfers between devices: 26.7 us -> none  [the longest x2 10 us: to_own_seqs(): lax.all_to_all(values, 'fs', split_axis=0, concat_axis=0)]
  transfers between devices with their start and end apart: 14 -> 0, of which waited for: 10 -> 0; matrix products, arithmetic and copies ran while one was open for 10% -> 0% of each run, Pallas kernels for 6% -> 0%
where the time goes in v2:
time: 623 us; the launch traced here: 614 us
  Pallas kernels  486 us (78%)
  matrix products  93.2 us (15%)
  local copies, waits for them, and re-layouts  20.4 us (3%)
  other arithmetic  13 us (2%)
    pallas_call x1, Pallas kernels, gather_all(): pl.pallas_call(functools.partial(gather_kernel, count), name='gather_all'...  155 us
    pallas_call x1, Pallas kernels, reduce_all(): pl.pallas_call(functools.partial(reduce_kernel, count), name='reduce_all'...  150 us
    pallas_call x4, Pallas kernels, heads_call(): pl.pallas_call(functools.partial(heads_kernel, features, into), name='to_...  104 us
    pallas_call x1, Pallas kernels, attention_backward(): pl.pallas_call(functools.partial(backward_kernel, heads, width, block), n...  45.8 us
    dot_general x4, matrix products, matmul(): return jnp.dot(left_side, right_side, preferred_element_type=f32)  33.6 us
    pallas_call x1, Pallas kernels, attention_forward(): pl.pallas_call(functools.partial(forward_kernel, heads, width, block), na...  30.9 us
    dot_general x4, matrix products, matmul_rt(): lax.dot_general(left_side, right_side, (((1,), (1,)), ((), ())), preferre...  30.5 us
    dot_general x4, matrix products, matmul_lt(): lax.dot_general(left_side, right_side, (((0,), (0,)), ((), ())), preferre...  29.1 us

profile of v2, /device:TPU:0, one launch (start us, length us, event | category | flops | bytes accessed | tf_op | source)
XLA Modules:
  0.0 614.0 jit_solution(16378904816552620847)
XLA Ops:
  8.6 154.5 %gather_all.1 = (bf16[2,4,64,1024]{3,2,1,0:T(8,128)(2,1)}, bf16[2,4,64,1024]{3,2,1,0:T(8,128)(2,1)}, bf16[4,24,128]{2,1,0:T(8,128)(2,1)}, bf16[4,8,32,3072]{3,2,...) custom-call(bf16[4,2,64,1024]{3,2,1,0:T(8,128)(2,1)} %bitcast.132, ...), custom_call_target="tpu_custom_call" | custom-call | tf_op jit(solution)/shard_map/gather_all/pallas_call | solution.py:446
  167.8 7.6 %add_convert_fusion = bf16[512,3072]{1,0:T(8,128)(2,1)} fusion(bf16[512,1024]{1,0:T(8,128)(2,1)S(1)} %bitcast.134, bf16[1024,3072]{1,0:T(8,128)(2,1)} %bitcast.170, f32[3072]{0:T(1024)S(1)} %add.104), kind=kOutput, calls=%fused_computation.16 | convolution fusion | flops 3224371200 | bytes 10498048 | tf_op jit(solution)/shard_map/dot_general | solution.py:35
  175.4 37.0 %to_heads.2 = bf16[2,4,8,64,384]{4,3,2,1,0:T(8,128)(2,1)} custom-call(bf16[2,4,64,3072]{3,2,1,0:T(8,128)(2,1)} %bitcast.127), custom_call_target="tpu_custom_call" | custom-call | tf_op jit(solution)/shard_map/to_heads/pallas_call | solution.py:506
  212.4 30.9 %attention_forward.1 = (bf16[2,2048,128]{2,1,0:T(8,128)(2,1)}, f32[2,2,64,2048]{3,2,1,0:T(8,128)}, f32[2,2,1,2048]{3,2,1,0:T(1,128)}) custom-call(f32[2]{0:T(128)} %dynamic_slice.3.slopes, bf16[2,2048,384]{2,1,0:T(8,128)(2,1)} %bitcast.116), custom_call_target="tpu_custom_call" | custom-call | tf_op jit(solution)/shard_map/attention_forward/pallas_call | solution.py:152
  243.3 15.0 %from_heads.2 = bf16[2,4,64,1024]{3,2,1,0:T(8,128)(2,1)} custom-call(bf16[2,4,8,64,128]{4,3,2,1,0:T(8,128)(2,1)} %bitcast.139), custom_call_target="tpu_custom_call" | custom-call | tf_op jit(solution)/shard_map/from_heads/pallas_call | solution.py:506
  258.4 2.6 fusion.28
  261.4 11.1 %fusion.22 = f32[512,4096]{1,0:T(8,128)} fusion(bf16[1024,4096]{1,0:T(8,128)(2,1)} %bitcast.164, f32[512,1024]{1,0:T(8,128)S(1)} %get-tuple-element.85, f32[1024]{0:T(1024)S(1)} %bitcast.160, f32[1024]{0:T(1024)S(1)} %bitcast.155, f32[512]{0:T(512)S(1)} %fusion.19, f32[512]{0:T(512)S(1)} %broadcast_multiply_fusion.1), kind=kOutput, calls=%fused_computation.77 | convolution fusion | flops 4297588736 | bytes 18886656 | tf_op jit(solution)/shard_map/dot_general | solution.py:35
  272.5 12.3 %add_convert_fusion.2 = bf16[512,1024]{1,0:T(8,128)(2,1)} fusion(f32[512,1024]{1,0:T(8,128)S(1)} %get-tuple-element.85, bf16[4096,1024]{1,0:T(8,128)(2,1)} %bitcast.168, f32[1024]{0:T(1024)S(1)} %bitcast.163, f32[512,4096]{1,0:T(8,128)} %fusion.22, f32[4096]{0:T(1024)S(1)} %bitcast.152), kind=kOutput, calls=%fused_computation.41 | convolution fusion | flops 4317511680 | bytes 19943424 | tf_op jit(solution)/shard_map/dot_general | solution.py:35
  284.9 14.6 %convert_reduce_fusion = (f32[4096]{0:T(1024)S(1)}, bf16[512,4096]{1,0:T(8,128)(2,1)S(1)}) fusion(f32[512,4096]{1,0:T(8,128)} %fusion.22, f32[4096]{0:T(1024)S(1)} %bitcast.153, bf16[512,1024]{1,0:T(8,128)(2,1)S(1)} %bitcast.120, bf16[4096,1024]{1,0:T(8,128)(2,1)} %bitcast.169), kind=kOutput, calls=%fused_computation.11 | convolution fusion | flops 4351586304 | bytes 22052864 | tf_op jit(solution)/shard_map/dot_general | solution.py:45
  299.5 5.0 multiply_reduce_fusion
  307.2 2.3 convolution_convert_fusion.3
  309.5 15.0 %to_heads.3 = bf16[2,4,8,64,128]{4,3,2,1,0:T(8,128)(2,1)} custom-call(bf16[2,4,64,1024]{3,2,1,0:T(8,128)(2,1)} %bitcast.140), custom_call_target="tpu_custom_call" | custom-call | tf_op jit(solution)/shard_map/to_heads/pallas_call | solution.py:506
  324.5 45.8 %attention_backward.1 = bf16[2,2048,384]{2,1,0:T(8,128)(2,1)} custom-call(f32[2]{0:T(128)} %dynamic_slice.3.slopes, bf16[2,2048,384]{2,1,0:T(8,128)(2,1)} %bitcast.117, bf16[2,2048,128]{2,1,0:T(8,128)(2,1)} %bitcast.125, f32[2,2,64,2048]{3,2,1,0:T(8,128)} %get-tuple-element.40.out_t, f32[2,2,1,2048]{3,2,1,0:T(1,128)} %get-tuple-element.41.lse), custom_call_target="tpu_custom_call" | custom-call | tf_op jit(solution)/shard_map/attention_backward/pallas_call | solution.py:257
  370.3 37.5 %from_heads.3 = bf16[2,4,64,3072]{3,2,1,0:T(8,128)(2,1)} custom-call(bf16[2,4,8,64,384]{4,3,2,1,0:T(8,128)(2,1)} %bitcast.119), custom_call_target="tpu_custom_call" | custom-call | tf_op jit(solution)/shard_map/from_heads/pallas_call | solution.py:506
  407.8 8.6 %fusion.23 = (f32[1024]{0:T(1024)S(1)}, f32[512]{0:T(512)S(1)}, f32[512,1024]{1,0:T(8,128)}) fusion(f32[1024]{0:T(1024)S(1)} %bitcast.146, f32[512]{0:T(512)S(1)} %div.45, bf16[2,4,64,1024]{3,2,1,0:T(8,128)(2,1)S(1)} %copy-done, bf16[512,3072]{1,0:T(8,128)(2,1)} %bitcast.118, bf16[1024,3072]{1,0:T(8,128)(2,1)} %bitcast.171), kind=kOutput, calls=%fused_computation.78 | convolution fusion | flops 3224369664 | bytes 12595200 | tf_op jit(solution)/shard_map/dot_general | solution.py:45
  416.6 2.7 fusion.17
  419.3 2.0 add_convert_fusion.1
  421.4 2.6 convert_reduce_fusion.1
  425.4 13.4 %convolution_convert_fusion.1 = bf16[4096,1024]{1,0:T(8,128)(2,1)} fusion(bf16[512,1024]{1,0:T(8,128)(2,1)S(1)} %bitcast.121, f32[512,4096]{1,0:T(8,128)} %fusion.22, f32[4096]{0:T(1024)S(1)} %bitcast.154), kind=kOutput, calls=%fused_computation.14 | convolution fusion | flops 4320133120 | bytes 17842176 | tf_op jit(solution)/shard_map/dot_general | solution.py:39
  438.9 7.5 %convolution_convert_fusion = bf16[1024,4096]{1,0:T(8,128)(2,1)} fusion(bf16[512,4096]{1,0:T(8,128)(2,1)S(1)} %copy-done.23, f32[512,1024]{1,0:T(8,128)S(1)} %copy-done.7, f32[1024]{0:T(1024)S(1)} %bitcast.161, f32[1024]{0:T(1024)S(1)} %bitcast.158, f32[512]{0:T(512)S(1)} %fusion.19, f32[512]{0:T(512)S(1)} %broadcast_multiply_fusion.1), kind=kOutput, calls=%fused_computation.13 | convolution fusion | flops 4301783040 | bytes 14692352 | tf_op jit(solution)/shard_map/dot_general | solution.py:39
  446.4 5.5 bitcast_convert_fusion
  452.0 2.6 convolution_convert_fusion.2
  454.6 150.0 %reduce_all.1 = (bf16[4,2,64,1024]{3,2,1,0:T(8,128)(2,1)}, bf16[4,2,64,1024]{3,2,1,0:T(8,128)(2,1)}, f32[8,128]{1,0:T(8,128)}, f32[128,1024]{1,0:T(8,128)}, f32[...) custom-call(bf16[2,4,64,1024]{3,2,1,0:T(8,128)(2,1)} %bitcast.141, bf16[2,4,64,1024]{3,2,1,0:T(8,128)(2,1)} %bitcast.126, ...), custom_call_target="tpu_custom_call" | custom-call | tf_op jit(solution)/shard_map/reduce_all/pallas_call | solution.py:664
  607.2 2.3 copy.62
  (116 shorter events, 23.8 us)
Async XLA Ops:
  8.6 155.4 %copy-start.21 = (f32[16]{0:T(128)S(1)}, f32[16]{0:T(128)}, u32[]{:S(2)}) copy-start(f32[16]{0:T(128)} %param.30) | copy-start | bytes 196
  163.2 3.4 copy-start
  167.4 8.0 %copy-start.10 = (bf16[2,4,64,1024]{3,2,1,0:T(8,128)(2,1)}, bf16[2,4,64,1024]{3,2,1,0:T(8,128)(2,1)S(1)}, u32[]{:S(2)}) copy-start(bf16[2,4,64,1024]{3,2,1,0:T(8,128)(2,1)S(1)} %fusion.14) | copy-start | bytes 3145732
  212.4 46.0 %copy-start.19 = (bf16[4,8,32,1024]{3,2,1,0:T(8,128)(2,1)S(1)}, bf16[4,8,32,1024]{3,2,1,0:T(8,128)(2,1)}, u32[]{:S(2)}) copy-start(bf16[4,8,32,1024]{3,2,1,0:T(8,128)(2,1)} %get-tuple-element.36) | copy-start | bytes 6291460
  261.0 43.5 %copy-start.6 = (f32[512,1024]{1,0:T(8,128)}, f32[512,1024]{1,0:T(8,128)S(1)}, u32[]{:S(2)}) copy-start(f32[512,1024]{1,0:T(8,128)S(1)} %get-tuple-element.85) | copy-start | bytes 6291460
  261.4 38.1 %slice-start = ((s8[8388608]{0:T(1024)(128)(4,1)}), s8[4194304]{0:T(1024)(128)(4,1)S(1)}, s32[]{:S(2)}) async-start(s8[8388608]{0:T(1024)(128)(4,1)} %bitcast.165), calls=%async_computation | async-start | bytes 8388608
  272.5 12.3 %copy-start.2 = (bf16[2,4,64,1024]{3,2,1,0:T(8,128)(2,1)S(1)}, bf16[2,4,64,1024]{3,2,1,0:T(8,128)(2,1)}, u32[]{:S(2)}) copy-start(bf16[2,4,64,1024]{3,2,1,0:T(8,128)(2,1)} %get-tuple-element.39) | copy-start | bytes 3145732
  272.5 27.0 %slice-start.1 = ((s8[8388608]{0:T(1024)(128)(4,1)}), s8[4194304]{0:T(1024)(128)(4,1)S(1)}, s32[]{:S(2)}) async-start(s8[8388608]{0:T(1024)(128)(4,1)} %bitcast.165), calls=%async_computation.1 | async-start | bytes 8388608
  299.5 5.0 copy-start.22
  307.1 2.4 copy-start.8
  416.5 2.7 copy-start.3
  416.5 2.7 copy-start.5
  421.3 4.1 copy-start.4
  425.4 13.4 %copy-start.7 = (f32[512,1024]{1,0:T(8,128)S(1)}, f32[512,1024]{1,0:T(8,128)}, u32[]{:S(2)}) copy-start(f32[512,1024]{1,0:T(8,128)} %copy-done.6) | copy-start | bytes 6291460
  425.4 13.4 %copy-start.23 = (bf16[512,4096]{1,0:T(8,128)(2,1)S(1)}, bf16[512,4096]{1,0:T(8,128)(2,1)}, u32[]{:S(2)}) copy-start(bf16[512,4096]{1,0:T(8,128)(2,1)} %copy-done.22) | copy-start | bytes 12582916
  438.9 7.6 %copy-start.1 = (bf16[2,4,64,3072]{3,2,1,0:T(8,128)(2,1)S(1)}, bf16[2,4,64,3072]{3,2,1,0:T(8,128)(2,1)}, u32[]{:S(2)}) copy-start(bf16[2,4,64,3072]{3,2,1,0:T(8,128)(2,1)} %from_heads.3) | copy-start | bytes 9437188
  438.9 7.6 %copy-start.11 = (bf16[2,4,64,1024]{3,2,1,0:T(8,128)(2,1)S(1)}, bf16[2,4,64,1024]{3,2,1,0:T(8,128)(2,1)}, u32[]{:S(2)}) copy-start(bf16[2,4,64,1024]{3,2,1,0:T(8,128)(2,1)} %copy-done.10) | copy-start | bytes 3145732
  446.4 5.5 copy-start.9
  446.4 5.5 copy-start.12
  604.6 4.9 copy-start.13
  607.2 3.3 copy-start.16
  607.2 4.1 copy-start.17
  609.5 2.4 copy-start.15
  609.5 3.2 copy-start.14
  (2 other events, 2.5 us)

commit v3 on v1

v3 whole, which is shorter than its diff:
```python
import functools
import math

import jax
import jax.numpy as jnp
from jax import lax
from jax.experimental import pallas as pl
from jax.experimental.pallas import tpu as pltpu
from jax.sharding import PartitionSpec as P

norm_eps = 1e-05
gelu_coef = 0.7978845608028654
masked_value = -1e30
f32 = jnp.float32
bf16 = jnp.bfloat16
MESH = pl.DeviceIdType.MESH
HBM = pl.BlockSpec(memory_space=pl.ANY)
VMEM = pl.BlockSpec(memory_space=pltpu.VMEM)
SMEM = pl.BlockSpec(memory_space=pltpu.SMEM)
vmem_bytes = 60 * 1024 * 1024


def normalize(values, norm_gain, norm_shift):
    center = values - jnp.mean(values, axis=-1, keepdims=True)
    variance = jnp.mean(center * center, axis=-1, keepdims=True)
    return center * lax.rsqrt(variance + norm_eps) * norm_gain + norm_shift


def gelu_tanh(values):
    return (
        0.5 * values * (1.0 + jnp.tanh(gelu_coef * (values + 0.044715 * values * values * values)))
    )


def matmul(left_side, right_side):
    return jnp.dot(left_side, right_side, preferred_element_type=f32)


def matmul_lt(left_side, right_side):
    return lax.dot_general(
        left_side, right_side, (((0,), (0,)), ((), ())), preferred_element_type=f32
    )


def matmul_rt(left_side, right_side):
    return lax.dot_general(
        left_side, right_side, (((1,), (1,)), ((), ())), preferred_element_type=f32
    )


def joined_bias_of(query_bias, value_bias, head_count):
    query_part = query_bias.astype(f32).reshape(head_count, -1)
    value_part = value_bias.astype(f32).reshape(head_count, -1)
    return jnp.stack([query_part, jnp.zeros_like(query_part), value_part], axis=1).reshape(-1)


def split_three(values):
    high = values.astype(bf16).astype(f32)
    rest = values - high
    middle = rest.astype(bf16).astype(f32)
    return high, middle, rest - middle


def key_columns(key_rows, slope, start):
    rows, width = key_rows.shape
    position = (start + lax.broadcasted_iota(jnp.int32, (rows, width), 0)).astype(f32)
    lane = lax.broadcasted_iota(jnp.int32, (rows, width), 1)
    high, middle, low = split_three(slope * position)
    extra = jnp.where(lane == 0, high, jnp.where(lane == 1, middle, jnp.where(lane == 2, low, 0.0)))
    return jnp.concatenate([key_rows.astype(f32), extra], axis=1).astype(bf16)


def query_columns(queries, scale):
    rows, width = queries.shape
    lane = lax.broadcasted_iota(jnp.int32, (rows, width), 1)
    ones = jnp.where(lane < 3, 1.0, 0.0)
    return jnp.concatenate([queries.astype(f32) * scale, ones], axis=1).astype(bf16)


class Forward:
    def __init__(self, heads, width, slopes, qkv, out, out_t, lse, keys, queries, values_t):
        self.heads, self.width, self.slopes, self.qkv, self.out = heads, width, slopes, qkv, out
        self.out_t, self.lse = out_t, lse
        self.keys, self.queries, self.values_t = keys, queries, values_t
        self.blocks = qkv.shape[1]
        self.block = qkv.shape[2] * qkv.shape[3]

    def rows(self, i):
        return pl.ds(pl.multiple_of(i * self.block, self.block), self.block)

    def prepare(self, b):
        width, block, qkv = self.width, self.block, self.qkv
        scale = 1.0 / math.sqrt(width)

        def body(i, _):
            rows = self.rows(i)
            for h in range(self.heads):
                base = h * 3 * width
                query, key, value = [
                    qkv[b, i, :, :, base + n * width : base + (n + 1) * width].reshape(block, width)
                    for n in range(3)
                ]
                self.keys[h, rows, :] = key_columns(key, self.slopes[h], i * block)
                self.queries[h, rows, :] = query_columns(query, scale)
                self.values_t[h, :, rows] = value.astype(f32).T.astype(bf16)
            return 0

        lax.fori_loop(0, self.blocks, body, 0)

    def run(self, b, low, high):
        heads, width, block = self.heads, self.width, self.block

        def one_block(i, _):
            rows = self.rows(i)
            query = [self.queries[h, rows, :] for h in range(heads)]

            def step(j, state, diagonal):
                columns = self.rows(j)
                result = []
                for h in range(heads):
                    top, total, acc = state[h]
                    scores = matmul_rt(self.keys[h, columns, :], query[h])
                    if diagonal:
                        key_at = lax.broadcasted_iota(jnp.int32, (block, block), 0)
                        query_at = lax.broadcasted_iota(jnp.int32, (block, block), 1)
                        scores = jnp.where(key_at <= query_at, scores, masked_value)
                    newest = jnp.maximum(top, jnp.max(scores, axis=0, keepdims=True))
                    shrink = jnp.exp(top - newest)
                    probs = jnp.exp(scores - newest)
                    total = total * shrink + jnp.sum(probs, axis=0, keepdims=True)
                    acc = acc * shrink + matmul(self.values_t[h, :, columns], probs.astype(bf16))
                    result.append((newest, total, acc))
                return tuple(result)

            state = tuple(
                (
                    jnp.full((1, block), masked_value, f32),
                    jnp.zeros((1, block), f32),
                    jnp.zeros((width, block), f32),
                )
                for h in range(heads)
            )
            state = lax.fori_loop(0, i, lambda j, s: step(j, s, False), state)
            state = step(i, state, True)
            finished = []
            for h in range(heads):
                top, total, acc = state[h]
                result = acc / total
                self.out_t[b, h, :, rows] = result
                self.lse[b, h, :, rows] = top + jnp.log(total)
                finished.append(result)
            joined = finished[0] if heads == 1 else jnp.concatenate(finished, axis=0)
            self.out[b, i] = joined.T.astype(bf16).reshape(self.out.shape[2:])
            return 0

        lax.fori_loop(low, high, one_block, 0)


def forward_kernel(heads, width, *refs):
    attention = Forward(heads, width, *refs)

    def one_seq(b, _):
        attention.prepare(b)
        attention.run(b, 0, attention.blocks)
        return 0

    lax.fori_loop(0, attention.qkv.shape[0], one_seq, 0)


def saved_shapes(seqs, length, heads, width):
    return (
        jax.ShapeDtypeStruct((seqs, heads, width, length), f32),
        jax.ShapeDtypeStruct((seqs, heads, 1, length), f32),
    )


def forward_scratch(length, heads, width):
    return [
        pltpu.VMEM((heads, length, 2 * width), bf16),
        pltpu.VMEM((heads, length, 2 * width), bf16),
        pltpu.VMEM((heads, width, length), bf16),
    ]


def attention_forward(qkv, slopes, heads, width):
    seqs, blocks, ranks, piece, _ = qkv.shape
    length = blocks * ranks * piece
    return pl.pallas_call(
        functools.partial(forward_kernel, heads, width),
        name="attention_forward",
        out_shape=(
            jax.ShapeDtypeStruct((seqs, blocks, ranks, piece, heads * width), bf16),
            *saved_shapes(seqs, length, heads, width),
        ),
        in_specs=[SMEM, VMEM],
        out_specs=(VMEM, VMEM, VMEM),
        scratch_shapes=forward_scratch(length, heads, width),
        compiler_params=pltpu.CompilerParams(vmem_limit_bytes=vmem_bytes),
    )(slopes, qkv)


class Backward:
    def __init__(
        self, heads, width, slopes, qkv, diff, out_t, lse, joined,
        keys, queries, keys_t, values, diffs, delta, query_acc,
    ):
        self.heads, self.width, self.slopes, self.qkv, self.diff = heads, width, slopes, qkv, diff
        self.out_t, self.lse, self.joined = out_t, lse, joined
        self.keys, self.queries, self.keys_t, self.values = keys, queries, keys_t, values
        self.diffs, self.delta, self.query_acc = diffs, delta, query_acc
        self.blocks = qkv.shape[1]
        self.block = qkv.shape[2] * qkv.shape[3]

    def rows(self, i):
        return pl.ds(pl.multiple_of(i * self.block, self.block), self.block)

    def prepare(self, b):
        width, block, qkv = self.width, self.block, self.qkv
        scale = 1.0 / math.sqrt(width)

        def body(i, _):
            rows = self.rows(i)
            for h in range(self.heads):
                base = h * 3 * width
                query, key, value = [
                    qkv[b, i, :, :, base + n * width : base + (n + 1) * width].reshape(block, width)
                    for n in range(3)
                ]
                self.keys[h, rows, :] = key_columns(key, self.slopes[h], i * block)
                self.keys_t[h, :, rows] = key.astype(f32).T.astype(bf16)
                self.queries[h, rows, :] = query_columns(query, scale)
                self.values[h, rows, :] = value
                part = self.diff[b, i, :, :, h * width : (h + 1) * width].reshape(block, width)
                self.diffs[h, rows, :] = part
                self.delta[h, :, rows] = jnp.sum(
                    part.astype(f32).T * self.out_t[b, h, :, rows], axis=0, keepdims=True
                )
                self.query_acc[h, :, rows] = jnp.zeros((width, block), f32)
            return 0

        lax.fori_loop(0, self.blocks, body, 0)

    def run(self, b, low, high):
        heads, width, block = self.heads, self.width, self.block
        tail = self.joined.shape[2:4] + (width,)

        def one_block(j, _):
            columns = self.rows(j)

            def step(i, state, diagonal):
                rows = self.rows(i)
                result = []
                for h in range(heads):
                    key_acc, value_acc = state[h]
                    query = self.queries[h, rows, :]
                    part = self.diffs[h, rows, :]
                    scores = matmul_rt(self.keys[h, columns, :], query)
                    probs = jnp.exp(scores - self.lse[b, h, :, rows])
                    if diagonal:
                        key_at = lax.broadcasted_iota(jnp.int32, (block, block), 0)
                        query_at = lax.broadcasted_iota(jnp.int32, (block, block), 1)
                        probs = jnp.where(key_at <= query_at, probs, 0.0)
                    prob_diff = matmul_rt(self.values[h, columns, :], part)
                    score_diff = (probs * (prob_diff - self.delta[h, :, rows])).astype(bf16)
                    value_acc = value_acc + matmul(probs.astype(bf16), part)
                    key_acc = key_acc + matmul(score_diff, query)
                    self.query_acc[h, :, rows] += matmul(self.keys_t[h, :, columns], score_diff)
                    result.append((key_acc, value_acc))
                return tuple(result)

            state = tuple(
                (jnp.zeros((block, 2 * width), f32), jnp.zeros((block, width), f32))
                for h in range(heads)
            )
            state = step(j, state, True)
            state = lax.fori_loop(j + 1, self.blocks, lambda i, s: step(i, s, False), state)
            for h in range(heads):
                base = (h * 3 + 1) * width
                key_acc, value_acc = state[h]
                self.joined[b, j, :, :, base : base + width] = (
                    key_acc[:, :width].astype(bf16).reshape(tail)
                )
                self.joined[b, j, :, :, base + width : base + 2 * width] = value_acc.astype(
                    bf16
                ).reshape(tail)
            return 0

        lax.fori_loop(low, high, one_block, 0)

    def finish(self, b):
        width = self.width
        scale = 1.0 / math.sqrt(width)
        tail = self.joined.shape[2:4] + (width,)

        def body(i, _):
            for h in range(self.heads):
                base = h * 3 * width
                result = (self.query_acc[h, :, self.rows(i)] * scale).T.astype(bf16)
                self.joined[b, i, :, :, base : base + width] = result.reshape(tail)
            return 0

        lax.fori_loop(0, self.blocks, body, 0)


def backward_kernel(heads, width, *refs):
    attention = Backward(heads, width, *refs)

    def one_seq(b, _):
        attention.prepare(b)
        attention.run(b, 0, attention.blocks)
        attention.finish(b)
        return 0

    lax.fori_loop(0, attention.qkv.shape[0], one_seq, 0)


def backward_scratch(length, heads, width):
    return [
        pltpu.VMEM((heads, length, 2 * width), bf16),
        pltpu.VMEM((heads, length, 2 * width), bf16),
        pltpu.VMEM((heads, width, length), bf16),
        pltpu.VMEM((heads, length, width), bf16),
        pltpu.VMEM((heads, length, width), bf16),
        pltpu.VMEM((heads, 1, length), f32),
        pltpu.VMEM((heads, width, length), f32),
    ]


def attention_backward(qkv, diff, out_t, lse, slopes, heads, width):
    length = qkv.shape[1] * qkv.shape[2] * qkv.shape[3]
    return pl.pallas_call(
        functools.partial(backward_kernel, heads, width),
        name="attention_backward",
        out_shape=jax.ShapeDtypeStruct(qkv.shape, bf16),
        in_specs=[SMEM, VMEM, VMEM, VMEM, VMEM],
        out_specs=VMEM,
        scratch_shapes=backward_scratch(length, heads, width),
        compiler_params=pltpu.CompilerParams(vmem_limit_bytes=vmem_bytes),
    )(slopes, qkv, diff, out_t, lse)


def to_own_seqs(values):
    seqs, piece, features = values.shape
    parts = lax.axis_size("fs")
    values = values.reshape(parts, seqs // parts, piece, features)
    return lax.all_to_all(values, "fs", split_axis=0, concat_axis=0).transpose(1, 0, 2, 3)


def from_own_seqs(values):
    own, parts, piece, features = values.shape
    values = lax.all_to_all(values.transpose(1, 0, 2, 3), "fs", split_axis=0, concat_axis=0)
    return values.reshape(parts * own, piece, features)


def to_heads(values):
    own, parts, piece, features = values.shape
    ranks = lax.axis_size("sp")
    values = values.reshape(own, parts, piece, ranks, features // ranks)
    return lax.all_to_all(values, "sp", split_axis=3, concat_axis=2)


def from_heads(values):
    own, parts, ranks, piece, features = values.shape
    values = lax.all_to_all(values, "sp", split_axis=2, concat_axis=3)
    return values.reshape(own, parts, piece, ranks * features)


class Copies:
    def __init__(self, send, recv):
        self.send, self.recv, self.used, self.made = send, recv, 0, []

    def start(self, source, target, device):
        copy = pltpu.make_async_remote_copy(
            src_ref=source,
            dst_ref=target,
            send_sem=self.send.at[self.used],
            recv_sem=self.recv.at[self.used],
            device_id=device,
            device_id_type=MESH,
        )
        self.used += 1
        self.made.append(copy)
        copy.start()
        return copy

    def finish(self):
        assert self.used == self.send.shape[0]
        for copy in self.made:
            copy.wait_send()


class Locals:
    def __init__(self, sems):
        self.sems, self.used = sems, 0

    def start(self, source, target):
        copy = pltpu.make_async_copy(source, target, self.sems.at[self.used])
        self.used += 1
        copy.start()
        return copy


def arrive(copies):
    for copy in copies:
        copy.wait_recv()


def greet(devices):
    barrier = pltpu.get_barrier_semaphore()
    for device in devices:
        pl.semaphore_signal(barrier, inc=1, device_id=device, device_id_type=MESH)
    pl.semaphore_wait(barrier, len(devices))


def place():
    z, s = lax.axis_index("fs"), lax.axis_index("sp")
    along_x = s + 2 - 4 * ((s // 2) % 2)
    along_y = s + 4 - 8 * (s // 4)
    partner = s + 1 - 2 * (s % 2)
    return z, s, along_x, along_y, partner


def line_of(z, s):
    return [(lax.rem(z + k, 4), s) for k in range(1, 4)]


def plane_of(z, s):
    return [(z, lax.rem(s + d, 8)) for d in range(1, 8)]


class Gather:
    copies_each = 45

    def __init__(self, weights, wholes, kept, copies, locals_):
        self.weights, self.wholes, self.kept = weights, wholes, kept
        self.copies, self.locals_ = copies, locals_
        self.z, self.s, self.along_x, self.along_y, self.partner = place()
        self.lines = line_of(self.z, self.s)
        self.first, self.second, self.third = {}, {}, {}
        self.waiting = []

    def load(self):
        self.loads = [self.locals_.start(w, k) for w, k in zip(self.weights, self.kept)]

    def keep(self):
        for copy in self.loads:
            copy.wait()
        self.own = [
            self.locals_.start(k, whole.at[self.z]) for k, whole in zip(self.kept, self.wholes)
        ]

    def start(self, t):
        self.first[t] = [
            self.copies.start(self.weights[t].at[self.s], self.wholes[t].at[self.z, self.s], to)
            for to in self.lines
        ]

    def refs(self, t):
        whole = self.wholes[t]
        half = whole.shape[2] // 2

        def same(k, rank, part, to):
            rows = pl.ds(part * half, half)
            where = (k, rank, rows)
            return self.copies.start(whole.at[where], whole.at[where], (self.z, to))

        return same

    def exchange(self, t):
        same = self.refs(t)
        arrive(self.first[t])
        step = []
        for k, _ in self.lines:
            step.append(same(k, self.s, 0, self.along_x))
            step.append(same(k, self.s, 1, self.along_y))
        for k, _ in self.lines:
            self.waiting.append(same(k, self.s, 0, self.partner))
            self.waiting.append(same(k, self.s, 1, self.partner))
        self.second[t] = step

    def spread(self, t):
        same = self.refs(t)
        arrive(self.second[t])
        step = []
        for k, _ in self.lines:
            step.append(same(k, self.s, 0, self.along_y))
            step.append(same(k, self.s, 1, self.along_x))
            step.append(same(k, self.along_x, 0, self.along_y))
            step.append(same(k, self.along_y, 1, self.along_x))
        for k, _ in self.lines:
            self.waiting.append(same(k, self.along_x, 0, self.partner))
            self.waiting.append(same(k, self.along_y, 1, self.partner))
        self.third[t] = step

    def share(self, t):
        same = self.refs(t)
        arrive(self.third[t])
        diagonal = self.along_x + self.along_y - self.s
        for k, _ in self.lines:
            self.waiting.append(same(k, self.along_y, 0, self.partner))
            self.waiting.append(same(k, self.along_x, 1, self.partner))
            self.waiting.append(same(k, diagonal, 0, self.partner))
            self.waiting.append(same(k, diagonal, 1, self.partner))

    def finish(self):
        arrive(self.waiting)
        for copy in self.own:
            copy.wait()


def add_blocks(steps, block_of):
    def body(i, _):
        target, other = block_of(i)
        target[...] = (target[...].astype(f32) + other[...].astype(f32)).astype(target.dtype)
        return 0

    lax.fori_loop(0, steps, body, 0)


class Reduce:
    copies_each = 10

    def __init__(self, grads, outs, bufs, copies, locals_):
        self.grads, self.outs, self.copies, self.locals_ = grads, outs, copies, locals_
        self.bufs = [bufs[7 * t : 7 * t + 7] for t in range(len(grads))]
        self.z, self.s, along_x, along_y, partner = place()
        self.core, self.chip = self.s % 2, self.s // 2
        self.x, self.y = self.chip % 2, self.chip // 2
        self.chip_x, self.chip_y = along_x // 2, along_y // 2
        self.lines = line_of(self.z, self.s)
        self.to_x, self.to_y, self.to_core = [(self.z, to) for to in (along_x, along_y, partner)]
        self.first, self.second, self.third, self.fourth = {}, {}, {}, {}

    def load(self):
        self.loads = [
            self.locals_.start(g.at[:, :, self.core], b[0]) for g, b in zip(self.grads, self.bufs)
        ]

    def start(self, t):
        self.first[t] = self.copies.start(
            self.grads[t].at[:, :, 1 - self.core], self.bufs[t][1], self.to_core
        )

    def halves(self, t):
        half = self.bufs[t][0].shape[2] // 2
        return pl.ds(0, half), pl.ds(half, half)

    def exchange(self, t):
        own, from_core, from_x, from_y = self.bufs[t][:4]
        low, high = self.halves(t)
        self.loads[t].wait()
        arrive([self.first[t]])
        add_blocks(16, lambda i: (own.at[i // 4, i % 4], from_core.at[i // 4, i % 4]))
        step = []
        for k in range(2):
            step.append(
                self.copies.start(own.at[:, 2 * k + 1 - self.x, low], from_x.at[:, k], self.to_x)
            )
            step.append(
                self.copies.start(
                    own.at[:, 2 * (1 - self.y) + k, high], from_y.at[:, k], self.to_y
                )
            )
        self.second[t] = step

    def spread(self, t):
        own, _, from_x, from_y, late_y, late_x, _ = self.bufs[t]
        low, high = self.halves(t)
        arrive(self.second[t])
        add_blocks(
            8, lambda i: (own.at[i // 2, 2 * (i % 2) + self.x, low], from_x.at[i // 2, i % 2])
        )
        add_blocks(
            8, lambda i: (own.at[i // 2, 2 * self.y + i % 2, high], from_y.at[i // 2, i % 2])
        )
        self.third[t] = [
            self.copies.start(own.at[:, self.chip_y, low], late_y, self.to_y),
            self.copies.start(own.at[:, self.chip_x, high], late_x, self.to_x),
        ]

    def send(self, t):
        own, _, _, _, late_y, late_x, from_z = self.bufs[t]
        low, high = self.halves(t)
        arrive(self.third[t])
        add_blocks(4, lambda i: (own.at[i, self.chip, low], late_y.at[i]))
        add_blocks(4, lambda i: (own.at[i, self.chip, high], late_x.at[i]))
        self.fourth[t] = [
            self.copies.start(own.at[to[0], self.chip], from_z.at[k], to)
            for k, to in enumerate(self.lines)
        ]

    def finish(self, t):
        own, from_z = self.bufs[t][0], self.bufs[t][6]
        arrive(self.fourth[t])
        total = own[self.z, self.chip].astype(f32)
        for k in range(3):
            total = total + from_z[k].astype(f32)
        self.outs[t][...] = total


def reduce_scratch(cut):
    scratch = []
    for item in cut:
        rows, columns = item.shape[3:]
        half = rows // 2
        scratch += [
            pltpu.VMEM((4, 4, rows, columns), bf16),
            pltpu.VMEM((4, 4, rows, columns), bf16),
            pltpu.VMEM((4, 2, half, columns), bf16),
            pltpu.VMEM((4, 2, half, columns), bf16),
            pltpu.VMEM((4, half, columns), bf16),
            pltpu.VMEM((4, half, columns), bf16),
            pltpu.VMEM((3, rows, columns), bf16),
        ]
    return scratch


def split_grad(item):
    return item.reshape(4, 4, 2, item.shape[0] // 32, item.shape[1])


def semaphores(remote, local):
    return [pltpu.SemaphoreType.DMA((n,)) for n in (remote, remote, local)]


def remote_call(kernel, name, collective, **options):
    return pl.pallas_call(
        kernel,
        name=name,
        compiler_params=pltpu.CompilerParams(
            collective_id=collective, has_side_effects=True, vmem_limit_bytes=vmem_bytes
        ),
        **options,
    )


def begin_kernel(
    tokens, vector, weight, tokens_out, vector_out, whole,
    tokens_own, vector_own, kept, send, recv, local,
):
    z, s, along_x, along_y, partner = place()
    lines = line_of(z, s)
    copies, locals_ = Copies(send, recv), Locals(local)
    gather = Gather([weight], [whole], [kept], copies, locals_)
    gather.load()
    own = [locals_.start(tokens.at[z], tokens_own), locals_.start(vector, vector_own)]
    greet(lines + [(z, to) for to in (along_x, along_y, partner)])
    waiting = []
    gather.start(0)
    for to in lines:
        waiting.append(copies.start(tokens.at[to[0]], tokens_out.at[:, z], to))
        waiting.append(copies.start(vector, vector_out.at[z], to))
    for copy in own:
        copy.wait()
    own = [
        locals_.start(tokens_own, tokens_out.at[:, z]),
        locals_.start(vector_own, vector_out.at[z]),
    ]
    gather.keep()
    gather.exchange(0)
    gather.spread(0)
    gather.share(0)
    gather.finish()
    arrive(waiting)
    copies.finish()
    for copy in own:
        copy.wait()


def begin(tokens, vector, weight):
    seqs, piece, features = tokens.shape
    own = seqs // 4
    vector = vector.reshape(-1, 128)
    cut = weight.reshape(8, weight.shape[0] // 8, weight.shape[1])
    out = remote_call(
        begin_kernel,
        "begin",
        0,
        out_shape=(
            jax.ShapeDtypeStruct((own, 4, piece, features), bf16),
            jax.ShapeDtypeStruct((4, *vector.shape), bf16),
            jax.ShapeDtypeStruct((4, *cut.shape), bf16),
        ),
        in_specs=[HBM] * 3,
        out_specs=(HBM,) * 3,
        scratch_shapes=[
            pltpu.VMEM((own, piece, features), bf16),
            pltpu.VMEM(vector.shape, bf16),
            pltpu.VMEM(cut.shape, bf16),
            *semaphores(6 + Gather.copies_each, 6),
        ],
    )(tokens.reshape(4, own, piece, features), vector, cut)
    return out[0], out[1].reshape(4, -1), out[2].reshape(4 * weight.shape[0], -1)


def columns_of(rank, features):
    return pl.ds(pl.multiple_of(rank * features, 128), features)


def forward_fused_kernel(
    heads, width, count, slopes, source, upstream, *refs
):
    weights, refs = refs[:count], refs[count:]
    qkv_out, attended, out_t, lse, upstream_out = refs[:5]
    wholes, refs = refs[5 : 5 + count], refs[5 + count :]
    qkv, result, upstream_own = refs[:3]
    attention = Forward(heads, width, slopes, qkv, result, out_t, lse, *refs[3:6])
    kept, (send, recv, local) = refs[6 : 6 + count], refs[6 + count :]
    z, s, along_x, along_y, partner = place()
    lines, plane = line_of(z, s), plane_of(z, s)
    copies, locals_ = Copies(send, recv), Locals(local)
    gather = Gather(weights, wholes, kept, copies, locals_)
    features = heads * width

    gather.load()
    own = [
        locals_.start(source.at[:, :, :, columns_of(s, 3 * features)], qkv.at[:, :, s]),
        locals_.start(upstream.at[z], upstream_own),
    ]
    greet(lines + plane)
    arriving = [
        copies.start(source.at[:, :, :, columns_of(to[1], 3 * features)], qkv.at[:, :, s], to)
        for to in plane
    ]
    for t in range(count):
        gather.start(t)
    waiting = [copies.start(upstream.at[to[0]], upstream_out.at[:, z], to) for to in lines]
    for copy in own:
        copy.wait()
    finishing = [locals_.start(upstream_own, upstream_out.at[:, z])]
    gather.keep()
    arrive(arriving)
    finishing.append(locals_.start(qkv, qkv_out))

    def hand_back(b):
        for to in plane:
            waiting.append(
                copies.start(
                    result.at[b, :, to[1]], attended.at[b, :, :, columns_of(s, features)], to
                )
            )
        finishing.append(
            locals_.start(result.at[b, :, s], attended.at[b, :, :, columns_of(s, features)])
        )

    gather.exchange(0)
    gather.exchange(1)
    attention.prepare(0)
    attention.run(0, 0, 3)
    gather.spread(0)
    gather.exchange(2)
    attention.run(0, 3, 4)
    hand_back(0)
    gather.spread(1)
    attention.prepare(1)
    attention.run(1, 0, 3)
    gather.share(0)
    gather.spread(2)
    attention.run(1, 3, 4)
    hand_back(1)
    gather.share(1)
    gather.share(2)
    gather.finish()
    arrive(waiting)
    copies.finish()
    for copy in finishing:
        copy.wait()


def forward_fused(joined_all, upstream, weights, slopes, heads, width):
    own, parts, piece, columns = joined_all.shape
    features = heads * width
    length = parts * 8 * piece
    count = len(weights)
    cut = [item.reshape(8, item.shape[0] // 8, item.shape[1]) for item in weights]
    seq_shape = (own, parts, piece, 8 * features)
    qkv_shape = (own, parts, 8, piece, 3 * features)
    out = remote_call(
        functools.partial(forward_fused_kernel, heads, width, count),
        "forward_fused",
        1,
        out_shape=(
            jax.ShapeDtypeStruct(qkv_shape, bf16),
            jax.ShapeDtypeStruct(seq_shape, bf16),
            *saved_shapes(own, length, heads, width),
            jax.ShapeDtypeStruct(seq_shape, bf16),
            *[jax.ShapeDtypeStruct((4, *item.shape), bf16) for item in cut],
        ),
        in_specs=[SMEM] + [HBM] * (2 + count),
        out_specs=(HBM, HBM, VMEM, VMEM, HBM) + (HBM,) * count,
        scratch_shapes=[
            pltpu.VMEM(qkv_shape, bf16),
            pltpu.VMEM((own, parts, 8, piece, features), bf16),
            pltpu.VMEM((own, piece, 8 * features), bf16),
            *forward_scratch(length, heads, width),
            *[pltpu.VMEM(item.shape, bf16) for item in cut],
            *semaphores(7 + 3 + 14 + count * Gather.copies_each, 2 * count + 6),
        ],
    )(slopes, joined_all, upstream.reshape(parts, own, piece, 8 * features), *cut)
    wholes = [
        whole.reshape(4 * item.shape[0], item.shape[1]) for whole, item in zip(out[5:], weights)
    ]
    return out[0], out[1], (out[2], out[3]), out[4], wholes


def backward_fused_kernel(heads, width, count, *refs):
    slopes, diff_in, qkv_in, out_t_in, lse_in, layer_output = refs[:6]
    grads, refs = refs[6 : 6 + count], refs[6 + count :]
    joined_out, layer_out = refs[:2]
    outs, refs = refs[2 : 2 + count], refs[2 + count :]
    diff, qkv, out_t, lse, joined, layer_own = refs[:6]
    attention = Backward(heads, width, slopes, qkv, diff, out_t, lse, joined, *refs[6:13])
    bufs, (send, recv, local) = refs[13 : 13 + 7 * count], refs[13 + 7 * count :]
    z, s, along_x, along_y, partner = place()
    lines, plane = line_of(z, s), plane_of(z, s)
    copies, locals_ = Copies(send, recv), Locals(local)
    features = heads * width
    reduce = Reduce(grads, outs, bufs, copies, locals_)

    own = [locals_.start(diff_in.at[:, :, :, columns_of(s, features)], diff.at[:, :, s])]
    own += [locals_.start(a, b) for a, b in ((qkv_in, qkv), (out_t_in, out_t), (lse_in, lse))]
    reduce.load()
    layer_load = locals_.start(layer_output.at[:, z], layer_own)
    greet(lines + plane)
    arriving = [
        copies.start(diff_in.at[:, :, :, columns_of(to[1], features)], diff.at[:, :, s], to)
        for to in plane
    ]
    for t in range(count):
        reduce.start(t)
    waiting = [copies.start(layer_output.at[:, to[0]], layer_out.at[z], to) for to in lines]
    finishing = []

    def hand_back(b):
        for to in plane:
            waiting.append(
                copies.start(
                    joined.at[b, :, to[1]], joined_out.at[b, :, :, columns_of(s, 3 * features)], to
                )
            )
        finishing.append(
            locals_.start(joined.at[b, :, s], joined_out.at[b, :, :, columns_of(s, 3 * features)])
        )

    reduce.exchange(0)
    layer_load.wait()
    finishing.append(locals_.start(layer_own, layer_out.at[z]))
    for copy in own:
        copy.wait()
    arrive(arriving)
    attention.prepare(0)
    attention.run(0, 0, 1)
    reduce.exchange(1)
    attention.run(0, 1, 4)
    reduce.spread(0)
    attention.finish(0)
    hand_back(0)
    attention.prepare(1)
    attention.run(1, 0, 1)
    reduce.exchange(2)
    reduce.spread(1)
    attention.run(1, 1, 4)
    attention.finish(1)
    reduce.spread(2)
    reduce.send(0)
    hand_back(1)
    reduce.send(1)
    reduce.send(2)
    for t in range(count):
        reduce.finish(t)
    arrive(waiting)
    copies.finish()
    for copy in finishing:
        copy.wait()


def backward_fused(attended_diff, qkv, saved, layer_output, grads, slopes, heads, width):
    own, parts, piece, columns = attended_diff.shape
    features = heads * width
    length = parts * 8 * piece
    cut = [split_grad(item) for item in grads]
    count = len(cut)
    out = remote_call(
        functools.partial(backward_fused_kernel, heads, width, count),
        "backward_fused",
        2,
        out_shape=(
            jax.ShapeDtypeStruct((own, parts, piece, 24 * features), bf16),
            jax.ShapeDtypeStruct((parts, own, piece, columns), bf16),
            *[jax.ShapeDtypeStruct(item.shape[3:], f32) for item in cut],
        ),
        in_specs=[SMEM] + [HBM] * (5 + count),
        out_specs=(HBM, HBM) + (VMEM,) * count,
        scratch_shapes=[
            pltpu.VMEM((own, parts, 8, piece, features), bf16),
            pltpu.VMEM(qkv.shape, bf16),
            *[pltpu.VMEM(item.shape, f32) for item in saved],
            pltpu.VMEM(qkv.shape, bf16),
            pltpu.VMEM((own, piece, columns), bf16),
            *backward_scratch(length, heads, width),
            *reduce_scratch(cut),
            *semaphores(7 + 3 + 14 + count * Reduce.copies_each, count + 8),
        ],
    )(slopes, attended_diff, qkv, *saved, layer_output, *cut)
    return out[0], out[1].reshape(parts * own, piece, columns), out[2:]


def end_kernel(input_grad, vector, grad, input_out, vector_out, out, *refs):
    input_own, ranks, plane_sum, others = refs[:4]
    bufs, (send, recv, local) = refs[4:11], refs[11:]
    z, s, _, _, _ = place()
    lines, plane = line_of(z, s), plane_of(z, s)
    copies, locals_ = Copies(send, recv), Locals(local)
    reduce = Reduce([grad], [out], bufs, copies, locals_)
    reduce.load()
    load = locals_.start(input_grad.at[:, z], input_own)
    load_vector = locals_.start(vector.at[:, s], ranks.at[0])
    greet(lines + plane)
    reduce.start(0)
    waiting = [copies.start(input_grad.at[:, to[0]], input_out.at[z], to) for to in lines]
    vectors = [
        copies.start(vector.at[:, to[1]], ranks.at[d + 1], to) for d, to in enumerate(plane)
    ]
    load.wait()
    keep = locals_.start(input_own, input_out.at[z])
    reduce.exchange(0)
    load_vector.wait()
    arrive(vectors)
    total = ranks[0]
    for d in range(1, 8):
        total = total + ranks[d]
    plane_sum[...] = total
    vectors = [
        copies.start(plane_sum.at[to[0]], others.at[k], to) for k, to in enumerate(lines)
    ]
    reduce.spread(0)
    reduce.send(0)
    arrive(vectors)
    total = plane_sum[z]
    for k in range(3):
        total = total + others[k]
    vector_out[...] = total
    reduce.finish(0)
    arrive(waiting)
    copies.finish()
    keep.wait()


def end(input_grad, vector, grad):
    own, parts, piece, features = input_grad.shape
    lanes = vector.shape[-1]
    padded = -(-lanes // 1024) * 1024
    vector = jnp.pad(vector, ((0, 0), (0, padded - lanes))).reshape(4, 8, padded // 128, 128)
    cut = split_grad(grad)
    out = remote_call(
        end_kernel,
        "end",
        3,
        out_shape=(
            jax.ShapeDtypeStruct((parts, own, piece, features), bf16),
            jax.ShapeDtypeStruct(vector.shape[2:], f32),
            jax.ShapeDtypeStruct(cut.shape[3:], f32),
        ),
        in_specs=[HBM] * 3,
        out_specs=(HBM, VMEM, VMEM),
        scratch_shapes=[
            pltpu.VMEM((own, piece, features), bf16),
            pltpu.VMEM((8, 4, padded // 128, 128), f32),
            pltpu.VMEM((4, padded // 128, 128), f32),
            pltpu.VMEM((3, padded // 128, 128), f32),
            *reduce_scratch([cut]),
            *semaphores(3 + 7 + 3 + Reduce.copies_each, 4),
        ],
    )(input_grad, vector, cut)
    return out[0].reshape(parts * own, piece, features), out[1].reshape(-1)[:lanes], out[2]


def per_device(
    layer_input,
    first_gain,
    first_shift,
    joined_weight,
    query_bias,
    value_bias,
    output_weight,
    output_bias,
    second_gain,
    second_shift,
    expand_weight,
    expand_bias,
    contract_weight,
    contract_bias,
    alibi_slopes,
    upstream,
):
    seqs, piece, features = layer_input.shape
    fs_count = lax.axis_size("fs")
    sp_count = lax.axis_size("sp")
    head_count = alibi_slopes.shape[0]
    width = features // head_count
    heads = head_count // sp_count
    rows = seqs * piece
    own = seqs // fs_count
    shape = (own, fs_count, piece)
    slopes = lax.dynamic_slice_in_dim(alibi_slopes, lax.axis_index("sp") * heads, heads)

    vectors = (
        first_gain, first_shift, query_bias, value_bias, output_bias,
        second_gain, second_shift, contract_bias, expand_bias,
    )
    fast = (fs_count, sp_count) == (4, 8) and own >= 1
    weights = (output_weight, expand_weight, contract_weight)
    gather = lambda item: lax.all_gather(item, "fs", axis=0, tiled=True)
    if fast:
        tokens, packed, joined_full = begin(layer_input, jnp.concatenate(vectors), joined_weight)
    else:
        tokens, joined_full = to_own_seqs(layer_input), gather(joined_weight)
        packed = lax.all_gather(jnp.concatenate(vectors), "fs", axis=0)
    tokens = tokens.reshape(rows, features).astype(f32)
    whole, at = [], 0
    for item in vectors:
        whole.append(packed[:, at : at + item.shape[0]].reshape(-1))
        at += item.shape[0]
    gain_one, shift_one, qbias, vbias, obias, gain_two, shift_two, cbias, ebias = [
        item.astype(f32) for item in whole
    ]

    normed_f, norm_back_one = jax.vjp(normalize, tokens, gain_one, shift_one)
    normed = normed_f.astype(bf16)
    joined_all = (matmul(normed, joined_full) + joined_bias_of(qbias, vbias, head_count)).astype(
        bf16
    )
    joined_all = joined_all.reshape(*shape, 3 * features)
    if fast:
        qkv, attended, saved, upstream_low, weights = forward_fused(
            joined_all, upstream, weights, slopes, heads, width
        )
    else:
        qkv = to_heads(joined_all)
        attended, *saved = attention_forward(qkv, slopes, heads, width)
        attended, upstream_low = from_heads(attended), to_own_seqs(upstream)
        weights = [gather(item) for item in weights]
    out_full, expand_full, contract_full = weights
    attended = attended.reshape(rows, features)
    upstream_low = upstream_low.reshape(rows, features)

    residual = tokens + (matmul(attended, out_full) + obias)
    second_f, norm_back_two = jax.vjp(normalize, residual, gain_two, shift_two)
    second = second_f.astype(bf16)
    expanded = matmul(second, expand_full) + ebias
    activated_f, gelu_back = jax.vjp(gelu_tanh, expanded)
    activated = activated_f.astype(bf16)
    result = residual + (matmul(activated, contract_full) + cbias)
    layer_output = result.astype(bf16).reshape(*shape, features)

    upstream_f = upstream_low.astype(f32)
    contract_grad = matmul_lt(activated, upstream_low)
    contract_bias_grad = jnp.sum(upstream_f, axis=0)
    act_grad = matmul_rt(upstream_low, contract_full)
    expand_diff = gelu_back(act_grad)[0].astype(bf16)
    expand_grad = matmul_lt(second, expand_diff)
    expand_bias_grad = jnp.sum(expand_diff.astype(f32), axis=0)
    second_back = matmul_rt(expand_diff, expand_full)
    resid_part, second_gain_grad, second_shift_grad = norm_back_two(second_back)
    residual_grad = upstream_f + resid_part

    branch_diff = residual_grad.astype(bf16)
    output_weight_grad = matmul_lt(attended, branch_diff)
    output_bias_grad = jnp.sum(branch_diff.astype(f32), axis=0)
    attended_diff = matmul_rt(branch_diff, out_full).astype(bf16)
    attended_diff = attended_diff.reshape(*shape, features)
    grads = (contract_grad, expand_grad, output_weight_grad)
    scatter = functools.partial(
        lax.psum_scatter, axis_name=("fs", "sp"), scatter_dimension=0, tiled=True
    )
    if fast:
        joined_diff, layer_output, grads = backward_fused(
            attended_diff, qkv, saved, layer_output, [item.astype(bf16) for item in grads],
            slopes, heads, width,
        )
    else:
        joined_diff = attention_backward(
            qkv, to_heads(attended_diff), *saved, slopes, heads, width
        )
        joined_diff, layer_output = from_heads(joined_diff), from_own_seqs(layer_output)
        grads = [scatter(item) for item in grads]
    contract_grad, expand_grad, output_weight_grad = grads
    joined_diff = joined_diff.reshape(rows, 3 * features)

    joined_grad = matmul_lt(normed, joined_diff)
    column_sums = jnp.sum(joined_diff.astype(f32), axis=0).reshape(head_count, 3, width)
    query_bias_grad = column_sums[:, 0].reshape(features)
    value_bias_grad = column_sums[:, 2].reshape(features)
    normed_back = matmul_rt(joined_diff, joined_full)
    input_part, first_gain_grad, first_shift_grad = norm_back_one(normed_back)
    input_grad = (residual_grad + input_part).astype(bf16).reshape(*shape, features)

    vector_grads = (
        first_gain_grad, first_shift_grad, query_bias_grad, value_bias_grad, output_bias_grad,
        second_gain_grad, second_shift_grad, contract_bias_grad, expand_bias_grad,
    )
    devices = fs_count * sp_count
    packed = jnp.concatenate([item.reshape(devices, -1) for item in vector_grads], axis=1)
    if fast:
        input_grad, packed, joined_grad = end(input_grad, packed, joined_grad.astype(bf16))
    else:
        input_grad, joined_grad = from_own_seqs(input_grad), scatter(joined_grad)
        packed = scatter(packed.reshape(-1))
    own_grads, at = [], 0
    for item in vector_grads:
        size = item.shape[0] // devices
        own_grads.append(packed[at : at + size])
        at += size
    g1, s1, qb, vb, ob, g2, s2, cb, eb = own_grads
    return (
        layer_output,
        input_grad,
        g1,
        s1,
        joined_grad,
        qb,
        vb,
        output_weight_grad,
        ob,
        g2,
        s2,
        expand_grad,
        eb,
        contract_grad,
        cb,
    )


def solution(mesh):
    tokens = P(None, ("fs", "sp"), None)
    both, both_rows = P(("fs", "sp")), P(("fs", "sp"), None)
    one, one_rows = P("fs"), P("fs", None)
    return jax.shard_map(
        per_device,
        mesh=mesh,
        in_specs=(
            tokens, one, one, one_rows, one, one, one_rows, one, one, one, one_rows, one,
            one_rows, one, P(), tokens,
        ),
        out_specs=(
            tokens, tokens, both, both, both_rows, both, both, both_rows, both, both, both,
            both_rows, both, both_rows, both,
        ),
        check_vma=False,
    )
```

time: 1260 us -> 531 us (0.42)
  waiting for transfers between devices: 816 us -> 0 us
  Pallas kernels: 76.4 us -> 394 us
  blocking collectives: 165 us -> 0 us
  starting transfers between devices: 27.5 us -> 0 us
  local copies, waits for them, and re-layouts: 36.4 us -> 20.4 us
  between operations: 15.1 us -> 1.39 us
  matrix products: 106 us -> 92.5 us
    reduce_scatter x4 -> x0, waiting for transfers between devices: 407 us -> none  [per_device(): lax.psum_scatter(item, ('fs', 'sp'), scatter_dimension=0, tiled=True)]
    pallas_call x2 -> x4, Pallas kernels: 76.4 us -> 394 us  [the longest x1 156 us: backward_fused(): remote_call(functools.partial(backward_fused_kernel, heads, width, count)...]
    all_gather x4 -> x0, waiting for transfers between devices: 286 us -> none  [per_device(): gather = lambda item: lax.all_gather(item, 'fs', axis=0, tiled=True)]
    all_to_all x6 -> x0, waiting for transfers between devices: 120 us -> none  [the longest x2 64.3 us: from_heads(): values = lax.all_to_all(values, 'sp', split_axis=2, concat_axis=3)]
    all_to_all x2 -> x0, blocking collectives: 66.7 us -> none  [to_heads(): values = lax.all_to_all(values, 'sp', split_axis=3, concat_axis=2)]
    all_gather x1 -> x0, blocking collectives: 55.8 us -> none  [per_device(): packed = lax.all_gather(jnp.concatenate(vectors), 'fs', axis=0)]
    unnamed x1 -> x0, blocking collectives: 42.3 us -> none
    all_to_all x6 -> x0, starting transfers between devices: 26.7 us -> none  [the longest x2 10 us: to_own_seqs(): lax.all_to_all(values, 'fs', split_axis=0, concat_axis=0)]
  transfers between devices with their start and end apart: 14 -> 0, of which waited for: 10 -> 0; matrix products, arithmetic and copies ran while one was open for 10% -> 0% of each run, Pallas kernels for 6% -> 0%
where the time goes in v3:
time: 531 us; the launch traced here: 522 us
  Pallas kernels  394 us (74%)
  matrix products  92.5 us (17%)
  local copies, waits for them, and re-layouts  20.4 us (4%)
  other arithmetic  13.6 us (3%)
    pallas_call x1, Pallas kernels, backward_fused(): remote_call(functools.partial(backward_fused_kernel, heads, width, count)...  156 us
    pallas_call x1, Pallas kernels, forward_fused(): remote_call(functools.partial(forward_fused_kernel, heads, width, count),...  136 us
    pallas_call x1, Pallas kernels, end(): remote_call(end_kernel, 'end', 3, out_shape=(jax.ShapeDtypeStruct((parts,...  56.8 us
    pallas_call x1, Pallas kernels, begin(): remote_call(begin_kernel, 'begin', 0, out_shape=(jax.ShapeDtypeStruct((ow...  44.8 us
    dot_general x4, matrix products, matmul_rt(): lax.dot_general(left_side, right_side, (((1,), (1,)), ((), ())), preferre...  32.7 us
    dot_general x4, matrix products, matmul_lt(): lax.dot_general(left_side, right_side, (((0,), (0,)), ((), ())), preferre...  31.3 us
    dot_general x4, matrix products, matmul(): return jnp.dot(left_side, right_side, preferred_element_type=f32)  28.5 us
    unnamed x64, local copies, waits for them, and re-layouts  14.6 us

profile of v3, /device:TPU:0, one launch (start us, length us, event | category | flops | bytes accessed | tf_op | source)
XLA Modules:
  0.0 521.6 jit_solution(9098261034747841436)
XLA Ops:
  0.6 1.2 dynamic_slice.3.slopes.refs_0_
  9.9 44.8 %begin.1 = (bf16[2,4,64,1024]{3,2,1,0:T(8,128)(2,1)}, bf16[4,24,128]{2,1,0:T(8,128)(2,1)}, bf16[4,8,32,3072]{3,2,1,0:T(8,128)(2,1)}) custom-call(bf16[4,2,64,1024]{3,2,1,0:T(8,128)(2,1)} %bitcast.127, bf16[24,128]{1,0:T(8,128)(2,1)} %bitcast.148, bf16[8,32,3072]{2,1,0:T(8,128)(2,1)} %bitcast.123), custom_call_target="tpu_custom_call" | custom-call | tf_op jit(solution)/shard_map/begin/pallas_call | solution.py:675
  55.5 1.4 convert_reduce_fusion.2
  57.1 1.6 fusion.11
  59.7 8.0 %add_convert_fusion = bf16[512,3072]{1,0:T(8,128)(2,1)} fusion(bf16[512,1024]{1,0:T(8,128)(2,1)S(1)} %bitcast.128, bf16[1024,3072]{1,0:T(8,128)(2,1)} %bitcast.159, f32[3072]{0:T(1024)S(1)} %add.104), kind=kOutput, calls=%fused_computation.16 | convolution fusion | flops 3224371200 | bytes 10498048 | tf_op jit(solution)/shard_map/dot_general | solution.py:36
  67.7 136.0 %forward_fused.1 = (bf16[2,4,8,64,384]{4,3,2,1,0:T(8,128)(2,1)}, bf16[2,4,64,1024]{3,2,1,0:T(8,128)(2,1)}, f32[2,2,64,2048]{3,2,1,0:T(8,128)}, f32[2,2,1,2048]{3...) custom-call(f32[2]{0:T(128)} %dynamic_slice.3.slopes.refs_0_, ...), custom_call_target="tpu_custom_call" | custom-call | tf_op jit(solution)/shard_map/forward_fused/pallas_call | solution.py:778
  203.7 1.4 convert_reduce_fusion.3
  205.2 3.4 fusion.28
  209.5 7.0 %fusion.22 = f32[512,4096]{1,0:T(8,128)} fusion(bf16[1024,4096]{1,0:T(8,128)(2,1)S(1)} %bitcast.153, f32[512,1024]{1,0:T(8,128)S(1)} %get-tuple-element.89, f32[1024]{0:T(1024)S(1)} %bitcast.149, f32[1024]{0:T(1024)S(1)} %bitcast.144, f32[512]{0:T(512)S(1)} %fusion.19, f32[512]{0:T(512)S(1)} %broadcast_multiply_fusion.1), kind=kOutput, calls=%fused_computation.77 | convolution fusion | flops 4297588736 | bytes 18886656 | tf_op jit(solution)/shard_map/dot_general | solution.py:36
  216.5 10.1 %add_convert_fusion.2 = bf16[512,1024]{1,0:T(8,128)(2,1)} fusion(f32[512,1024]{1,0:T(8,128)S(1)} %get-tuple-element.89, bf16[4096,1024]{1,0:T(8,128)(2,1)S(1)} %bitcast.158, f32[1024]{0:T(1024)S(1)} %bitcast.151, f32[512,4096]{1,0:T(8,128)} %fusion.22, f32[4096]{0:T(1024)S(1)} %bitcast.141), kind=kOutput, calls=%fused_computation.39 | convolution fusion | flops 4317511680 | bytes 19943424 | tf_op jit(solution)/shard_map/dot_general | solution.py:36
  226.6 16.3 %convert_reduce_fusion = (f32[4096]{0:T(1024)S(1)}, bf16[512,4096]{1,0:T(8,128)(2,1)}) fusion(f32[512,4096]{1,0:T(8,128)} %fusion.22, f32[4096]{0:T(1024)S(1)} %bitcast.142, bf16[512,1024]{1,0:T(8,128)(2,1)S(1)} %bitcast.112, bf16[4096,1024]{1,0:T(8,128)(2,1)} %bitcast.155), kind=kOutput, calls=%fused_computation.11 | convolution fusion | flops 4351586304 | bytes 22052864 | tf_op jit(solution)/shard_map/dot_general | solution.py:46
  242.8 13.2 %convolution_convert_fusion.1 = bf16[4096,1024]{1,0:T(8,128)(2,1)} fusion(bf16[512,1024]{1,0:T(8,128)(2,1)S(1)} %bitcast.113, f32[512,4096]{1,0:T(8,128)} %fusion.22, f32[4096]{0:T(1024)S(1)} %bitcast.143), kind=kOutput, calls=%fused_computation.14 | convolution fusion | flops 4320133120 | bytes 17842176 | tf_op jit(solution)/shard_map/dot_general | solution.py:40
  256.0 7.2 %multiply_reduce_fusion = (f32[1024]{0:T(1024)S(1)}, f32[512]{0:T(512)S(1)}, f32[1024]{0:T(1024)S(1)}, f32[512,1024]{1,0:T(8,128)S(1)}) fusion(f32[512,1024]{1,0:T(8,128)S(1)} %get-tuple-element.89, f32[512]{0:T(512)S(1)} %fusion.19, f32[512]{0:T(512)S(1)} %broadcast_multiply_fusion.1, f32[1024]{0:T(1024)S(1)} %bitcast.145, ...), kind=kOutput, calls=%fused_computation.36 | convolution fusion | flops 4299159040 | bytes 16795648 | tf_op jit(solution)/shard_map/dot_general | solution.py:46
  264.1 1.8 convert_reduce_fusion.4
  266.0 2.3 convolution_convert_fusion.3
  268.4 4.3 convolution_convert_fusion.2
  272.6 7.2 %convolution_convert_fusion = bf16[1024,4096]{1,0:T(8,128)(2,1)} fusion(bf16[512,4096]{1,0:T(8,128)(2,1)S(1)} %copy-done.17, f32[512,1024]{1,0:T(8,128)S(1)} %copy-done.4, f32[1024]{0:T(1024)S(1)} %bitcast.150, f32[1024]{0:T(1024)S(1)} %bitcast.147, f32[512]{0:T(512)S(1)} %fusion.19, f32[512]{0:T(512)S(1)} %broadcast_multiply_fusion.1), kind=kOutput, calls=%fused_computation.13 | convolution fusion | flops 4301783040 | bytes 14692352 | tf_op jit(solution)/shard_map/dot_general | solution.py:40
  279.9 156.2 %backward_fused.1 = (bf16[2,4,64,3072]{3,2,1,0:T(8,128)(2,1)}, bf16[4,2,64,1024]{3,2,1,0:T(8,128)(2,1)}, f32[128,1024]{1,0:T(8,128)}, f32[32,4096]{1,0:T(8,128)}, f32[32,1024]{1,0:T(8,128)}) custom-call(f32[2]{0:T(128)} %dynamic_slice.3.slopes.refs_0_, bf16[2,4,64,1024]{3,2,1,0:T(8,128)(2,1)} %bitcast.126, ...), custom_call_target="tpu_custom_call" | custom-call | tf_op jit(solution)/shard_map/backward_fused/pallas_call | solution.py:883
  436.1 7.0 %fusion.23 = (f32[1024]{0:T(1024)S(1)}, f32[512]{0:T(512)S(1)}, f32[512,1024]{1,0:T(8,128)S(1)}) fusion(f32[1024]{0:T(1024)S(1)} %bitcast.135, f32[512]{0:T(512)S(1)} %div.45, bf16[2,4,64,1024]{3,2,1,0:T(8,128)(2,1)S(1)} %copy-done, bf16[512,3072]{1,0:T(8,128)(2,1)} %bitcast.118, bf16[1024,3072]{1,0:T(8,128)(2,1)} %bitcast.160), kind=kOutput, calls=%fused_computation.78 | convolution fusion | flops 3224369664 | bytes 12595200 | tf_op jit(solution)/shard_map/dot_general | solution.py:46
  444.3 2.0 add_convert_fusion.1
  446.4 2.7 convert_reduce_fusion.1
  450.2 6.6 %bitcast_convert_fusion = bf16[1024,3072]{1,0:T(8,128)(2,1)} fusion(bf16[2,4,64,1024]{3,2,1,0:T(8,128)(2,1)} %copy-done.7, bf16[2,4,64,3072]{3,2,1,0:T(8,128)(2,1)S(1)} %copy-done.5), kind=kOutput, calls=%fused_computation | convolution fusion | flops 3224371200 | bytes 10485760 | tf_op jit(solution)/shard_map/dot_general | solution.py:40
  456.8 56.8 %end.1 = (bf16[4,2,64,1024]{3,2,1,0:T(8,128)(2,1)}, f32[8,128]{1,0:T(8,128)}, f32[32,3072]{1,0:T(8,128)}) custom-call(bf16[2,4,64,1024]{3,2,1,0:T(8,128)(2,1)} %bitcast.117, f32[4,8,8,128]{3,2,1,0:T(8,128)} %copy.44, bf16[4,4,2,32,3072]{4,3,2,1,0:T(8,128)(2,1)} %bitcast.116), custom_call_target="tpu_custom_call" | custom-call | tf_op jit(solution)/shard_map/end/pallas_call | solution.py:955
  513.6 1.3 slice_bitcast_fusion.1
  (101 shorter events, 20.6 us)
Async XLA Ops:
  9.3 0.6 copy-start.14
  54.7 4.5 copy-start
  59.7 8.0 %copy-start.7 = (bf16[2,4,64,1024]{3,2,1,0:T(8,128)(2,1)}, bf16[2,4,64,1024]{3,2,1,0:T(8,128)(2,1)S(1)}, u32[]{:S(2)}) copy-start(bf16[2,4,64,1024]{3,2,1,0:T(8,128)(2,1)S(1)} %fusion.14) | copy-start | bytes 3145732
  205.2 4.3 copy-start.15
  208.6 54.6 %copy-start.3 = (f32[512,1024]{1,0:T(8,128)}, f32[512,1024]{1,0:T(8,128)S(1)}, u32[]{:S(2)}) copy-start(f32[512,1024]{1,0:T(8,128)S(1)} %get-tuple-element.89) | copy-start | bytes 6291460
  208.6 7.9 %slice-start = ((s8[8388608]{0:T(1024)(128)(4,1)}), s8[4194304]{0:T(1024)(128)(4,1)S(1)}, s32[]{:S(2)}) async-start(s8[8388608]{0:T(1024)(128)(4,1)} %bitcast.156), calls=%async_computation | async-start | bytes 8388608
  209.5 7.0 %slice-start.1 = ((s8[8388608]{0:T(1024)(128)(4,1)}), s8[4194304]{0:T(1024)(128)(4,1)S(1)}, s32[]{:S(2)}) async-start(s8[8388608]{0:T(1024)(128)(4,1)} %bitcast.156), calls=%async_computation.1 | async-start | bytes 8388608
  216.5 10.1 %copy-start.1 = (bf16[2,4,64,1024]{3,2,1,0:T(8,128)(2,1)S(1)}, bf16[2,4,64,1024]{3,2,1,0:T(8,128)(2,1)}, u32[]{:S(2)}) copy-start(bf16[2,4,64,1024]{3,2,1,0:T(8,128)(2,1)} %get-tuple-element.37) | copy-start | bytes 3145732
  264.1 1.9 copy-start.16
  265.9 2.4 copy-start.6
  268.3 4.3 copy-start.4
  268.3 4.3 copy-start.17
  443.1 1.2 copy-start.2
  446.3 3.9 copy-start.5
  456.8 59.4 %copy-start.8 = (bf16[4,2,64,1024]{3,2,1,0:T(8,128)(2,1)S(1)}, bf16[4,2,64,1024]{3,2,1,0:T(8,128)(2,1)}, u32[]{:S(2)}) copy-start(bf16[4,2,64,1024]{3,2,1,0:T(8,128)(2,1)} %get-tuple-element.45) | copy-start | bytes 3145732
  513.6 3.6 copy-start.9
  516.2 2.0 copy-start.12
  516.2 2.7 copy-start.13
  517.2 2.4 copy-start.11
  517.2 3.2 copy-start.10

commit v4 on v3

v4 whole, which is shorter than its diff:
```python
import functools
import math

import jax
import jax.numpy as jnp
from jax import lax
from jax.experimental import pallas as pl
from jax.experimental.pallas import tpu as pltpu
from jax.sharding import PartitionSpec as P

norm_eps = 1e-05
gelu_coef = 0.7978845608028654
masked_value = -1e30
f32 = jnp.float32
bf16 = jnp.bfloat16
MESH = pl.DeviceIdType.MESH
HBM = pl.BlockSpec(memory_space=pl.ANY)
VMEM = pl.BlockSpec(memory_space=pltpu.VMEM)
SMEM = pl.BlockSpec(memory_space=pltpu.SMEM)
vmem_bytes = 60 * 1024 * 1024


def normalize(values, norm_gain, norm_shift):
    center = values - jnp.mean(values, axis=-1, keepdims=True)
    variance = jnp.mean(center * center, axis=-1, keepdims=True)
    return center * lax.rsqrt(variance + norm_eps) * norm_gain + norm_shift


def gelu_tanh(values):
    return (
        0.5 * values * (1.0 + jnp.tanh(gelu_coef * (values + 0.044715 * values * values * values)))
    )


def matmul(left_side, right_side):
    return jnp.dot(left_side, right_side, preferred_element_type=f32)


def matmul_lt(left_side, right_side):
    return lax.dot_general(
        left_side, right_side, (((0,), (0,)), ((), ())), preferred_element_type=f32
    )


def matmul_rt(left_side, right_side):
    return lax.dot_general(
        left_side, right_side, (((1,), (1,)), ((), ())), preferred_element_type=f32
    )


def joined_bias_of(query_bias, value_bias, head_count):
    query_part = query_bias.astype(f32).reshape(head_count, -1)
    value_part = value_bias.astype(f32).reshape(head_count, -1)
    return jnp.stack([query_part, jnp.zeros_like(query_part), value_part], axis=1).reshape(-1)


def split_three(values):
    high = values.astype(bf16).astype(f32)
    rest = values - high
    middle = rest.astype(bf16).astype(f32)
    return high, middle, rest - middle


def key_columns(key_rows, slope, start):
    rows, width = key_rows.shape
    position = (start + lax.broadcasted_iota(jnp.int32, (rows, width), 0)).astype(f32)
    lane = lax.broadcasted_iota(jnp.int32, (rows, width), 1)
    high, middle, low = split_three(slope * position)
    extra = jnp.where(lane == 0, high, jnp.where(lane == 1, middle, jnp.where(lane == 2, low, 0.0)))
    return jnp.concatenate([key_rows.astype(f32), extra], axis=1).astype(bf16)


def query_columns(queries, scale):
    rows, width = queries.shape
    lane = lax.broadcasted_iota(jnp.int32, (rows, width), 1)
    ones = jnp.where(lane < 3, 1.0, 0.0)
    return jnp.concatenate([queries.astype(f32) * scale, ones], axis=1).astype(bf16)


def follow(n, after):
    for at, steps in after.items():

        def act(steps=steps):
            for step, *given in steps:
                step(*given)

        pl.when(n == at)(act)


class Forward:
    def __init__(self, heads, width, slopes, qkv, out, out_t, lse, keys, queries, values_t):
        self.heads, self.width, self.slopes, self.qkv, self.out = heads, width, slopes, qkv, out
        self.out_t, self.lse = out_t, lse
        self.keys, self.queries, self.values_t = keys, queries, values_t
        self.blocks = qkv.shape[1]
        self.block = qkv.shape[2] * qkv.shape[3]

    def rows(self, i):
        return pl.ds(pl.multiple_of(i * self.block, self.block), self.block)

    def prepare(self, b):
        width, block, qkv = self.width, self.block, self.qkv
        scale = 1.0 / math.sqrt(width)

        def body(i, _):
            rows = self.rows(i)
            for h in range(self.heads):
                base = h * 3 * width
                query, key, value = [
                    qkv[b, i, :, :, base + n * width : base + (n + 1) * width].reshape(block, width)
                    for n in range(3)
                ]
                self.keys[h, rows, :] = key_columns(key, self.slopes[h], i * block)
                self.queries[h, rows, :] = query_columns(query, scale)
                self.values_t[h, :, rows] = value.astype(f32).T.astype(bf16)
            return 0

        lax.fori_loop(0, self.blocks, body, 0)

    def one(self, b, i):
        heads, width, block = self.heads, self.width, self.block
        rows = self.rows(i)
        query = [self.queries[h, rows, :] for h in range(heads)]

        def step(j, state, diagonal):
            columns = self.rows(j)
            result = []
            for h in range(heads):
                top, total, acc = state[h]
                scores = matmul_rt(self.keys[h, columns, :], query[h])
                if diagonal:
                    key_at = lax.broadcasted_iota(jnp.int32, (block, block), 0)
                    query_at = lax.broadcasted_iota(jnp.int32, (block, block), 1)
                    scores = jnp.where(key_at <= query_at, scores, masked_value)
                newest = jnp.maximum(top, jnp.max(scores, axis=0, keepdims=True))
                shrink = jnp.exp(top - newest)
                probs = jnp.exp(scores - newest)
                total = total * shrink + jnp.sum(probs, axis=0, keepdims=True)
                acc = acc * shrink + matmul(self.values_t[h, :, columns], probs.astype(bf16))
                result.append((newest, total, acc))
            return tuple(result)

        state = tuple(
            (
                jnp.full((1, block), masked_value, f32),
                jnp.zeros((1, block), f32),
                jnp.zeros((width, block), f32),
            )
            for h in range(heads)
        )
        state = lax.fori_loop(0, i, lambda j, s: step(j, s, False), state)
        state = step(i, state, True)
        finished = []
        for h in range(heads):
            top, total, acc = state[h]
            result = acc / total
            self.out_t[b, h, :, rows] = result
            self.lse[b, h, :, rows] = top + jnp.log(total)
            finished.append(result)
        joined = finished[0] if heads == 1 else jnp.concatenate(finished, axis=0)
        self.out[b, i] = joined.T.astype(bf16).reshape(self.out.shape[2:])

    def run(self, after):
        blocks = self.blocks

        def body(n, _):
            b, i = n // blocks, n % blocks
            pl.when(i == 0)(lambda: self.prepare(b))
            self.one(b, i)
            follow(n, after)
            return 0

        lax.fori_loop(0, self.qkv.shape[0] * blocks, body, 0)


def forward_kernel(heads, width, *refs):
    Forward(heads, width, *refs).run({})


def saved_shapes(seqs, length, heads, width):
    return (
        jax.ShapeDtypeStruct((seqs, heads, width, length), f32),
        jax.ShapeDtypeStruct((seqs, heads, 1, length), f32),
    )


def forward_scratch(length, heads, width):
    return [
        pltpu.VMEM((heads, length, 2 * width), bf16),
        pltpu.VMEM((heads, length, 2 * width), bf16),
        pltpu.VMEM((heads, width, length), bf16),
    ]


def attention_forward(qkv, slopes, heads, width):
    seqs, blocks, ranks, piece, _ = qkv.shape
    length = blocks * ranks * piece
    return pl.pallas_call(
        functools.partial(forward_kernel, heads, width),
        name="attention_forward",
        out_shape=(
            jax.ShapeDtypeStruct((seqs, blocks, ranks, piece, heads * width), bf16),
            *saved_shapes(seqs, length, heads, width),
        ),
        in_specs=[SMEM, VMEM],
        out_specs=(VMEM, VMEM, VMEM),
        scratch_shapes=forward_scratch(length, heads, width),
        compiler_params=pltpu.CompilerParams(vmem_limit_bytes=vmem_bytes),
    )(slopes, qkv)


class Backward:
    def __init__(
        self, heads, width, slopes, qkv, diff, out_t, lse, joined,
        keys, queries, keys_t, values, diffs, delta, query_acc,
    ):
        self.heads, self.width, self.slopes, self.qkv, self.diff = heads, width, slopes, qkv, diff
        self.out_t, self.lse, self.joined = out_t, lse, joined
        self.keys, self.queries, self.keys_t, self.values = keys, queries, keys_t, values
        self.diffs, self.delta, self.query_acc = diffs, delta, query_acc
        self.blocks = qkv.shape[1]
        self.block = qkv.shape[2] * qkv.shape[3]

    def rows(self, i):
        return pl.ds(pl.multiple_of(i * self.block, self.block), self.block)

    def prepare(self, b):
        width, block, qkv = self.width, self.block, self.qkv
        scale = 1.0 / math.sqrt(width)

        def body(i, _):
            rows = self.rows(i)
            for h in range(self.heads):
                base = h * 3 * width
                query, key, value = [
                    qkv[b, i, :, :, base + n * width : base + (n + 1) * width].reshape(block, width)
                    for n in range(3)
                ]
                self.keys[h, rows, :] = key_columns(key, self.slopes[h], i * block)
                self.keys_t[h, :, rows] = key.astype(f32).T.astype(bf16)
                self.queries[h, rows, :] = query_columns(query, scale)
                self.values[h, rows, :] = value
                part = self.diff[b, i, :, :, h * width : (h + 1) * width].reshape(block, width)
                self.diffs[h, rows, :] = part
                self.delta[h, :, rows] = jnp.sum(
                    part.astype(f32).T * self.out_t[b, h, :, rows], axis=0, keepdims=True
                )
                self.query_acc[h, :, rows] = jnp.zeros((width, block), f32)
            return 0

        lax.fori_loop(0, self.blocks, body, 0)

    def one(self, b, j):
        heads, width, block = self.heads, self.width, self.block
        tail = self.joined.shape[2:4] + (width,)
        columns = self.rows(j)

        def step(i, state, diagonal):
            rows = self.rows(i)
            result = []
            for h in range(heads):
                key_acc, value_acc = state[h]
                query = self.queries[h, rows, :]
                part = self.diffs[h, rows, :]
                scores = matmul_rt(self.keys[h, columns, :], query)
                probs = jnp.exp(scores - self.lse[b, h, :, rows])
                if diagonal:
                    key_at = lax.broadcasted_iota(jnp.int32, (block, block), 0)
                    query_at = lax.broadcasted_iota(jnp.int32, (block, block), 1)
                    probs = jnp.where(key_at <= query_at, probs, 0.0)
                prob_diff = matmul_rt(self.values[h, columns, :], part)
                score_diff = (probs * (prob_diff - self.delta[h, :, rows])).astype(bf16)
                value_acc = value_acc + matmul(probs.astype(bf16), part)
                key_acc = key_acc + matmul(score_diff, query)
                self.query_acc[h, :, rows] += matmul(self.keys_t[h, :, columns], score_diff)
                result.append((key_acc, value_acc))
            return tuple(result)

        state = tuple(
            (jnp.zeros((block, 2 * width), f32), jnp.zeros((block, width), f32))
            for h in range(heads)
        )
        state = step(j, state, True)
        state = lax.fori_loop(j + 1, self.blocks, lambda i, s: step(i, s, False), state)
        for h in range(heads):
            base = (h * 3 + 1) * width
            key_acc, value_acc = state[h]
            self.joined[b, j, :, :, base : base + width] = (
                key_acc[:, :width].astype(bf16).reshape(tail)
            )
            self.joined[b, j, :, :, base + width : base + 2 * width] = value_acc.astype(
                bf16
            ).reshape(tail)

    def run(self, after):
        blocks = self.blocks

        def body(n, _):
            b, j = n // blocks, n % blocks
            pl.when(j == 0)(lambda: self.prepare(b))
            self.one(b, j)
            pl.when(j == blocks - 1)(lambda: self.finish(b))
            follow(n, after)
            return 0

        lax.fori_loop(0, self.qkv.shape[0] * blocks, body, 0)

    def finish(self, b):
        width = self.width
        scale = 1.0 / math.sqrt(width)
        tail = self.joined.shape[2:4] + (width,)

        def body(i, _):
            for h in range(self.heads):
                base = h * 3 * width
                result = (self.query_acc[h, :, self.rows(i)] * scale).T.astype(bf16)
                self.joined[b, i, :, :, base : base + width] = result.reshape(tail)
            return 0

        lax.fori_loop(0, self.blocks, body, 0)


def backward_kernel(heads, width, *refs):
    Backward(heads, width, *refs).run({})


def backward_scratch(length, heads, width):
    return [
        pltpu.VMEM((heads, length, 2 * width), bf16),
        pltpu.VMEM((heads, length, 2 * width), bf16),
        pltpu.VMEM((heads, width, length), bf16),
        pltpu.VMEM((heads, length, width), bf16),
        pltpu.VMEM((heads, length, width), bf16),
        pltpu.VMEM((heads, 1, length), f32),
        pltpu.VMEM((heads, width, length), f32),
    ]


def attention_backward(qkv, diff, out_t, lse, slopes, heads, width):
    length = qkv.shape[1] * qkv.shape[2] * qkv.shape[3]
    return pl.pallas_call(
        functools.partial(backward_kernel, heads, width),
        name="attention_backward",
        out_shape=jax.ShapeDtypeStruct(qkv.shape, bf16),
        in_specs=[SMEM, VMEM, VMEM, VMEM, VMEM],
        out_specs=VMEM,
        scratch_shapes=backward_scratch(length, heads, width),
        compiler_params=pltpu.CompilerParams(vmem_limit_bytes=vmem_bytes),
    )(slopes, qkv, diff, out_t, lse)


def to_own_seqs(values):
    seqs, piece, features = values.shape
    parts = lax.axis_size("fs")
    values = values.reshape(parts, seqs // parts, piece, features)
    return lax.all_to_all(values, "fs", split_axis=0, concat_axis=0).transpose(1, 0, 2, 3)


def from_own_seqs(values):
    own, parts, piece, features = values.shape
    values = lax.all_to_all(values.transpose(1, 0, 2, 3), "fs", split_axis=0, concat_axis=0)
    return values.reshape(parts * own, piece, features)


def to_heads(values):
    own, parts, piece, features = values.shape
    ranks = lax.axis_size("sp")
    values = values.reshape(own, parts, piece, ranks, features // ranks)
    return lax.all_to_all(values, "sp", split_axis=3, concat_axis=2)


def from_heads(values):
    own, parts, ranks, piece, features = values.shape
    values = lax.all_to_all(values, "sp", split_axis=2, concat_axis=3)
    return values.reshape(own, parts, piece, ranks * features)


class Copies:
    def __init__(self, send, recv, local):
        self.send, self.recv, self.local = send, recv, local
        self.used, self.used_local, self.made = 0, 0, []

    def plan(self, source, target, device):
        copy = pltpu.make_async_remote_copy(
            src_ref=source,
            dst_ref=target,
            send_sem=self.send.at[self.used],
            recv_sem=self.recv.at[self.used],
            device_id=device,
            device_id_type=MESH,
        )
        self.used += 1
        self.made.append(copy)
        return copy

    def inside(self, source, target):
        copy = pltpu.make_async_copy(source, target, self.local.at[self.used_local])
        self.used_local += 1
        return copy

    def finish(self):
        assert (self.used, self.used_local) == (self.send.shape[0], self.local.shape[0])
        for copy in self.made:
            copy.wait_send()


def go(copies):
    for copy in copies:
        copy.start()


def arrive(copies):
    for copy in copies:
        copy.wait_recv()


def done(copies):
    for copy in copies:
        copy.wait()


def greet(devices):
    barrier = pltpu.get_barrier_semaphore()
    for device in devices:
        pl.semaphore_signal(barrier, inc=1, device_id=device, device_id_type=MESH)
    pl.semaphore_wait(barrier, len(devices))


class Place:
    def __init__(self):
        z, s = lax.axis_index("fs"), lax.axis_index("sp")
        self.z, self.s = z, s
        self.core, self.chip = s % 2, s // 2
        self.x, self.y = self.chip % 2, self.chip // 2
        self.along_x = s + 2 - 4 * self.x
        self.along_y = s + 4 - 8 * self.y
        self.partner = s + 1 - 2 * self.core
        self.diagonal = self.along_x + self.along_y - s
        self.chip_x, self.chip_y = self.along_x // 2, self.along_y // 2
        self.lines = [(lax.rem(z + k, 4), s) for k in range(1, 4)]
        self.plane = [(z, lax.rem(s + d, 8)) for d in range(1, 8)]
        self.to_x, self.to_y, self.to_core = [
            (z, to) for to in (self.along_x, self.along_y, self.partner)
        ]
        self.near = self.lines + [self.to_x, self.to_y, self.to_core]


class Gather:
    copies_each = 33

    def __init__(self, place, weights, wholes, kept, chunks, copies):
        z, s, lines = place.z, place.s, place.lines
        self.loads = [copies.inside(w, k) for w, k in zip(weights, kept)]
        self.own = [copies.inside(k, whole.at[z]) for k, whole in zip(kept, wholes)]
        self.first, self.second, self.third, self.cores, self.last = [], [], [], [], []
        for t, row, rows, column, columns in chunks:
            whole = wholes[t]
            wide = pl.ds(column, columns)
            every = pl.ds(row, rows)
            low, high = pl.ds(row, rows // 2), pl.ds(row + rows // 2, rows // 2)

            def same(k, rank, part, to):
                where = (k, rank, part, wide)
                return copies.plan(whole.at[where], whole.at[where], to)

            self.first.append(
                [
                    copies.plan(weights[t].at[s, every, wide], whole.at[z, s, every, wide], to)
                    for to in lines
                ]
            )
            second, third, cores, last = [], [], [], []
            for k, _ in lines:
                second.append(same(k, s, low, place.to_x))
                second.append(same(k, s, high, place.to_y))
                cores.append(same(k, s, every, place.to_core))
                third.append(same(k, s, low, place.to_y))
                third.append(same(k, s, high, place.to_x))
                third.append(same(k, place.along_x, low, place.to_y))
                third.append(same(k, place.along_y, high, place.to_x))
                for rank in (place.along_x, place.along_y, place.diagonal):
                    last.append(same(k, rank, every, place.to_core))
            self.second.append(second)
            self.third.append(third)
            self.cores.append(cores)
            self.last.append(last)

    def keep(self):
        done(self.loads)
        go(self.own)

    def start(self, t):
        go(self.first[t])

    def exchange(self, t):
        arrive(self.first[t])
        go(self.second[t])
        go(self.cores[t])

    def spread(self, t):
        arrive(self.second[t])
        go(self.third[t])

    def share(self, t):
        arrive(self.third[t])
        go(self.last[t])

    def finish(self):
        for copies in self.cores + self.last:
            arrive(copies)
        done(self.own)


def add_into(target, other):
    target[...] = (target[...].astype(f32) + other[...].astype(f32)).astype(target.dtype)


def add_blocks(steps, block_of):
    def body(i, _):
        add_into(*block_of(i))
        return 0

    lax.fori_loop(0, steps, body, 0)


class Reduce:
    copies_each = 10

    def __init__(self, place, grads, outs, bufs, chunks, copies):
        self.place, self.outs, self.chunks = place, outs, chunks
        self.bufs = [bufs[7 * t : 7 * t + 7] for t in range(len(chunks))]
        self.loads, self.first, self.second, self.third, self.fourth = [], [], [], [], []
        for (t, row, rows, column, columns), buf in zip(chunks, self.bufs):
            own, from_core, from_x, from_y, late_y, late_x, from_z = buf
            every, wide = pl.ds(row, rows), pl.ds(column, columns)
            low, high = pl.ds(0, rows // 2), pl.ds(rows // 2, rows // 2)
            self.loads.append(
                copies.inside(grads[t].at[:, :, place.core, every, wide], own)
            )
            self.first.append(
                copies.plan(
                    grads[t].at[:, :, 1 - place.core, every, wide], from_core, place.to_core
                )
            )
            step = []
            for k in range(2):
                step.append(
                    copies.plan(own.at[:, 2 * k + 1 - place.x, low], from_x.at[:, k], place.to_x)
                )
                step.append(
                    copies.plan(
                        own.at[:, 2 * (1 - place.y) + k, high], from_y.at[:, k], place.to_y
                    )
                )
            self.second.append(step)
            self.third.append(
                [
                    copies.plan(own.at[:, place.chip_y, low], late_y, place.to_y),
                    copies.plan(own.at[:, place.chip_x, high], late_x, place.to_x),
                ]
            )
            self.fourth.append(
                [
                    copies.plan(own.at[to[0], place.chip], from_z.at[k], to)
                    for k, to in enumerate(place.lines)
                ]
            )

    def start(self):
        go(self.first)

    def halves(self, t):
        half = self.chunks[t][2] // 2
        return pl.ds(0, half), pl.ds(half, half)

    def exchange(self, t):
        own, from_core = self.bufs[t][:2]
        self.loads[t].wait()
        arrive([self.first[t]])
        add_blocks(16, lambda i: (own.at[i // 4, i % 4], from_core.at[i // 4, i % 4]))
        go(self.second[t])

    def spread(self, t):
        own, _, from_x, from_y = self.bufs[t][:4]
        low, high = self.halves(t)
        x, y = self.place.x, self.place.y
        arrive(self.second[t])
        add_blocks(8, lambda i: (own.at[i // 2, 2 * (i % 2) + x, low], from_x.at[i // 2, i % 2]))
        add_blocks(8, lambda i: (own.at[i // 2, 2 * y + i % 2, high], from_y.at[i // 2, i % 2]))
        go(self.third[t])

    def send(self, t):
        own, _, _, _, late_y, late_x, _ = self.bufs[t]
        low, high = self.halves(t)
        chip = self.place.chip
        arrive(self.third[t])
        add_blocks(4, lambda i: (own.at[i, chip, low], late_y.at[i]))
        add_blocks(4, lambda i: (own.at[i, chip, high], late_x.at[i]))
        go(self.fourth[t])

    def finish(self, t):
        own, from_z = self.bufs[t][0], self.bufs[t][6]
        index, row, rows, column, columns = self.chunks[t]
        arrive(self.fourth[t])
        total = own[self.place.z, self.place.chip].astype(f32)
        for k in range(3):
            total = total + from_z[k].astype(f32)
        self.outs[index][row : row + rows, column : column + columns] = total


def reduce_scratch(chunks):
    scratch = []
    for _, _, rows, _, columns in chunks:
        half = rows // 2
        scratch += [
            pltpu.VMEM((4, 4, rows, columns), bf16),
            pltpu.VMEM((4, 4, rows, columns), bf16),
            pltpu.VMEM((4, 2, half, columns), bf16),
            pltpu.VMEM((4, 2, half, columns), bf16),
            pltpu.VMEM((4, half, columns), bf16),
            pltpu.VMEM((4, half, columns), bf16),
            pltpu.VMEM((3, rows, columns), bf16),
        ]
    return scratch


class ReduceLines:
    copies = 4 * 7 + 3

    def __init__(self, place, grad, out, bufs, copies):
        self.place, self.grad, self.out, self.bufs = place, grad, out, bufs
        from_core, from_x, from_y, late_y, late_x, from_z = bufs
        core, x, y = place.core, place.x, place.y
        self.order = [to[0] for to in place.lines] + [place.z]
        rows = grad.shape[3]
        self.low, self.high = pl.ds(0, rows // 2), pl.ds(rows // 2, rows // 2)
        self.first, self.second, self.third, self.fourth = [], [], [], []
        for k, at in enumerate(self.order):
            self.first.append(
                copies.plan(grad.at[at, :, 1 - core], from_core.at[k], place.to_core)
            )
            step = []
            for j in range(2):
                step.append(
                    copies.plan(
                        grad.at[at, 2 * j + 1 - x, core, self.low], from_x.at[k, j], place.to_x
                    )
                )
                step.append(
                    copies.plan(
                        grad.at[at, 2 * (1 - y) + j, core, self.high], from_y.at[k, j], place.to_y
                    )
                )
            self.second.append(step)
            self.third.append(
                [
                    copies.plan(grad.at[at, place.chip_y, core, self.low], late_y.at[k], place.to_y),
                    copies.plan(
                        grad.at[at, place.chip_x, core, self.high], late_x.at[k], place.to_x
                    ),
                ]
            )
            if k < 3:
                self.fourth.append(
                    copies.plan(grad.at[at, place.chip, core], from_z.at[k], place.lines[k])
                )

    def start(self, k):
        go([self.first[k]])

    def exchange(self, k):
        arrive([self.first[k]])
        at, core = self.order[k], self.place.core
        add_blocks(4, lambda i: (self.grad.at[at, i, core], self.bufs[0].at[k, i]))
        go(self.second[k])

    def spread(self, k):
        arrive(self.second[k])
        at, core, x, y = self.order[k], self.place.core, self.place.x, self.place.y
        add_blocks(
            2, lambda j: (self.grad.at[at, 2 * j + x, core, self.low], self.bufs[1].at[k, j])
        )
        add_blocks(
            2, lambda j: (self.grad.at[at, 2 * y + j, core, self.high], self.bufs[2].at[k, j])
        )
        go(self.third[k])

    def send(self, k):
        arrive(self.third[k])
        at, core, chip = self.order[k], self.place.core, self.place.chip
        add_into(self.grad.at[at, chip, core, self.low], self.bufs[3].at[k])
        add_into(self.grad.at[at, chip, core, self.high], self.bufs[4].at[k])
        go(self.fourth[k : k + 1])

    def finish(self):
        arrive(self.fourth)
        place = self.place
        total = self.grad[place.z, place.chip, place.core].astype(f32)
        for k in range(3):
            total = total + self.bufs[5][k].astype(f32)
        self.out[...] = total


def reduce_lines_scratch(rows, columns):
    half = rows // 2
    return [
        pltpu.VMEM((4, 4, rows, columns), bf16),
        pltpu.VMEM((4, 2, half, columns), bf16),
        pltpu.VMEM((4, 2, half, columns), bf16),
        pltpu.VMEM((4, half, columns), bf16),
        pltpu.VMEM((4, half, columns), bf16),
        pltpu.VMEM((3, rows, columns), bf16),
    ]


def split_grad(item):
    return item.reshape(4, 4, 2, item.shape[0] // 32, item.shape[1])


def split_weight(item):
    return item.reshape(8, item.shape[0] // 8, item.shape[1])


def chunks_of(index, rows, columns, count):
    if rows >= 64:
        return [(index, rows // count * n, rows // count, 0, columns) for n in range(count)]
    return [(index, 0, rows, columns // count * n, columns // count) for n in range(count)]


def semaphores(remote, local):
    return [pltpu.SemaphoreType.DMA((n,)) for n in (remote, remote, local)]


def remote_call(kernel, name, collective, **options):
    return pl.pallas_call(
        kernel,
        name=name,
        compiler_params=pltpu.CompilerParams(
            collective_id=collective, has_side_effects=True, vmem_limit_bytes=vmem_bytes
        ),
        **options,
    )


def begin_kernel(count, chunks, tokens, weight, *refs):
    vectors, refs = refs[:count], refs[count:]
    tokens_out, whole = refs[:2]
    vectors_out, refs = refs[2 : 2 + count], refs[2 + count :]
    tokens_own, kept = refs[:2]
    copies = Copies(*refs[2:])
    place = Place()
    z, lines = place.z, place.lines
    gather = Gather(place, [weight], [whole], [kept], chunks, copies)
    load = copies.inside(tokens.at[z], tokens_own)
    own = [copies.inside(tokens_own, tokens_out.at[:, z])]
    small = [copies.inside(item, out.at[z]) for item, out in zip(vectors, vectors_out)]
    waiting = []
    for to in lines:
        waiting.append(copies.plan(tokens.at[to[0]], tokens_out.at[:, z], to))
        waiting += [
            copies.plan(item, out.at[z], to) for item, out in zip(vectors, vectors_out)
        ]
    go(gather.loads)
    go([load])
    go(small)
    greet(place.near)
    gather.start(0)
    go(waiting)
    for t in range(1, len(chunks)):
        gather.start(t)
    load.wait()
    go(own)
    gather.keep()
    for t in range(len(chunks) + 2):
        if t < len(chunks):
            gather.exchange(t)
        if 0 <= t - 1 < len(chunks):
            gather.spread(t - 1)
        if 0 <= t - 2:
            gather.share(t - 2)
    gather.finish()
    arrive(waiting)
    copies.finish()
    done(own + small)


def begin(tokens, vectors, weight):
    seqs, piece, features = tokens.shape
    own = seqs // 4
    vectors = [item.reshape(-1, 128) for item in vectors]
    count = len(vectors)
    cut = split_weight(weight)
    chunks = chunks_of(0, cut.shape[1], cut.shape[2], 3)
    out = remote_call(
        functools.partial(begin_kernel, count, chunks),
        "begin",
        0,
        out_shape=(
            jax.ShapeDtypeStruct((own, 4, piece, features), bf16),
            jax.ShapeDtypeStruct((4, *cut.shape), bf16),
            *[jax.ShapeDtypeStruct((4, *item.shape), bf16) for item in vectors],
        ),
        in_specs=[HBM] * (2 + count),
        out_specs=(HBM,) * (2 + count),
        scratch_shapes=[
            pltpu.VMEM((own, piece, features), bf16),
            pltpu.VMEM(cut.shape, bf16),
            *semaphores(3 + 3 * count + len(chunks) * Gather.copies_each, 4 + count),
        ],
    )(tokens.reshape(4, own, piece, features), cut, *vectors)
    return out[0], out[1].reshape(4 * weight.shape[0], -1), [item.reshape(-1) for item in out[2:]]


def columns_of(rank, features):
    return pl.ds(pl.multiple_of(rank * features, 128), features)


def forward_fused_kernel(heads, width, count, chunks, slopes, source, upstream, *refs):
    weights, refs = refs[:count], refs[count:]
    qkv_out, attended, out_t, lse, upstream_out = refs[:5]
    wholes, refs = refs[5 : 5 + count], refs[5 + count :]
    qkv, result, upstream_own = refs[:3]
    attention = Forward(heads, width, slopes, qkv, result, out_t, lse, *refs[3:6])
    kept, refs = refs[6 : 6 + count], refs[6 + count :]
    copies = Copies(*refs)
    place = Place()
    z, s, lines, plane = place.z, place.s, place.lines, place.plane
    gather = Gather(place, weights, wholes, kept, chunks, copies)
    features = heads * width
    mine = columns_of(s, features)

    own = [
        copies.inside(source.at[:, :, :, columns_of(s, 3 * features)], qkv.at[:, :, s]),
        copies.inside(upstream.at[z], upstream_own),
    ]
    arriving = [
        copies.plan(source.at[:, :, :, columns_of(to[1], 3 * features)], qkv.at[:, :, s], to)
        for to in plane
    ]
    later = [copies.plan(upstream.at[to[0]], upstream_out.at[:, z], to) for to in lines]
    keeping = [copies.inside(upstream_own, upstream_out.at[:, z]), copies.inside(qkv, qkv_out)]
    back = [
        [copies.plan(result.at[b, :, to[1]], attended.at[b, :, :, mine], to) for to in plane]
        for b in range(2)
    ]
    stay = [copies.inside(result.at[b, :, s], attended.at[b, :, :, mine]) for b in range(2)]

    def hand_back(b):
        go(back[b] + stay[b : b + 1])

    go(gather.loads + own)
    greet(lines + plane)
    go(arriving)
    for t in range(len(chunks)):
        gather.start(t)
    go(later)
    done(own)
    gather.keep()
    arrive(arriving)
    go(keeping)
    for t in range(3):
        gather.exchange(t)
    attention.run(
        {
            2: [(gather.spread, 0), (gather.spread, 1), (gather.exchange, 3)],
            3: [(hand_back, 0)],
            5: [(gather.spread, 2), (gather.exchange, 4)],
            6: [(gather.spread, 3), (gather.share, 0), (gather.share, 1)],
            7: [(hand_back, 1)],
        }
    )
    gather.share(2)
    gather.spread(4)
    gather.share(3)
    gather.share(4)
    gather.finish()
    arrive(later + back[0] + back[1])
    copies.finish()
    done(keeping + stay)


def forward_fused(joined_all, upstream, weights, slopes, heads, width):
    own, parts, piece, columns = joined_all.shape
    features = heads * width
    length = parts * 8 * piece
    count = len(weights)
    cut = [split_weight(item) for item in weights]
    chunks = []
    for t, pieces in enumerate((1, 2, 2)):
        chunks += chunks_of(t, *cut[t].shape[1:], pieces)
    seq_shape = (own, parts, piece, 8 * features)
    qkv_shape = (own, parts, 8, piece, 3 * features)
    out = remote_call(
        functools.partial(forward_fused_kernel, heads, width, count, chunks),
        "forward_fused",
        1,
        out_shape=(
            jax.ShapeDtypeStruct(qkv_shape, bf16),
            jax.ShapeDtypeStruct(seq_shape, bf16),
            *saved_shapes(own, length, heads, width),
            jax.ShapeDtypeStruct(seq_shape, bf16),
            *[jax.ShapeDtypeStruct((4, *item.shape), bf16) for item in cut],
        ),
        in_specs=[SMEM] + [HBM] * (2 + count),
        out_specs=(HBM, HBM, VMEM, VMEM, HBM) + (HBM,) * count,
        scratch_shapes=[
            pltpu.VMEM(qkv_shape, bf16),
            pltpu.VMEM((own, parts, 8, piece, features), bf16),
            pltpu.VMEM((own, piece, 8 * features), bf16),
            *forward_scratch(length, heads, width),
            *[pltpu.VMEM(item.shape, bf16) for item in cut],
            *semaphores(7 + 3 + 14 + len(chunks) * Gather.copies_each, 2 * count + 6),
        ],
    )(slopes, joined_all, upstream.reshape(parts, own, piece, 8 * features), *cut)
    wholes = [
        whole.reshape(4 * item.shape[0], item.shape[1]) for whole, item in zip(out[5:], weights)
    ]
    return out[0], out[1], (out[2], out[3]), out[4], wholes


def feed_forward_kernel(
    expand, contract, expand_bias, second, upstream, residual,
    layer_out, second_back, expand_grad, bias_grad, contract_grad,
    expand_in, contract_in, second_t, expanded, grad, layer, staged, *refs,
):
    bufs, refs = refs[:6], refs[6:]
    loaded, stored, refs = refs[0], refs[1], refs[2:]
    copies = Copies(*refs)
    place = Place()
    z, lines = place.z, place.lines
    reduce = ReduceLines(place, grad, contract_grad, bufs, copies)
    rows, features = second.shape
    steps = 8
    wide = expand.shape[1] // steps
    own, parts, piece, _ = layer.shape

    def at(n):
        part = (z + 1 + n // 2) % 4
        return part, n % 2, pl.ds(pl.multiple_of((2 * part + n % 2) * wide, wide), wide)

    def load(n):
        _, _, where = at(n)
        return (
            pltpu.make_async_copy(expand.at[:, where], expand_in.at[:, where], loaded.at[0, n]),
            pltpu.make_async_copy(contract.at[where], contract_in.at[where], loaded.at[1, n]),
        )

    def store(n):
        _, _, where = at(n)
        slot = n % 2
        return pltpu.make_async_copy(
            staged.at[slot], expand_grad.at[:, where], stored.at[slot]
        )

    returned = [copies.plan(layer.at[:, to[0]], layer_out.at[z], to) for to in lines]
    stay = copies.inside(layer.at[:, z], layer_out.at[z])
    for n in range(steps):
        go(load(n))
    greet(place.near)
    second_t[...] = second[...].T
    second_back[...] = residual[...]

    def forward(n, after):
        part, side, where = at(n)
        done(load(n))
        values = matmul(second[...], expand_in[:, where]) + expand_bias[:, where]
        expanded[:, where] = values
        activated = gelu_tanh(values).astype(bf16)
        made = matmul(activated.T, upstream[...]).astype(bf16)
        grad[part, pl.ds(2 * side, 2)] = made.reshape(2, 2, wide // 4, features)
        second_back[...] += matmul(activated, contract_in[where, :])
        follow(n, after)
        return 0

    def backward(n, after):
        _, _, where = at(n)
        values = expanded[:, where]
        act_grad = matmul_rt(upstream[...], contract_in[where, :])
        bent = jnp.tanh(gelu_coef * (values + 0.044715 * values * values * values))
        slope = 0.5 * (1.0 + bent) + 0.5 * values * (1.0 - bent * bent) * (
            gelu_coef * (1.0 + 3.0 * 0.044715 * values * values)
        )
        diff = (act_grad * slope).astype(bf16)
        bias_grad[:, where] = jnp.sum(diff.astype(f32), axis=0, keepdims=True)
        pl.when(n >= 2)(lambda: store(n - 2).wait())
        staged[n % 2] = matmul(second_t[...], diff).astype(bf16)
        store(n).start()
        second_back[...] += matmul_rt(diff, expand_in[:, where])
        follow(n, after)
        return 0

    first = {
        1: [(reduce.start, 0)],
        2: [(reduce.exchange, 0)],
        3: [(reduce.start, 1)],
        4: [(reduce.spread, 0), (reduce.exchange, 1)],
        5: [(reduce.start, 2)],
        6: [(reduce.send, 0), (reduce.spread, 1), (reduce.exchange, 2)],
        7: [(reduce.start, 3)],
    }
    second_steps = {
        0: [(reduce.send, 1), (reduce.spread, 2), (reduce.exchange, 3)],
        2: [(reduce.send, 2), (reduce.spread, 3)],
        4: [(reduce.send, 3)],
    }
    lax.fori_loop(0, steps, lambda n, _: forward(n, first), 0)
    layer[...] = second_back[...].astype(bf16).reshape(layer.shape)
    second_back[...] = jnp.zeros_like(second_back)
    go(returned + [stay])
    lax.fori_loop(0, steps, lambda n, _: backward(n, second_steps), 0)
    reduce.finish()
    store(steps - 2).wait()
    store(steps - 1).wait()
    arrive(returned)
    copies.finish()
    done([stay])


def feed_forward(shape, expand, contract, expand_bias, second, upstream, residual):
    own, parts, piece = shape
    rows, features = second.shape
    hidden = expand.shape[1]
    wide = hidden // 8
    each = hidden // 32
    out = remote_call(
        feed_forward_kernel,
        "feed_forward",
        4,
        out_shape=(
            jax.ShapeDtypeStruct((parts, own, piece, features), bf16),
            jax.ShapeDtypeStruct((rows, features), f32),
            jax.ShapeDtypeStruct((features, hidden), bf16),
            jax.ShapeDtypeStruct((1, hidden), f32),
            jax.ShapeDtypeStruct((each, features), f32),
        ),
        in_specs=[HBM, HBM, VMEM, VMEM, VMEM, VMEM],
        out_specs=(HBM, VMEM, HBM, VMEM, VMEM),
        scratch_shapes=[
            pltpu.VMEM((features, hidden), bf16),
            pltpu.VMEM((hidden, features), bf16),
            pltpu.VMEM((features, rows), bf16),
            pltpu.VMEM((rows, hidden), f32),
            pltpu.VMEM((4, 4, 2, each, features), bf16),
            pltpu.VMEM((own, parts, piece, features), bf16),
            pltpu.VMEM((2, features, wide), bf16),
            *reduce_lines_scratch(each, features),
            pltpu.SemaphoreType.DMA((2, 8)),
            pltpu.SemaphoreType.DMA((2,)),
            *semaphores(ReduceLines.copies + 3, 1),
        ],
    )(expand, contract, expand_bias, second, upstream, residual)
    return out[0].reshape(parts * own, piece, features), *out[1:]


def backward_fused_kernel(heads, width, count, chunks, *refs):
    slopes, diff_in, qkv_in, out_t_in, lse_in = refs[:5]
    grads, refs = refs[5 : 5 + count], refs[5 + count :]
    joined_out, outs, refs = refs[0], refs[1 : 1 + count], refs[1 + count :]
    diff, qkv, out_t, lse, joined = refs[:5]
    attention = Backward(heads, width, slopes, qkv, diff, out_t, lse, joined, *refs[5:12])
    bufs, refs = refs[12 : 12 + 7 * len(chunks)], refs[12 + 7 * len(chunks) :]
    copies = Copies(*refs)
    place = Place()
    s, plane = place.s, place.plane
    features = heads * width
    mine = columns_of(s, 3 * features)
    reduce = Reduce(place, grads, outs, bufs, chunks, copies)

    own = [copies.inside(diff_in.at[:, :, :, columns_of(s, features)], diff.at[:, :, s])]
    own += [copies.inside(a, b) for a, b in ((qkv_in, qkv), (out_t_in, out_t), (lse_in, lse))]
    arriving = [
        copies.plan(diff_in.at[:, :, :, columns_of(to[1], features)], diff.at[:, :, s], to)
        for to in plane
    ]
    back = [
        [copies.plan(joined.at[b, :, to[1]], joined_out.at[b, :, :, mine], to) for to in plane]
        for b in range(2)
    ]
    stay = [copies.inside(joined.at[b, :, s], joined_out.at[b, :, :, mine]) for b in range(2)]

    def hand_back(b):
        go(back[b] + stay[b : b + 1])

    go(own + reduce.loads)
    greet(place.lines + plane)
    go(arriving)
    reduce.start()
    for t in range(3):
        reduce.exchange(t)
    done(own)
    arrive(arriving)
    attention.run(
        {
            1: [(reduce.spread, 0)],
            3: [(hand_back, 0)],
            4: [(reduce.spread, 1), (reduce.spread, 2), (reduce.send, 0)],
            7: [(hand_back, 1)],
        }
    )
    reduce.send(1)
    reduce.send(2)
    for t in range(3):
        reduce.finish(t)
    arrive(back[0] + back[1])
    copies.finish()
    done(stay)


def backward_fused(attended_diff, qkv, saved, grads, slopes, heads, width):
    own, parts, piece, columns = attended_diff.shape
    features = heads * width
    length = parts * 8 * piece
    cut = [split_grad(item) for item in grads]
    count = len(cut)
    chunks = []
    for t, pieces in enumerate((2, 1)):
        chunks += chunks_of(t, *cut[t].shape[3:], pieces)
    out = remote_call(
        functools.partial(backward_fused_kernel, heads, width, count, chunks),
        "backward_fused",
        2,
        out_shape=(
            jax.ShapeDtypeStruct((own, parts, piece, 24 * features), bf16),
            *[jax.ShapeDtypeStruct(item.shape[3:], f32) for item in cut],
        ),
        in_specs=[SMEM] + [HBM] * (4 + count),
        out_specs=(HBM,) + (VMEM,) * count,
        scratch_shapes=[
            pltpu.VMEM((own, parts, 8, piece, features), bf16),
            pltpu.VMEM(qkv.shape, bf16),
            *[pltpu.VMEM(item.shape, f32) for item in saved],
            pltpu.VMEM(qkv.shape, bf16),
            *backward_scratch(length, heads, width),
            *reduce_scratch(chunks),
            *semaphores(7 + 14 + len(chunks) * Reduce.copies_each, len(chunks) + 6),
        ],
    )(slopes, attended_diff, qkv, *saved, *cut)
    return out[0], out[1:]


def end_kernel(chunks, input_grad, vector, grad, input_out, vector_out, out, *refs):
    input_own, ranks, plane_sum, others = refs[:4]
    bufs, refs = refs[4 : 4 + 7 * len(chunks)], refs[4 + 7 * len(chunks) :]
    copies = Copies(*refs)
    place = Place()
    z, s, lines, plane = place.z, place.s, place.lines, place.plane
    count = len(chunks)
    reduce = Reduce(place, [grad], [out], bufs, chunks, copies)
    load = copies.inside(input_grad.at[:, z], input_own)
    load_vector = copies.inside(vector.at[:, s], ranks.at[0])
    keep = copies.inside(input_own, input_out.at[z])
    waiting = [copies.plan(input_grad.at[:, to[0]], input_out.at[z], to) for to in lines]
    vectors = [
        copies.plan(vector.at[:, to[1]], ranks.at[d + 1], to) for d, to in enumerate(plane)
    ]
    sums = [copies.plan(plane_sum.at[to[0]], others.at[k], to) for k, to in enumerate(lines)]
    go(reduce.loads + [load, load_vector])
    greet(lines + plane)
    reduce.start()
    go(waiting + vectors)
    load.wait()
    go([keep])
    for t in range(count + 2):
        if t < count:
            reduce.exchange(t)
        if t == 0:
            load_vector.wait()
            arrive(vectors)
            total = ranks[0]
            for d in range(1, 8):
                total = total + ranks[d]
            plane_sum[...] = total
            go(sums)
        if 0 <= t - 1 < count:
            reduce.spread(t - 1)
        if 0 <= t - 2:
            reduce.send(t - 2)
    arrive(sums)
    total = plane_sum[z]
    for k in range(3):
        total = total + others[k]
    vector_out[...] = total
    for t in range(count):
        reduce.finish(t)
    arrive(waiting)
    copies.finish()
    keep.wait()


def end(input_grad, vector, grad):
    own, parts, piece, features = input_grad.shape
    lanes = vector.shape[-1]
    padded = -(-lanes // 1024) * 1024
    vector = jnp.pad(vector, ((0, 0), (0, padded - lanes))).reshape(4, 8, padded // 128, 128)
    cut = split_grad(grad)
    chunks = chunks_of(0, *cut.shape[3:], 3)
    out = remote_call(
        functools.partial(end_kernel, chunks),
        "end",
        3,
        out_shape=(
            jax.ShapeDtypeStruct((parts, own, piece, features), bf16),
            jax.ShapeDtypeStruct(vector.shape[2:], f32),
            jax.ShapeDtypeStruct(cut.shape[3:], f32),
        ),
        in_specs=[HBM] * 3,
        out_specs=(HBM, VMEM, VMEM),
        scratch_shapes=[
            pltpu.VMEM((own, piece, features), bf16),
            pltpu.VMEM((8, 4, padded // 128, 128), f32),
            pltpu.VMEM((4, padded // 128, 128), f32),
            pltpu.VMEM((3, padded // 128, 128), f32),
            *reduce_scratch(chunks),
            *semaphores(3 + 7 + 3 + len(chunks) * Reduce.copies_each, 3 + len(chunks)),
        ],
    )(input_grad, vector, cut)
    return out[0].reshape(parts * own, piece, features), out[1].reshape(-1)[:lanes], out[2]


def per_device(
    layer_input,
    first_gain,
    first_shift,
    joined_weight,
    query_bias,
    value_bias,
    output_weight,
    output_bias,
    second_gain,
    second_shift,
    expand_weight,
    expand_bias,
    contract_weight,
    contract_bias,
    alibi_slopes,
    upstream,
):
    seqs, piece, features = layer_input.shape
    fs_count = lax.axis_size("fs")
    sp_count = lax.axis_size("sp")
    head_count = alibi_slopes.shape[0]
    width = features // head_count
    heads = head_count // sp_count
    rows = seqs * piece
    own = seqs // fs_count
    shape = (own, fs_count, piece)
    slopes = lax.dynamic_slice_in_dim(alibi_slopes, lax.axis_index("sp") * heads, heads)

    vectors = (
        first_gain, first_shift, query_bias, value_bias, output_bias,
        second_gain, second_shift, contract_bias, expand_bias,
    )
    fast = (fs_count, sp_count) == (4, 8) and (own, heads) == (2, 2)
    weights = (output_weight, expand_weight, contract_weight)
    gather = lambda item: lax.all_gather(item, "fs", axis=0, tiled=True)
    if fast:
        tokens, joined_full, whole = begin(layer_input, vectors, joined_weight)
    else:
        tokens, joined_full = to_own_seqs(layer_input), gather(joined_weight)
        whole = [gather(item) for item in vectors]
    tokens = tokens.reshape(rows, features).astype(f32)
    gain_one, shift_one, qbias, vbias, obias, gain_two, shift_two, cbias, ebias = [
        item.astype(f32) for item in whole
    ]

    normed_f, norm_back_one = jax.vjp(normalize, tokens, gain_one, shift_one)
    normed = normed_f.astype(bf16)
    joined_all = (matmul(normed, joined_full) + joined_bias_of(qbias, vbias, head_count)).astype(
        bf16
    )
    joined_all = joined_all.reshape(*shape, 3 * features)
    if fast:
        qkv, attended, saved, upstream_low, weights = forward_fused(
            joined_all, upstream, weights, slopes, heads, width
        )
    else:
        qkv = to_heads(joined_all)
        attended, *saved = attention_forward(qkv, slopes, heads, width)
        attended, upstream_low = from_heads(attended), to_own_seqs(upstream)
        weights = [gather(item) for item in weights]
    out_full, expand_full, contract_full = weights
    attended = attended.reshape(rows, features)
    upstream_low = upstream_low.reshape(rows, features)

    residual = tokens + (matmul(attended, out_full) + obias)
    second_f, norm_back_two = jax.vjp(normalize, residual, gain_two, shift_two)
    second = second_f.astype(bf16)
    upstream_f = upstream_low.astype(f32)
    contract_bias_grad = jnp.sum(upstream_f, axis=0)
    if fast:
        layer_output, second_back, expand_grad, expand_bias_grad, contract_grad = feed_forward(
            shape, expand_full, contract_full, ebias.reshape(1, -1), second, upstream_low,
            residual + cbias,
        )
        expand_bias_grad = expand_bias_grad.reshape(-1)
    else:
        expanded = matmul(second, expand_full) + ebias
        activated_f, gelu_back = jax.vjp(gelu_tanh, expanded)
        activated = activated_f.astype(bf16)
        result = residual + (matmul(activated, contract_full) + cbias)
        layer_output = result.astype(bf16).reshape(*shape, features)

        contract_grad = matmul_lt(activated, upstream_low)
        act_grad = matmul_rt(upstream_low, contract_full)
        expand_diff = gelu_back(act_grad)[0].astype(bf16)
        expand_grad = matmul_lt(second, expand_diff)
        expand_bias_grad = jnp.sum(expand_diff.astype(f32), axis=0)
        second_back = matmul_rt(expand_diff, expand_full)
    resid_part, second_gain_grad, second_shift_grad = norm_back_two(second_back)
    residual_grad = upstream_f + resid_part

    branch_diff = residual_grad.astype(bf16)
    output_weight_grad = matmul_lt(attended, branch_diff)
    output_bias_grad = jnp.sum(branch_diff.astype(f32), axis=0)
    attended_diff = matmul_rt(branch_diff, out_full).astype(bf16)
    attended_diff = attended_diff.reshape(*shape, features)
    grads = (expand_grad, output_weight_grad)
    scatter = functools.partial(
        lax.psum_scatter, axis_name=("fs", "sp"), scatter_dimension=0, tiled=True
    )
    if fast:
        joined_diff, grads = backward_fused(
            attended_diff, qkv, saved, [item.astype(bf16) for item in grads], slopes, heads, width
        )
    else:
        joined_diff = attention_backward(
            qkv, to_heads(attended_diff), *saved, slopes, heads, width
        )
        joined_diff, layer_output = from_heads(joined_diff), from_own_seqs(layer_output)
        grads = [scatter(item) for item in grads]
        contract_grad = scatter(contract_grad)
    expand_grad, output_weight_grad = grads
    joined_diff = joined_diff.reshape(rows, 3 * features)

    joined_grad = matmul_lt(normed, joined_diff)
    column_sums = jnp.sum(joined_diff.astype(f32), axis=0).reshape(head_count, 3, width)
    query_bias_grad = column_sums[:, 0].reshape(features)
    value_bias_grad = column_sums[:, 2].reshape(features)
    normed_back = matmul_rt(joined_diff, joined_full)
    input_part, first_gain_grad, first_shift_grad = norm_back_one(normed_back)
    input_grad = (residual_grad + input_part).astype(bf16).reshape(*shape, features)

    vector_grads = (
        first_gain_grad, first_shift_grad, query_bias_grad, value_bias_grad, output_bias_grad,
        second_gain_grad, second_shift_grad, contract_bias_grad, expand_bias_grad,
    )
    devices = fs_count * sp_count
    packed = jnp.concatenate([item.reshape(devices, -1) for item in vector_grads], axis=1)
    if fast:
        input_grad, packed, joined_grad = end(input_grad, packed, joined_grad.astype(bf16))
    else:
        input_grad, joined_grad = from_own_seqs(input_grad), scatter(joined_grad)
        packed = scatter(packed.reshape(-1))
    own_grads, at = [], 0
    for item in vector_grads:
        size = item.shape[0] // devices
        own_grads.append(packed[at : at + size])
        at += size
    g1, s1, qb, vb, ob, g2, s2, cb, eb = own_grads
    return (
        layer_output,
        input_grad,
        g1,
        s1,
        joined_grad,
        qb,
        vb,
        output_weight_grad,
        ob,
        g2,
        s2,
        expand_grad,
        eb,
        contract_grad,
        cb,
    )


def solution(mesh):
    tokens = P(None, ("fs", "sp"), None)
    both, both_rows = P(("fs", "sp")), P(("fs", "sp"), None)
    one, one_rows = P("fs"), P("fs", None)
    return jax.shard_map(
        per_device,
        mesh=mesh,
        in_specs=(
            tokens, one, one, one_rows, one, one, one_rows, one, one, one, one_rows, one,
            one_rows, one, P(), tokens,
        ),
        out_specs=(
            tokens, tokens, both, both, both_rows, both, both, both_rows, both, both, both,
            both_rows, both, both_rows, both,
        ),
        check_vma=False,
    )
```

time: 531 us -> 465 us (0.88); the launches traced: 522 us -> 464 us
  matrix products: 92.5 us -> 30.2 us
  local copies, waits for them, and re-layouts: 20.4 us -> 12.2 us
  Pallas kernels: 394 us -> 402 us
    dot_general x4 -> x2, matrix products: 32.7 us -> 9 us  [matmul_rt(): lax.dot_general(left_side, right_side, (((1,), (1,)), ((), ())), preferre...]
    dot_general x4 -> x2, matrix products: 31.3 us -> 10.3 us  [matmul_lt(): lax.dot_general(left_side, right_side, (((0,), (0,)), ((), ())), preferre...]
    dot_general x4 -> x2, matrix products: 28.5 us -> 11 us  [matmul(): return jnp.dot(left_side, right_side, preferred_element_type=f32)]
    pallas_call x4 -> x5, Pallas kernels: 394 us -> 402 us  [the longest x1 118 us: forward_fused(): remote_call(functools.partial(forward_fused_kernel, heads, width, count,...]
    unnamed x64 -> x62, local copies, waits for them, and re-layouts: 14.6 us -> 7.79 us
where the time goes in v4:
time: 465 us; the launch traced here: 464 us
  Pallas kernels  402 us (86%)
  matrix products  30.2 us (6%)
  other arithmetic  18.8 us (4%)
  local copies, waits for them, and re-layouts  12.2 us (3%)
    pallas_call x1, Pallas kernels, forward_fused(): remote_call(functools.partial(forward_fused_kernel, heads, width, count,...  118 us
    pallas_call x1, Pallas kernels, backward_fused(): remote_call(functools.partial(backward_fused_kernel, heads, width, count,...  94.9 us
    pallas_call x1, Pallas kernels, feed_forward(): remote_call(feed_forward_kernel, 'feed_forward', 4, out_shape=(jax.ShapeD...  77.6 us
    pallas_call x1, Pallas kernels, begin(): remote_call(functools.partial(begin_kernel, count, chunks), 'begin', 0, o...  65 us
    pallas_call x1, Pallas kernels, end(): remote_call(functools.partial(end_kernel, chunks), 'end', 3, out_shape=(j...  46.5 us
    dot_general x2, matrix products, matmul(): return jnp.dot(left_side, right_side, preferred_element_type=f32)  11 us
    dot_general x2, matrix products, matmul_lt(): lax.dot_general(left_side, right_side, (((0,), (0,)), ((), ())), preferre...  10.3 us

profile of v4, /device:TPU:0, one launch (start us, length us, event | category | flops | bytes accessed | tf_op | source)
XLA Modules:
  0.0 464.4 jit_solution(573376495695464070)
XLA Ops:
  0.6 65.0 %begin.1 = (bf16[2,4,64,1024]{3,2,1,0:T(8,128)(2,1)}, bf16[4,8,32,3072]{3,2,1,0:T(8,128)(2,1)}, bf16[4,2,128]{2,1,0:T(2,128)(2,1)}, bf16[4,2,128]{2,1,0:T(2,128)...) custom-call(bf16[4,2,64,1024]{3,2,1,0:T(8,128)(2,1)} %bitcast.112, ...), custom_call_target="tpu_custom_call" | custom-call | tf_op jit(solution)/shard_map/begin/pallas_call | solution.py:794
  65.7 1.5 convert_reduce_fusion.1
  67.2 1.6 fusion.5
  69.8 7.7 %add_convert_fusion = bf16[512,3072]{1,0:T(8,128)(2,1)} fusion(bf16[512,1024]{1,0:T(8,128)(2,1)S(1)} %bitcast.114, bf16[1024,3072]{1,0:T(8,128)(2,1)} %bitcast.136, f32[3072]{0:T(1024)S(1)} %add.86), kind=kOutput, calls=%fused_computation.2 | convolution fusion | flops 3224371200 | bytes 10498048 | tf_op jit(solution)/shard_map/dot_general | solution.py:36
  78.1 118.2 %forward_fused.1 = (bf16[2,4,8,64,384]{4,3,2,1,0:T(8,128)(2,1)}, bf16[2,4,64,1024]{3,2,1,0:T(8,128)(2,1)}, f32[2,2,64,2048]{3,2,1,0:T(8,128)}, f32[2,2,1,2048]{3...) custom-call(f32[2]{0:T(128)} %dynamic_slice.3.slopes.refs_0_, ...), custom_call_target="tpu_custom_call" | custom-call | tf_op jit(solution)/shard_map/forward_fused/pallas_call | solution.py:893
  196.3 3.3 fusion.20
  200.3 2.2 broadcast_add_fusion
  203.1 77.6 %feed_forward.1 = (bf16[4,2,64,1024]{3,2,1,0:T(8,128)(2,1)}, f32[512,1024]{1,0:T(8,128)}, bf16[1024,4096]{1,0:T(8,128)(2,1)}, f32[1,4096]{1,0:T(1,128)}, f32[128,1024]{1,0:T(8,128)}) custom-call(bf16[1024,4096]{1,0:T(8,128)(2,1)} %bitcast.100, bf16[4096,1024]{1,0:T(8,128)(2,1)} %bitcast.101, f32[1,4096]{1,0:T(1,128)} %bitcast.117, ...), custom_call_target="tpu_custom_call" | custom-call | tf_op jit(solution)/shard_map/feed_forward/pallas_call | solution.py:1025
  280.7 2.5 multiply_reduce_fusion
  285.9 2.7 convolution_convert_fusion
  288.6 2.3 convolution_convert_fusion.1
  290.9 94.9 %backward_fused.1 = (bf16[2,4,64,3072]{3,2,1,0:T(8,128)(2,1)}, f32[32,4096]{1,0:T(8,128)}, f32[32,1024]{1,0:T(8,128)}) custom-call(f32[2]{0:T(128)} %dynamic_slice.3.slopes.refs_0_, bf16[2,4,64,1024]{3,2,1,0:T(8,128)(2,1)} %bitcast.111, bf16[2,4,8,64,384]{4,3,2,1,0:T(8,128)(2,1)} %get-tuple-element.63.refs_2_, f32[2,2,64,2048]{3,2,1,0:T(8,128)} %get-tuple-element.64.refs_3_, ...), custom_call_target="tpu_custom_call" | custom-call | tf_op jit(solution)/shard_map/backward_fused/pallas_call | solution.py:1118
  385.8 7.6 %bitcast_convert_fusion = bf16[1024,3072]{1,0:T(8,128)(2,1)} fusion(bf16[2,4,64,1024]{3,2,1,0:T(8,128)(2,1)S(1)} %copy-done.8, bf16[2,4,64,3072]{3,2,1,0:T(8,128)(2,1)} %get-tuple-element.67), kind=kOutput, calls=%fused_computation | convolution fusion | flops 3224371200 | bytes 10485760 | tf_op jit(solution)/shard_map/dot_general | solution.py:40
  393.4 6.7 %fusion.16 = (f32[1024]{0:T(1024)S(1)}, f32[512]{0:T(512)S(1)}, f32[512,1024]{1,0:T(8,128)S(1)}) fusion(f32[1024]{0:T(1024)S(1)} %convert.10, f32[512]{0:T(512)S(1)} %div.45, bf16[2,4,64,1024]{3,2,1,0:T(8,128)(2,1)S(1)} %copy-done, bf16[512,3072]{1,0:T(8,128)(2,1)} %bitcast.104, bf16[1024,3072]{1,0:T(8,128)(2,1)} %bitcast.137), kind=kOutput, calls=%fused_computation.51 | convolution fusion | flops 3224369664 | bytes 12595200 | tf_op jit(solution)/shard_map/dot_general | solution.py:46
  400.3 1.0 fusion.11
  401.7 2.7 convert_reduce_fusion
  404.8 1.4 convert_reduce_fusion.2
  407.1 3.2 add_convert_fusion.1
  410.4 46.5 %end.1 = (bf16[4,2,64,1024]{3,2,1,0:T(8,128)(2,1)}, f32[8,128]{1,0:T(8,128)}, f32[32,3072]{1,0:T(8,128)}) custom-call(bf16[2,4,64,1024]{3,2,1,0:T(8,128)(2,1)} %bitcast.103, f32[4,8,8,128]{3,2,1,0:T(8,128)} %copy.36, bf16[4,4,2,32,3072]{4,3,2,1,0:T(8,128)(2,1)} %bitcast.102), custom_call_target="tpu_custom_call" | custom-call | tf_op jit(solution)/shard_map/end/pallas_call | solution.py:1197
  458.2 1.2 slice_bitcast_fusion.1
  459.4 1.0 copy.43
  460.4 1.0 copy.44
  462.8 0.8 copy.47
  463.6 0.8 copy.48
  (98 shorter events, 10.2 us)
Async XLA Ops:
  65.6 3.2 copy-start.23
  65.6 3.2 copy-start.22
  65.7 3.3 copy-start
  65.7 3.7 copy-start.21
  65.7 3.8 copy-start.20
  69.4 8.1 %copy-start.7 = (bf16[2,4,64,1024]{3,2,1,0:T(8,128)(2,1)}, bf16[2,4,64,1024]{3,2,1,0:T(8,128)(2,1)S(1)}, u32[]{:S(2)}) copy-start(bf16[2,4,64,1024]{3,2,1,0:T(8,128)(2,1)S(1)} %fusion.8) | copy-start | bytes 3145732
  69.8 7.7 %copy-start.26 = (f32[16]{0:T(128)S(1)}, f32[16]{0:T(128)}, u32[]{:S(2)}) copy-start(f32[16]{0:T(128)} %param.30) | copy-start | bytes 196
  78.1 118.3 %copy-start.19 = (bf16[4,2,128]{2,1,0:T(2,128)(2,1)S(1)}, bf16[4,2,128]{2,1,0:T(2,128)(2,1)}, u32[]{:S(2)}) copy-start(bf16[4,2,128]{2,1,0:T(2,128)(2,1)} %get-tuple-element.56) | copy-start | bytes 6148
  200.3 2.2 copy-start.15
  280.7 2.5 copy-start.5
  283.2 1.2 copy-start.3
  283.9 1.3 copy-start.1
  284.4 1.5 copy-start.25
  285.9 2.7 copy-start.24
  290.9 94.9 %copy-start.8 = (bf16[2,4,64,1024]{3,2,1,0:T(8,128)(2,1)S(1)}, bf16[2,4,64,1024]{3,2,1,0:T(8,128)(2,1)}, u32[]{:S(2)}) copy-start(bf16[2,4,64,1024]{3,2,1,0:T(8,128)(2,1)} %copy-done.7) | copy-start | bytes 3145732
  400.2 1.4 copy-start.4
  401.7 4.7 %copy-start.14 = (f32[1,4096]{1,0:T(1,128)S(1)}, f32[1,4096]{1,0:T(1,128)}, u32[]{:S(2)}) copy-start(f32[1,4096]{1,0:T(1,128)} %get-tuple-element.68) | copy-start | bytes 49156
  401.7 5.5 %copy-start.2 = (f32[512,1024]{1,0:T(8,128)S(1)}, f32[512,1024]{1,0:T(8,128)}, u32[]{:S(2)}) copy-start(f32[512,1024]{1,0:T(8,128)} %copy-done.1) | copy-start | bytes 6291460
  410.4 49.1 %copy-start.6 = (bf16[4,2,64,1024]{3,2,1,0:T(8,128)(2,1)S(1)}, bf16[4,2,64,1024]{3,2,1,0:T(8,128)(2,1)}, u32[]{:S(2)}) copy-start(bf16[4,2,64,1024]{3,2,1,0:T(8,128)(2,1)} %get-tuple-element.61) | copy-start | bytes 3145732
  456.8 3.6 copy-start.9
  459.4 2.0 copy-start.12
  459.4 2.7 copy-start.13
  459.4 3.4 copy-start.11
  460.4 3.2 copy-start.10
  (3 other events, 2.0 us)

commit v5 on v4

--- a/solution.py
+++ b/solution.py
@@ -450,8 +450,13 @@
 
     def __init__(self, place, weights, wholes, kept, chunks, copies):
         z, s, lines = place.z, place.s, place.lines
-        self.loads = [copies.inside(w, k) for w, k in zip(weights, kept)]
-        self.own = [copies.inside(k, whole.at[z]) for k, whole in zip(kept, wholes)]
+        self.loads, self.own = [], []
+        for weight, whole, keep in zip(weights, wholes, kept):
+            if keep is None:
+                self.loads.append(copies.inside(weight, whole.at[z]))
+            else:
+                self.loads.append(copies.inside(weight, keep))
+                self.own.append(copies.inside(keep, whole.at[z]))
         self.first, self.second, self.third, self.cores, self.last = [], [], [], [], []
         for t, row, rows, column, columns in chunks:
             whole = wholes[t]
@@ -505,10 +510,8 @@
         arrive(self.third[t])
         go(self.last[t])
 
-    def finish(self):
-        for copies in self.cores + self.last:
-            arrive(copies)
-        done(self.own)
+    def complete(self, t):
+        arrive(self.cores[t] + self.last[t])
 
 
 def add_into(target, other):
@@ -742,180 +745,215 @@
     )
 
 
-def begin_kernel(count, chunks, tokens, weight, *refs):
-    vectors, refs = refs[:count], refs[count:]
-    tokens_out, whole = refs[:2]
-    vectors_out, refs = refs[2 : 2 + count], refs[2 + count :]
-    tokens_own, kept = refs[:2]
+def columns_of(rank, features):
+    return pl.ds(pl.multiple_of(rank * features, 128), features)
+
+
+def forward_fused_kernel(heads, width, count, vector_count, chunks, slopes, tokens, upstream, *refs):
+    vectors, refs = refs[:vector_count], refs[vector_count:]
+    weights, refs = refs[:count], refs[count:]
+    tokens_out, vectors_out, joined_out, qkv_out, attended, out_t, lse, upstream_out = refs[:8]
+    wholes, refs = refs[8 : 7 + count], refs[7 + count :]
+    held, small, values_of, joined, normed, outgoing, qkv, result, upstream_own = refs[:9]
+    attention = Forward(heads, width, slopes, qkv, result, out_t, lse, *refs[9:12])
+    kept, refs = refs[12 : 11 + count], refs[11 + count :]
+    head_send, head_recv = refs[:2]
     copies = Copies(*refs[2:])
     place = Place()
-    z, lines = place.z, place.lines
-    gather = Gather(place, [weight], [whole], [kept], chunks, copies)
-    load = copies.inside(tokens.at[z], tokens_own)
-    own = [copies.inside(tokens_own, tokens_out.at[:, z])]
-    small = [copies.inside(item, out.at[z]) for item, out in zip(vectors, vectors_out)]
-    waiting = []
-    for to in lines:
-        waiting.append(copies.plan(tokens.at[to[0]], tokens_out.at[:, z], to))
-        waiting += [
-            copies.plan(item, out.at[z], to) for item, out in zip(vectors, vectors_out)
-        ]
-    go(gather.loads)
-    go([load])
-    go(small)
-    greet(place.near)
-    gather.start(0)
-    go(waiting)
-    for t in range(1, len(chunks)):
-        gather.start(t)
-    load.wait()
-    go(own)
-    gather.keep()
-    for t in range(len(chunks) + 2):
-        if t < len(chunks):
-            gather.exchange(t)
-        if 0 <= t - 1 < len(chunks):
-            gather.spread(t - 1)
-        if 0 <= t - 2:
-            gather.share(t - 2)
-    gather.finish()
-    arrive(waiting)
-    copies.finish()
-    done(own + small)
-
-
-def begin(tokens, vectors, weight):
-    seqs, piece, features = tokens.shape
-    own = seqs // 4
-    vectors = [item.reshape(-1, 128) for item in vectors]
-    count = len(vectors)
-    cut = split_weight(weight)
-    chunks = chunks_of(0, cut.shape[1], cut.shape[2], 3)
-    out = remote_call(
-        functools.partial(begin_kernel, count, chunks),
-        "begin",
-        0,
-        out_shape=(
-            jax.ShapeDtypeStruct((own, 4, piece, features), bf16),
-            jax.ShapeDtypeStruct((4, *cut.shape), bf16),
-            *[jax.ShapeDtypeStruct((4, *item.shape), bf16) for item in vectors],
-        ),
-        in_specs=[HBM] * (2 + count),
-        out_specs=(HBM,) * (2 + count),
-        scratch_shapes=[
-            pltpu.VMEM((own, piece, features), bf16),
-            pltpu.VMEM(cut.shape, bf16),
-            *semaphores(3 + 3 * count + len(chunks) * Gather.copies_each, 4 + count),
-        ],
-    )(tokens.reshape(4, own, piece, features), cut, *vectors)
-    return out[0], out[1].reshape(4 * weight.shape[0], -1), [item.reshape(-1) for item in out[2:]]
-
-
-def columns_of(rank, features):
-    return pl.ds(pl.multiple_of(rank * features, 128), features)
-
-
-def forward_fused_kernel(heads, width, count, chunks, slopes, source, upstream, *refs):
-    weights, refs = refs[:count], refs[count:]
-    qkv_out, attended, out_t, lse, upstream_out = refs[:5]
-    wholes, refs = refs[5 : 5 + count], refs[5 + count :]
-    qkv, result, upstream_own = refs[:3]
-    attention = Forward(heads, width, slopes, qkv, result, out_t, lse, *refs[3:6])
-    kept, refs = refs[6 : 6 + count], refs[6 + count :]
-    copies = Copies(*refs)
-    place = Place()
     z, s, lines, plane = place.z, place.s, place.lines, place.plane
-    gather = Gather(place, weights, wholes, kept, chunks, copies)
+    gather = Gather(place, weights, [joined, *wholes], [None, *kept], chunks, copies)
+    first = [t for t, chunk in enumerate(chunks) if chunk[0] == 0]
+    later = [t for t, chunk in enumerate(chunks) if chunk[0] > 0]
     features = heads * width
     mine = columns_of(s, features)
-
-    own = [
-        copies.inside(source.at[:, :, :, columns_of(s, 3 * features)], qkv.at[:, :, s]),
-        copies.inside(upstream.at[z], upstream_own),
+    own_seqs, parts, piece, wide = held.shape
+
+    load = copies.inside(tokens.at[z], held.at[:, z])
+    load_upstream = copies.inside(upstream.at[z], upstream_own)
+    seqs = [copies.plan(tokens.at[to[0]], held.at[:, z], to) for to in lines]
+    vector_copies = [copies.plan(small.at[z], small.at[z], to) for to in lines]
+    upstreams = [copies.plan(upstream.at[to[0]], upstream_out.at[:, z], to) for to in lines]
+    keep_upstream = copies.inside(upstream_own, upstream_out.at[:, z])
+    keeping = [
+        copies.inside(held, tokens_out),
+        copies.inside(small, vectors_out),
+        copies.inside(joined, joined_out),
     ]
-    arriving = [
-        copies.plan(source.at[:, :, :, columns_of(to[1], 3 * features)], qkv.at[:, :, s], to)
-        for to in plane
-    ]
-    later = [copies.plan(upstream.at[to[0]], upstream_out.at[:, z], to) for to in lines]
-    keeping = [copies.inside(upstream_own, upstream_out.at[:, z]), copies.inside(qkv, qkv_out)]
+    keep_qkv = copies.inside(qkv, qkv_out)
     back = [
         [copies.plan(result.at[b, :, to[1]], attended.at[b, :, :, mine], to) for to in plane]
         for b in range(2)
     ]
     stay = [copies.inside(result.at[b, :, s], attended.at[b, :, :, mine]) for b in range(2)]
 
+    def to_head(d):
+        return pltpu.make_async_remote_copy(
+            src_ref=outgoing.at[d],
+            dst_ref=qkv.at[:, :, s],
+            send_sem=head_send.at[d],
+            recv_sem=head_recv.at[d],
+            device_id=(z, lax.rem(s + 1 + d, 8)),
+            device_id_type=MESH,
+        )
+
     def hand_back(b):
         go(back[b] + stay[b : b + 1])
 
-    go(gather.loads + own)
+    go(gather.loads + [load, load_upstream])
+    small[z] = jnp.zeros(small.shape[1:], bf16)
+    for n, item in enumerate(vectors):
+        small[z, n, : item.shape[0], :] = item[...]
     greet(lines + plane)
-    go(arriving)
-    for t in range(len(chunks)):
+    for t in first:
         gather.start(t)
-    go(later)
-    done(own)
+    go(seqs + vector_copies)
+    for t in later:
+        gather.start(t)
+    go(upstreams)
     gather.keep()
-    arrive(arriving)
+    load.wait()
+    for t in range(len(first) + 2):
+        if t < len(first):
+            gather.exchange(t)
+        if 0 <= t - 1 < len(first):
+            gather.spread(t - 1)
+        if 0 <= t - 2:
+            gather.share(t - 2)
+    load_upstream.wait()
+    keep_upstream.start()
+    arrive(seqs + vector_copies)
+    values_of[...] = small[...].astype(f32)
+
+    def row_of(n):
+        found = [values_of[k, n, r : r + 1, :] for k in range(4) for r in range(wide // 512)]
+        return jnp.concatenate(found, axis=1)
+
+    gain, shift = row_of(0), row_of(1)
+
+    def norm(i, _):
+        values = held[i // parts, i % parts].astype(f32)
+        rows = pl.ds(pl.multiple_of(i * piece, piece), piece)
+        normed[rows, :] = normalize(values, gain, shift).astype(bf16)
+        return 0
+
+    lax.fori_loop(0, own_seqs * parts, norm, 0)
+    for t in first:
+        gather.complete(t)
     go(keeping)
-    for t in range(3):
-        gather.exchange(t)
+
+    def project(d, _):
+        rank = lax.rem(s + 1 + d, 8)
+        per = 8 // 4
+        query_bias = values_of[rank // per, 2, pl.ds(rank % per, 1), :]
+        value_bias = values_of[rank // per, 3, pl.ds(rank % per, 1), :]
+        low = lax.broadcasted_iota(jnp.int32, query_bias.shape, 1) < width
+        bias = jnp.concatenate(
+            [
+                jnp.where(low, query_bias, 0.0),
+                jnp.where(low, value_bias, query_bias),
+                jnp.where(low, 0.0, value_bias),
+            ],
+            axis=1,
+        )
+        weight = joined[:, :, :, columns_of(rank, 3 * features)].reshape(wide, 3 * features)
+        made = (matmul(normed[...], weight) + bias).astype(bf16)
+        outgoing[d] = made.reshape(outgoing.shape[1:])
+        pl.when(d < 7)(lambda: to_head(d).start())
+        return 0
+
+    lax.fori_loop(0, 8, project, 0)
+    own_copy = copies.inside(outgoing.at[7], qkv.at[:, :, s])
+    own_copy.start()
+    base = later[0]
+    gather.exchange(base)
+    gather.exchange(base + 1)
+    own_copy.wait()
+    for d in range(7):
+        to_head(d).wait_recv()
+    keep_qkv.start()
+    gather.exchange(base + 2)
     attention.run(
         {
-            2: [(gather.spread, 0), (gather.spread, 1), (gather.exchange, 3)],
+            2: [(gather.spread, base), (gather.spread, base + 1), (gather.exchange, base + 3)],
             3: [(hand_back, 0)],
-            5: [(gather.spread, 2), (gather.exchange, 4)],
-            6: [(gather.spread, 3), (gather.share, 0), (gather.share, 1)],
+            5: [(gather.spread, base + 2), (gather.exchange, base + 4)],
+            6: [(gather.spread, base + 3), (gather.share, base), (gather.share, base + 1)],
             7: [(hand_back, 1)],
         }
     )
-    gather.share(2)
-    gather.spread(4)
-    gather.share(3)
-    gather.share(4)
-    gather.finish()
-    arrive(later + back[0] + back[1])
+    gather.share(base + 2)
+    gather.spread(base + 4)
+    gather.share(base + 3)
+    gather.share(base + 4)
+    for t in later:
+        gather.complete(t)
+    arrive(upstreams + back[0] + back[1])
+    for d in range(7):
+        to_head(d).wait_send()
     copies.finish()
-    done(keeping + stay)
-
-
-def forward_fused(joined_all, upstream, weights, slopes, heads, width):
-    own, parts, piece, columns = joined_all.shape
-    features = heads * width
+    done(gather.own + [keep_upstream, keep_qkv] + keeping + stay)
+
+
+def forward_fused(tokens, upstream, vectors, weights, slopes, heads, width):
+    seqs, piece, features = tokens.shape
+    parts = 4
+    own = seqs // parts
+    columns = heads * width
     length = parts * 8 * piece
-    count = len(weights)
+    vectors = [item.reshape(-1, 128) for item in vectors]
     cut = [split_weight(item) for item in weights]
+    count, tall = len(cut), 8 * -(-max(item.shape[0] for item in vectors) // 8)
     chunks = []
-    for t, pieces in enumerate((1, 2, 2)):
+    for t, pieces in enumerate((3, 1, 2, 2)):
         chunks += chunks_of(t, *cut[t].shape[1:], pieces)
-    seq_shape = (own, parts, piece, 8 * features)
-    qkv_shape = (own, parts, 8, piece, 3 * features)
+    seq_shape = (own, parts, piece, features)
+    qkv_shape = (own, parts, 8, piece, 3 * columns)
+    small = (parts, len(vectors), tall, 128)
     out = remote_call(
-        functools.partial(forward_fused_kernel, heads, width, count, chunks),
+        functools.partial(forward_fused_kernel, heads, width, count, len(vectors), chunks),
         "forward_fused",
         1,
         out_shape=(
+            jax.ShapeDtypeStruct(seq_shape, bf16),
+            jax.ShapeDtypeStruct(small, bf16),
+            jax.ShapeDtypeStruct((parts, *cut[0].shape), bf16),
             jax.ShapeDtypeStruct(qkv_shape, bf16),
             jax.ShapeDtypeStruct(seq_shape, bf16),
             *saved_shapes(own, length, heads, width),
             jax.ShapeDtypeStruct(seq_shape, bf16),
-            *[jax.ShapeDtypeStruct((4, *item.shape), bf16) for item in cut],
+            *[jax.ShapeDtypeStruct((parts, *item.shape), bf16) for item in cut[1:]],
         ),
-        in_specs=[SMEM] + [HBM] * (2 + count),
-        out_specs=(HBM, HBM, VMEM, VMEM, HBM) + (HBM,) * count,
+        in_specs=[SMEM, HBM, HBM] + [VMEM] * len(vectors) + [HBM] * count,
+        out_specs=(HBM,) * 5 + (VMEM, VMEM) + (HBM,) * count,
         scratch_shapes=[
+            pltpu.VMEM(seq_shape, bf16),
+            pltpu.VMEM(small, bf16),
+            pltpu.VMEM(small, f32),
+            pltpu.VMEM((parts, *cut[0].shape), bf16),
+            pltpu.VMEM((own * parts * piece, features), bf16),
+            pltpu.VMEM((8, own, parts, piece, 3 * columns), bf16),
             pltpu.VMEM(qkv_shape, bf16),
-            pltpu.VMEM((own, parts, 8, piece, features), bf16),
-            pltpu.VMEM((own, piece, 8 * features), bf16),
+            pltpu.VMEM((own, parts, 8, piece, columns), bf16),
+            pltpu.VMEM((own, piece, features), bf16),
             *forward_scratch(length, heads, width),
-            *[pltpu.VMEM(item.shape, bf16) for item in cut],
-            *semaphores(7 + 3 + 14 + len(chunks) * Gather.copies_each, 2 * count + 6),
+            *[pltpu.VMEM(item.shape, bf16) for item in cut[1:]],
+            pltpu.SemaphoreType.DMA((7,)),
+            pltpu.SemaphoreType.DMA((7,)),
+            *semaphores(9 + 14 + len(chunks) * Gather.copies_each, 2 * count - 1 + 10),
         ],
-    )(slopes, joined_all, upstream.reshape(parts, own, piece, 8 * features), *cut)
+    )(
+        slopes,
+        tokens.reshape(parts, own, piece, features),
+        upstream.reshape(parts, own, piece, features),
+        *vectors,
+        *cut,
+    )
     wholes = [
-        whole.reshape(4 * item.shape[0], item.shape[1]) for whole, item in zip(out[5:], weights)
+        whole.reshape(4 * item.shape[0], item.shape[1])
+        for whole, item in zip((out[2], *out[8:]), weights)
     ]
-    return out[0], out[1], (out[2], out[3]), out[4], wholes
+    found = [out[1][:, n, : item.shape[0]].reshape(-1) for n, item in enumerate(vectors)]
+    return out[0], found, wholes, out[3], out[4], (out[5], out[6]), out[7]
 
 
 def feed_forward_kernel(
@@ -1250,14 +1288,17 @@
         first_gain, first_shift, query_bias, value_bias, output_bias,
         second_gain, second_shift, contract_bias, expand_bias,
     )
-    fast = (fs_count, sp_count) == (4, 8) and (own, heads) == (2, 2)
-    weights = (output_weight, expand_weight, contract_weight)
+    fast = (fs_count, sp_count) == (4, 8) and (own, heads, width) == (2, 2, 64)
+    weights = (joined_weight, output_weight, expand_weight, contract_weight)
     gather = lambda item: lax.all_gather(item, "fs", axis=0, tiled=True)
     if fast:
-        tokens, joined_full, whole = begin(layer_input, vectors, joined_weight)
+        tokens, whole, weights, qkv, attended, saved, upstream_low = forward_fused(
+            layer_input, upstream, vectors, weights, slopes, heads, width
+        )
     else:
-        tokens, joined_full = to_own_seqs(layer_input), gather(joined_weight)
-        whole = [gather(item) for item in vectors]
+        tokens, upstream_low = to_own_seqs(layer_input), to_own_seqs(upstream)
+        whole, weights = [gather(item) for item in vectors], [gather(item) for item in weights]
+    joined_full, out_full, expand_full, contract_full = weights
     tokens = tokens.reshape(rows, features).astype(f32)
     gain_one, shift_one, qbias, vbias, obias, gain_two, shift_two, cbias, ebias = [
         item.astype(f32) for item in whole
@@ -1265,20 +1306,12 @@
 
     normed_f, norm_back_one = jax.vjp(normalize, tokens, gain_one, shift_one)
     normed = normed_f.astype(bf16)
-    joined_all = (matmul(normed, joined_full) + joined_bias_of(qbias, vbias, head_count)).astype(
-        bf16
-    )
-    joined_all = joined_all.reshape(*shape, 3 * features)
-    if fast:
-        qkv, attended, saved, upstream_low, weights = forward_fused(
-            joined_all, upstream, weights, slopes, heads, width
-        )
-    else:
-        qkv = to_heads(joined_all)
+    if not fast:
+        joined_bias = joined_bias_of(qbias, vbias, head_count)
+        joined_all = (matmul(normed, joined_full) + joined_bias).astype(bf16)
+        qkv = to_heads(joined_all.reshape(*shape, 3 * features))
         attended, *saved = attention_forward(qkv, slopes, heads, width)
-        attended, upstream_low = from_heads(attended), to_own_seqs(upstream)
-        weights = [gather(item) for item in weights]
-    out_full, expand_full, contract_full = weights
+        attended = from_heads(attended)
     attended = attended.reshape(rows, features)
     upstream_low = upstream_low.reshape(rows, features)
 

time: 465 us -> 452 us (0.972)
  matrix products: 30.2 us -> 22.8 us
  Pallas kernels: 402 us -> 397 us
    pallas_call x1, Pallas kernels: 118 us -> 184 us  [forward_fused(): remote_call(functools.partial(forward_fused_kernel, heads, width, count,...]
    pallas_call x1 -> x0, Pallas kernels: 65 us -> none  [begin(): remote_call(functools.partial(begin_kernel, count, chunks), 'begin', 0, o...]
    dot_general x2 -> x1, matrix products: 11 us -> 3.53 us  [matmul(): return jnp.dot(left_side, right_side, preferred_element_type=f32)]
    pallas_call x1, Pallas kernels: 77.6 us -> 71.9 us  [feed_forward(): remote_call(feed_forward_kernel, 'feed_forward', 4, out_shape=(jax.ShapeD...]
where the time goes in v5:
time: 452 us
  Pallas kernels  397 us (88%)
  matrix products  22.8 us (5%)
  other arithmetic  16.7 us (4%)
  local copies, waits for them, and re-layouts  13.8 us (3%)
    pallas_call x1, Pallas kernels, forward_fused(): remote_call(functools.partial(forward_fused_kernel, heads, width, count,...  184 us
    pallas_call x1, Pallas kernels, backward_fused(): remote_call(functools.partial(backward_fused_kernel, heads, width, count,...  95.3 us
    pallas_call x1, Pallas kernels, feed_forward(): remote_call(feed_forward_kernel, 'feed_forward', 4, out_shape=(jax.ShapeD...  71.9 us
    pallas_call x1, Pallas kernels, end(): remote_call(functools.partial(end_kernel, chunks), 'end', 3, out_shape=(j...  46.2 us
    dot_general x2, matrix products, matmul_rt(): lax.dot_general(left_side, right_side, (((1,), (1,)), ((), ())), preferre...  10.9 us

profile of v5, /device:TPU:0, one launch (start us, length us, event | category | flops | bytes accessed | tf_op | source)
XLA Modules:
  0.0 451.6 jit_solution(18293524506677223561)
XLA Ops:
  0.6 1.2 dynamic_slice.3.slopes.refs_0_
  1.9 184.1 %forward_fused.1 = (bf16[2,4,64,1024]{3,2,1,0:T(8,128)(2,1)}, bf16[4,9,8,128]{3,2,1,0:T(8,128)(2,1)}, bf16[4,8,32,3072]{3,2,1,0:T(8,128)(2,1)}, bf16[2,4,8,64,38...) custom-call(f32[2]{0:T(128)} %dynamic_slice.3.slopes.refs_0_, ...), custom_call_target="tpu_custom_call" | custom-call | tf_op jit(solution)/shard_map/forward_fused/pallas_call | solution.py:912
  186.0 0.8 fusion.24
  186.8 3.5 fusion.26
  190.7 2.2 broadcast_add_fusion
  192.8 1.3 slice_convert_fusion
  194.1 71.9 %feed_forward.1 = (bf16[4,2,64,1024]{3,2,1,0:T(8,128)(2,1)}, f32[512,1024]{1,0:T(8,128)}, bf16[1024,4096]{1,0:T(8,128)(2,1)}, f32[1,4096]{1,0:T(1,128)}, f32[128,1024]{1,0:T(8,128)}) custom-call(bf16[1024,4096]{1,0:T(8,128)(2,1)} %bitcast.92, bf16[4096,1024]{1,0:T(8,128)(2,1)} %bitcast.93, f32[1,4096]{1,0:T(1,128)} %bitcast.107, ...), custom_call_target="tpu_custom_call" | custom-call | tf_op jit(solution)/shard_map/feed_forward/pallas_call | solution.py:1063
  266.1 2.5 multiply_reduce_fusion
  271.3 2.6 convolution_convert_fusion
  273.8 2.3 convolution_convert_fusion.1
  276.1 95.3 %backward_fused.1 = (bf16[2,4,64,3072]{3,2,1,0:T(8,128)(2,1)}, f32[32,4096]{1,0:T(8,128)}, f32[32,1024]{1,0:T(8,128)}) custom-call(f32[2]{0:T(128)} %dynamic_slice.3.slopes.refs_0_, bf16[2,4,64,1024]{3,2,1,0:T(8,128)(2,1)} %bitcast.103, bf16[2,4,8,64,384]{4,3,2,1,0:T(8,128)(2,1)} %get-tuple-element.46.refs_2_, f32[2,2,64,2048]{3,2,1,0:T(8,128)} %get-tuple-element.47.refs_3_, ...), custom_call_target="tpu_custom_call" | custom-call | tf_op jit(solution)/shard_map/backward_fused/pallas_call | solution.py:1156
  372.2 1.1 copy-done.5
  373.3 5.8 %bitcast_convert_fusion = bf16[1024,3072]{1,0:T(8,128)(2,1)} fusion(bf16[2,4,64,3072]{3,2,1,0:T(8,128)(2,1)S(1)} %copy-done.5, bf16[2,4,64,1024]{3,2,1,0:T(8,128)(2,1)S(1)} %copy-done.3, f32[1024]{0:T(1024)S(1)} %convert.13, f32[1024]{0:T(1024)S(1)} %convert.8, f32[2,4,64]{2,1,0:T(4,128)S(1)} %get-tuple-element.80, f32[2,4,64]{2,1,0:T(4,128)S(1)} %broadcast_multiply_fusion), kind=kOutput, calls=%fused_computation | convolution fusion | flops 3227516928 | bytes 10498048 | tf_op jit(solution)/shard_map/dot_general | solution.py:40
  379.1 8.7 %fusion.21 = (f32[1024]{0:T(1024)S(1)}, f32[512]{0:T(512)S(1)}, f32[512,1024]{1,0:T(8,128)}) fusion(f32[1024]{0:T(1024)S(1)} %convert.8, f32[512]{0:T(512)S(1)} %div.45, bf16[2,4,64,1024]{3,2,1,0:T(8,128)(2,1)S(1)} %copy-done.3, bf16[512,3072]{1,0:T(8,128)(2,1)} %bitcast.96, bf16[1024,3072]{1,0:T(8,128)(2,1)} %bitcast.124), kind=kOutput, calls=%fused_computation.54 | convolution fusion | flops 3224369664 | bytes 12595200 | tf_op jit(solution)/shard_map/dot_general | solution.py:46
  387.9 2.6 fusion.11
  390.6 2.7 convert_reduce_fusion
  394.6 3.3 add_convert_fusion
  397.9 46.2 %end.1 = (bf16[4,2,64,1024]{3,2,1,0:T(8,128)(2,1)}, f32[8,128]{1,0:T(8,128)}, f32[32,3072]{1,0:T(8,128)}) custom-call(bf16[2,4,64,1024]{3,2,1,0:T(8,128)(2,1)} %bitcast.95, f32[4,8,8,128]{3,2,1,0:T(8,128)} %copy.34, bf16[4,4,2,32,3072]{4,3,2,1,0:T(8,128)(2,1)} %bitcast.94), custom_call_target="tpu_custom_call" | custom-call | tf_op jit(solution)/shard_map/end/pallas_call | solution.py:1235
  444.1 0.8 slice_bitcast_fusion
  445.4 1.2 slice_bitcast_fusion.1
  446.6 1.0 copy.41
  447.6 1.0 copy.42
  450.0 0.8 copy.45
  450.8 0.8 copy.46
  (66 shorter events, 7.5 us)
Async XLA Ops:
  266.1 2.5 copy-start.4
  268.6 1.2 copy-start.2
  269.3 1.4 copy-start
  269.8 1.4 copy-start.14
  271.2 2.6 copy-start.13
  276.1 95.3 %copy-start.3 = (bf16[2,4,64,1024]{3,2,1,0:T(8,128)(2,1)S(1)}, bf16[2,4,64,1024]{3,2,1,0:T(8,128)(2,1)}, u32[]{:S(2)}) copy-start(bf16[2,4,64,1024]{3,2,1,0:T(8,128)(2,1)} %get-tuple-element.40) | copy-start | bytes 3145732
  371.4 1.9 copy-start.5
  390.4 3.4 copy-start.12
  390.4 4.2 copy-start.1
  397.9 48.8 %copy-start.6 = (bf16[4,2,64,1024]{3,2,1,0:T(8,128)(2,1)S(1)}, bf16[4,2,64,1024]{3,2,1,0:T(8,128)(2,1)}, u32[]{:S(2)}) copy-start(bf16[4,2,64,1024]{3,2,1,0:T(8,128)(2,1)} %get-tuple-element.44) | copy-start | bytes 3145732
  444.1 3.6 copy-start.7
  446.6 2.0 copy-start.10
  446.6 2.7 copy-start.11
  447.6 2.4 copy-start.9
  447.6 3.2 copy-start.8

commit v6 on v5

--- a/solution.py
+++ b/solution.py
@@ -160,13 +160,15 @@
         joined = finished[0] if heads == 1 else jnp.concatenate(finished, axis=0)
         self.out[b, i] = joined.T.astype(bf16).reshape(self.out.shape[2:])
 
-    def run(self, after):
+    def run(self, after, each=None):
         blocks = self.blocks
 
         def body(n, _):
             b, i = n // blocks, n % blocks
             pl.when(i == 0)(lambda: self.prepare(b))
             self.one(b, i)
+            if each is not None:
+                each(b, i)
             follow(n, after)
             return 0
 
@@ -292,32 +294,30 @@
                 bf16
             ).reshape(tail)
 
-    def run(self, after):
+    def run(self, after, each=None):
         blocks = self.blocks
 
         def body(n, _):
             b, j = n // blocks, n % blocks
             pl.when(j == 0)(lambda: self.prepare(b))
             self.one(b, j)
-            pl.when(j == blocks - 1)(lambda: self.finish(b))
+            self.finish(b, j)
+            if each is not None:
+                each(b, j)
             follow(n, after)
             return 0
 
         lax.fori_loop(0, self.qkv.shape[0] * blocks, body, 0)
 
-    def finish(self, b):
+    def finish(self, b, j):
         width = self.width
         scale = 1.0 / math.sqrt(width)
-        tail = self.joined.shape[2:4] + (width,)
-
-        def body(i, _):
-            for h in range(self.heads):
-                base = h * 3 * width
-                result = (self.query_acc[h, :, self.rows(i)] * scale).T.astype(bf16)
-                self.joined[b, i, :, :, base : base + width] = result.reshape(tail)
-            return 0
-
-        lax.fori_loop(0, self.blocks, body, 0)
+        for h in range(self.heads):
+            base = h * 3 * width
+            result = (self.query_acc[h, :, self.rows(j)] * scale).T.astype(bf16)
+            self.joined[b, j, :, :, base : base + width] = result.reshape(
+                self.joined.shape[2:4] + (width,)
+            )
 
 
 def backward_kernel(heads, width, *refs):
@@ -448,8 +448,9 @@
 class Gather:
     copies_each = 33
 
-    def __init__(self, place, weights, wholes, kept, chunks, copies):
+    def __init__(self, place, weights, wholes, kept, chunks, copies, given=None):
         z, s, lines = place.z, place.s, place.lines
+        self.ready = arrive if given is None else done
         self.loads, self.own = [], []
         for weight, whole, keep in zip(weights, wholes, kept):
             if keep is None:
@@ -468,12 +469,17 @@
                 where = (k, rank, part, wide)
                 return copies.plan(whole.at[where], whole.at[where], to)
 
-            self.first.append(
-                [
+            if given is None:
+                first = [
                     copies.plan(weights[t].at[s, every, wide], whole.at[z, s, every, wide], to)
                     for to in lines
                 ]
-            )
+            else:
+                first = [
+                    copies.inside(given.at[k, every, wide], whole.at[k, s, every, wide])
+                    for k, _ in lines
+                ]
+            self.first.append(first)
             second, third, cores, last = [], [], [], []
             for k, _ in lines:
                 second.append(same(k, s, low, place.to_x))
@@ -498,7 +504,7 @@
         go(self.first[t])
 
     def exchange(self, t):
-        arrive(self.first[t])
+        self.ready(self.first[t])
         go(self.second[t])
         go(self.cores[t])
 
@@ -627,6 +633,143 @@
     return scratch
 
 
+class ReduceAlong(Reduce):
+    def __init__(self, place, grad, out, buf, chunk, copies):
+        self.place, self.grad, self.out, self.buf, self.chunk = place, grad, out, buf, chunk
+        own, from_core, from_z, from_x, from_y, late_y, late_x = buf
+        _, row, rows, column, columns = chunk
+        every, wide = pl.ds(row, rows), pl.ds(column, columns)
+        self.low, self.high = low, high = pl.ds(0, rows // 2), pl.ds(rows // 2, rows // 2)
+        z, x, y = place.z, place.x, place.y
+        self.load = copies.inside(grad.at[:, :, place.core, every, wide], own)
+        self.first = copies.plan(
+            grad.at[:, :, 1 - place.core, every, wide], from_core, place.to_core
+        )
+        self.second = [
+            copies.plan(own.at[to[0]], from_z.at[k], to) for k, to in enumerate(place.lines)
+        ]
+        self.third = []
+        for k in range(2):
+            self.third.append(
+                copies.plan(own.at[z, 2 * k + 1 - x, low], from_x.at[k], place.to_x)
+            )
+            self.third.append(
+                copies.plan(own.at[z, 2 * (1 - y) + k, high], from_y.at[k], place.to_y)
+            )
+        self.fourth = [
+            copies.plan(own.at[z, place.chip_y, low], late_y, place.to_y),
+            copies.plan(own.at[z, place.chip_x, high], late_x, place.to_x),
+        ]
+
+    def exchange(self):
+        own, from_core = self.buf[:2]
+        self.load.wait()
+        arrive([self.first])
+        add_blocks(16, lambda i: (own.at[i // 4, i % 4], from_core.at[i // 4, i % 4]))
+        go(self.second)
+
+    def spread(self):
+        own, _, from_z = self.buf[:3]
+        z = self.place.z
+        arrive(self.second)
+
+        def body(i, _):
+            total = own[z, i].astype(f32)
+            for k in range(3):
+                total = total + from_z[k, i].astype(f32)
+            own[z, i] = total.astype(bf16)
+            return 0
+
+        lax.fori_loop(0, 4, body, 0)
+        go(self.third)
+
+    def send(self):
+        own, _, _, from_x, from_y = self.buf[:5]
+        z, x, y = self.place.z, self.place.x, self.place.y
+        arrive(self.third)
+        add_blocks(2, lambda j: (own.at[z, 2 * j + x, self.low], from_x.at[j]))
+        add_blocks(2, lambda j: (own.at[z, 2 * y + j, self.high], from_y.at[j]))
+        go(self.fourth)
+
+    def finish(self):
+        own, late_y, late_x = self.buf[0], self.buf[5], self.buf[6]
+        z, chip = self.place.z, self.place.chip
+        _, row, rows, column, columns = self.chunk
+        arrive(self.fourth)
+        half = rows // 2
+        wide = slice(column, column + columns)
+        self.out[row : row + half, wide] = own[z, chip, self.low].astype(f32) + late_y[...].astype(
+            f32
+        )
+        self.out[row + half : row + rows, wide] = own[z, chip, self.high].astype(f32) + late_x[
+            ...
+        ].astype(f32)
+
+
+def reduce_along_scratch(chunk):
+    _, _, rows, _, columns = chunk
+    half = rows // 2
+    return [
+        pltpu.VMEM((4, 4, rows, columns), bf16),
+        pltpu.VMEM((4, 4, rows, columns), bf16),
+        pltpu.VMEM((3, 4, rows, columns), bf16),
+        pltpu.VMEM((2, half, columns), bf16),
+        pltpu.VMEM((2, half, columns), bf16),
+        pltpu.VMEM((half, columns), bf16),
+        pltpu.VMEM((half, columns), bf16),
+    ]
+
+
+class HandBack:
+    def __init__(self, place, source, target, features, send, recv, local):
+        self.place, self.source, self.target = place, source, target
+        self.mine = columns_of(place.s, features)
+        self.send, self.recv, self.local = send, recv, local
+        self.blocks = source.shape[1]
+
+    def copy(self, b, i, d):
+        rank = self.place.plane[d][1]
+        n = b * self.blocks + i
+        return pltpu.make_async_remote_copy(
+            src_ref=self.source.at[b, i, rank],
+            dst_ref=self.target.at[b, i, :, self.mine],
+            send_sem=self.send.at[n, d],
+            recv_sem=self.recv.at[n, d],
+            device_id=self.place.plane[d],
+            device_id_type=MESH,
+        )
+
+    def own(self, b, i):
+        return pltpu.make_async_copy(
+            self.source.at[b, i, self.place.s],
+            self.target.at[b, i, :, self.mine],
+            self.local.at[b * self.blocks + i],
+        )
+
+    def each(self, b, i):
+        for d in range(7):
+            self.copy(b, i, d).start()
+        self.own(b, i).start()
+
+    def finish(self):
+        def body(n, _):
+            b, i = n // self.blocks, n % self.blocks
+            for d in range(7):
+                self.copy(b, i, d).wait()
+            self.own(b, i).wait()
+            return 0
+
+        lax.fori_loop(0, self.source.shape[0] * self.blocks, body, 0)
+
+
+def hand_back_semaphores(steps):
+    return [
+        pltpu.SemaphoreType.DMA((steps, 7)),
+        pltpu.SemaphoreType.DMA((steps, 7)),
+        pltpu.SemaphoreType.DMA((steps,)),
+    ]
+
+
 class ReduceLines:
     copies = 4 * 7 + 3
 
@@ -751,21 +894,22 @@
 
 def forward_fused_kernel(heads, width, count, vector_count, chunks, slopes, tokens, upstream, *refs):
     vectors, refs = refs[:vector_count], refs[vector_count:]
-    weights, refs = refs[:count], refs[count:]
+    weights, contract, refs = refs[:count], refs[count], refs[count + 1 :]
     tokens_out, vectors_out, joined_out, qkv_out, attended, out_t, lse, upstream_out = refs[:8]
-    wholes, refs = refs[8 : 7 + count], refs[7 + count :]
+    contract_out = refs[8]
+    wholes, refs = refs[9 : 8 + count], refs[8 + count :]
     held, small, values_of, joined, normed, outgoing, qkv, result, upstream_own = refs[:9]
     attention = Forward(heads, width, slopes, qkv, result, out_t, lse, *refs[9:12])
     kept, refs = refs[12 : 11 + count], refs[11 + count :]
     head_send, head_recv = refs[:2]
-    copies = Copies(*refs[2:])
+    copies = Copies(*refs[5:])
     place = Place()
     z, s, lines, plane = place.z, place.s, place.lines, place.plane
     gather = Gather(place, weights, [joined, *wholes], [None, *kept], chunks, copies)
     first = [t for t, chunk in enumerate(chunks) if chunk[0] == 0]
     later = [t for t, chunk in enumerate(chunks) if chunk[0] > 0]
     features = heads * width
-    mine = columns_of(s, features)
+    back = HandBack(place, result, attended, features, *refs[2:5])
     own_seqs, parts, piece, wide = held.shape
 
     load = copies.inside(tokens.at[z], held.at[:, z])
@@ -780,11 +924,7 @@
         copies.inside(joined, joined_out),
     ]
     keep_qkv = copies.inside(qkv, qkv_out)
-    back = [
-        [copies.plan(result.at[b, :, to[1]], attended.at[b, :, :, mine], to) for to in plane]
-        for b in range(2)
-    ]
-    stay = [copies.inside(result.at[b, :, s], attended.at[b, :, :, mine]) for b in range(2)]
+    contracts = [copies.plan(contract.at[s], contract_out.at[z], to) for to in lines]
 
     def to_head(d):
         return pltpu.make_async_remote_copy(
@@ -795,9 +935,6 @@
             device_id=(z, lax.rem(s + 1 + d, 8)),
             device_id_type=MESH,
         )
-
-    def hand_back(b):
-        go(back[b] + stay[b : b + 1])
 
     go(gather.loads + [load, load_upstream])
     small[z] = jnp.zeros(small.shape[1:], bf16)
@@ -809,7 +946,7 @@
     go(seqs + vector_copies)
     for t in later:
         gather.start(t)
-    go(upstreams)
+    go(contracts + upstreams)
     gather.keep()
     load.wait()
     for t in range(len(first) + 2):
@@ -868,33 +1005,32 @@
     gather.exchange(base)
     gather.exchange(base + 1)
     own_copy.wait()
+    gather.spread(base)
+    gather.exchange(base + 2)
+    gather.spread(base + 1)
     for d in range(7):
         to_head(d).wait_recv()
     keep_qkv.start()
-    gather.exchange(base + 2)
+    gather.share(base)
     attention.run(
         {
-            2: [(gather.spread, base), (gather.spread, base + 1), (gather.exchange, base + 3)],
-            3: [(hand_back, 0)],
-            5: [(gather.spread, base + 2), (gather.exchange, base + 4)],
-            6: [(gather.spread, base + 3), (gather.share, base), (gather.share, base + 1)],
-            7: [(hand_back, 1)],
-        }
+            1: [(gather.spread, base + 2)],
+            3: [(gather.share, base + 1)],
+            5: [(gather.share, base + 2)],
+        },
+        back.each,
     )
-    gather.share(base + 2)
-    gather.spread(base + 4)
-    gather.share(base + 3)
-    gather.share(base + 4)
     for t in later:
         gather.complete(t)
-    arrive(upstreams + back[0] + back[1])
+    arrive(contracts + upstreams)
+    back.finish()
     for d in range(7):
         to_head(d).wait_send()
     copies.finish()
-    done(gather.own + [keep_upstream, keep_qkv] + keeping + stay)
-
-
-def forward_fused(tokens, upstream, vectors, weights, slopes, heads, width):
+    done(gather.own + [keep_upstream, keep_qkv] + keeping)
+
+
+def forward_fused(tokens, upstream, vectors, weights, contract, slopes, heads, width):
     seqs, piece, features = tokens.shape
     parts = 4
     own = seqs // parts
@@ -902,9 +1038,10 @@
     length = parts * 8 * piece
     vectors = [item.reshape(-1, 128) for item in vectors]
     cut = [split_weight(item) for item in weights]
+    contract = split_weight(contract)
     count, tall = len(cut), 8 * -(-max(item.shape[0] for item in vectors) // 8)
     chunks = []
-    for t, pieces in enumerate((3, 1, 2, 2)):
+    for t, pieces in enumerate((3, 1, 2)):
         chunks += chunks_of(t, *cut[t].shape[1:], pieces)
     seq_shape = (own, parts, piece, features)
     qkv_shape = (own, parts, 8, piece, 3 * columns)
@@ -921,10 +1058,11 @@
             jax.ShapeDtypeStruct(seq_shape, bf16),
             *saved_shapes(own, length, heads, width),
             jax.ShapeDtypeStruct(seq_shape, bf16),
+            jax.ShapeDtypeStruct((parts, *contract.shape[1:]), bf16),
             *[jax.ShapeDtypeStruct((parts, *item.shape), bf16) for item in cut[1:]],
         ),
-        in_specs=[SMEM, HBM, HBM] + [VMEM] * len(vectors) + [HBM] * count,
-        out_specs=(HBM,) * 5 + (VMEM, VMEM) + (HBM,) * count,
+        in_specs=[SMEM, HBM, HBM] + [VMEM] * len(vectors) + [HBM] * (count + 1),
+        out_specs=(HBM,) * 5 + (VMEM, VMEM) + (HBM,) * (count + 1),
         scratch_shapes=[
             pltpu.VMEM(seq_shape, bf16),
             pltpu.VMEM(small, bf16),
@@ -939,7 +1077,8 @@
             *[pltpu.VMEM(item.shape, bf16) for item in cut[1:]],
             pltpu.SemaphoreType.DMA((7,)),
             pltpu.SemaphoreType.DMA((7,)),
-            *semaphores(9 + 14 + len(chunks) * Gather.copies_each, 2 * count - 1 + 10),
+            *hand_back_semaphores(own * parts),
+            *semaphores(12 + len(chunks) * Gather.copies_each, 2 * count - 1 + 8),
         ],
     )(
         slopes,
@@ -947,19 +1086,20 @@
         upstream.reshape(parts, own, piece, features),
         *vectors,
         *cut,
+        contract,
     )
     wholes = [
         whole.reshape(4 * item.shape[0], item.shape[1])
-        for whole, item in zip((out[2], *out[8:]), weights)
+        for whole, item in zip((out[2], *out[9:]), weights)
     ]
     found = [out[1][:, n, : item.shape[0]].reshape(-1) for n, item in enumerate(vectors)]
-    return out[0], found, wholes, out[3], out[4], (out[5], out[6]), out[7]
+    return out[0], found, [*wholes, out[8]], out[3], out[4], (out[5], out[6]), out[7]
 
 
 def feed_forward_kernel(
-    expand, contract, expand_bias, second, upstream, residual,
+    chunks, expand, contract, contract_line, expand_bias, second, upstream, residual,
     layer_out, second_back, expand_grad, bias_grad, contract_grad,
-    expand_in, contract_in, second_t, expanded, grad, layer, staged, *refs,
+    expand_in, contract_in, second_t, expanded, activated, grad, layer, staged, *refs,
 ):
     bufs, refs = refs[:6], refs[6:]
     loaded, stored, refs = refs[0], refs[1], refs[2:]
@@ -967,6 +1107,9 @@
     place = Place()
     z, lines = place.z, place.lines
     reduce = ReduceLines(place, grad, contract_grad, bufs, copies)
+    gather = Gather(
+        place, [contract], [contract_in], [None], chunks, copies, given=contract_line
+    )
     rows, features = second.shape
     steps = 8
     wide = expand.shape[1] // steps
@@ -978,10 +1121,11 @@
 
     def load(n):
         _, _, where = at(n)
-        return (
-            pltpu.make_async_copy(expand.at[:, where], expand_in.at[:, where], loaded.at[0, n]),
-            pltpu.make_async_copy(contract.at[where], contract_in.at[where], loaded.at[1, n]),
-        )
+        return pltpu.make_async_copy(expand.at[:, where], expand_in.at[:, where], loaded.at[n])
+
+    def contract_at(n):
+        part, side, _ = at(n)
+        return contract_in[part, pl.ds(4 * side, 4)].reshape(wide, features)
 
     def store(n):
         _, _, where = at(n)
@@ -992,28 +1136,39 @@
 
     returned = [copies.plan(layer.at[:, to[0]], layer_out.at[z], to) for to in lines]
     stay = copies.inside(layer.at[:, z], layer_out.at[z])
+    for n in range(len(chunks)):
+        gather.start(n)
     for n in range(steps):
-        go(load(n))
+        load(n).start()
+    go(gather.loads)
     greet(place.near)
+    for n in range(len(chunks)):
+        gather.exchange(n)
     second_t[...] = second[...].T
     second_back[...] = residual[...]
 
     def forward(n, after):
         part, side, where = at(n)
-        done(load(n))
+        load(n).wait()
         values = matmul(second[...], expand_in[:, where]) + expand_bias[:, where]
         expanded[:, where] = values
-        activated = gelu_tanh(values).astype(bf16)
-        made = matmul(activated.T, upstream[...]).astype(bf16)
+        low = gelu_tanh(values).astype(bf16)
+        activated[:, where] = low
+        made = matmul(low.T, upstream[...]).astype(bf16)
         grad[part, pl.ds(2 * side, 2)] = made.reshape(2, 2, wide // 4, features)
-        second_back[...] += matmul(activated, contract_in[where, :])
+        follow(n, after)
+        return 0
+
+    def shrink(n, after):
+        _, _, where = at(n)
+        second_back[...] += matmul(activated[:, where], contract_at(n))
         follow(n, after)
         return 0
 
     def backward(n, after):
         _, _, where = at(n)
         values = expanded[:, where]
-        act_grad = matmul_rt(upstream[...], contract_in[where, :])
+        act_grad = matmul_rt(upstream[...], contract_at(n))
         bent = jnp.tanh(gelu_coef * (values + 0.044715 * values * values * values))
         slope = 0.5 * (1.0 + bent) + 0.5 * values * (1.0 - bent * bent) * (
             gelu_coef * (1.0 + 3.0 * 0.044715 * values * values)
@@ -1027,25 +1182,36 @@
         follow(n, after)
         return 0
 
-    first = {
-        1: [(reduce.start, 0)],
-        2: [(reduce.exchange, 0)],
-        3: [(reduce.start, 1)],
-        4: [(reduce.spread, 0), (reduce.exchange, 1)],
-        5: [(reduce.start, 2)],
-        6: [(reduce.send, 0), (reduce.spread, 1), (reduce.exchange, 2)],
-        7: [(reduce.start, 3)],
+    last = len(chunks) - 1
+    forward_steps = {
+        1: [(reduce.start, 0)] + [(gather.spread, n) for n in range(last)],
+        2: [(gather.spread, last)],
+        3: [(reduce.exchange, 0), (reduce.start, 1)],
+        4: [(reduce.exchange, 1)],
+        5: [(reduce.start, 2)] + [(gather.share, n) for n in range(last)],
+        7: [(reduce.start, 3), (reduce.exchange, 2)],
     }
-    second_steps = {
-        0: [(reduce.send, 1), (reduce.spread, 2), (reduce.exchange, 3)],
-        2: [(reduce.send, 2), (reduce.spread, 3)],
-        4: [(reduce.send, 3)],
+    shrink_steps = {
+        1: [(reduce.spread, 0)],
+        3: [(reduce.exchange, 3)],
+        5: [(reduce.spread, 1), (reduce.send, 0)],
     }
-    lax.fori_loop(0, steps, lambda n, _: forward(n, first), 0)
+    backward_steps = {
+        0: [(reduce.spread, 2)],
+        1: [(reduce.send, 1), (reduce.spread, 3)],
+        3: [(reduce.send, 2)],
+        5: [(reduce.send, 3)],
+    }
+    lax.fori_loop(0, steps, lambda n, _: forward(n, forward_steps), 0)
+    gather.share(last)
+    for n in range(len(chunks)):
+        gather.complete(n)
+    done(gather.loads)
+    lax.fori_loop(0, steps, lambda n, _: shrink(n, shrink_steps), 0)
     layer[...] = second_back[...].astype(bf16).reshape(layer.shape)
     second_back[...] = jnp.zeros_like(second_back)
     go(returned + [stay])
-    lax.fori_loop(0, steps, lambda n, _: backward(n, second_steps), 0)
+    lax.fori_loop(0, steps, lambda n, _: backward(n, backward_steps), 0)
     reduce.finish()
     store(steps - 2).wait()
     store(steps - 1).wait()
@@ -1054,14 +1220,16 @@
     done([stay])
 
 
-def feed_forward(shape, expand, contract, expand_bias, second, upstream, residual):
+def feed_forward(shape, expand, contract, line, expand_bias, second, upstream, residual):
     own, parts, piece = shape
     rows, features = second.shape
     hidden = expand.shape[1]
     wide = hidden // 8
     each = hidden // 32
+    contract = split_weight(contract)
+    chunks = chunks_of(0, *contract.shape[1:], 2)
     out = remote_call(
-        feed_forward_kernel,
+        functools.partial(feed_forward_kernel, chunks),
         "feed_forward",
         4,
         out_shape=(
@@ -1071,22 +1239,26 @@
             jax.ShapeDtypeStruct((1, hidden), f32),
             jax.ShapeDtypeStruct((each, features), f32),
         ),
-        in_specs=[HBM, HBM, VMEM, VMEM, VMEM, VMEM],
+        in_specs=[HBM, HBM, HBM, VMEM, VMEM, VMEM, VMEM],
         out_specs=(HBM, VMEM, HBM, VMEM, VMEM),
         scratch_shapes=[
             pltpu.VMEM((features, hidden), bf16),
-            pltpu.VMEM((hidden, features), bf16),
+            pltpu.VMEM((4, *contract.shape), bf16),
             pltpu.VMEM((features, rows), bf16),
             pltpu.VMEM((rows, hidden), f32),
+            pltpu.VMEM((rows, hidden), bf16),
             pltpu.VMEM((4, 4, 2, each, features), bf16),
             pltpu.VMEM((own, parts, piece, features), bf16),
             pltpu.VMEM((2, features, wide), bf16),
             *reduce_lines_scratch(each, features),
-            pltpu.SemaphoreType.DMA((2, 8)),
+            pltpu.SemaphoreType.DMA((8,)),
             pltpu.SemaphoreType.DMA((2,)),
-            *semaphores(ReduceLines.copies + 3, 1),
+            *semaphores(
+                ReduceLines.copies + 3 + len(chunks) * (Gather.copies_each - 3),
+                2 + 3 * len(chunks),
+            ),
         ],
-    )(expand, contract, expand_bias, second, upstream, residual)
+    )(expand, contract, line, expand_bias, second, upstream, residual)
     return out[0].reshape(parts * own, piece, features), *out[1:]
 
 
@@ -1097,12 +1269,13 @@
     diff, qkv, out_t, lse, joined = refs[:5]
     attention = Backward(heads, width, slopes, qkv, diff, out_t, lse, joined, *refs[5:12])
     bufs, refs = refs[12 : 12 + 7 * len(chunks)], refs[12 + 7 * len(chunks) :]
-    copies = Copies(*refs)
+    copies = Copies(*refs[3:])
     place = Place()
     s, plane = place.s, place.plane
     features = heads * width
-    mine = columns_of(s, 3 * features)
-    reduce = Reduce(place, grads, outs, bufs, chunks, copies)
+    along = ReduceAlong(place, grads[0], outs[0], bufs[:7], chunks[0], copies)
+    reduce = Reduce(place, grads, outs, bufs[7:], chunks[1:], copies)
+    back = HandBack(place, joined, joined_out, 3 * features, *refs[:3])
 
     own = [copies.inside(diff_in.at[:, :, :, columns_of(s, features)], diff.at[:, :, s])]
     own += [copies.inside(a, b) for a, b in ((qkv_in, qkv), (out_t_in, out_t), (lse_in, lse))]
@@ -1110,38 +1283,30 @@
         copies.plan(diff_in.at[:, :, :, columns_of(to[1], features)], diff.at[:, :, s], to)
         for to in plane
     ]
-    back = [
-        [copies.plan(joined.at[b, :, to[1]], joined_out.at[b, :, :, mine], to) for to in plane]
-        for b in range(2)
-    ]
-    stay = [copies.inside(joined.at[b, :, s], joined_out.at[b, :, :, mine]) for b in range(2)]
-
-    def hand_back(b):
-        go(back[b] + stay[b : b + 1])
-
-    go(own + reduce.loads)
+    go(own + reduce.loads + [along.load])
     greet(place.lines + plane)
-    go(arriving)
+    go(arriving + [along.first])
     reduce.start()
-    for t in range(3):
+    along.exchange()
+    for t in range(2):
         reduce.exchange(t)
     done(own)
     arrive(arriving)
     attention.run(
         {
             1: [(reduce.spread, 0)],
-            3: [(hand_back, 0)],
-            4: [(reduce.spread, 1), (reduce.spread, 2), (reduce.send, 0)],
-            7: [(hand_back, 1)],
-        }
+            3: [(reduce.spread, 1)],
+            4: [(reduce.send, 0), (along.spread,)],
+            5: [(reduce.send, 1)],
+            6: [(along.send,)],
+        },
+        back.each,
     )
-    reduce.send(1)
-    reduce.send(2)
-    for t in range(3):
+    for t in range(2):
         reduce.finish(t)
-    arrive(back[0] + back[1])
+    along.finish()
+    back.finish()
     copies.finish()
-    done(stay)
 
 
 def backward_fused(attended_diff, qkv, saved, grads, slopes, heads, width):
@@ -1169,8 +1334,10 @@
             *[pltpu.VMEM(item.shape, f32) for item in saved],
             pltpu.VMEM(qkv.shape, bf16),
             *backward_scratch(length, heads, width),
-            *reduce_scratch(chunks),
-            *semaphores(7 + 14 + len(chunks) * Reduce.copies_each, len(chunks) + 6),
+            *reduce_along_scratch(chunks[0]),
+            *reduce_scratch(chunks[1:]),
+            *hand_back_semaphores(own * parts),
+            *semaphores(7 + len(chunks) * Reduce.copies_each, len(chunks) + 4),
         ],
     )(slopes, attended_diff, qkv, *saved, *cut)
     return out[0], out[1:]
@@ -1289,15 +1456,16 @@
         second_gain, second_shift, contract_bias, expand_bias,
     )
     fast = (fs_count, sp_count) == (4, 8) and (own, heads, width) == (2, 2, 64)
-    weights = (joined_weight, output_weight, expand_weight, contract_weight)
+    weights = (joined_weight, output_weight, expand_weight)
     gather = lambda item: lax.all_gather(item, "fs", axis=0, tiled=True)
     if fast:
         tokens, whole, weights, qkv, attended, saved, upstream_low = forward_fused(
-            layer_input, upstream, vectors, weights, slopes, heads, width
+            layer_input, upstream, vectors, weights, contract_weight, slopes, heads, width
         )
     else:
         tokens, upstream_low = to_own_seqs(layer_input), to_own_seqs(upstream)
-        whole, weights = [gather(item) for item in vectors], [gather(item) for item in weights]
+        whole = [gather(item) for item in vectors]
+        weights = [gather(item) for item in (*weights, contract_weight)]
     joined_full, out_full, expand_full, contract_full = weights
     tokens = tokens.reshape(rows, features).astype(f32)
     gain_one, shift_one, qbias, vbias, obias, gain_two, shift_two, cbias, ebias = [
@@ -1322,8 +1490,8 @@
     contract_bias_grad = jnp.sum(upstream_f, axis=0)
     if fast:
         layer_output, second_back, expand_grad, expand_bias_grad, contract_grad = feed_forward(
-            shape, expand_full, contract_full, ebias.reshape(1, -1), second, upstream_low,
-            residual + cbias,
+            shape, expand_full, contract_weight, contract_full, ebias.reshape(1, -1), second,
+            upstream_low, residual + cbias,
         )
         expand_bias_grad = expand_bias_grad.reshape(-1)
     else:

time: 452 us -> 455 us (level)
    pallas_call x1, Pallas kernels: 71.9 us -> 96.1 us  [feed_forward(): remote_call(functools.partial(feed_forward_kernel, chunks), 'feed_forward...]
    pallas_call x1, Pallas kernels: 184 us -> 170 us  [forward_fused(): remote_call(functools.partial(forward_fused_kernel, heads, width, count,...]
    pallas_call x1, Pallas kernels: 95.3 us -> 85.4 us  [backward_fused(): remote_call(functools.partial(backward_fused_kernel, heads, width, count,...]
where the time goes in v6:
time: 455 us; the launch traced here: 454 us
  Pallas kernels  400 us (88%)
  matrix products  22.8 us (5%)
  other arithmetic  16.7 us (4%)
  local copies, waits for them, and re-layouts  13.8 us (3%)
    pallas_call x1, Pallas kernels, forward_fused(): remote_call(functools.partial(forward_fused_kernel, heads, width, count,...  170 us
    pallas_call x1, Pallas kernels, feed_forward(): remote_call(functools.partial(feed_forward_kernel, chunks), 'feed_forward...  96.1 us
    pallas_call x1, Pallas kernels, backward_fused(): remote_call(functools.partial(backward_fused_kernel, heads, width, count,...  85.4 us
    pallas_call x1, Pallas kernels, end(): remote_call(functools.partial(end_kernel, chunks), 'end', 3, out_shape=(j...  48.7 us
    dot_general x2, matrix products, matmul_rt(): lax.dot_general(left_side, right_side, (((1,), (1,)), ((), ())), preferre...  10.9 us

profile of v6, /device:TPU:0, one launch (start us, length us, event | category | flops | bytes accessed | tf_op | source)
XLA Modules:
  0.0 454.1 jit_solution(9113227250744798427)
XLA Ops:
  0.6 1.2 dynamic_slice.3.slopes.refs_0_
  1.9 169.7 %forward_fused.1 = (bf16[2,4,64,1024]{3,2,1,0:T(8,128)(2,1)}, bf16[4,9,8,128]{3,2,1,0:T(8,128)(2,1)}, bf16[4,8,32,3072]{3,2,1,0:T(8,128)(2,1)}, bf16[2,4,8,64,38...) custom-call(f32[2]{0:T(128)} %dynamic_slice.3.slopes.refs_0_, ...), custom_call_target="tpu_custom_call" | custom-call | tf_op jit(solution)/shard_map/forward_fused/pallas_call | solution.py:1049
  171.6 0.8 fusion.24
  172.4 3.5 fusion.26
  176.4 2.2 broadcast_add_fusion
  178.5 1.3 slice_convert_fusion
  179.8 96.1 %feed_forward.1 = (bf16[4,2,64,1024]{3,2,1,0:T(8,128)(2,1)}, f32[512,1024]{1,0:T(8,128)}, bf16[1024,4096]{1,0:T(8,128)(2,1)}, f32[1,4096]{1,0:T(1,128)}, f32[128,1024]{1,0:T(8,128)}) custom-call(bf16[1024,4096]{1,0:T(8,128)(2,1)} %bitcast.93, bf16[8,128,1024]{2,1,0:T(8,128)(2,1)} %bitcast.91, bf16[4,128,1024]{2,1,0:T(8,128)(2,1)} %get-tuple-element.38.contract_line, ...), custom_call_target="tpu_custom_call" | custom-call | tf_op jit(solution)/shard_map/feed_forward/pallas_call | solution.py:1231
  275.9 2.5 multiply_reduce_fusion
  281.1 2.6 convolution_convert_fusion
  283.7 2.3 convolution_convert_fusion.1
  286.0 85.4 %backward_fused.1 = (bf16[2,4,64,3072]{3,2,1,0:T(8,128)(2,1)}, f32[32,4096]{1,0:T(8,128)}, f32[32,1024]{1,0:T(8,128)}) custom-call(f32[2]{0:T(128)} %dynamic_slice.3.slopes.refs_0_, bf16[2,4,64,1024]{3,2,1,0:T(8,128)(2,1)} %bitcast.102, bf16[2,4,8,64,384]{4,3,2,1,0:T(8,128)(2,1)} %get-tuple-element.46.refs_2_, f32[2,2,64,2048]{3,2,1,0:T(8,128)} %get-tuple-element.47.refs_3_, ...), custom_call_target="tpu_custom_call" | custom-call | tf_op jit(solution)/shard_map/backward_fused/pallas_call | solution.py:1321
  372.2 1.1 copy-done.5
  373.3 5.8 %bitcast_convert_fusion = bf16[1024,3072]{1,0:T(8,128)(2,1)} fusion(bf16[2,4,64,3072]{3,2,1,0:T(8,128)(2,1)S(1)} %copy-done.5, bf16[2,4,64,1024]{3,2,1,0:T(8,128)(2,1)S(1)} %copy-done.3, f32[1024]{0:T(1024)S(1)} %convert.13, f32[1024]{0:T(1024)S(1)} %convert.8, f32[2,4,64]{2,1,0:T(4,128)S(1)} %get-tuple-element.80, f32[2,4,64]{2,1,0:T(4,128)S(1)} %broadcast_multiply_fusion), kind=kOutput, calls=%fused_computation | convolution fusion | flops 3227516928 | bytes 10498048 | tf_op jit(solution)/shard_map/dot_general | solution.py:40
  379.1 8.7 %fusion.21 = (f32[1024]{0:T(1024)S(1)}, f32[512]{0:T(512)S(1)}, f32[512,1024]{1,0:T(8,128)}) fusion(f32[1024]{0:T(1024)S(1)} %convert.8, f32[512]{0:T(512)S(1)} %div.45, bf16[2,4,64,1024]{3,2,1,0:T(8,128)(2,1)S(1)} %copy-done.3, bf16[512,3072]{1,0:T(8,128)(2,1)} %bitcast.96, bf16[1024,3072]{1,0:T(8,128)(2,1)} %bitcast.123), kind=kOutput, calls=%fused_computation.54 | convolution fusion | flops 3224369664 | bytes 12595200 | tf_op jit(solution)/shard_map/dot_general | solution.py:46
  387.9 2.6 fusion.11
  390.6 2.7 convert_reduce_fusion
  394.6 3.3 add_convert_fusion
  397.9 48.7 %end.1 = (bf16[4,2,64,1024]{3,2,1,0:T(8,128)(2,1)}, f32[8,128]{1,0:T(8,128)}, f32[32,3072]{1,0:T(8,128)}) custom-call(bf16[2,4,64,1024]{3,2,1,0:T(8,128)(2,1)} %bitcast.95, f32[4,8,8,128]{3,2,1,0:T(8,128)} %copy.34, bf16[4,4,2,32,3072]{4,3,2,1,0:T(8,128)(2,1)} %bitcast.94), custom_call_target="tpu_custom_call" | custom-call | tf_op jit(solution)/shard_map/end/pallas_call | solution.py:1402
  446.6 0.8 slice_bitcast_fusion
  448.0 1.2 slice_bitcast_fusion.1
  449.2 1.0 copy.41
  450.2 1.0 copy.42
  452.5 0.8 copy.45
  453.3 0.8 copy.46
  (66 shorter events, 7.5 us)
Async XLA Ops:
  275.9 2.5 copy-start.4
  278.4 1.2 copy-start.2
  279.2 1.4 copy-start
  279.7 1.4 copy-start.14
  281.1 2.6 copy-start.13
  286.0 85.4 %copy-start.3 = (bf16[2,4,64,1024]{3,2,1,0:T(8,128)(2,1)S(1)}, bf16[2,4,64,1024]{3,2,1,0:T(8,128)(2,1)}, u32[]{:S(2)}) copy-start(bf16[2,4,64,1024]{3,2,1,0:T(8,128)(2,1)} %get-tuple-element.40) | copy-start | bytes 3145732
  371.4 1.9 copy-start.5
  390.4 3.4 copy-start.12
  390.4 4.2 copy-start.1
  397.9 51.3 %copy-start.6 = (bf16[4,2,64,1024]{3,2,1,0:T(8,128)(2,1)S(1)}, bf16[4,2,64,1024]{3,2,1,0:T(8,128)(2,1)}, u32[]{:S(2)}) copy-start(bf16[4,2,64,1024]{3,2,1,0:T(8,128)(2,1)} %get-tuple-element.44) | copy-start | bytes 3145732
  446.6 3.5 copy-start.7
  449.2 2.0 copy-start.10
  449.2 2.7 copy-start.11
  450.1 2.4 copy-start.9
  450.2 3.2 copy-start.8

commit v7 on v6

--- a/solution.py
+++ b/solution.py
@@ -944,9 +944,6 @@
     for t in first:
         gather.start(t)
     go(seqs + vector_copies)
-    for t in later:
-        gather.start(t)
-    go(contracts + upstreams)
     gather.keep()
     load.wait()
     for t in range(len(first) + 2):
@@ -959,6 +956,8 @@
     load_upstream.wait()
     keep_upstream.start()
     arrive(seqs + vector_copies)
+    for t in later:
+        gather.start(t)
     values_of[...] = small[...].astype(f32)
 
     def row_of(n):
@@ -1006,17 +1005,16 @@
     gather.exchange(base + 1)
     own_copy.wait()
     gather.spread(base)
-    gather.exchange(base + 2)
-    gather.spread(base + 1)
     for d in range(7):
         to_head(d).wait_recv()
     keep_qkv.start()
-    gather.share(base)
     attention.run(
         {
-            1: [(gather.spread, base + 2)],
-            3: [(gather.share, base + 1)],
-            5: [(gather.share, base + 2)],
+            0: [(gather.exchange, base + 2), (go, contracts), (gather.spread, base + 1)],
+            2: [(gather.spread, base + 2), (gather.share, base)],
+            3: [(go, upstreams)],
+            5: [(gather.share, base + 1)],
+            6: [(gather.share, base + 2)],
         },
         back.each,
     )
@@ -1098,14 +1096,14 @@
 
 def feed_forward_kernel(
     chunks, expand, contract, contract_line, expand_bias, second, upstream, residual,
-    layer_out, second_back, expand_grad, bias_grad, contract_grad,
-    expand_in, contract_in, second_t, expanded, activated, grad, layer, staged, *refs,
+    layer, second_back, expand_grad, bias_grad, contract_grad,
+    expand_in, contract_in, second_t, expanded, activated, grad, staged, *refs,
 ):
     bufs, refs = refs[:6], refs[6:]
     loaded, stored, refs = refs[0], refs[1], refs[2:]
     copies = Copies(*refs)
     place = Place()
-    z, lines = place.z, place.lines
+    z = place.z
     reduce = ReduceLines(place, grad, contract_grad, bufs, copies)
     gather = Gather(
         place, [contract], [contract_in], [None], chunks, copies, given=contract_line
@@ -1113,7 +1111,6 @@
     rows, features = second.shape
     steps = 8
     wide = expand.shape[1] // steps
-    own, parts, piece, _ = layer.shape
 
     def at(n):
         part = (z + 1 + n // 2) % 4
@@ -1134,8 +1131,6 @@
             staged.at[slot], expand_grad.at[:, where], stored.at[slot]
         )
 
-    returned = [copies.plan(layer.at[:, to[0]], layer_out.at[z], to) for to in lines]
-    stay = copies.inside(layer.at[:, z], layer_out.at[z])
     for n in range(len(chunks)):
         gather.start(n)
     for n in range(steps):
@@ -1187,20 +1182,21 @@
         1: [(reduce.start, 0)] + [(gather.spread, n) for n in range(last)],
         2: [(gather.spread, last)],
         3: [(reduce.exchange, 0), (reduce.start, 1)],
-        4: [(reduce.exchange, 1)],
-        5: [(reduce.start, 2)] + [(gather.share, n) for n in range(last)],
-        7: [(reduce.start, 3), (reduce.exchange, 2)],
+        5: [(reduce.start, 2), (reduce.exchange, 1)],
+        7: [(reduce.start, 3), (reduce.exchange, 2)] + [(gather.share, n) for n in range(last)],
     }
     shrink_steps = {
-        1: [(reduce.spread, 0)],
-        3: [(reduce.exchange, 3)],
-        5: [(reduce.spread, 1), (reduce.send, 0)],
+        1: [(reduce.exchange, 3)],
+        3: [(reduce.spread, 0)],
+        7: [(reduce.spread, 1)],
     }
     backward_steps = {
-        0: [(reduce.spread, 2)],
-        1: [(reduce.send, 1), (reduce.spread, 3)],
-        3: [(reduce.send, 2)],
-        5: [(reduce.send, 3)],
+        1: [(reduce.spread, 2)],
+        2: [(reduce.spread, 3)],
+        3: [(reduce.send, 0)],
+        4: [(reduce.send, 1)],
+        5: [(reduce.send, 2)],
+        6: [(reduce.send, 3)],
     }
     lax.fori_loop(0, steps, lambda n, _: forward(n, forward_steps), 0)
     gather.share(last)
@@ -1210,14 +1206,11 @@
     lax.fori_loop(0, steps, lambda n, _: shrink(n, shrink_steps), 0)
     layer[...] = second_back[...].astype(bf16).reshape(layer.shape)
     second_back[...] = jnp.zeros_like(second_back)
-    go(returned + [stay])
     lax.fori_loop(0, steps, lambda n, _: backward(n, backward_steps), 0)
     reduce.finish()
     store(steps - 2).wait()
     store(steps - 1).wait()
-    arrive(returned)
     copies.finish()
-    done([stay])
 
 
 def feed_forward(shape, expand, contract, line, expand_bias, second, upstream, residual):
@@ -1228,19 +1221,19 @@
     each = hidden // 32
     contract = split_weight(contract)
     chunks = chunks_of(0, *contract.shape[1:], 2)
-    out = remote_call(
+    return remote_call(
         functools.partial(feed_forward_kernel, chunks),
         "feed_forward",
         4,
         out_shape=(
-            jax.ShapeDtypeStruct((parts, own, piece, features), bf16),
+            jax.ShapeDtypeStruct((own, parts, piece, features), bf16),
             jax.ShapeDtypeStruct((rows, features), f32),
             jax.ShapeDtypeStruct((features, hidden), bf16),
             jax.ShapeDtypeStruct((1, hidden), f32),
             jax.ShapeDtypeStruct((each, features), f32),
         ),
         in_specs=[HBM, HBM, HBM, VMEM, VMEM, VMEM, VMEM],
-        out_specs=(HBM, VMEM, HBM, VMEM, VMEM),
+        out_specs=(VMEM, VMEM, HBM, VMEM, VMEM),
         scratch_shapes=[
             pltpu.VMEM((features, hidden), bf16),
             pltpu.VMEM((4, *contract.shape), bf16),
@@ -1248,24 +1241,23 @@
             pltpu.VMEM((rows, hidden), f32),
             pltpu.VMEM((rows, hidden), bf16),
             pltpu.VMEM((4, 4, 2, each, features), bf16),
-            pltpu.VMEM((own, parts, piece, features), bf16),
             pltpu.VMEM((2, features, wide), bf16),
             *reduce_lines_scratch(each, features),
             pltpu.SemaphoreType.DMA((8,)),
             pltpu.SemaphoreType.DMA((2,)),
             *semaphores(
-                ReduceLines.copies + 3 + len(chunks) * (Gather.copies_each - 3),
-                2 + 3 * len(chunks),
+                ReduceLines.copies + len(chunks) * (Gather.copies_each - 3),
+                1 + 3 * len(chunks),
             ),
         ],
     )(expand, contract, line, expand_bias, second, upstream, residual)
-    return out[0].reshape(parts * own, piece, features), *out[1:]
 
 
 def backward_fused_kernel(heads, width, count, chunks, *refs):
-    slopes, diff_in, qkv_in, out_t_in, lse_in = refs[:5]
-    grads, refs = refs[5 : 5 + count], refs[5 + count :]
-    joined_out, outs, refs = refs[0], refs[1 : 1 + count], refs[1 + count :]
+    slopes, diff_in, qkv_in, out_t_in, lse_in, layer = refs[:6]
+    grads, refs = refs[6 : 6 + count], refs[6 + count :]
+    joined_out, layer_out, layer_own = refs[0], refs[1], refs[2 + count]
+    outs, refs = refs[2 : 2 + count], refs[3 + count :]
     diff, qkv, out_t, lse, joined = refs[:5]
     attention = Backward(heads, width, slopes, qkv, diff, out_t, lse, joined, *refs[5:12])
     bufs, refs = refs[12 : 12 + 7 * len(chunks)], refs[12 + 7 * len(chunks) :]
@@ -1283,52 +1275,67 @@
         copies.plan(diff_in.at[:, :, :, columns_of(to[1], features)], diff.at[:, :, s], to)
         for to in plane
     ]
-    go(own + reduce.loads + [along.load])
+    returned = [copies.plan(layer.at[:, to[0]], layer_out.at[place.z], to) for to in place.lines]
+    load_layer = copies.inside(layer.at[:, place.z], layer_own)
+    keep_layer = copies.inside(layer_own, layer_out.at[place.z])
+    go(own + reduce.loads + [along.load, load_layer])
     greet(place.lines + plane)
     go(arriving + [along.first])
     reduce.start()
     along.exchange()
-    for t in range(2):
+    go(returned)
+    for t in range(3):
         reduce.exchange(t)
-    done(own)
+    done(own + [load_layer])
+    keep_layer.start()
     arrive(arriving)
     attention.run(
         {
             1: [(reduce.spread, 0)],
-            3: [(reduce.spread, 1)],
-            4: [(reduce.send, 0), (along.spread,)],
+            2: [(along.spread,)],
+            3: [(reduce.spread, 1), (reduce.spread, 2)],
+            4: [(reduce.send, 0), (along.send,)],
             5: [(reduce.send, 1)],
-            6: [(along.send,)],
+            6: [(reduce.send, 2)],
         },
         back.each,
     )
-    for t in range(2):
+    for t in range(3):
         reduce.finish(t)
     along.finish()
     back.finish()
+    arrive(returned)
     copies.finish()
-
-
-def backward_fused(attended_diff, qkv, saved, grads, slopes, heads, width):
+    keep_layer.wait()
+
+
+def backward_fused(attended_diff, qkv, saved, layer, grads, slopes, heads, width):
     own, parts, piece, columns = attended_diff.shape
     features = heads * width
     length = parts * 8 * piece
     cut = [split_grad(item) for item in grads]
     count = len(cut)
-    chunks = []
-    for t, pieces in enumerate((2, 1)):
-        chunks += chunks_of(t, *cut[t].shape[3:], pieces)
+    rows, wide = cut[0].shape[3:]
+    part = 3 * wide // 8
+    chunks = [
+        (0, 0, rows, 0, wide // 4),
+        (0, 0, rows, wide // 4, part),
+        (0, 0, rows, wide // 4 + part, part),
+        *chunks_of(1, *cut[1].shape[3:], 1),
+    ]
     out = remote_call(
         functools.partial(backward_fused_kernel, heads, width, count, chunks),
         "backward_fused",
         2,
         out_shape=(
             jax.ShapeDtypeStruct((own, parts, piece, 24 * features), bf16),
+            jax.ShapeDtypeStruct((parts, own, piece, columns), bf16),
             *[jax.ShapeDtypeStruct(item.shape[3:], f32) for item in cut],
         ),
-        in_specs=[SMEM] + [HBM] * (4 + count),
-        out_specs=(HBM,) + (VMEM,) * count,
+        in_specs=[SMEM] + [HBM] * (5 + count),
+        out_specs=(HBM, HBM) + (VMEM,) * count,
         scratch_shapes=[
+            pltpu.VMEM((own, piece, columns), bf16),
             pltpu.VMEM((own, parts, 8, piece, features), bf16),
             pltpu.VMEM(qkv.shape, bf16),
             *[pltpu.VMEM(item.shape, f32) for item in saved],
@@ -1337,10 +1344,10 @@
             *reduce_along_scratch(chunks[0]),
             *reduce_scratch(chunks[1:]),
             *hand_back_semaphores(own * parts),
-            *semaphores(7 + len(chunks) * Reduce.copies_each, len(chunks) + 4),
+            *semaphores(10 + len(chunks) * Reduce.copies_each, len(chunks) + 6),
         ],
-    )(slopes, attended_diff, qkv, *saved, *cut)
-    return out[0], out[1:]
+    )(slopes, attended_diff, qkv, *saved, layer, *cut)
+    return out[0], out[1].reshape(parts * own, piece, columns), out[2:]
 
 
 def end_kernel(chunks, input_grad, vector, grad, input_out, vector_out, out, *refs):
@@ -1520,8 +1527,9 @@
         lax.psum_scatter, axis_name=("fs", "sp"), scatter_dimension=0, tiled=True
     )
     if fast:
-        joined_diff, grads = backward_fused(
-            attended_diff, qkv, saved, [item.astype(bf16) for item in grads], slopes, heads, width
+        joined_diff, layer_output, grads = backward_fused(
+            attended_diff, qkv, saved, layer_output, [item.astype(bf16) for item in grads],
+            slopes, heads, width,
         )
     else:
         joined_diff = attention_backward(

time: 455 us -> 420 us (0.923)
  Pallas kernels: 400 us -> 365 us
    pallas_call x1, Pallas kernels: 170 us -> 143 us  [forward_fused(): remote_call(functools.partial(forward_fused_kernel, heads, width, count,...]
    pallas_call x1, Pallas kernels: 96.1 us -> 85.6 us  [feed_forward(): remote_call(functools.partial(feed_forward_kernel, chunks), 'feed_forward...]
    pallas_call x1, Pallas kernels: 85.4 us -> 90.7 us  [backward_fused(): remote_call(functools.partial(backward_fused_kernel, heads, width, count,...]
where the time goes in v7:
time: 420 us; the launch traced here: 419 us
  Pallas kernels  365 us (87%)
  matrix products  22.8 us (5%)
  other arithmetic  16.7 us (4%)
  local copies, waits for them, and re-layouts  13.8 us (3%)
    pallas_call x1, Pallas kernels, forward_fused(): remote_call(functools.partial(forward_fused_kernel, heads, width, count,...  143 us
    pallas_call x1, Pallas kernels, backward_fused(): remote_call(functools.partial(backward_fused_kernel, heads, width, count,...  90.7 us
    pallas_call x1, Pallas kernels, feed_forward(): remote_call(functools.partial(feed_forward_kernel, chunks), 'feed_forward...  85.6 us
    pallas_call x1, Pallas kernels, end(): remote_call(functools.partial(end_kernel, chunks), 'end', 3, out_shape=(j...  46.1 us
    dot_general x2, matrix products, matmul_rt(): lax.dot_general(left_side, right_side, (((1,), (1,)), ((), ())), preferre...  10.9 us

profile of v7, /device:TPU:0, one launch (start us, length us, event | category | flops | bytes accessed | tf_op | source)
XLA Modules:
  0.0 419.3 jit_solution(4812472355462819761)
XLA Ops:
  0.6 1.2 dynamic_slice.3.slopes.refs_0_
  1.9 142.7 %forward_fused.1 = (bf16[2,4,64,1024]{3,2,1,0:T(8,128)(2,1)}, bf16[4,9,8,128]{3,2,1,0:T(8,128)(2,1)}, bf16[4,8,32,3072]{3,2,1,0:T(8,128)(2,1)}, bf16[2,4,8,64,38...) custom-call(f32[2]{0:T(128)} %dynamic_slice.3.slopes.refs_0_, ...), custom_call_target="tpu_custom_call" | custom-call | tf_op jit(solution)/shard_map/forward_fused/pallas_call | solution.py:1047
  144.6 0.8 fusion.24
  145.4 3.5 fusion.26
  149.4 2.2 broadcast_add_fusion
  151.5 1.3 slice_convert_fusion
  152.8 85.6 %feed_forward.1 = (bf16[2,4,64,1024]{3,2,1,0:T(8,128)(2,1)}, f32[512,1024]{1,0:T(8,128)}, bf16[1024,4096]{1,0:T(8,128)(2,1)}, f32[1,4096]{1,0:T(1,128)}, f32[128,1024]{1,0:T(8,128)}) custom-call(bf16[1024,4096]{1,0:T(8,128)(2,1)} %bitcast.93, bf16[8,128,1024]{2,1,0:T(8,128)(2,1)} %bitcast.91, bf16[4,128,1024]{2,1,0:T(8,128)(2,1)} %get-tuple-element.40.contract_line, ...), custom_call_target="tpu_custom_call" | custom-call | tf_op jit(solution)/shard_map/feed_forward/pallas_call | solution.py:1224
  238.5 2.5 multiply_reduce_fusion
  243.7 2.6 convolution_convert_fusion
  246.3 2.3 convolution_convert_fusion.1
  248.5 90.7 %backward_fused.1 = (bf16[2,4,64,3072]{3,2,1,0:T(8,128)(2,1)}, bf16[4,2,64,1024]{3,2,1,0:T(8,128)(2,1)}, f32[32,4096]{1,0:T(8,128)}, f32[32,1024]{1,0:T(8,128)}) custom-call(f32[2]{0:T(128)} %dynamic_slice.3.slopes.refs_0_, bf16[2,4,64,1024]{3,2,1,0:T(8,128)(2,1)} %bitcast.102, bf16[2,4,8,64,384]{4,3,2,1,0:T(8,128)(2,1)} %get-tuple-element.46.refs_2_, ...), custom_call_target="tpu_custom_call" | custom-call | tf_op jit(solution)/shard_map/backward_fused/pallas_call | solution.py:1326
  340.0 1.1 copy-done.5
  341.1 5.8 %bitcast_convert_fusion = bf16[1024,3072]{1,0:T(8,128)(2,1)} fusion(bf16[2,4,64,3072]{3,2,1,0:T(8,128)(2,1)S(1)} %copy-done.5, bf16[2,4,64,1024]{3,2,1,0:T(8,128)(2,1)S(1)} %copy-done.3, f32[1024]{0:T(1024)S(1)} %convert.13, f32[1024]{0:T(1024)S(1)} %convert.8, f32[2,4,64]{2,1,0:T(4,128)S(1)} %get-tuple-element.82, f32[2,4,64]{2,1,0:T(4,128)S(1)} %broadcast_multiply_fusion), kind=kOutput, calls=%fused_computation | convolution fusion | flops 3227516928 | bytes 10498048 | tf_op jit(solution)/shard_map/dot_general | solution.py:40
  346.9 8.7 %fusion.21 = (f32[1024]{0:T(1024)S(1)}, f32[512]{0:T(512)S(1)}, f32[512,1024]{1,0:T(8,128)}) fusion(f32[1024]{0:T(1024)S(1)} %convert.8, f32[512]{0:T(512)S(1)} %div.45, bf16[2,4,64,1024]{3,2,1,0:T(8,128)(2,1)S(1)} %copy-done.3, bf16[512,3072]{1,0:T(8,128)(2,1)} %bitcast.96, bf16[1024,3072]{1,0:T(8,128)(2,1)} %bitcast.123), kind=kOutput, calls=%fused_computation.54 | convolution fusion | flops 3224369664 | bytes 12595200 | tf_op jit(solution)/shard_map/dot_general | solution.py:46
  355.6 2.6 fusion.11
  358.4 2.7 convert_reduce_fusion
  362.4 3.3 add_convert_fusion
  365.6 46.1 %end.1 = (bf16[4,2,64,1024]{3,2,1,0:T(8,128)(2,1)}, f32[8,128]{1,0:T(8,128)}, f32[32,3072]{1,0:T(8,128)}) custom-call(bf16[2,4,64,1024]{3,2,1,0:T(8,128)(2,1)} %bitcast.95, f32[4,8,8,128]{3,2,1,0:T(8,128)} %copy.34, bf16[4,4,2,32,3072]{4,3,2,1,0:T(8,128)(2,1)} %bitcast.94), custom_call_target="tpu_custom_call" | custom-call | tf_op jit(solution)/shard_map/end/pallas_call | solution.py:1409
  411.8 0.8 slice_bitcast_fusion
  413.2 1.2 slice_bitcast_fusion.1
  414.4 1.0 copy.41
  415.3 1.0 copy.42
  417.7 0.8 copy.45
  418.5 0.8 copy.46
  (66 shorter events, 7.5 us)
Async XLA Ops:
  238.5 2.5 copy-start.4
  241.0 1.2 copy-start.2
  241.7 1.4 copy-start
  242.2 1.4 copy-start.14
  243.7 2.6 copy-start.13
  248.5 90.7 %copy-start.3 = (bf16[2,4,64,1024]{3,2,1,0:T(8,128)(2,1)S(1)}, bf16[2,4,64,1024]{3,2,1,0:T(8,128)(2,1)}, u32[]{:S(2)}) copy-start(bf16[2,4,64,1024]{3,2,1,0:T(8,128)(2,1)} %get-tuple-element.42) | copy-start | bytes 3145732
  339.2 1.9 copy-start.5
  358.2 3.4 copy-start.12
  358.2 4.2 copy-start.1
  365.6 48.7 %copy-start.6 = (bf16[4,2,64,1024]{3,2,1,0:T(8,128)(2,1)S(1)}, bf16[4,2,64,1024]{3,2,1,0:T(8,128)(2,1)}, u32[]{:S(2)}) copy-start(bf16[4,2,64,1024]{3,2,1,0:T(8,128)(2,1)} %get-tuple-element.51) | copy-start | bytes 3145732
  411.8 3.6 copy-start.7
  414.4 2.0 copy-start.10
  414.4 2.7 copy-start.11
  415.3 2.4 copy-start.9
  415.3 3.2 copy-start.8

commit v8 on v7

--- a/solution.py
+++ b/solution.py
@@ -17,7 +17,7 @@
 HBM = pl.BlockSpec(memory_space=pl.ANY)
 VMEM = pl.BlockSpec(memory_space=pltpu.VMEM)
 SMEM = pl.BlockSpec(memory_space=pltpu.SMEM)
-vmem_bytes = 60 * 1024 * 1024
+vmem_bytes = 63 * 1024 * 1024
 
 
 def normalize(values, norm_gain, norm_shift):
@@ -1095,10 +1095,13 @@
 
 
 def feed_forward_kernel(
-    chunks, expand, contract, contract_line, expand_bias, second, upstream, residual,
-    layer, second_back, expand_grad, bias_grad, contract_grad,
-    expand_in, contract_in, second_t, expanded, activated, grad, staged, *refs,
+    chunks, expand, contract, contract_line, out_weight,
+    expand_bias, upstream, tokens, attended, out_bias, gain, shift, contract_bias,
+    layer, residual_grad, attended_diff, expand_grad, out_grad, contract_grad,
+    bias_grad, gain_grad, shift_grad, out_bias_grad,
+    expand_in, contract_in, residual, second, second_t, expanded, activated, grad, staged, *refs,
 ):
+    second_back = residual_grad
     bufs, refs = refs[:6], refs[6:]
     loaded, stored, refs = refs[0], refs[1], refs[2:]
     copies = Copies(*refs)
@@ -1131,16 +1134,45 @@
             staged.at[slot], expand_grad.at[:, where], stored.at[slot]
         )
 
+    halves = [pl.ds(0, wide), pl.ds(wide, wide)]
+    out_loads = [
+        pltpu.make_async_copy(out_weight.at[:, half], staged.at[n], stored.at[n])
+        for n, half in enumerate(halves)
+    ]
+    out_stores = [
+        pltpu.make_async_copy(staged.at[n], out_grad.at[:, half], stored.at[n])
+        for n, half in enumerate(halves)
+    ]
+    part_rows = rows // 8
+
+    def rows_at(i):
+        return pl.ds(pl.multiple_of(i * part_rows, part_rows), part_rows)
+
     for n in range(len(chunks)):
         gather.start(n)
+    go(out_loads)
     for n in range(steps):
         load(n).start()
     go(gather.loads)
     greet(place.near)
     for n in range(len(chunks)):
         gather.exchange(n)
+    for n, half in enumerate(halves):
+        out_loads[n].wait()
+        residual[:, half] = (
+            tokens[:, half].astype(f32) + (matmul(attended[...], staged[n]) + out_bias[:, half])
+        )
+
+    def norm(i, _):
+        values = residual[rows_at(i), :]
+        second[rows_at(i), :] = normalize(values, gain[...], shift[...]).astype(bf16)
+        second_back[rows_at(i), :] = values + contract_bias[...]
+        return 0
+
+    lax.fori_loop(0, 8, norm, 0)
+    for n in range(len(chunks) - 1):
+        gather.spread(n)
     second_t[...] = second[...].T
-    second_back[...] = residual[...]
 
     def forward(n, after):
         part, side, where = at(n)
@@ -1179,8 +1211,8 @@
 
     last = len(chunks) - 1
     forward_steps = {
-        1: [(reduce.start, 0)] + [(gather.spread, n) for n in range(last)],
-        2: [(gather.spread, last)],
+        0: [(gather.spread, last)],
+        1: [(reduce.start, 0)],
         3: [(reduce.exchange, 0), (reduce.start, 1)],
         5: [(reduce.start, 2), (reduce.exchange, 1)],
         7: [(reduce.start, 3), (reduce.exchange, 2)] + [(gather.share, n) for n in range(last)],
@@ -1207,36 +1239,75 @@
     layer[...] = second_back[...].astype(bf16).reshape(layer.shape)
     second_back[...] = jnp.zeros_like(second_back)
     lax.fori_loop(0, steps, lambda n, _: backward(n, backward_steps), 0)
-    reduce.finish()
     store(steps - 2).wait()
     store(steps - 1).wait()
+    go(out_loads)
+    second_t[...] = attended[...].T
+
+    def norm_back(i, sums):
+        values, back = residual[rows_at(i), :], second_back[rows_at(i), :]
+        center = values - jnp.mean(values, axis=-1, keepdims=True)
+        inverse = lax.rsqrt(jnp.mean(center * center, axis=-1, keepdims=True) + norm_eps)
+        normal = center * inverse
+        scaled = back * gain[...]
+        even = jnp.mean(scaled, axis=-1, keepdims=True)
+        along = jnp.mean(scaled * normal, axis=-1, keepdims=True)
+        total = upstream[rows_at(i), :].astype(f32) + inverse * (scaled - even - normal * along)
+        low = total.astype(bf16)
+        residual_grad[rows_at(i), :] = total
+        second[rows_at(i), :] = low
+        found = (back * normal, back, low.astype(f32))
+        return tuple(
+            kept + jnp.sum(item, axis=0, keepdims=True) for kept, item in zip(sums, found)
+        )
+
+    nothing = jnp.zeros((1, features), f32)
+    sums = lax.fori_loop(0, 8, norm_back, (nothing, nothing, nothing))
+    gain_grad[...], shift_grad[...], out_bias_grad[...] = sums
+    done(out_loads)
+    branch_diff = second
+    made = matmul_rt(branch_diff[:, halves[0]], staged[0])
+    made = (made + matmul_rt(branch_diff[:, halves[1]], staged[1])).astype(bf16)
+    attended_diff[...] = made.reshape(attended_diff.shape)
+    for n, half in enumerate(halves):
+        staged[n] = matmul(second_t[...], branch_diff[:, half]).astype(bf16)
+        out_stores[n].start()
+    reduce.finish()
+    done(out_stores)
     copies.finish()
 
 
-def feed_forward(shape, expand, contract, line, expand_bias, second, upstream, residual):
+def feed_forward(shape, expand, contract, line, out_weight, tokens, upstream, attended, vectors):
     own, parts, piece = shape
-    rows, features = second.shape
+    rows, features = tokens.shape
     hidden = expand.shape[1]
     wide = hidden // 8
     each = hidden // 32
     contract = split_weight(contract)
     chunks = chunks_of(0, *contract.shape[1:], 2)
+    out_bias, gain, shift, expand_bias, contract_bias = [item.reshape(1, -1) for item in vectors]
+    seq_shape = (own, parts, piece, features)
     return remote_call(
         functools.partial(feed_forward_kernel, chunks),
         "feed_forward",
         4,
         out_shape=(
-            jax.ShapeDtypeStruct((own, parts, piece, features), bf16),
+            jax.ShapeDtypeStruct(seq_shape, bf16),
             jax.ShapeDtypeStruct((rows, features), f32),
+            jax.ShapeDtypeStruct(seq_shape, bf16),
             jax.ShapeDtypeStruct((features, hidden), bf16),
+            jax.ShapeDtypeStruct((features, features), bf16),
+            jax.ShapeDtypeStruct((each, features), f32),
             jax.ShapeDtypeStruct((1, hidden), f32),
-            jax.ShapeDtypeStruct((each, features), f32),
+            *[jax.ShapeDtypeStruct((1, features), f32)] * 3,
         ),
-        in_specs=[HBM, HBM, HBM, VMEM, VMEM, VMEM, VMEM],
-        out_specs=(VMEM, VMEM, HBM, VMEM, VMEM),
+        in_specs=[HBM] * 4 + [VMEM] * 8,
+        out_specs=(VMEM, VMEM, VMEM, HBM, HBM) + (VMEM,) * 5,
         scratch_shapes=[
             pltpu.VMEM((features, hidden), bf16),
             pltpu.VMEM((4, *contract.shape), bf16),
+            pltpu.VMEM((rows, features), f32),
+            pltpu.VMEM((rows, features), bf16),
             pltpu.VMEM((features, rows), bf16),
             pltpu.VMEM((rows, hidden), f32),
             pltpu.VMEM((rows, hidden), bf16),
@@ -1250,7 +1321,10 @@
                 1 + 3 * len(chunks),
             ),
         ],
-    )(expand, contract, line, expand_bias, second, upstream, residual)
+    )(
+        expand, contract, line, out_weight,
+        expand_bias, upstream, tokens, attended, out_bias, gain, shift, contract_bias,
+    )
 
 
 def backward_fused_kernel(heads, width, count, chunks, *refs):
@@ -1463,6 +1537,7 @@
         second_gain, second_shift, contract_bias, expand_bias,
     )
     fast = (fs_count, sp_count) == (4, 8) and (own, heads, width) == (2, 2, 64)
+    fast = fast and expand_weight.shape[1] == 4 * features
     weights = (joined_weight, output_weight, expand_weight)
     gather = lambda item: lax.all_gather(item, "fs", axis=0, tiled=True)
     if fast:
@@ -1474,7 +1549,8 @@
         whole = [gather(item) for item in vectors]
         weights = [gather(item) for item in (*weights, contract_weight)]
     joined_full, out_full, expand_full, contract_full = weights
-    tokens = tokens.reshape(rows, features).astype(f32)
+    tokens_low = tokens.reshape(rows, features)
+    tokens = tokens_low.astype(f32)
     gain_one, shift_one, qbias, vbias, obias, gain_two, shift_two, cbias, ebias = [
         item.astype(f32) for item in whole
     ]
@@ -1490,18 +1566,23 @@
     attended = attended.reshape(rows, features)
     upstream_low = upstream_low.reshape(rows, features)
 
-    residual = tokens + (matmul(attended, out_full) + obias)
-    second_f, norm_back_two = jax.vjp(normalize, residual, gain_two, shift_two)
-    second = second_f.astype(bf16)
     upstream_f = upstream_low.astype(f32)
     contract_bias_grad = jnp.sum(upstream_f, axis=0)
     if fast:
-        layer_output, second_back, expand_grad, expand_bias_grad, contract_grad = feed_forward(
-            shape, expand_full, contract_weight, contract_full, ebias.reshape(1, -1), second,
-            upstream_low, residual + cbias,
-        )
-        expand_bias_grad = expand_bias_grad.reshape(-1)
+        (
+            layer_output, residual_grad, attended_diff, expand_grad, output_weight_grad,
+            contract_grad, *small,
+        ) = feed_forward(
+            shape, expand_full, contract_weight, contract_full, out_full, tokens_low, upstream_low,
+            attended, (obias, gain_two, shift_two, ebias, cbias),
+        )
+        expand_bias_grad, second_gain_grad, second_shift_grad, output_bias_grad = [
+            item.reshape(-1) for item in small
+        ]
     else:
+        residual = tokens + (matmul(attended, out_full) + obias)
+        second_f, norm_back_two = jax.vjp(normalize, residual, gain_two, shift_two)
+        second = second_f.astype(bf16)
         expanded = matmul(second, expand_full) + ebias
         activated_f, gelu_back = jax.vjp(gelu_tanh, expanded)
         activated = activated_f.astype(bf16)
@@ -1514,14 +1595,14 @@
         expand_grad = matmul_lt(second, expand_diff)
         expand_bias_grad = jnp.sum(expand_diff.astype(f32), axis=0)
         second_back = matmul_rt(expand_diff, expand_full)
-    resid_part, second_gain_grad, second_shift_grad = norm_back_two(second_back)
-    residual_grad = upstream_f + resid_part
-
-    branch_diff = residual_grad.astype(bf16)
-    output_weight_grad = matmul_lt(attended, branch_diff)
-    output_bias_grad = jnp.sum(branch_diff.astype(f32), axis=0)
-    attended_diff = matmul_rt(branch_diff, out_full).astype(bf16)
-    attended_diff = attended_diff.reshape(*shape, features)
+        resid_part, second_gain_grad, second_shift_grad = norm_back_two(second_back)
+        residual_grad = upstream_f + resid_part
+
+        branch_diff = residual_grad.astype(bf16)
+        output_weight_grad = matmul_lt(attended, branch_diff)
+        output_bias_grad = jnp.sum(branch_diff.astype(f32), axis=0)
+        attended_diff = matmul_rt(branch_diff, out_full).astype(bf16)
+        attended_diff = attended_diff.reshape(*shape, features)
     grads = (expand_grad, output_weight_grad)
     scatter = functools.partial(
         lax.psum_scatter, axis_name=("fs", "sp"), scatter_dimension=0, tiled=True

time: 420 us -> 407 us (0.969)
  matrix products: 22.8 us -> 14.5 us
    dot_general x2 -> x1, matrix products: 10.9 us -> 6.92 us  [matmul_rt(): lax.dot_general(left_side, right_side, (((1,), (1,)), ((), ())), preferre...]
where the time goes in v8:
time: 407 us; the launch traced here: 406 us
  Pallas kernels  365 us (90%)
  matrix products  14.5 us (4%)
  other arithmetic  13.9 us (3%)
  local copies, waits for them, and re-layouts  12.3 us (3%)
    pallas_call x1, Pallas kernels, forward_fused(): remote_call(functools.partial(forward_fused_kernel, heads, width, count,...  143 us
    pallas_call x1, Pallas kernels, backward_fused(): remote_call(functools.partial(backward_fused_kernel, heads, width, count,...  90.5 us
    pallas_call x1, Pallas kernels, feed_forward(): remote_call(functools.partial(feed_forward_kernel, chunks), 'feed_forward...  85.7 us
    pallas_call x1, Pallas kernels, end(): remote_call(functools.partial(end_kernel, chunks), 'end', 3, out_shape=(j...  46.2 us

profile of v8, /device:TPU:0, one launch (start us, length us, event | category | flops | bytes accessed | tf_op | source)
XLA Modules:
  0.0 406.4 jit_solution(16891015332760445185)
XLA Ops:
  0.6 1.2 dynamic_slice.3.slopes.refs_0_
  1.9 142.7 %forward_fused.1 = (bf16[2,4,64,1024]{3,2,1,0:T(8,128)(2,1)}, bf16[4,9,8,128]{3,2,1,0:T(8,128)(2,1)}, bf16[4,8,32,3072]{3,2,1,0:T(8,128)(2,1)}, bf16[2,4,8,64,38...) custom-call(f32[2]{0:T(128)} %dynamic_slice.3.slopes.refs_0_, ...), custom_call_target="tpu_custom_call" | custom-call | tf_op jit(solution)/shard_map/forward_fused/pallas_call | solution.py:1047
  144.6 1.4 fusion.14
  146.0 1.3 slice_convert_fusion
  147.3 85.7 %feed_forward.1 = (bf16[2,4,64,1024]{3,2,1,0:T(8,128)(2,1)}, f32[512,1024]{1,0:T(8,128)}, bf16[2,4,64,1024]{3,2,1,0:T(8,128)(2,1)}, bf16[1024,4096]{1,0:T(8,128)...) custom-call(bf16[1024,4096]{1,0:T(8,128)(2,1)} %bitcast.64, ...), custom_call_target="tpu_custom_call" | custom-call | tf_op jit(solution)/shard_map/feed_forward/pallas_call | solution.py:1290
  233.0 90.5 %backward_fused.1 = (bf16[2,4,64,3072]{3,2,1,0:T(8,128)(2,1)}, bf16[4,2,64,1024]{3,2,1,0:T(8,128)(2,1)}, f32[32,4096]{1,0:T(8,128)}, f32[32,1024]{1,0:T(8,128)}) custom-call(f32[2]{0:T(128)} %dynamic_slice.3.slopes.refs_0_, bf16[2,4,64,1024]{3,2,1,0:T(8,128)(2,1)} %get-tuple-element.50.refs_1_, bf16[2,4,8,64,384]{4,3,2,1,0:T(8,128)(2,1)} %get-tuple-element.51.refs_2_, ...), custom_call_target="tpu_custom_call" | custom-call | tf_op jit(solution)/shard_map/backward_fused/pallas_call | solution.py:1400
  323.5 1.9 convert_reduce_fusion.1
  325.9 7.5 %bitcast_convert_fusion = bf16[1024,3072]{1,0:T(8,128)(2,1)} fusion(bf16[2,4,64,3072]{3,2,1,0:T(8,128)(2,1)} %get-tuple-element.59, bf16[2,4,64,1024]{3,2,1,0:T(8,128)(2,1)S(1)} %copy-done, f32[1024]{0:T(1024)S(1)} %convert.8, f32[1024]{0:T(1024)S(1)} %convert.7, f32[2,4,64]{2,1,0:T(4,128)S(1)} %get-tuple-element.83, f32[2,4,64]{2,1,0:T(4,128)S(1)} %broadcast_multiply_fusion), kind=kOutput, calls=%fused_computation | convolution fusion | flops 3227516928 | bytes 10498048 | tf_op jit(solution)/shard_map/dot_general | solution.py:40
  333.5 6.9 %fusion.13 = (f32[1024]{0:T(1024)S(1)}, f32[512]{0:T(512)S(1)}, f32[512,1024]{1,0:T(8,128)S(1)}) fusion(f32[1024]{0:T(1024)S(1)} %convert.7, f32[512]{0:T(512)S(1)} %div.22, bf16[2,4,64,1024]{3,2,1,0:T(8,128)(2,1)S(1)} %copy-done, bf16[512,3072]{1,0:T(8,128)(2,1)} %bitcast.70, bf16[1024,3072]{1,0:T(8,128)(2,1)} %bitcast.98), kind=kOutput, calls=%fused_computation.37 | convolution fusion | flops 3224369664 | bytes 12595200 | tf_op jit(solution)/shard_map/dot_general | solution.py:46
  340.5 1.0 multiply_reduce_fusion
  341.7 2.5 convert_reduce_fusion
  345.0 0.7 reduce.21
  345.7 0.7 reduce.22
  346.5 0.7 reduce.23
  347.4 0.7 copy.34
  348.1 3.3 add_convert_fusion
  351.4 46.2 %end.1 = (bf16[4,2,64,1024]{3,2,1,0:T(8,128)(2,1)}, f32[8,128]{1,0:T(8,128)}, f32[32,3072]{1,0:T(8,128)}) custom-call(bf16[2,4,64,1024]{3,2,1,0:T(8,128)(2,1)} %bitcast.69, f32[4,8,8,128]{3,2,1,0:T(8,128)} %copy.34, bf16[4,4,2,32,3072]{4,3,2,1,0:T(8,128)(2,1)} %bitcast.67), custom_call_target="tpu_custom_call" | custom-call | tf_op jit(solution)/shard_map/end/pallas_call | solution.py:1483
  397.6 0.8 slice_bitcast_fusion
  398.9 1.2 slice_bitcast_fusion.1
  400.1 2.3 copy.41
  402.5 1.0 copy.42
  403.4 0.7 copy.43
  404.8 0.8 copy.45
  405.6 0.8 copy.46
  (44 shorter events, 3.2 us)
Async XLA Ops:
  323.5 2.0 copy-start
  341.5 3.5 copy-start.9
  341.5 4.2 %copy-start.8 = (f32[1,1024]{1,0:T(1,128)S(1)}, f32[1,1024]{1,0:T(1,128)}, u32[]{:S(2)}) copy-start(f32[1,1024]{1,0:T(1,128)} %get-tuple-element.62) | copy-start | bytes 12292
  341.5 5.0 %copy-start.7 = (f32[1,1024]{1,0:T(1,128)S(1)}, f32[1,1024]{1,0:T(1,128)}, u32[]{:S(2)}) copy-start(f32[1,1024]{1,0:T(1,128)} %get-tuple-element.63) | copy-start | bytes 12292
  341.5 5.8 %copy-start.6 = (f32[1,4096]{1,0:T(1,128)S(1)}, f32[1,4096]{1,0:T(1,128)}, u32[]{:S(2)}) copy-start(f32[1,4096]{1,0:T(1,128)} %get-tuple-element.64) | copy-start | bytes 49156
  397.6 4.9 %copy-start.1 = (bf16[4,2,64,1024]{3,2,1,0:T(8,128)(2,1)S(1)}, bf16[4,2,64,1024]{3,2,1,0:T(8,128)(2,1)}, u32[]{:S(2)}) copy-start(bf16[4,2,64,1024]{3,2,1,0:T(8,128)(2,1)} %get-tuple-element.65) | copy-start | bytes 3145732
  400.1 3.3 copy-start.4
  400.1 4.1 copy-start.5
  402.4 2.4 copy-start.3
  402.5 3.2 copy-start.2

commit v9 on v8

--- a/solution.py
+++ b/solution.py
@@ -24,6 +24,16 @@
     center = values - jnp.mean(values, axis=-1, keepdims=True)
     variance = jnp.mean(center * center, axis=-1, keepdims=True)
     return center * lax.rsqrt(variance + norm_eps) * norm_gain + norm_shift
+
+
+def normalize_back(values, back, norm_gain):
+    center = values - jnp.mean(values, axis=-1, keepdims=True)
+    inverse = lax.rsqrt(jnp.mean(center * center, axis=-1, keepdims=True) + norm_eps)
+    normal = center * inverse
+    scaled = back * norm_gain
+    even = jnp.mean(scaled, axis=-1, keepdims=True)
+    along = jnp.mean(scaled * normal, axis=-1, keepdims=True)
+    return inverse * (scaled - even - normal * along), normal
 
 
 def gelu_tanh(values):
@@ -577,6 +587,9 @@
 
     def start(self):
         go(self.first)
+
+    def begin(self, t):
+        go([self.loads[t], self.first[t]])
 
     def halves(self, t):
         half = self.chunks[t][2] // 2
@@ -1245,14 +1258,9 @@
     second_t[...] = attended[...].T
 
     def norm_back(i, sums):
-        values, back = residual[rows_at(i), :], second_back[rows_at(i), :]
-        center = values - jnp.mean(values, axis=-1, keepdims=True)
-        inverse = lax.rsqrt(jnp.mean(center * center, axis=-1, keepdims=True) + norm_eps)
-        normal = center * inverse
-        scaled = back * gain[...]
-        even = jnp.mean(scaled, axis=-1, keepdims=True)
-        along = jnp.mean(scaled * normal, axis=-1, keepdims=True)
-        total = upstream[rows_at(i), :].astype(f32) + inverse * (scaled - even - normal * along)
+        back = second_back[rows_at(i), :]
+        part, normal = normalize_back(residual[rows_at(i), :], back, gain[...])
+        total = upstream[rows_at(i), :].astype(f32) + part
         low = total.astype(bf16)
         residual_grad[rows_at(i), :] = total
         second[rows_at(i), :] = low
@@ -1424,83 +1432,158 @@
     return out[0], out[1].reshape(parts * own, piece, columns), out[2:]
 
 
-def end_kernel(chunks, input_grad, vector, grad, input_out, vector_out, out, *refs):
-    input_own, ranks, plane_sum, others = refs[:4]
-    bufs, refs = refs[4 : 4 + 7 * len(chunks)], refs[4 + 7 * len(chunks) :]
-    copies = Copies(*refs)
+def end_kernel(
+    width, joined_diff, joined_weight, tokens, residual_grad, gain, shift, out_bias_grad,
+    second_gain_grad, second_shift_grad, contract_bias_grad, expand_bias_grad,
+    input_out, vector_out, out,
+    diff_in, weight_in, normed, normed_t, back, grads, held, vectors, others, ranks, *refs,
+):
+    count = grads.shape[0]
+    bufs, refs = refs[: 7 * count], refs[7 * count :]
+    loaded, copies = refs[0], Copies(*refs[1:])
     place = Place()
-    z, s, lines, plane = place.z, place.s, place.lines, place.plane
-    count = len(chunks)
-    reduce = Reduce(place, [grad], [out], bufs, chunks, copies)
-    load = copies.inside(input_grad.at[:, z], input_own)
-    load_vector = copies.inside(vector.at[:, s], ranks.at[0])
-    keep = copies.inside(input_own, input_out.at[z])
-    waiting = [copies.plan(input_grad.at[:, to[0]], input_out.at[z], to) for to in lines]
-    vectors = [
-        copies.plan(vector.at[:, to[1]], ranks.at[d + 1], to) for d, to in enumerate(plane)
+    z, lines, plane = place.z, place.lines, place.plane
+    rows, features = tokens.shape
+    own_seqs, parts, piece, _ = held.shape
+    columns = [pl.ds(features * n, features) for n in range(count)]
+    chunks = [(n, 0, grads.shape[4], 0, features) for n in range(count)]
+    outs = [out.at[:, where] for where in columns]
+    reduce = Reduce(place, [grads.at[n] for n in range(count)], outs, bufs, chunks, copies)
+    loads = [
+        (
+            pltpu.make_async_copy(joined_diff.at[:, c], diff_in.at[:, c], loaded.at[0, n]),
+            pltpu.make_async_copy(joined_weight.at[:, c], weight_in.at[:, c], loaded.at[1, n]),
+        )
+        for n, c in enumerate(columns)
     ]
-    sums = [copies.plan(plane_sum.at[to[0]], others.at[k], to) for k, to in enumerate(lines)]
-    go(reduce.loads + [load, load_vector])
+    returned = [copies.plan(held.at[:, to[0]], input_out.at[z], to) for to in lines]
+    stay = copies.inside(held.at[:, z], input_out.at[z])
+    along = [copies.plan(vectors.at[to[0]], others.at[k], to) for k, to in enumerate(lines)]
+    across = [copies.plan(ranks.at[0], ranks.at[d + 1], to) for d, to in enumerate(plane)]
+
+    for load in loads:
+        go(load)
     greet(lines + plane)
-    reduce.start()
-    go(waiting + vectors)
-    load.wait()
-    go([keep])
-    for t in range(count + 2):
-        if t < count:
-            reduce.exchange(t)
-        if t == 0:
-            load_vector.wait()
-            arrive(vectors)
-            total = ranks[0]
-            for d in range(1, 8):
-                total = total + ranks[d]
-            plane_sum[...] = total
-            go(sums)
-        if 0 <= t - 1 < count:
-            reduce.spread(t - 1)
-        if 0 <= t - 2:
-            reduce.send(t - 2)
-    arrive(sums)
-    total = plane_sum[z]
+    for n, where in enumerate(columns):
+        done(loads[n])
+        part = matmul_rt(diff_in[:, where], weight_in[:, where])
+        back[...] = part if n == 0 else back[...] + part
+
+    def norm_back(i, sums):
+        at = pl.ds(pl.multiple_of(i * piece, piece), piece)
+        values, given = tokens[at, :].astype(f32), back[at, :]
+        part, normal = normalize_back(values, given, gain[...])
+        normed[at, :] = (normal * gain[...] + shift[...]).astype(bf16)
+        total = (residual_grad[at, :] + part).astype(bf16)
+        held[i // parts, i % parts] = total
+        found = (given * normal, given)
+        return tuple(
+            kept + jnp.sum(item, axis=0, keepdims=True) for kept, item in zip(sums, found)
+        )
+
+    nothing = jnp.zeros((1, features), f32)
+    gain_grad, shift_grad = lax.fori_loop(0, own_seqs * parts, norm_back, (nothing, nothing))
+    go(returned + [stay])
+    normed_t[...] = normed[...].T
+    sums = []
+    for n, where in enumerate(columns):
+        made = matmul(normed_t[...], diff_in[:, where]).astype(bf16)
+        grads[n] = made.reshape(grads.shape[1:])
+        reduce.begin(n)
+        sums.append(jnp.sum(diff_in[:, where].astype(f32), axis=0, keepdims=True))
+        if n > 0:
+            reduce.exchange(n - 1)
+
+    sums = jnp.concatenate(sums, axis=1)
+    low = lax.broadcasted_iota(jnp.int32, (1, 128), 1) < width
+    query_grad, value_grad = [], []
+    for r in range(features // 128):
+        first, middle, last = [sums[:, (3 * r + n) * 128 : (3 * r + n + 1) * 128] for n in range(3)]
+        query_grad.append(jnp.where(low, first, middle))
+        value_grad.append(jnp.where(low, middle, last))
+    given = [
+        gain_grad, shift_grad, jnp.concatenate(query_grad, axis=1),
+        jnp.concatenate(value_grad, axis=1), out_bias_grad[...], second_gain_grad[...],
+        second_shift_grad[...], contract_bias_grad[...], expand_bias_grad[...],
+    ]
+    row = 0
+    for item in given:
+        each = item.shape[1] // 512
+        for k in range(4):
+            for r in range(each):
+                start = (k * each + r) * 128
+                vectors[k, row + r : row + r + 1, :] = item[:, start : start + 128]
+        row += each
+    go(along)
+    reduce.spread(0)
+    reduce.exchange(count - 1)
+    arrive(along)
+    total = vectors[z]
     for k in range(3):
         total = total + others[k]
+    ranks[0] = total
+    go(across)
+    for n in range(1, count):
+        reduce.send(n - 1)
+        reduce.spread(n)
+    reduce.send(count - 1)
+    arrive(across)
+    total = ranks[0]
+    for d in range(1, 8):
+        total = total + ranks[d]
     vector_out[...] = total
-    for t in range(count):
-        reduce.finish(t)
-    arrive(waiting)
+    for n in range(count):
+        reduce.finish(n)
+    arrive(returned)
     copies.finish()
-    keep.wait()
-
-
-def end(input_grad, vector, grad):
-    own, parts, piece, features = input_grad.shape
-    lanes = vector.shape[-1]
-    padded = -(-lanes // 1024) * 1024
-    vector = jnp.pad(vector, ((0, 0), (0, padded - lanes))).reshape(4, 8, padded // 128, 128)
-    cut = split_grad(grad)
-    chunks = chunks_of(0, *cut.shape[3:], 3)
+    stay.wait()
+
+
+def end(shape, joined_diff, joined_weight, tokens, residual_grad, gain, shift, vectors, width):
+    own, parts, piece = shape
+    rows, features = tokens.shape
+    count = joined_diff.shape[1] // features
+    each = features // 32
+    vectors = [item.reshape(1, -1) for item in (gain, shift, *vectors)]
+    tall = (4 * features + sum(item.shape[1] for item in vectors[2:])) // 512
+    chunks = [(n, 0, each, 0, features) for n in range(count)]
     out = remote_call(
-        functools.partial(end_kernel, chunks),
+        functools.partial(end_kernel, width),
         "end",
         3,
         out_shape=(
             jax.ShapeDtypeStruct((parts, own, piece, features), bf16),
-            jax.ShapeDtypeStruct(vector.shape[2:], f32),
-            jax.ShapeDtypeStruct(cut.shape[3:], f32),
+            jax.ShapeDtypeStruct((tall, 128), f32),
+            jax.ShapeDtypeStruct((each, count * features), f32),
         ),
-        in_specs=[HBM] * 3,
+        in_specs=[HBM, HBM] + [VMEM] * (2 + len(vectors)),
         out_specs=(HBM, VMEM, VMEM),
         scratch_shapes=[
-            pltpu.VMEM((own, piece, features), bf16),
-            pltpu.VMEM((8, 4, padded // 128, 128), f32),
-            pltpu.VMEM((4, padded // 128, 128), f32),
-            pltpu.VMEM((3, padded // 128, 128), f32),
+            pltpu.VMEM((rows, count * features), bf16),
+            pltpu.VMEM((features, count * features), bf16),
+            pltpu.VMEM((rows, features), bf16),
+            pltpu.VMEM((features, rows), bf16),
+            pltpu.VMEM((rows, features), f32),
+            pltpu.VMEM((count, 4, 4, 2, each, features), bf16),
+            pltpu.VMEM((own, parts, piece, features), bf16),
+            pltpu.VMEM((4, tall, 128), f32),
+            pltpu.VMEM((3, tall, 128), f32),
+            pltpu.VMEM((8, tall, 128), f32),
             *reduce_scratch(chunks),
-            *semaphores(3 + 7 + 3 + len(chunks) * Reduce.copies_each, 3 + len(chunks)),
+            pltpu.SemaphoreType.DMA((2, count)),
+            *semaphores(3 + 3 + 7 + count * Reduce.copies_each, 1 + count),
         ],
-    )(input_grad, vector, cut)
-    return out[0].reshape(parts * own, piece, features), out[1].reshape(-1)[:lanes], out[2]
+    )(joined_diff, joined_weight, tokens, residual_grad, *vectors)
+    each = features // 32
+    split = 8 * features // 512
+    place = lax.axis_index("sp")
+    short = out[1][:split].reshape(8, features // 4)
+    short = lax.dynamic_slice_in_dim(short, place * each, each, 1)
+    long = out[1][split:].reshape(-1)
+    size = long.shape[0] // 8
+    long = lax.dynamic_slice_in_dim(long, place * size, size)
+    own_grads = [short[n] for n in range(8)] + [long]
+    return out[0].reshape(parts * own, piece, features), own_grads, out[2]
 
 
 def per_device(
@@ -1622,30 +1705,38 @@
     expand_grad, output_weight_grad = grads
     joined_diff = joined_diff.reshape(rows, 3 * features)
 
-    joined_grad = matmul_lt(normed, joined_diff)
-    column_sums = jnp.sum(joined_diff.astype(f32), axis=0).reshape(head_count, 3, width)
-    query_bias_grad = column_sums[:, 0].reshape(features)
-    value_bias_grad = column_sums[:, 2].reshape(features)
-    normed_back = matmul_rt(joined_diff, joined_full)
-    input_part, first_gain_grad, first_shift_grad = norm_back_one(normed_back)
-    input_grad = (residual_grad + input_part).astype(bf16).reshape(*shape, features)
-
-    vector_grads = (
-        first_gain_grad, first_shift_grad, query_bias_grad, value_bias_grad, output_bias_grad,
-        second_gain_grad, second_shift_grad, contract_bias_grad, expand_bias_grad,
-    )
-    devices = fs_count * sp_count
-    packed = jnp.concatenate([item.reshape(devices, -1) for item in vector_grads], axis=1)
     if fast:
-        input_grad, packed, joined_grad = end(input_grad, packed, joined_grad.astype(bf16))
+        input_grad, own_grads, joined_grad = end(
+            shape, joined_diff, joined_full, tokens_low, residual_grad, gain_one, shift_one,
+            (
+                output_bias_grad, second_gain_grad, second_shift_grad, contract_bias_grad,
+                expand_bias_grad,
+            ),
+            width,
+        )
     else:
+        joined_grad = matmul_lt(normed, joined_diff)
+        column_sums = jnp.sum(joined_diff.astype(f32), axis=0).reshape(head_count, 3, width)
+        query_bias_grad = column_sums[:, 0].reshape(features)
+        value_bias_grad = column_sums[:, 2].reshape(features)
+        normed_back = matmul_rt(joined_diff, joined_full)
+        input_part, first_gain_grad, first_shift_grad = norm_back_one(normed_back)
+        input_grad = (residual_grad + input_part).astype(bf16).reshape(*shape, features)
+
+        vector_grads = (
+            first_gain_grad, first_shift_grad, query_bias_grad, value_bias_grad,
+            output_bias_grad, second_gain_grad, second_shift_grad, contract_bias_grad,
+            expand_bias_grad,
+        )
+        devices = fs_count * sp_count
+        packed = jnp.concatenate([item.reshape(devices, -1) for item in vector_grads], axis=1)
         input_grad, joined_grad = from_own_seqs(input_grad), scatter(joined_grad)
         packed = scatter(packed.reshape(-1))
-    own_grads, at = [], 0
-    for item in vector_grads:
-        size = item.shape[0] // devices
-        own_grads.append(packed[at : at + size])
-        at += size
+        own_grads, at = [], 0
+        for item in vector_grads:
+            size = item.shape[0] // devices
+            own_grads.append(packed[at : at + size])
+            at += size
     g1, s1, qb, vb, ob, g2, s2, cb, eb = own_grads
     return (
         layer_output,

time: 407 us -> 393 us (0.966)
  matrix products: 14.5 us -> 0 us
  Pallas kernels: 365 us -> 377 us
  other arithmetic: 13.9 us -> 4.7 us
    dot_general x2 -> x0, matrix products: 14.5 us -> none  [the longest x1 7.54 us: matmul_lt(): lax.dot_general(left_side, right_side, (((0,), (0,)), ((), ())), preferre...]
    pallas_call x1, Pallas kernels: 46.2 us -> 58.2 us  [end(): remote_call(functools.partial(end_kernel, width), 'end', 3, out_shape=(ja...]
where the time goes in v9:
time: 393 us
  Pallas kernels  377 us (96%)
  local copies, waits for them, and re-layouts  10.2 us (3%)
  other arithmetic  4.7 us (1%)
    pallas_call x1, Pallas kernels, forward_fused(): remote_call(functools.partial(forward_fused_kernel, heads, width, count,...  143 us
    pallas_call x1, Pallas kernels, backward_fused(): remote_call(functools.partial(backward_fused_kernel, heads, width, count,...  90.4 us
    pallas_call x1, Pallas kernels, feed_forward(): remote_call(functools.partial(feed_forward_kernel, chunks), 'feed_forward...  85.7 us
    pallas_call x1, Pallas kernels, end(): remote_call(functools.partial(end_kernel, width), 'end', 3, out_shape=(ja...  58.2 us

profile of v9, /device:TPU:0, one launch (start us, length us, event | category | flops | bytes accessed | tf_op | source)
XLA Modules:
  0.0 392.8 jit_solution(7011039744428861211)
XLA Ops:
  0.6 1.2 dynamic_slice.9.slopes.refs_0_
  1.9 142.9 %forward_fused.1 = (bf16[2,4,64,1024]{3,2,1,0:T(8,128)(2,1)}, bf16[4,9,8,128]{3,2,1,0:T(8,128)(2,1)}, bf16[4,8,32,3072]{3,2,1,0:T(8,128)(2,1)}, bf16[2,4,8,64,38...) custom-call(f32[2]{0:T(128)} %dynamic_slice.9.slopes.refs_0_, ...), custom_call_target="tpu_custom_call" | custom-call | tf_op jit(solution)/shard_map/forward_fused/pallas_call | solution.py:1060
  144.8 1.4 slice_convert_fusion.1
  146.2 1.3 slice_convert_fusion
  147.5 85.7 %feed_forward.1 = (bf16[2,4,64,1024]{3,2,1,0:T(8,128)(2,1)}, f32[512,1024]{1,0:T(8,128)}, bf16[2,4,64,1024]{3,2,1,0:T(8,128)(2,1)}, bf16[1024,4096]{1,0:T(8,128)...) custom-call(bf16[1024,4096]{1,0:T(8,128)(2,1)} %bitcast.53, ...), custom_call_target="tpu_custom_call" | custom-call | tf_op jit(solution)/shard_map/feed_forward/pallas_call | solution.py:1298
  233.1 90.4 %backward_fused.1 = (bf16[2,4,64,3072]{3,2,1,0:T(8,128)(2,1)}, bf16[4,2,64,1024]{3,2,1,0:T(8,128)(2,1)}, f32[32,4096]{1,0:T(8,128)}, f32[32,1024]{1,0:T(8,128)}) custom-call(f32[2]{0:T(128)} %dynamic_slice.9.slopes.refs_0_, bf16[2,4,64,1024]{3,2,1,0:T(8,128)(2,1)} %get-tuple-element.50.refs_1_, bf16[2,4,8,64,384]{4,3,2,1,0:T(8,128)(2,1)} %get-tuple-element.51.refs_2_, ...), custom_call_target="tpu_custom_call" | custom-call | tf_op jit(solution)/shard_map/backward_fused/pallas_call | solution.py:1408
  323.6 2.0 convert_reduce_fusion
  325.6 58.2 %end.1 = (bf16[4,2,64,1024]{3,2,1,0:T(8,128)(2,1)}, f32[24,128]{1,0:T(8,128)}, f32[32,3072]{1,0:T(8,128)}) custom-call(bf16[512,3072]{1,0:T(8,128)(2,1)} %bitcast.60, bf16[1024,3072]{1,0:T(8,128)(2,1)} %bitcast.56, bf16[512,1024]{1,0:T(8,128)(2,1)} %bitcast.59, f32[512,1024]{1,0:T(8,128)} %get-tuple-element.60.residual_grad, f32[1,1024]{1,0:T(1,128)} %bitcast.74, ...), custom_call_target="tpu_custom_call" | custom-call | tf_op jit(solution)/shard_map/end/pallas_call | solution.py:1550
  383.8 0.0 copy-start
  383.8 0.8 slice.58
  384.6 0.1 constant_dynamic-slice_fusion
  384.7 0.5 slice_bitcast_fusion.1
  385.2 0.7 slice_bitcast_fusion
  385.9 0.6 dynamic_slice.11
  386.5 2.3 copy.37
  388.8 0.0 copy-done
  388.8 1.0 copy.38
  389.8 0.7 copy.39
  390.5 0.0 copy-done.4
  390.5 0.7 copy.40
  391.2 0.0 copy-done.2
  391.2 0.8 copy.41
  392.0 0.0 copy-done.1
  392.0 0.8 copy.42
  (6 shorter events, 0.0 us)
Async XLA Ops:
  383.8 5.0 %copy-start = (bf16[4,2,64,1024]{3,2,1,0:T(8,128)(2,1)S(1)}, bf16[4,2,64,1024]{3,2,1,0:T(8,128)(2,1)}, u32[]{:S(2)}) copy-start(bf16[4,2,64,1024]{3,2,1,0:T(8,128)(2,1)} %get-tuple-element.65) | copy-start | bytes 3145732
  386.5 3.3 copy-start.3
  386.5 4.1 %copy-start.4 = (f32[32,1024]{1,0:T(8,128)S(1)}, f32[32,1024]{1,0:T(8,128)}, u32[]{:S(2)}) copy-start(f32[32,1024]{1,0:T(8,128)} %get-tuple-element.107) | copy-start | bytes 393220
  388.8 2.4 copy-start.2
  388.8 3.2 copy-start.1

commit v10 on v9

--- a/solution.py
+++ b/solution.py
@@ -102,6 +102,7 @@
         self.heads, self.width, self.slopes, self.qkv, self.out = heads, width, slopes, qkv, out
         self.out_t, self.lse = out_t, lse
         self.keys, self.queries, self.values_t = keys, queries, values_t
+        self.head = 0
         self.blocks = qkv.shape[1]
         self.block = qkv.shape[2] * qkv.shape[3]
 
@@ -120,7 +121,7 @@
                     qkv[b, i, :, :, base + n * width : base + (n + 1) * width].reshape(block, width)
                     for n in range(3)
                 ]
-                self.keys[h, rows, :] = key_columns(key, self.slopes[h], i * block)
+                self.keys[h, rows, :] = key_columns(key, self.slopes[self.head + h], i * block)
                 self.queries[h, rows, :] = query_columns(query, scale)
                 self.values_t[h, :, rows] = value.astype(f32).T.astype(bf16)
             return 0
@@ -230,6 +231,7 @@
         self.out_t, self.lse, self.joined = out_t, lse, joined
         self.keys, self.queries, self.keys_t, self.values = keys, queries, keys_t, values
         self.diffs, self.delta, self.query_acc = diffs, delta, query_acc
+        self.head = 0
         self.blocks = qkv.shape[1]
         self.block = qkv.shape[2] * qkv.shape[3]
 
@@ -248,7 +250,7 @@
                     qkv[b, i, :, :, base + n * width : base + (n + 1) * width].reshape(block, width)
                     for n in range(3)
                 ]
-                self.keys[h, rows, :] = key_columns(key, self.slopes[h], i * block)
+                self.keys[h, rows, :] = key_columns(key, self.slopes[self.head + h], i * block)
                 self.keys_t[h, :, rows] = key.astype(f32).T.astype(bf16)
                 self.queries[h, rows, :] = query_columns(query, scale)
                 self.values[h, rows, :] = value
@@ -784,15 +786,46 @@
 
 
 class ReduceLines:
-    copies = 4 * 7 + 3
+    copies = 4 * 7 + 3 + 3 + 6
 
     def __init__(self, place, grad, out, bufs, copies):
         self.place, self.grad, self.out, self.bufs = place, grad, out, bufs
-        from_core, from_x, from_y, late_y, late_x, from_z = bufs
+        from_core, from_x, from_y, late_y, late_x, from_z = bufs[:6]
+        early_z, own_x, own_y, own_late_y, own_late_x = bufs[6:]
         core, x, y = place.core, place.x, place.y
         self.order = [to[0] for to in place.lines] + [place.z]
         rows = grad.shape[3]
-        self.low, self.high = pl.ds(0, rows // 2), pl.ds(rows // 2, rows // 2)
+        low, high = pl.ds(0, rows // 2), pl.ds(rows // 2, rows // 2)
+        cut = from_z.shape[2]
+        most, rest = pl.ds(0, cut), pl.ds(cut, grad.shape[4] - cut)
+        self.low, self.high, self.all = (low, most), (high, most), (pl.ds(0, rows), most)
+        self.low_rest, self.high_rest = (low, rest), (high, rest)
+        self.all_rest = (pl.ds(0, rows), rest)
+        z = place.z
+        self.early = [
+            copies.plan(grad.at[(to[0], pl.ds(0, 4), core, *self.all_rest)], early_z.at[k], to)
+            for k, to in enumerate(place.lines)
+        ]
+        self.own_second, self.own_third = [], []
+        for j in range(2):
+            self.own_second.append(
+                copies.plan(
+                    grad.at[(z, 2 * j + 1 - x, core, *self.low_rest)], own_x.at[j], place.to_x
+                )
+            )
+            self.own_second.append(
+                copies.plan(
+                    grad.at[(z, 2 * (1 - y) + j, core, *self.high_rest)], own_y.at[j], place.to_y
+                )
+            )
+        self.own_third = [
+            copies.plan(
+                grad.at[(z, place.chip_y, core, *self.low_rest)], own_late_y, place.to_y
+            ),
+            copies.plan(
+                grad.at[(z, place.chip_x, core, *self.high_rest)], own_late_x, place.to_x
+            ),
+        ]
         self.first, self.second, self.third, self.fourth = [], [], [], []
         for k, at in enumerate(self.order):
             self.first.append(
@@ -802,26 +835,30 @@
             for j in range(2):
                 step.append(
                     copies.plan(
-                        grad.at[at, 2 * j + 1 - x, core, self.low], from_x.at[k, j], place.to_x
+                        grad.at[(at, 2 * j + 1 - x, core, *self.low)], from_x.at[k, j], place.to_x
                     )
                 )
                 step.append(
                     copies.plan(
-                        grad.at[at, 2 * (1 - y) + j, core, self.high], from_y.at[k, j], place.to_y
+                        grad.at[(at, 2 * (1 - y) + j, core, *self.high)], from_y.at[k, j], place.to_y
                     )
                 )
             self.second.append(step)
             self.third.append(
                 [
-                    copies.plan(grad.at[at, place.chip_y, core, self.low], late_y.at[k], place.to_y),
                     copies.plan(
-                        grad.at[at, place.chip_x, core, self.high], late_x.at[k], place.to_x
+                        grad.at[(at, place.chip_y, core, *self.low)], late_y.at[k], place.to_y
+                    ),
+                    copies.plan(
+                        grad.at[(at, place.chip_x, core, *self.high)], late_x.at[k], place.to_x
                     ),
                 ]
             )
             if k < 3:
                 self.fourth.append(
-                    copies.plan(grad.at[at, place.chip, core], from_z.at[k], place.lines[k])
+                    copies.plan(
+                        grad.at[(at, place.chip, core, *self.all)], from_z.at[k], place.lines[k]
+                    )
                 )
 
     def start(self, k):
@@ -831,44 +868,82 @@
         arrive([self.first[k]])
         at, core = self.order[k], self.place.core
         add_blocks(4, lambda i: (self.grad.at[at, i, core], self.bufs[0].at[k, i]))
-        go(self.second[k])
+        go(self.second[k] + self.early[k : k + 1])
 
     def spread(self, k):
         arrive(self.second[k])
         at, core, x, y = self.order[k], self.place.core, self.place.x, self.place.y
         add_blocks(
-            2, lambda j: (self.grad.at[at, 2 * j + x, core, self.low], self.bufs[1].at[k, j])
+            2, lambda j: (self.grad.at[(at, 2 * j + x, core, *self.low)], self.bufs[1].at[k, j])
         )
         add_blocks(
-            2, lambda j: (self.grad.at[at, 2 * y + j, core, self.high], self.bufs[2].at[k, j])
+            2, lambda j: (self.grad.at[(at, 2 * y + j, core, *self.high)], self.bufs[2].at[k, j])
         )
         go(self.third[k])
 
     def send(self, k):
         arrive(self.third[k])
         at, core, chip = self.order[k], self.place.core, self.place.chip
-        add_into(self.grad.at[at, chip, core, self.low], self.bufs[3].at[k])
-        add_into(self.grad.at[at, chip, core, self.high], self.bufs[4].at[k])
+        add_into(self.grad.at[(at, chip, core, *self.low)], self.bufs[3].at[k])
+        add_into(self.grad.at[(at, chip, core, *self.high)], self.bufs[4].at[k])
         go(self.fourth[k : k + 1])
 
+    def own_spread(self):
+        arrive(self.early)
+        z, core = self.place.z, self.place.core
+
+        def body(i, _):
+            target = self.grad.at[(z, i, core, *self.all_rest)]
+            total = target[...].astype(f32)
+            for k in range(3):
+                total = total + self.bufs[6][k, i].astype(f32)
+            target[...] = total.astype(bf16)
+            return 0
+
+        lax.fori_loop(0, 4, body, 0)
+        go(self.own_second)
+
+    def own_send(self):
+        arrive(self.own_second)
+        z, core, x, y = self.place.z, self.place.core, self.place.x, self.place.y
+        for j in range(2):
+            add_into(self.grad.at[(z, 2 * j + x, core, *self.low_rest)], self.bufs[7].at[j])
+            add_into(self.grad.at[(z, 2 * y + j, core, *self.high_rest)], self.bufs[8].at[j])
+        go(self.own_third)
+
     def finish(self):
-        arrive(self.fourth)
+        arrive(self.fourth + self.own_third)
         place = self.place
-        total = self.grad[place.z, place.chip, place.core].astype(f32)
+        at = (place.z, place.chip, place.core)
+        total = self.grad[(*at, *self.all)].astype(f32)
         for k in range(3):
             total = total + self.bufs[5][k].astype(f32)
-        self.out[...] = total
-
-
-def reduce_lines_scratch(rows, columns):
+        cut = total.shape[1]
+        half = total.shape[0] // 2
+        self.out[:, :cut] = total
+        self.out[:half, cut:] = self.grad[(*at, *self.low_rest)].astype(f32) + self.bufs[9][
+            ...
+        ].astype(f32)
+        self.out[half:, cut:] = self.grad[(*at, *self.high_rest)].astype(f32) + self.bufs[10][
+            ...
+        ].astype(f32)
+
+
+def reduce_lines_scratch(rows, columns, rest):
     half = rows // 2
+    most = columns - rest
     return [
         pltpu.VMEM((4, 4, rows, columns), bf16),
-        pltpu.VMEM((4, 2, half, columns), bf16),
-        pltpu.VMEM((4, 2, half, columns), bf16),
-        pltpu.VMEM((4, half, columns), bf16),
-        pltpu.VMEM((4, half, columns), bf16),
-        pltpu.VMEM((3, rows, columns), bf16),
+        pltpu.VMEM((4, 2, half, most), bf16),
+        pltpu.VMEM((4, 2, half, most), bf16),
+        pltpu.VMEM((4, half, most), bf16),
+        pltpu.VMEM((4, half, most), bf16),
+        pltpu.VMEM((3, rows, most), bf16),
+        pltpu.VMEM((3, 4, rows, rest), bf16),
+        pltpu.VMEM((2, half, rest), bf16),
+        pltpu.VMEM((2, half, rest), bf16),
+        pltpu.VMEM((half, rest), bf16),
+        pltpu.VMEM((half, rest), bf16),
     ]
 
 
@@ -899,6 +974,11 @@
         ),
         **options,
     )
+
+
+def row_of(packed, n, size):
+    found = [packed[k, n, r : r + 1, :] for k in range(4) for r in range(size // 512)]
+    return jnp.concatenate(found, axis=1)
 
 
 def columns_of(rank, features):
@@ -918,6 +998,7 @@
     copies = Copies(*refs[5:])
     place = Place()
     z, s, lines, plane = place.z, place.s, place.lines, place.plane
+    attention.head = s * heads
     gather = Gather(place, weights, [joined, *wholes], [None, *kept], chunks, copies)
     first = [t for t, chunk in enumerate(chunks) if chunk[0] == 0]
     later = [t for t, chunk in enumerate(chunks) if chunk[0] > 0]
@@ -973,11 +1054,7 @@
         gather.start(t)
     values_of[...] = small[...].astype(f32)
 
-    def row_of(n):
-        found = [values_of[k, n, r : r + 1, :] for k in range(4) for r in range(wide // 512)]
-        return jnp.concatenate(found, axis=1)
-
-    gain, shift = row_of(0), row_of(1)
+    gain, shift = row_of(values_of, 0, wide), row_of(values_of, 1, wide)
 
     def norm(i, _):
         values = held[i // parts, i % parts].astype(f32)
@@ -1103,19 +1180,18 @@
         whole.reshape(4 * item.shape[0], item.shape[1])
         for whole, item in zip((out[2], *out[9:]), weights)
     ]
-    found = [out[1][:, n, : item.shape[0]].reshape(-1) for n, item in enumerate(vectors)]
-    return out[0], found, [*wholes, out[8]], out[3], out[4], (out[5], out[6]), out[7]
+    return out[0], out[1], [*wholes, out[8]], out[3], out[4], (out[5], out[6]), out[7]
 
 
 def feed_forward_kernel(
     chunks, expand, contract, contract_line, out_weight,
-    expand_bias, upstream, tokens, attended, out_bias, gain, shift, contract_bias,
+    small, upstream, tokens, attended,
     layer, residual_grad, attended_diff, expand_grad, out_grad, contract_grad,
-    bias_grad, gain_grad, shift_grad, out_bias_grad,
-    expand_in, contract_in, residual, second, second_t, expanded, activated, grad, staged, *refs,
+    bias_grad, gain_grad, shift_grad, out_bias_grad, contract_bias_grad,
+    values_of, expand_bias, expand_in, contract_in, residual, second, second_t, expanded, activated, grad, staged, *refs,
 ):
     second_back = residual_grad
-    bufs, refs = refs[:6], refs[6:]
+    bufs, refs = refs[:11], refs[11:]
     loaded, stored, refs = refs[0], refs[1], refs[2:]
     copies = Copies(*refs)
     place = Place()
@@ -1170,16 +1246,22 @@
     greet(place.near)
     for n in range(len(chunks)):
         gather.exchange(n)
+    values_of[...] = small[...].astype(f32)
+    out_bias, gain, shift, contract_bias = [
+        row_of(values_of, n, features) for n in (4, 5, 6, 7)
+    ]
+    expand_bias[...] = row_of(values_of, 8, steps * wide)
     for n, half in enumerate(halves):
         out_loads[n].wait()
+        bias = out_bias[:, n * wide : (n + 1) * wide]
         residual[:, half] = (
-            tokens[:, half].astype(f32) + (matmul(attended[...], staged[n]) + out_bias[:, half])
+            tokens[:, half].astype(f32) + (matmul(attended[...], staged[n]) + bias)
         )
 
     def norm(i, _):
         values = residual[rows_at(i), :]
-        second[rows_at(i), :] = normalize(values, gain[...], shift[...]).astype(bf16)
-        second_back[rows_at(i), :] = values + contract_bias[...]
+        second[rows_at(i), :] = normalize(values, gain, shift).astype(bf16)
+        second_back[rows_at(i), :] = values + contract_bias
         return 0
 
     lax.fori_loop(0, 8, norm, 0)
@@ -1238,10 +1320,10 @@
     backward_steps = {
         1: [(reduce.spread, 2)],
         2: [(reduce.spread, 3)],
-        3: [(reduce.send, 0)],
+        3: [(reduce.send, 0), (reduce.own_spread,)],
         4: [(reduce.send, 1)],
         5: [(reduce.send, 2)],
-        6: [(reduce.send, 3)],
+        6: [(reduce.send, 3), (reduce.own_send,)],
     }
     lax.fori_loop(0, steps, lambda n, _: forward(n, forward_steps), 0)
     gather.share(last)
@@ -1259,19 +1341,20 @@
 
     def norm_back(i, sums):
         back = second_back[rows_at(i), :]
-        part, normal = normalize_back(residual[rows_at(i), :], back, gain[...])
-        total = upstream[rows_at(i), :].astype(f32) + part
+        part, normal = normalize_back(residual[rows_at(i), :], back, gain)
+        given = upstream[rows_at(i), :].astype(f32)
+        total = given + part
         low = total.astype(bf16)
         residual_grad[rows_at(i), :] = total
         second[rows_at(i), :] = low
-        found = (back * normal, back, low.astype(f32))
+        found = (back * normal, back, low.astype(f32), given)
         return tuple(
             kept + jnp.sum(item, axis=0, keepdims=True) for kept, item in zip(sums, found)
         )
 
     nothing = jnp.zeros((1, features), f32)
-    sums = lax.fori_loop(0, 8, norm_back, (nothing, nothing, nothing))
-    gain_grad[...], shift_grad[...], out_bias_grad[...] = sums
+    sums = lax.fori_loop(0, 8, norm_back, (nothing,) * 4)
+    gain_grad[...], shift_grad[...], out_bias_grad[...], contract_bias_grad[...] = sums
     done(out_loads)
     branch_diff = second
     made = matmul_rt(branch_diff[:, halves[0]], staged[0])
@@ -1285,7 +1368,7 @@
     copies.finish()
 
 
-def feed_forward(shape, expand, contract, line, out_weight, tokens, upstream, attended, vectors):
+def feed_forward(shape, expand, contract, line, out_weight, tokens, upstream, attended, small):
     own, parts, piece = shape
     rows, features = tokens.shape
     hidden = expand.shape[1]
@@ -1293,7 +1376,6 @@
     each = hidden // 32
     contract = split_weight(contract)
     chunks = chunks_of(0, *contract.shape[1:], 2)
-    out_bias, gain, shift, expand_bias, contract_bias = [item.reshape(1, -1) for item in vectors]
     seq_shape = (own, parts, piece, features)
     return remote_call(
         functools.partial(feed_forward_kernel, chunks),
@@ -1307,11 +1389,13 @@
             jax.ShapeDtypeStruct((features, features), bf16),
             jax.ShapeDtypeStruct((each, features), f32),
             jax.ShapeDtypeStruct((1, hidden), f32),
-            *[jax.ShapeDtypeStruct((1, features), f32)] * 3,
+            *[jax.ShapeDtypeStruct((1, features), f32)] * 4,
         ),
-        in_specs=[HBM] * 4 + [VMEM] * 8,
-        out_specs=(VMEM, VMEM, VMEM, HBM, HBM) + (VMEM,) * 5,
+        in_specs=[HBM] * 4 + [VMEM] * 4,
+        out_specs=(VMEM, VMEM, VMEM, HBM, HBM) + (VMEM,) * 6,
         scratch_shapes=[
+            pltpu.VMEM(small.shape, f32),
+            pltpu.VMEM((1, hidden), f32),
             pltpu.VMEM((features, hidden), bf16),
             pltpu.VMEM((4, *contract.shape), bf16),
             pltpu.VMEM((rows, features), f32),
@@ -1321,7 +1405,7 @@
             pltpu.VMEM((rows, hidden), bf16),
             pltpu.VMEM((4, 4, 2, each, features), bf16),
             pltpu.VMEM((2, features, wide), bf16),
-            *reduce_lines_scratch(each, features),
+            *reduce_lines_scratch(each, features, features // 4),
             pltpu.SemaphoreType.DMA((8,)),
             pltpu.SemaphoreType.DMA((2,)),
             *semaphores(
@@ -1329,10 +1413,7 @@
                 1 + 3 * len(chunks),
             ),
         ],
-    )(
-        expand, contract, line, out_weight,
-        expand_bias, upstream, tokens, attended, out_bias, gain, shift, contract_bias,
-    )
+    )(expand, contract, line, out_weight, small, upstream, tokens, attended)
 
 
 def backward_fused_kernel(heads, width, count, chunks, *refs):
@@ -1346,6 +1427,7 @@
     copies = Copies(*refs[3:])
     place = Place()
     s, plane = place.s, place.plane
+    attention.head = s * heads
     features = heads * width
     along = ReduceAlong(place, grads[0], outs[0], bufs[:7], chunks[0], copies)
     reduce = Reduce(place, grads, outs, bufs[7:], chunks[1:], copies)
@@ -1433,10 +1515,11 @@
 
 
 def end_kernel(
-    width, joined_diff, joined_weight, tokens, residual_grad, gain, shift, out_bias_grad,
+    width, joined_diff, joined_weight, tokens, residual_grad, small, out_bias_grad,
     second_gain_grad, second_shift_grad, contract_bias_grad, expand_bias_grad,
     input_out, vector_out, out,
-    diff_in, weight_in, normed, normed_t, back, grads, held, vectors, others, ranks, *refs,
+    values_of, diff_in, weight_in, normed, normed_t, back, grads, held, vectors, others, ranks,
+    *refs,
 ):
     count = grads.shape[0]
     bufs, refs = refs[: 7 * count], refs[7 * count :]
@@ -1463,6 +1546,8 @@
 
     for load in loads:
         go(load)
+    values_of[...] = small[...].astype(f32)
+    gain, shift = row_of(values_of, 0, features), row_of(values_of, 1, features)
     greet(lines + plane)
     for n, where in enumerate(columns):
         done(loads[n])
@@ -1472,8 +1557,8 @@
     def norm_back(i, sums):
         at = pl.ds(pl.multiple_of(i * piece, piece), piece)
         values, given = tokens[at, :].astype(f32), back[at, :]
-        part, normal = normalize_back(values, given, gain[...])
-        normed[at, :] = (normal * gain[...] + shift[...]).astype(bf16)
+        part, normal = normalize_back(values, given, gain)
+        normed[at, :] = (normal * gain + shift).astype(bf16)
         total = (residual_grad[at, :] + part).astype(bf16)
         held[i // parts, i % parts] = total
         found = (given * normal, given)
@@ -1539,13 +1624,12 @@
     stay.wait()
 
 
-def end(shape, joined_diff, joined_weight, tokens, residual_grad, gain, shift, vectors, width):
+def end(shape, joined_diff, joined_weight, tokens, residual_grad, small, vectors, width):
     own, parts, piece = shape
     rows, features = tokens.shape
     count = joined_diff.shape[1] // features
     each = features // 32
-    vectors = [item.reshape(1, -1) for item in (gain, shift, *vectors)]
-    tall = (4 * features + sum(item.shape[1] for item in vectors[2:])) // 512
+    tall = (4 * features + sum(item.shape[1] for item in vectors)) // 512
     chunks = [(n, 0, each, 0, features) for n in range(count)]
     out = remote_call(
         functools.partial(end_kernel, width),
@@ -1556,9 +1640,10 @@
             jax.ShapeDtypeStruct((tall, 128), f32),
             jax.ShapeDtypeStruct((each, count * features), f32),
         ),
-        in_specs=[HBM, HBM] + [VMEM] * (2 + len(vectors)),
+        in_specs=[HBM, HBM] + [VMEM] * (3 + len(vectors)),
         out_specs=(HBM, VMEM, VMEM),
         scratch_shapes=[
+            pltpu.VMEM(small.shape, f32),
             pltpu.VMEM((rows, count * features), bf16),
             pltpu.VMEM((features, count * features), bf16),
             pltpu.VMEM((rows, features), bf16),
@@ -1573,17 +1658,51 @@
             pltpu.SemaphoreType.DMA((2, count)),
             *semaphores(3 + 3 + 7 + count * Reduce.copies_each, 1 + count),
         ],
-    )(joined_diff, joined_weight, tokens, residual_grad, *vectors)
-    each = features // 32
-    split = 8 * features // 512
-    place = lax.axis_index("sp")
-    short = out[1][:split].reshape(8, features // 4)
-    short = lax.dynamic_slice_in_dim(short, place * each, each, 1)
-    long = out[1][split:].reshape(-1)
-    size = long.shape[0] // 8
-    long = lax.dynamic_slice_in_dim(long, place * size, size)
-    own_grads = [short[n] for n in range(8)] + [long]
-    return out[0].reshape(parts * own, piece, features), own_grads, out[2]
+    )(joined_diff, joined_weight, tokens, residual_grad, small, *vectors)
+    return out[0].reshape(parts * own, piece, features), out[1], out[2]
+
+
+def hand_out_kernel(sizes, vector, *refs):
+    count = (len(refs) - len(sizes) - 1) // 3
+    arrays, outs, smalls = refs[:count], refs[count : 2 * count], refs[2 * count :]
+    smalls, kept, sems = smalls[: len(sizes)], smalls[len(sizes) : -1], refs[-1]
+    s = lax.axis_index("sp")
+    loads = [pltpu.make_async_copy(a, k, sems.at[n]) for n, (a, k) in enumerate(zip(arrays, kept))]
+    stores = [
+        pltpu.make_async_copy(k, o, sems.at[count + n]) for n, (k, o) in enumerate(zip(kept, outs))
+    ]
+    go(loads)
+    row = 0
+    for out, size in zip(smalls, sizes):
+        per = 128 // size
+        found = vector[pl.ds(row + s // per, 1), :]
+        if per > 1:
+            found = pltpu.roll(found, lax.rem(128 - s % per * size, 128), 1)
+        out[...] = found[:, :size]
+        row += 8 // per
+    for load, store in zip(loads, stores):
+        load.wait()
+        store.start()
+    done(stores)
+
+
+def hand_out(vector, sizes, arrays):
+    out = pl.pallas_call(
+        functools.partial(hand_out_kernel, sizes),
+        name="hand_out",
+        out_shape=(
+            *[jax.ShapeDtypeStruct(item.shape, item.dtype) for item in arrays],
+            *[jax.ShapeDtypeStruct((1, size), f32) for size in sizes],
+        ),
+        in_specs=[VMEM] + [HBM] * len(arrays),
+        out_specs=(HBM,) * len(arrays) + (VMEM,) * len(sizes),
+        scratch_shapes=[
+            *[pltpu.VMEM(item.shape, item.dtype) for item in arrays],
+            pltpu.SemaphoreType.DMA((2 * len(arrays),)),
+        ],
+        compiler_params=pltpu.CompilerParams(vmem_limit_bytes=vmem_bytes),
+    )(vector, *arrays)
+    return out[: len(arrays)], [item.reshape(-1) for item in out[len(arrays) :]]
 
 
 def per_device(
@@ -1613,7 +1732,6 @@
     rows = seqs * piece
     own = seqs // fs_count
     shape = (own, fs_count, piece)
-    slopes = lax.dynamic_slice_in_dim(alibi_slopes, lax.axis_index("sp") * heads, heads)
 
     vectors = (
         first_gain, first_shift, query_bias, value_bias, output_bias,
@@ -1621,139 +1739,113 @@
     )
     fast = (fs_count, sp_count) == (4, 8) and (own, heads, width) == (2, 2, 64)
     fast = fast and expand_weight.shape[1] == 4 * features
-    weights = (joined_weight, output_weight, expand_weight)
-    gather = lambda item: lax.all_gather(item, "fs", axis=0, tiled=True)
     if fast:
-        tokens, whole, weights, qkv, attended, saved, upstream_low = forward_fused(
-            layer_input, upstream, vectors, weights, contract_weight, slopes, heads, width
-        )
-    else:
-        tokens, upstream_low = to_own_seqs(layer_input), to_own_seqs(upstream)
-        whole = [gather(item) for item in vectors]
-        weights = [gather(item) for item in (*weights, contract_weight)]
-    joined_full, out_full, expand_full, contract_full = weights
-    tokens_low = tokens.reshape(rows, features)
-    tokens = tokens_low.astype(f32)
-    gain_one, shift_one, qbias, vbias, obias, gain_two, shift_two, cbias, ebias = [
-        item.astype(f32) for item in whole
-    ]
-
-    normed_f, norm_back_one = jax.vjp(normalize, tokens, gain_one, shift_one)
-    normed = normed_f.astype(bf16)
-    if not fast:
-        joined_bias = joined_bias_of(qbias, vbias, head_count)
-        joined_all = (matmul(normed, joined_full) + joined_bias).astype(bf16)
-        qkv = to_heads(joined_all.reshape(*shape, 3 * features))
-        attended, *saved = attention_forward(qkv, slopes, heads, width)
-        attended = from_heads(attended)
-    attended = attended.reshape(rows, features)
-    upstream_low = upstream_low.reshape(rows, features)
-
-    upstream_f = upstream_low.astype(f32)
-    contract_bias_grad = jnp.sum(upstream_f, axis=0)
-    if fast:
+        weights = (joined_weight, output_weight, expand_weight)
+        tokens, small, weights, qkv, attended, saved, upstream_low = forward_fused(
+            layer_input, upstream, vectors, weights, contract_weight, alibi_slopes, heads, width
+        )
+        joined_full, out_full, expand_full, contract_line = weights
+        tokens = tokens.reshape(rows, features)
         (
             layer_output, residual_grad, attended_diff, expand_grad, output_weight_grad,
-            contract_grad, *small,
+            contract_grad, eb, g2, s2, ob, cb,
         ) = feed_forward(
-            shape, expand_full, contract_weight, contract_full, out_full, tokens_low, upstream_low,
-            attended, (obias, gain_two, shift_two, ebias, cbias),
-        )
-        expand_bias_grad, second_gain_grad, second_shift_grad, output_bias_grad = [
-            item.reshape(-1) for item in small
-        ]
-    else:
-        residual = tokens + (matmul(attended, out_full) + obias)
-        second_f, norm_back_two = jax.vjp(normalize, residual, gain_two, shift_two)
-        second = second_f.astype(bf16)
-        expanded = matmul(second, expand_full) + ebias
-        activated_f, gelu_back = jax.vjp(gelu_tanh, expanded)
-        activated = activated_f.astype(bf16)
-        result = residual + (matmul(activated, contract_full) + cbias)
-        layer_output = result.astype(bf16).reshape(*shape, features)
-
-        contract_grad = matmul_lt(activated, upstream_low)
-        act_grad = matmul_rt(upstream_low, contract_full)
-        expand_diff = gelu_back(act_grad)[0].astype(bf16)
-        expand_grad = matmul_lt(second, expand_diff)
-        expand_bias_grad = jnp.sum(expand_diff.astype(f32), axis=0)
-        second_back = matmul_rt(expand_diff, expand_full)
-        resid_part, second_gain_grad, second_shift_grad = norm_back_two(second_back)
-        residual_grad = upstream_f + resid_part
-
-        branch_diff = residual_grad.astype(bf16)
-        output_weight_grad = matmul_lt(attended, branch_diff)
-        output_bias_grad = jnp.sum(branch_diff.astype(f32), axis=0)
-        attended_diff = matmul_rt(branch_diff, out_full).astype(bf16)
-        attended_diff = attended_diff.reshape(*shape, features)
-    grads = (expand_grad, output_weight_grad)
+            shape, expand_full, contract_weight, contract_line, out_full, tokens,
+            upstream_low.reshape(rows, features), attended.reshape(rows, features), small,
+        )
+        joined_diff, layer_output, grads = backward_fused(
+            attended_diff, qkv, saved, layer_output, (expand_grad, output_weight_grad),
+            alibi_slopes, heads, width,
+        )
+        input_grad, vector, joined_grad = end(
+            shape, joined_diff.reshape(rows, 3 * features), joined_full, tokens, residual_grad,
+            small, (ob, g2, s2, cb, eb), width,
+        )
+        devices = fs_count * sp_count
+        sizes = [4 * item.shape[0] // devices for item in vectors]
+        arrays, (g1, s1, qb, vb, ob, g2, s2, cb, eb) = hand_out(
+            vector, sizes, (layer_output, input_grad, joined_grad, grads[1], grads[0], contract_grad)
+        )
+        layer_output, input_grad, joined_grad, output_grad, expand_grad, contract_grad = arrays
+        return (
+            layer_output, input_grad, g1, s1, joined_grad, qb, vb, output_grad, ob, g2, s2,
+            expand_grad, eb, contract_grad, cb,
+        )
+
+    slopes = lax.dynamic_slice_in_dim(alibi_slopes, lax.axis_index("sp") * heads, heads)
+    gather = lambda item: lax.all_gather(item, "fs", axis=0, tiled=True)
     scatter = functools.partial(
         lax.psum_scatter, axis_name=("fs", "sp"), scatter_dimension=0, tiled=True
     )
-    if fast:
-        joined_diff, layer_output, grads = backward_fused(
-            attended_diff, qkv, saved, layer_output, [item.astype(bf16) for item in grads],
-            slopes, heads, width,
-        )
-    else:
-        joined_diff = attention_backward(
-            qkv, to_heads(attended_diff), *saved, slopes, heads, width
-        )
-        joined_diff, layer_output = from_heads(joined_diff), from_own_seqs(layer_output)
-        grads = [scatter(item) for item in grads]
-        contract_grad = scatter(contract_grad)
-    expand_grad, output_weight_grad = grads
-    joined_diff = joined_diff.reshape(rows, 3 * features)
-
-    if fast:
-        input_grad, own_grads, joined_grad = end(
-            shape, joined_diff, joined_full, tokens_low, residual_grad, gain_one, shift_one,
-            (
-                output_bias_grad, second_gain_grad, second_shift_grad, contract_bias_grad,
-                expand_bias_grad,
-            ),
-            width,
-        )
-    else:
-        joined_grad = matmul_lt(normed, joined_diff)
-        column_sums = jnp.sum(joined_diff.astype(f32), axis=0).reshape(head_count, 3, width)
-        query_bias_grad = column_sums[:, 0].reshape(features)
-        value_bias_grad = column_sums[:, 2].reshape(features)
-        normed_back = matmul_rt(joined_diff, joined_full)
-        input_part, first_gain_grad, first_shift_grad = norm_back_one(normed_back)
-        input_grad = (residual_grad + input_part).astype(bf16).reshape(*shape, features)
-
-        vector_grads = (
-            first_gain_grad, first_shift_grad, query_bias_grad, value_bias_grad,
-            output_bias_grad, second_gain_grad, second_shift_grad, contract_bias_grad,
-            expand_bias_grad,
-        )
-        devices = fs_count * sp_count
-        packed = jnp.concatenate([item.reshape(devices, -1) for item in vector_grads], axis=1)
-        input_grad, joined_grad = from_own_seqs(input_grad), scatter(joined_grad)
-        packed = scatter(packed.reshape(-1))
-        own_grads, at = [], 0
-        for item in vector_grads:
-            size = item.shape[0] // devices
-            own_grads.append(packed[at : at + size])
-            at += size
+    gain_one, shift_one, qbias, vbias, obias, gain_two, shift_two, cbias, ebias = [
+        gather(item).astype(f32) for item in vectors
+    ]
+    joined_full, out_full, expand_full, contract_full = [
+        gather(item) for item in (joined_weight, output_weight, expand_weight, contract_weight)
+    ]
+    tokens = to_own_seqs(layer_input).reshape(rows, features).astype(f32)
+    upstream_low = to_own_seqs(upstream).reshape(rows, features)
+
+    normed_f, norm_back_one = jax.vjp(normalize, tokens, gain_one, shift_one)
+    normed = normed_f.astype(bf16)
+    joined_bias = joined_bias_of(qbias, vbias, head_count)
+    joined_all = (matmul(normed, joined_full) + joined_bias).astype(bf16)
+    qkv = to_heads(joined_all.reshape(*shape, 3 * features))
+    attended, *saved = attention_forward(qkv, slopes, heads, width)
+    attended = from_heads(attended).reshape(rows, features)
+    upstream_f = upstream_low.astype(f32)
+    contract_bias_grad = jnp.sum(upstream_f, axis=0)
+    residual = tokens + (matmul(attended, out_full) + obias)
+    second_f, norm_back_two = jax.vjp(normalize, residual, gain_two, shift_two)
+    second = second_f.astype(bf16)
+    expanded = matmul(second, expand_full) + ebias
+    activated_f, gelu_back = jax.vjp(gelu_tanh, expanded)
+    activated = activated_f.astype(bf16)
+    result = residual + (matmul(activated, contract_full) + cbias)
+    layer_output = result.astype(bf16).reshape(*shape, features)
+
+    contract_grad = matmul_lt(activated, upstream_low)
+    act_grad = matmul_rt(upstream_low, contract_full)
+    expand_diff = gelu_back(act_grad)[0].astype(bf16)
+    expand_grad = matmul_lt(second, expand_diff)
+    expand_bias_grad = jnp.sum(expand_diff.astype(f32), axis=0)
+    second_back = matmul_rt(expand_diff, expand_full)
+    resid_part, second_gain_grad, second_shift_grad = norm_back_two(second_back)
+    residual_grad = upstream_f + resid_part
+
+    branch_diff = residual_grad.astype(bf16)
+    output_weight_grad = matmul_lt(attended, branch_diff)
+    output_bias_grad = jnp.sum(branch_diff.astype(f32), axis=0)
+    attended_diff = matmul_rt(branch_diff, out_full).astype(bf16)
+    attended_diff = attended_diff.reshape(*shape, features)
+    joined_diff = attention_backward(qkv, to_heads(attended_diff), *saved, slopes, heads, width)
+    joined_diff = from_heads(joined_diff).reshape(rows, 3 * features)
+    joined_grad = matmul_lt(normed, joined_diff)
+    column_sums = jnp.sum(joined_diff.astype(f32), axis=0).reshape(head_count, 3, width)
+    query_bias_grad = column_sums[:, 0].reshape(features)
+    value_bias_grad = column_sums[:, 2].reshape(features)
+    normed_back = matmul_rt(joined_diff, joined_full)
+    input_part, first_gain_grad, first_shift_grad = norm_back_one(normed_back)
+    input_grad = (residual_grad + input_part).astype(bf16).reshape(*shape, features)
+
+    vector_grads = (
+        first_gain_grad, first_shift_grad, query_bias_grad, value_bias_grad,
+        output_bias_grad, second_gain_grad, second_shift_grad, contract_bias_grad,
+        expand_bias_grad,
+    )
+    devices = fs_count * sp_count
+    packed = jnp.concatenate([item.reshape(devices, -1) for item in vector_grads], axis=1)
+    packed = scatter(packed.reshape(-1))
+    own_grads, at = [], 0
+    for item in vector_grads:
+        size = item.shape[0] // devices
+        own_grads.append(packed[at : at + size])
+        at += size
     g1, s1, qb, vb, ob, g2, s2, cb, eb = own_grads
     return (
-        layer_output,
-        input_grad,
-        g1,
-        s1,
-        joined_grad,
-        qb,
-        vb,
-        output_weight_grad,
-        ob,
-        g2,
-        s2,
-        expand_grad,
-        eb,
-        contract_grad,
-        cb,
+        from_own_seqs(layer_output), from_own_seqs(input_grad), g1, s1, scatter(joined_grad), qb,
+        vb, scatter(output_weight_grad), ob, g2, s2, scatter(expand_grad), eb,
+        scatter(contract_grad), cb,
     )
 
 

time: 393 us -> 375 us (0.954)
  local copies, waits for them, and re-layouts: 10.2 us -> 0 us
  other arithmetic: 4.7 us -> 0 us
    unnamed x16 -> x0, local copies, waits for them, and re-layouts: 6.3 us -> none
    pallas_call x1, Pallas kernels: 85.7 us -> 80.2 us  [feed_forward(): remote_call(functools.partial(feed_forward_kernel, chunks), 'feed_forward...]
    pallas_call x0 -> x1, Pallas kernels: none -> 4.42 us  [hand_out(): pl.pallas_call(functools.partial(hand_out_kernel, sizes), name='hand_out'...]
where the time goes in v10:
time: 375 us
  Pallas kernels  374 us (100%)
    pallas_call x1, Pallas kernels, forward_fused(): remote_call(functools.partial(forward_fused_kernel, heads, width, count,...  143 us
    pallas_call x1, Pallas kernels, backward_fused(): remote_call(functools.partial(backward_fused_kernel, heads, width, count,...  89.5 us
    pallas_call x1, Pallas kernels, feed_forward(): remote_call(functools.partial(feed_forward_kernel, chunks), 'feed_forward...  80.2 us
    pallas_call x1, Pallas kernels, end(): remote_call(functools.partial(end_kernel, width), 'end', 3, out_shape=(ja...  56.7 us

profile of v10, /device:TPU:0, one launch (start us, length us, event | category | flops | bytes accessed | tf_op | source)
XLA Modules:
  0.0 374.6 jit_solution(2013309622498920859)
XLA Ops:
  0.7 142.9 %forward_fused.1 = (bf16[2,4,64,1024]{3,2,1,0:T(8,128)(2,1)}, bf16[4,9,8,128]{3,2,1,0:T(8,128)(2,1)}, bf16[4,8,32,3072]{3,2,1,0:T(8,128)(2,1)}, bf16[2,4,8,64,38...) custom-call(f32[16]{0:T(128)} %refs_0_.1, ...), custom_call_target="tpu_custom_call" | custom-call | tf_op jit(solution)/shard_map/forward_fused/pallas_call | solution.py:1137
  143.5 80.2 %feed_forward.1 = (bf16[2,4,64,1024]{3,2,1,0:T(8,128)(2,1)}, f32[512,1024]{1,0:T(8,128)}, bf16[2,4,64,1024]{3,2,1,0:T(8,128)(2,1)}, bf16[1024,4096]{1,0:T(8,128)...) custom-call(bf16[1024,4096]{1,0:T(8,128)(2,1)} %bitcast.36, ...), custom_call_target="tpu_custom_call" | custom-call | tf_op jit(solution)/shard_map/feed_forward/pallas_call | solution.py:1380
  223.7 89.5 %backward_fused.1 = (bf16[2,4,64,3072]{3,2,1,0:T(8,128)(2,1)}, bf16[4,2,64,1024]{3,2,1,0:T(8,128)(2,1)}, f32[32,4096]{1,0:T(8,128)}, f32[32,1024]{1,0:T(8,128)}) custom-call(f32[16]{0:T(128)} %refs_0_.1, bf16[2,4,64,1024]{3,2,1,0:T(8,128)(2,1)} %get-tuple-element.66.refs_1_, bf16[2,4,8,64,384]{4,3,2,1,0:T(8,128)(2,1)} %get-tuple-element.67.refs_2_, ...), custom_call_target="tpu_custom_call" | custom-call | tf_op jit(solution)/shard_map/backward_fused/pallas_call | solution.py:1490
  313.2 56.7 %end.1 = (bf16[4,2,64,1024]{3,2,1,0:T(8,128)(2,1)}, f32[24,128]{1,0:T(8,128)}, f32[32,3072]{1,0:T(8,128)}) custom-call(bf16[512,3072]{1,0:T(8,128)(2,1)} %bitcast.42, bf16[1024,3072]{1,0:T(8,128)(2,1)} %bitcast.39, bf16[512,1024]{1,0:T(8,128)(2,1)} %bitcast.41, f32[512,1024]{1,0:T(8,128)} %get-tuple-element.75.residual_grad, ...), custom_call_target="tpu_custom_call" | custom-call | tf_op jit(solution)/shard_map/end/pallas_call | solution.py:1634
  370.0 4.4 %hand_out.1 = (bf16[8,64,1024]{2,1,0:T(8,128)(2,1)}, bf16[8,64,1024]{2,1,0:T(8,128)(2,1)}, f32[32,3072]{1,0:T(8,128)}, f32[32,1024]{1,0:T(8,128)}, f32[32,4096]{...) custom-call(f32[24,128]{1,0:T(8,128)} %get-tuple-element.81.vector, ...), custom_call_target="tpu_custom_call" | custom-call | tf_op jit(solution)/shard_map/hand_out/pallas_call | solution.py:1690

commit v11 on v10

--- a/solution.py
+++ b/solution.py
@@ -390,20 +390,29 @@
 class Copies:
     def __init__(self, send, recv, local):
         self.send, self.recv, self.local = send, recv, local
-        self.used, self.used_local, self.made = 0, 0, []
-
-    def plan(self, source, target, device):
+        self.used, self.used_local, self.made, self.partial = 0, 0, [], []
+
+    def plan(self, source, target, device, at=None, only=None):
+        send, recv = (self.used, self.used) if at is None else at
         copy = pltpu.make_async_remote_copy(
             src_ref=source,
             dst_ref=target,
-            send_sem=self.send.at[self.used],
-            recv_sem=self.recv.at[self.used],
+            send_sem=self.send.at[send],
+            recv_sem=self.recv.at[recv],
             device_id=device,
             device_id_type=MESH,
         )
-        self.used += 1
-        self.made.append(copy)
+        if at is None:
+            self.used += 1
+        if only is None:
+            self.made.append(copy)
+        else:
+            self.partial.append((only, copy))
         return copy
+
+    def take(self, count):
+        self.used += count
+        return range(self.used - count, self.used)
 
     def inside(self, source, target):
         copy = pltpu.make_async_copy(source, target, self.local.at[self.used_local])
@@ -414,6 +423,8 @@
         assert (self.used, self.used_local) == (self.send.shape[0], self.local.shape[0])
         for copy in self.made:
             copy.wait_send()
+        for only, copy in self.partial:
+            pl.when(only)(copy.wait_send)
 
 
 def go(copies):
@@ -436,6 +447,10 @@
     for device in devices:
         pl.semaphore_signal(barrier, inc=1, device_id=device, device_id_type=MESH)
     pl.semaphore_wait(barrier, len(devices))
+
+
+def paired(z, mask):
+    return 2 * ((z // 2 + mask // 2) % 2) + (z + mask) % 2
 
 
 class Place:
@@ -449,20 +464,24 @@
         self.partner = s + 1 - 2 * self.core
         self.diagonal = self.along_x + self.along_y - s
         self.chip_x, self.chip_y = self.along_x // 2, self.along_y // 2
-        self.lines = [(lax.rem(z + k, 4), s) for k in range(1, 4)]
+        self.lines = [(paired(z, 3 - k), s) for k in range(3)]
         self.plane = [(z, lax.rem(s + d, 8)) for d in range(1, 8)]
         self.to_x, self.to_y, self.to_core = [
             (z, to) for to in (self.along_x, self.along_y, self.partner)
         ]
+        self.beside = z + 1 - 2 * (z % 2)
+        self.inner = ((z + 1) // 2) % 2
+        self.other_inner, self.other_outer = 2 - z // 2, 3 * (1 - z // 2)
         self.near = self.lines + [self.to_x, self.to_y, self.to_core]
 
 
 class Gather:
     copies_each = 33
 
-    def __init__(self, place, weights, wholes, kept, chunks, copies, given=None):
+    def __init__(self, place, weights, wholes, kept, chunks, copies, given=None, relayed=()):
         z, s, lines = place.z, place.s, place.lines
-        self.ready = arrive if given is None else done
+        self.is_given = given is not None
+        self.inner, self.passed = place.inner == 1, {}
         self.loads, self.own = [], []
         for weight, whole, keep in zip(weights, wholes, kept):
             if keep is None:
@@ -481,7 +500,30 @@
                 where = (k, rank, part, wide)
                 return copies.plan(whole.at[where], whole.at[where], to)
 
-            if given is None:
+            number = len(self.first)
+            if number in relayed:
+                near, middle, far, second = copies.take(4)
+                part = (s, every, wide)
+                beside = (place.beside, s)
+                first = [
+                    copies.plan(
+                        weights[t].at[part], whole.at[(z, *part)], beside, at=(near, near)
+                    ),
+                    copies.plan(
+                        weights[t].at[part],
+                        whole.at[(z, *part)],
+                        (place.other_inner, s),
+                        at=(second, middle + 1 - place.inner),
+                    ),
+                ]
+                self.passed[number] = [
+                    copies.plan(
+                        whole.at[(k, *part)], whole.at[(k, *part)], beside, at=(n, n),
+                        only=self.inner,
+                    )
+                    for k, n in ((place.other_inner, middle), (place.other_outer, far))
+                ]
+            elif given is None:
                 first = [
                     copies.plan(weights[t].at[s, every, wide], whole.at[z, s, every, wide], to)
                     for to in lines
@@ -516,7 +558,15 @@
         go(self.first[t])
 
     def exchange(self, t):
-        self.ready(self.first[t])
+        if t in self.passed:
+            arrive(self.first[t][:1])
+            for copy in self.passed[t]:
+                copy.wait_recv()
+                pl.when(self.inner)(copy.start)
+        elif self.is_given:
+            done(self.first[t])
+        else:
+            arrive(self.first[t])
         go(self.second[t])
         go(self.cores[t])
 
@@ -999,8 +1049,10 @@
     place = Place()
     z, s, lines, plane = place.z, place.s, place.lines, place.plane
     attention.head = s * heads
-    gather = Gather(place, weights, [joined, *wholes], [None, *kept], chunks, copies)
     first = [t for t, chunk in enumerate(chunks) if chunk[0] == 0]
+    gather = Gather(
+        place, weights, [joined, *wholes], [None, *kept], chunks, copies, relayed=first
+    )
     later = [t for t, chunk in enumerate(chunks) if chunk[0] > 0]
     features = heads * width
     back = HandBack(place, result, attended, features, *refs[2:5])
@@ -1095,14 +1147,14 @@
     gather.exchange(base + 1)
     own_copy.wait()
     gather.spread(base)
+    go(contracts)
     for d in range(7):
         to_head(d).wait_recv()
     keep_qkv.start()
     attention.run(
         {
-            0: [(gather.exchange, base + 2), (go, contracts), (gather.spread, base + 1)],
+            0: [(gather.exchange, base + 2), (go, upstreams), (gather.spread, base + 1)],
             2: [(gather.spread, base + 2), (gather.share, base)],
-            3: [(go, upstreams)],
             5: [(gather.share, base + 1)],
             6: [(gather.share, base + 2)],
         },
@@ -1166,7 +1218,7 @@
             pltpu.SemaphoreType.DMA((7,)),
             pltpu.SemaphoreType.DMA((7,)),
             *hand_back_semaphores(own * parts),
-            *semaphores(12 + len(chunks) * Gather.copies_each, 2 * count - 1 + 8),
+            *semaphores(12 + 3 + len(chunks) * Gather.copies_each, 2 * count - 1 + 8),
         ],
     )(
         slopes,
@@ -1205,7 +1257,7 @@
     wide = expand.shape[1] // steps
 
     def at(n):
-        part = (z + 1 + n // 2) % 4
+        part = paired(z, 3 - n // 2)
         return part, n % 2, pl.ds(pl.multiple_of((2 * part + n % 2) * wide, wide), wide)
 
     def load(n):

time: 375 us -> 367 us (0.979)
  Pallas kernels: 374 us -> 366 us
    pallas_call x1, Pallas kernels: 80.2 us -> 74.7 us  [feed_forward(): remote_call(functools.partial(feed_forward_kernel, chunks), 'feed_forward...]
where the time goes in v11:
time: 367 us
  Pallas kernels  366 us (100%)
    pallas_call x1, Pallas kernels, forward_fused(): remote_call(functools.partial(forward_fused_kernel, heads, width, count,...  143 us
    pallas_call x1, Pallas kernels, backward_fused(): remote_call(functools.partial(backward_fused_kernel, heads, width, count,...  88.2 us
    pallas_call x1, Pallas kernels, feed_forward(): remote_call(functools.partial(feed_forward_kernel, chunks), 'feed_forward...  74.7 us
    pallas_call x1, Pallas kernels, end(): remote_call(functools.partial(end_kernel, width), 'end', 3, out_shape=(ja...  55.6 us

profile of v11, /device:TPU:0, one launch (start us, length us, event | category | flops | bytes accessed | tf_op | source)
XLA Modules:
  0.0 366.6 jit_solution(12512655280213737977)
XLA Ops:
  0.7 142.8 %forward_fused.1 = (bf16[2,4,64,1024]{3,2,1,0:T(8,128)(2,1)}, bf16[4,9,8,128]{3,2,1,0:T(8,128)(2,1)}, bf16[4,8,32,3072]{3,2,1,0:T(8,128)(2,1)}, bf16[2,4,8,64,38...) custom-call(f32[16]{0:T(128)} %refs_0_.1, ...), custom_call_target="tpu_custom_call" | custom-call | tf_op jit(solution)/shard_map/forward_fused/pallas_call | solution.py:1189
  143.4 74.7 %feed_forward.1 = (bf16[2,4,64,1024]{3,2,1,0:T(8,128)(2,1)}, f32[512,1024]{1,0:T(8,128)}, bf16[2,4,64,1024]{3,2,1,0:T(8,128)(2,1)}, bf16[1024,4096]{1,0:T(8,128)...) custom-call(bf16[1024,4096]{1,0:T(8,128)(2,1)} %bitcast.36, ...), custom_call_target="tpu_custom_call" | custom-call | tf_op jit(solution)/shard_map/feed_forward/pallas_call | solution.py:1432
  218.2 88.2 %backward_fused.1 = (bf16[2,4,64,3072]{3,2,1,0:T(8,128)(2,1)}, bf16[4,2,64,1024]{3,2,1,0:T(8,128)(2,1)}, f32[32,4096]{1,0:T(8,128)}, f32[32,1024]{1,0:T(8,128)}) custom-call(f32[16]{0:T(128)} %refs_0_.1, bf16[2,4,64,1024]{3,2,1,0:T(8,128)(2,1)} %get-tuple-element.66.refs_1_, bf16[2,4,8,64,384]{4,3,2,1,0:T(8,128)(2,1)} %get-tuple-element.67.refs_2_, ...), custom_call_target="tpu_custom_call" | custom-call | tf_op jit(solution)/shard_map/backward_fused/pallas_call | solution.py:1542
  306.4 55.6 %end.1 = (bf16[4,2,64,1024]{3,2,1,0:T(8,128)(2,1)}, f32[24,128]{1,0:T(8,128)}, f32[32,3072]{1,0:T(8,128)}) custom-call(bf16[512,3072]{1,0:T(8,128)(2,1)} %bitcast.42, bf16[1024,3072]{1,0:T(8,128)(2,1)} %bitcast.39, bf16[512,1024]{1,0:T(8,128)(2,1)} %bitcast.41, f32[512,1024]{1,0:T(8,128)} %get-tuple-element.75.residual_grad, ...), custom_call_target="tpu_custom_call" | custom-call | tf_op jit(solution)/shard_map/end/pallas_call | solution.py:1686
  362.0 4.4 %hand_out.1 = (bf16[8,64,1024]{2,1,0:T(8,128)(2,1)}, bf16[8,64,1024]{2,1,0:T(8,128)(2,1)}, f32[32,3072]{1,0:T(8,128)}, f32[32,1024]{1,0:T(8,128)}, f32[32,4096]{...) custom-call(f32[24,128]{1,0:T(8,128)} %get-tuple-element.81.vector, ...), custom_call_target="tpu_custom_call" | custom-call | tf_op jit(solution)/shard_map/hand_out/pallas_call | solution.py:1742

commit v12 on v11

--- a/solution.py
+++ b/solution.py
@@ -557,12 +557,18 @@
     def start(self, t):
         go(self.first[t])
 
+    def pass_on(self, t):
+        def act():
+            for copy in self.passed[t]:
+                copy.wait_recv()
+                copy.start()
+
+        pl.when(self.inner)(act)
+
     def exchange(self, t):
         if t in self.passed:
             arrive(self.first[t][:1])
-            for copy in self.passed[t]:
-                copy.wait_recv()
-                pl.when(self.inner)(copy.start)
+            pl.when(jnp.logical_not(self.inner))(lambda: arrive(self.passed[t]))
         elif self.is_given:
             done(self.first[t])
         else:
@@ -1038,12 +1044,12 @@
 def forward_fused_kernel(heads, width, count, vector_count, chunks, slopes, tokens, upstream, *refs):
     vectors, refs = refs[:vector_count], refs[vector_count:]
     weights, contract, refs = refs[:count], refs[count], refs[count + 1 :]
-    tokens_out, vectors_out, joined_out, qkv_out, attended, out_t, lse, upstream_out = refs[:8]
+    tokens_out, vectors_out, joined_out, qkv_out, attended, *saved, upstream_out = refs[:8]
     contract_out = refs[8]
     wholes, refs = refs[9 : 8 + count], refs[8 + count :]
     held, small, values_of, joined, normed, outgoing, qkv, result, upstream_own = refs[:9]
-    attention = Forward(heads, width, slopes, qkv, result, out_t, lse, *refs[9:12])
-    kept, refs = refs[12 : 11 + count], refs[11 + count :]
+    attention = Forward(heads, width, slopes, qkv, result, *refs[9:14])
+    kept, refs = refs[14 : 13 + count], refs[13 + count :]
     head_send, head_recv = refs[:2]
     copies = Copies(*refs[5:])
     place = Place()
@@ -1070,6 +1076,7 @@
         copies.inside(joined, joined_out),
     ]
     keep_qkv = copies.inside(qkv, qkv_out)
+    keep_saved = [copies.inside(attention.out_t, saved[0]), copies.inside(attention.lse, saved[1])]
     contracts = [copies.plan(contract.at[s], contract_out.at[z], to) for to in lines]
 
     def to_head(d):
@@ -1089,6 +1096,8 @@
     greet(lines + plane)
     for t in first:
         gather.start(t)
+    for t in first:
+        gather.pass_on(t)
     go(seqs + vector_copies)
     gather.keep()
     load.wait()
@@ -1160,6 +1169,7 @@
         },
         back.each,
     )
+    go(keep_saved)
     for t in later:
         gather.complete(t)
     arrive(contracts + upstreams)
@@ -1167,7 +1177,7 @@
     for d in range(7):
         to_head(d).wait_send()
     copies.finish()
-    done(gather.own + [keep_upstream, keep_qkv] + keeping)
+    done(gather.own + [keep_upstream, keep_qkv] + keep_saved + keeping)
 
 
 def forward_fused(tokens, upstream, vectors, weights, contract, slopes, heads, width):
@@ -1202,7 +1212,7 @@
             *[jax.ShapeDtypeStruct((parts, *item.shape), bf16) for item in cut[1:]],
         ),
         in_specs=[SMEM, HBM, HBM] + [VMEM] * len(vectors) + [HBM] * (count + 1),
-        out_specs=(HBM,) * 5 + (VMEM, VMEM) + (HBM,) * (count + 1),
+        out_specs=(HBM,) * (8 + count),
         scratch_shapes=[
             pltpu.VMEM(seq_shape, bf16),
             pltpu.VMEM(small, bf16),
@@ -1213,12 +1223,13 @@
             pltpu.VMEM(qkv_shape, bf16),
             pltpu.VMEM((own, parts, 8, piece, columns), bf16),
             pltpu.VMEM((own, piece, features), bf16),
+            *[pltpu.VMEM(item.shape, f32) for item in saved_shapes(own, length, heads, width)],
             *forward_scratch(length, heads, width),
             *[pltpu.VMEM(item.shape, bf16) for item in cut[1:]],
             pltpu.SemaphoreType.DMA((7,)),
             pltpu.SemaphoreType.DMA((7,)),
             *hand_back_semaphores(own * parts),
-            *semaphores(12 + 3 + len(chunks) * Gather.copies_each, 2 * count - 1 + 8),
+            *semaphores(12 + 3 + len(chunks) * Gather.copies_each, 2 * count - 1 + 10),
         ],
     )(
         slopes,
@@ -1237,10 +1248,10 @@
 
 def feed_forward_kernel(
     chunks, expand, contract, contract_line, out_weight,
-    small, upstream, tokens, attended,
-    layer, residual_grad, attended_diff, expand_grad, out_grad, contract_grad,
+    small, upstream_in, tokens_in, attended_in,
+    layer_out, residual_out, diff_out, expand_grad, out_grad, contract_grad,
     bias_grad, gain_grad, shift_grad, out_bias_grad, contract_bias_grad,
-    values_of, expand_bias, expand_in, contract_in, residual, second, second_t, expanded, activated, grad, staged, *refs,
+    upstream, tokens, attended, layer, residual_grad, attended_diff, values_of, expand_bias, expand_in, contract_in, residual, second, second_t, expanded, activated, grad, staged, *refs,
 ):
     second_back = residual_grad
     bufs, refs = refs[:11], refs[11:]
@@ -1248,6 +1259,13 @@
     copies = Copies(*refs)
     place = Place()
     z = place.z
+    given = [
+        copies.inside(a, b)
+        for a, b in ((attended_in, attended), (tokens_in, tokens), (upstream_in, upstream))
+    ]
+    keep_layer = copies.inside(layer, layer_out)
+    keep_residual = copies.inside(residual_grad, residual_out)
+    keep_diff = copies.inside(attended_diff, diff_out)
     reduce = ReduceLines(place, grad, contract_grad, bufs, copies)
     gather = Gather(
         place, [contract], [contract_in], [None], chunks, copies, given=contract_line
@@ -1291,7 +1309,7 @@
 
     for n in range(len(chunks)):
         gather.start(n)
-    go(out_loads)
+    go(given[:2] + out_loads + given[2:])
     for n in range(steps):
         load(n).start()
     go(gather.loads)
@@ -1303,6 +1321,7 @@
         row_of(values_of, n, features) for n in (4, 5, 6, 7)
     ]
     expand_bias[...] = row_of(values_of, 8, steps * wide)
+    done(given)
     for n, half in enumerate(halves):
         out_loads[n].wait()
         bias = out_bias[:, n * wide : (n + 1) * wide]
@@ -1384,6 +1403,7 @@
     done(gather.loads)
     lax.fori_loop(0, steps, lambda n, _: shrink(n, shrink_steps), 0)
     layer[...] = second_back[...].astype(bf16).reshape(layer.shape)
+    keep_layer.start()
     second_back[...] = jnp.zeros_like(second_back)
     lax.fori_loop(0, steps, lambda n, _: backward(n, backward_steps), 0)
     store(steps - 2).wait()
@@ -1407,16 +1427,18 @@
     nothing = jnp.zeros((1, features), f32)
     sums = lax.fori_loop(0, 8, norm_back, (nothing,) * 4)
     gain_grad[...], shift_grad[...], out_bias_grad[...], contract_bias_grad[...] = sums
+    keep_residual.start()
     done(out_loads)
     branch_diff = second
     made = matmul_rt(branch_diff[:, halves[0]], staged[0])
     made = (made + matmul_rt(branch_diff[:, halves[1]], staged[1])).astype(bf16)
     attended_diff[...] = made.reshape(attended_diff.shape)
+    keep_diff.start()
     for n, half in enumerate(halves):
         staged[n] = matmul(second_t[...], branch_diff[:, half]).astype(bf16)
         out_stores[n].start()
     reduce.finish()
-    done(out_stores)
+    done(out_stores + [keep_layer, keep_residual, keep_diff])
     copies.finish()
 
 
@@ -1443,9 +1465,13 @@
             jax.ShapeDtypeStruct((1, hidden), f32),
             *[jax.ShapeDtypeStruct((1, features), f32)] * 4,
         ),
-        in_specs=[HBM] * 4 + [VMEM] * 4,
-        out_specs=(VMEM, VMEM, VMEM, HBM, HBM) + (VMEM,) * 6,
+        in_specs=[HBM] * 4 + [VMEM] + [HBM] * 3,
+        out_specs=(HBM,) * 5 + (VMEM,) * 6,
         scratch_shapes=[
+            *[pltpu.VMEM((rows, features), bf16)] * 3,
+            pltpu.VMEM(seq_shape, bf16),
+            pltpu.VMEM((rows, features), f32),
+            pltpu.VMEM(seq_shape, bf16),
             pltpu.VMEM(small.shape, f32),
             pltpu.VMEM((1, hidden), f32),
             pltpu.VMEM((features, hidden), bf16),
@@ -1462,7 +1488,7 @@
             pltpu.SemaphoreType.DMA((2,)),
             *semaphores(
                 ReduceLines.copies + len(chunks) * (Gather.copies_each - 3),
-                1 + 3 * len(chunks),
+                7 + 3 * len(chunks),
             ),
         ],
     )(expand, contract, line, out_weight, small, upstream, tokens, attended)
@@ -1532,11 +1558,11 @@
     cut = [split_grad(item) for item in grads]
     count = len(cut)
     rows, wide = cut[0].shape[3:]
-    part = 3 * wide // 8
+    early, part = 3 * wide // 8, 5 * wide // 16
     chunks = [
-        (0, 0, rows, 0, wide // 4),
-        (0, 0, rows, wide // 4, part),
-        (0, 0, rows, wide // 4 + part, part),
+        (0, 0, rows, 0, early),
+        (0, 0, rows, early, part),
+        (0, 0, rows, early + part, part),
         *chunks_of(1, *cut[1].shape[3:], 1),
     ]
     out = remote_call(
@@ -1567,11 +1593,11 @@
 
 
 def end_kernel(
-    width, joined_diff, joined_weight, tokens, residual_grad, small, out_bias_grad,
+    width, joined_diff, joined_weight, tokens_in, residual_in, small, out_bias_grad,
     second_gain_grad, second_shift_grad, contract_bias_grad, expand_bias_grad,
     input_out, vector_out, out,
-    values_of, diff_in, weight_in, normed, normed_t, back, grads, held, vectors, others, ranks,
-    *refs,
+    tokens, residual_grad, values_of, diff_in, weight_in, normed, normed_t, back, grads, held,
+    vectors, others, ranks, *refs,
 ):
     count = grads.shape[0]
     bufs, refs = refs[: 7 * count], refs[7 * count :]
@@ -1596,8 +1622,10 @@
     along = [copies.plan(vectors.at[to[0]], others.at[k], to) for k, to in enumerate(lines)]
     across = [copies.plan(ranks.at[0], ranks.at[d + 1], to) for d, to in enumerate(plane)]
 
+    given_loads = [copies.inside(tokens_in, tokens), copies.inside(residual_in, residual_grad)]
     for load in loads:
         go(load)
+    go(given_loads)
     values_of[...] = small[...].astype(f32)
     gain, shift = row_of(values_of, 0, features), row_of(values_of, 1, features)
     greet(lines + plane)
@@ -1618,6 +1646,7 @@
             kept + jnp.sum(item, axis=0, keepdims=True) for kept, item in zip(sums, found)
         )
 
+    done(given_loads)
     nothing = jnp.zeros((1, features), f32)
     gain_grad, shift_grad = lax.fori_loop(0, own_seqs * parts, norm_back, (nothing, nothing))
     go(returned + [stay])
@@ -1692,9 +1721,11 @@
             jax.ShapeDtypeStruct((tall, 128), f32),
             jax.ShapeDtypeStruct((each, count * features), f32),
         ),
-        in_specs=[HBM, HBM] + [VMEM] * (3 + len(vectors)),
+        in_specs=[HBM] * 4 + [VMEM] * (1 + len(vectors)),
         out_specs=(HBM, VMEM, VMEM),
         scratch_shapes=[
+            pltpu.VMEM((rows, features), bf16),
+            pltpu.VMEM((rows, features), f32),
             pltpu.VMEM(small.shape, f32),
             pltpu.VMEM((rows, count * features), bf16),
             pltpu.VMEM((features, count * features), bf16),
@@ -1708,7 +1739,7 @@
             pltpu.VMEM((8, tall, 128), f32),
             *reduce_scratch(chunks),
             pltpu.SemaphoreType.DMA((2, count)),
-            *semaphores(3 + 3 + 7 + count * Reduce.copies_each, 1 + count),
+            *semaphores(3 + 3 + 7 + count * Reduce.copies_each, 3 + count),
         ],
     )(joined_diff, joined_weight, tokens, residual_grad, small, *vectors)
     return out[0].reshape(parts * own, piece, features), out[1], out[2]

time: 367 us -> 357 us (0.973)
  Pallas kernels: 366 us -> 356 us
    pallas_call x1, Pallas kernels: 143 us -> 135 us  [forward_fused(): remote_call(functools.partial(forward_fused_kernel, heads, width, count,...]
where the time goes in v12:
time: 357 us
  Pallas kernels  356 us (100%)
    pallas_call x1, Pallas kernels, forward_fused(): remote_call(functools.partial(forward_fused_kernel, heads, width, count,...  135 us
    pallas_call x1, Pallas kernels, backward_fused(): remote_call(functools.partial(backward_fused_kernel, heads, width, count,...  89.4 us
    pallas_call x1, Pallas kernels, feed_forward(): remote_call(functools.partial(feed_forward_kernel, chunks), 'feed_forward...  72.2 us
    pallas_call x1, Pallas kernels, end(): remote_call(functools.partial(end_kernel, width), 'end', 3, out_shape=(ja...  55.1 us

profile of v12, /device:TPU:0, one launch (start us, length us, event | category | flops | bytes accessed | tf_op | source)
XLA Modules:
  0.0 357.2 jit_solution(1980511605870817794)
XLA Ops:
  0.7 135.3 %forward_fused.1 = (bf16[2,4,64,1024]{3,2,1,0:T(8,128)(2,1)}, bf16[4,9,8,128]{3,2,1,0:T(8,128)(2,1)}, bf16[4,8,32,3072]{3,2,1,0:T(8,128)(2,1)}, bf16[2,4,8,64,38...) custom-call(f32[16]{0:T(128)} %refs_0_.1, ...), custom_call_target="tpu_custom_call" | custom-call | tf_op jit(solution)/shard_map/forward_fused/pallas_call | solution.py:1199
  135.9 72.2 %feed_forward.1 = (bf16[2,4,64,1024]{3,2,1,0:T(8,128)(2,1)}, f32[512,1024]{1,0:T(8,128)}, bf16[2,4,64,1024]{3,2,1,0:T(8,128)(2,1)}, bf16[1024,4096]{1,0:T(8,128)...) custom-call(bf16[1024,4096]{1,0:T(8,128)(2,1)} %bitcast.36, ...), custom_call_target="tpu_custom_call" | custom-call | tf_op jit(solution)/shard_map/feed_forward/pallas_call | solution.py:1454
  208.1 89.4 %backward_fused.1 = (bf16[2,4,64,3072]{3,2,1,0:T(8,128)(2,1)}, bf16[4,2,64,1024]{3,2,1,0:T(8,128)(2,1)}, f32[32,4096]{1,0:T(8,128)}, f32[32,1024]{1,0:T(8,128)}) custom-call(f32[16]{0:T(128)} %refs_0_.1, bf16[2,4,64,1024]{3,2,1,0:T(8,128)(2,1)} %get-tuple-element.66.refs_1_, bf16[2,4,8,64,384]{4,3,2,1,0:T(8,128)(2,1)} %get-tuple-element.67.refs_2_, ...), custom_call_target="tpu_custom_call" | custom-call | tf_op jit(solution)/shard_map/backward_fused/pallas_call | solution.py:1568
  297.5 55.1 %end.1 = (bf16[4,2,64,1024]{3,2,1,0:T(8,128)(2,1)}, f32[24,128]{1,0:T(8,128)}, f32[32,3072]{1,0:T(8,128)}) custom-call(bf16[512,3072]{1,0:T(8,128)(2,1)} %bitcast.42, bf16[1024,3072]{1,0:T(8,128)(2,1)} %bitcast.39, bf16[512,1024]{1,0:T(8,128)(2,1)} %bitcast.41, f32[512,1024]{1,0:T(8,128)} %get-tuple-element.75.residual_in, ...), custom_call_target="tpu_custom_call" | custom-call | tf_op jit(solution)/shard_map/end/pallas_call | solution.py:1715
  352.6 4.4 %hand_out.1 = (bf16[8,64,1024]{2,1,0:T(8,128)(2,1)}, bf16[8,64,1024]{2,1,0:T(8,128)(2,1)}, f32[32,3072]{1,0:T(8,128)}, f32[32,1024]{1,0:T(8,128)}, f32[32,4096]{...) custom-call(f32[24,128]{1,0:T(8,128)} %get-tuple-element.81.vector, ...), custom_call_target="tpu_custom_call" | custom-call | tf_op jit(solution)/shard_map/hand_out/pallas_call | solution.py:1773

commit v13 on v12

--- a/solution.py
+++ b/solution.py
@@ -1353,8 +1353,9 @@
         return 0
 
     def shrink(n, after):
-        _, _, where = at(n)
-        second_back[...] += matmul(activated[:, where], contract_at(n))
+        where = pl.ds(pl.multiple_of(n * (features // 4), 128), features // 4)
+        weight = contract_in[:, :, :, where].reshape(steps * wide, features // 4)
+        second_back[:, where] += matmul(activated[...], weight)
         follow(n, after)
         return 0
 
@@ -1384,9 +1385,9 @@
         7: [(reduce.start, 3), (reduce.exchange, 2)] + [(gather.share, n) for n in range(last)],
     }
     shrink_steps = {
-        1: [(reduce.exchange, 3)],
-        3: [(reduce.spread, 0)],
-        7: [(reduce.spread, 1)],
+        0: [(reduce.exchange, 3)],
+        1: [(reduce.spread, 0)],
+        3: [(reduce.spread, 1)],
     }
     backward_steps = {
         1: [(reduce.spread, 2)],
@@ -1401,7 +1402,7 @@
     for n in range(len(chunks)):
         gather.complete(n)
     done(gather.loads)
-    lax.fori_loop(0, steps, lambda n, _: shrink(n, shrink_steps), 0)
+    lax.fori_loop(0, 4, lambda n, _: shrink(n, shrink_steps), 0)
     layer[...] = second_back[...].astype(bf16).reshape(layer.shape)
     keep_layer.start()
     second_back[...] = jnp.zeros_like(second_back)
@@ -1558,7 +1559,7 @@
     cut = [split_grad(item) for item in grads]
     count = len(cut)
     rows, wide = cut[0].shape[3:]
-    early, part = 3 * wide // 8, 5 * wide // 16
+    early, part = 5 * wide // 16, 11 * wide // 32
     chunks = [
         (0, 0, rows, 0, early),
         (0, 0, rows, early, part),

time: 357 us -> 354 us (level)
  no operation moved by 1% of the time
where the time goes in v13:
time: 354 us; the launch traced here: 353 us
  Pallas kernels  353 us (100%)
    pallas_call x1, Pallas kernels, forward_fused(): remote_call(functools.partial(forward_fused_kernel, heads, width, count,...  135 us
    pallas_call x1, Pallas kernels, backward_fused(): remote_call(functools.partial(backward_fused_kernel, heads, width, count,...  86.6 us
    pallas_call x1, Pallas kernels, feed_forward(): remote_call(functools.partial(feed_forward_kernel, chunks), 'feed_forward...  71.4 us
    pallas_call x1, Pallas kernels, end(): remote_call(functools.partial(end_kernel, width), 'end', 3, out_shape=(ja...  54.8 us

profile of v13, /device:TPU:0, one launch (start us, length us, event | category | flops | bytes accessed | tf_op | source)
XLA Modules:
  0.0 353.4 jit_solution(8683520321114644350)
XLA Ops:
  0.7 135.3 %forward_fused.1 = (bf16[2,4,64,1024]{3,2,1,0:T(8,128)(2,1)}, bf16[4,9,8,128]{3,2,1,0:T(8,128)(2,1)}, bf16[4,8,32,3072]{3,2,1,0:T(8,128)(2,1)}, bf16[2,4,8,64,38...) custom-call(f32[16]{0:T(128)} %refs_0_.1, ...), custom_call_target="tpu_custom_call" | custom-call | tf_op jit(solution)/shard_map/forward_fused/pallas_call | solution.py:1199
  135.9 71.4 %feed_forward.1 = (bf16[2,4,64,1024]{3,2,1,0:T(8,128)(2,1)}, f32[512,1024]{1,0:T(8,128)}, bf16[2,4,64,1024]{3,2,1,0:T(8,128)(2,1)}, bf16[1024,4096]{1,0:T(8,128)...) custom-call(bf16[1024,4096]{1,0:T(8,128)(2,1)} %bitcast.36, ...), custom_call_target="tpu_custom_call" | custom-call | tf_op jit(solution)/shard_map/feed_forward/pallas_call | solution.py:1455
  207.4 86.6 %backward_fused.1 = (bf16[2,4,64,3072]{3,2,1,0:T(8,128)(2,1)}, bf16[4,2,64,1024]{3,2,1,0:T(8,128)(2,1)}, f32[32,4096]{1,0:T(8,128)}, f32[32,1024]{1,0:T(8,128)}) custom-call(f32[16]{0:T(128)} %refs_0_.1, bf16[2,4,64,1024]{3,2,1,0:T(8,128)(2,1)} %get-tuple-element.66.refs_1_, bf16[2,4,8,64,384]{4,3,2,1,0:T(8,128)(2,1)} %get-tuple-element.67.refs_2_, ...), custom_call_target="tpu_custom_call" | custom-call | tf_op jit(solution)/shard_map/backward_fused/pallas_call | solution.py:1569
  294.0 54.8 %end.1 = (bf16[4,2,64,1024]{3,2,1,0:T(8,128)(2,1)}, f32[24,128]{1,0:T(8,128)}, f32[32,3072]{1,0:T(8,128)}) custom-call(bf16[512,3072]{1,0:T(8,128)(2,1)} %bitcast.42, bf16[1024,3072]{1,0:T(8,128)(2,1)} %bitcast.39, bf16[512,1024]{1,0:T(8,128)(2,1)} %bitcast.41, f32[512,1024]{1,0:T(8,128)} %get-tuple-element.75.residual_in, ...), custom_call_target="tpu_custom_call" | custom-call | tf_op jit(solution)/shard_map/end/pallas_call | solution.py:1716
  348.8 4.4 %hand_out.1 = (bf16[8,64,1024]{2,1,0:T(8,128)(2,1)}, bf16[8,64,1024]{2,1,0:T(8,128)(2,1)}, f32[32,3072]{1,0:T(8,128)}, f32[32,1024]{1,0:T(8,128)}, f32[32,4096]{...) custom-call(f32[24,128]{1,0:T(8,128)} %get-tuple-element.81.vector, ...), custom_call_target="tpu_custom_call" | custom-call | tf_op jit(solution)/shard_map/hand_out/pallas_call | solution.py:1774

commit v14 on v13

--- a/solution.py
+++ b/solution.py
@@ -1162,7 +1162,8 @@
     keep_qkv.start()
     attention.run(
         {
-            0: [(gather.exchange, base + 2), (go, upstreams), (gather.spread, base + 1)],
+            0: [(gather.exchange, base + 2), (gather.spread, base + 1)],
+            1: [(go, upstreams)],
             2: [(gather.spread, base + 2), (gather.share, base)],
             5: [(gather.share, base + 1)],
             6: [(gather.share, base + 2)],

time: 354 us -> 354 us (level)
  no operation moved by 1% of the time
where the time goes in v14:
time: 354 us; the launch traced here: 353 us
  Pallas kernels  353 us (100%)
    pallas_call x1, Pallas kernels, forward_fused(): remote_call(functools.partial(forward_fused_kernel, heads, width, count,...  135 us
    pallas_call x1, Pallas kernels, backward_fused(): remote_call(functools.partial(backward_fused_kernel, heads, width, count,...  86.6 us
    pallas_call x1, Pallas kernels, feed_forward(): remote_call(functools.partial(feed_forward_kernel, chunks), 'feed_forward...  71.4 us
    pallas_call x1, Pallas kernels, end(): remote_call(functools.partial(end_kernel, width), 'end', 3, out_shape=(ja...  54.8 us

profile of v14, /device:TPU:0, one launch (start us, length us, event | category | flops | bytes accessed | tf_op | source)
XLA Modules:
  0.0 353.4 jit_solution(9767994051311349222)
XLA Ops:
  0.7 135.3 %forward_fused.1 = (bf16[2,4,64,1024]{3,2,1,0:T(8,128)(2,1)}, bf16[4,9,8,128]{3,2,1,0:T(8,128)(2,1)}, bf16[4,8,32,3072]{3,2,1,0:T(8,128)(2,1)}, bf16[2,4,8,64,38...) custom-call(f32[16]{0:T(128)} %refs_0_.1, ...), custom_call_target="tpu_custom_call" | custom-call | tf_op jit(solution)/shard_map/forward_fused/pallas_call | solution.py:1200
  135.9 71.4 %feed_forward.1 = (bf16[2,4,64,1024]{3,2,1,0:T(8,128)(2,1)}, f32[512,1024]{1,0:T(8,128)}, bf16[2,4,64,1024]{3,2,1,0:T(8,128)(2,1)}, bf16[1024,4096]{1,0:T(8,128)...) custom-call(bf16[1024,4096]{1,0:T(8,128)(2,1)} %bitcast.36, ...), custom_call_target="tpu_custom_call" | custom-call | tf_op jit(solution)/shard_map/feed_forward/pallas_call | solution.py:1456
  207.4 86.6 %backward_fused.1 = (bf16[2,4,64,3072]{3,2,1,0:T(8,128)(2,1)}, bf16[4,2,64,1024]{3,2,1,0:T(8,128)(2,1)}, f32[32,4096]{1,0:T(8,128)}, f32[32,1024]{1,0:T(8,128)}) custom-call(f32[16]{0:T(128)} %refs_0_.1, bf16[2,4,64,1024]{3,2,1,0:T(8,128)(2,1)} %get-tuple-element.66.refs_1_, bf16[2,4,8,64,384]{4,3,2,1,0:T(8,128)(2,1)} %get-tuple-element.67.refs_2_, ...), custom_call_target="tpu_custom_call" | custom-call | tf_op jit(solution)/shard_map/backward_fused/pallas_call | solution.py:1570
  294.0 54.8 %end.1 = (bf16[4,2,64,1024]{3,2,1,0:T(8,128)(2,1)}, f32[24,128]{1,0:T(8,128)}, f32[32,3072]{1,0:T(8,128)}) custom-call(bf16[512,3072]{1,0:T(8,128)(2,1)} %bitcast.42, bf16[1024,3072]{1,0:T(8,128)(2,1)} %bitcast.39, bf16[512,1024]{1,0:T(8,128)(2,1)} %bitcast.41, f32[512,1024]{1,0:T(8,128)} %get-tuple-element.75.residual_in, ...), custom_call_target="tpu_custom_call" | custom-call | tf_op jit(solution)/shard_map/end/pallas_call | solution.py:1717
  348.8 4.4 %hand_out.1 = (bf16[8,64,1024]{2,1,0:T(8,128)(2,1)}, bf16[8,64,1024]{2,1,0:T(8,128)(2,1)}, f32[32,3072]{1,0:T(8,128)}, f32[32,1024]{1,0:T(8,128)}, f32[32,4096]{...) custom-call(f32[24,128]{1,0:T(8,128)} %get-tuple-element.81.vector, ...), custom_call_target="tpu_custom_call" | custom-call | tf_op jit(solution)/shard_map/hand_out/pallas_call | solution.py:1775
